TPU v7x, 32 devices: a whole 2x2x4 slice. The times are simulated.
32 devices in a mesh: group: 4 (over z), member: 8 (over y, x, core).
Axes of the slice: x: 2, y: 2, z: 4, core: 2. Of those that a mesh axis runs over, the one named last changes fastest.
Arguments:
- patterns: float32 [32, 2, 256, 512], P('group', None, 'member'), may hold values from -6 to 6
- operators: float32 [100, 2, 256, 512], P(None, None, 'member'), may hold values from -1 to 1
- partners: int32 [32, 8], P('group'), may hold values from 0 to 31, as said below
- operator_index: int32 [32, 8], P('group'), may hold values from 0 to 99
- child_parent: int32 [64], P('group'), may hold values from 0 to 31, as said below
- child_octant: int32 [64], P('group'), may hold values from 0 to 7, as said below
Outputs:
- child_patterns: float32 [64, 2, 128, 256], P('group', None, 'member')
Inputs may be any that keep to these rules, and one draw needn't show every extreme that they name: `partners`: an entry of cluster c's list lies in c's own group block (clusters g * 8 to (g + 1) * 8 - 1); only the first 2 clusters of a block may also name any of the last 2 clusters of the previous block, and only the last 2 clusters any of the first 2 clusters of the next block. `child_parent`: the parent of a child in child block g (children g * 16 to (g + 1) * 16 - 1) lies in cluster block g; every cluster has at least one child; every cluster has 1 to 3 children, and in every block some cluster has exactly 3. `child_octant`: children of one parent have different octants.
All inputs are finite; a program needn't handle non-finite values.
Results may differ from a plain program's by a relative error of at most 0.0003.
Values sent between devices are 32-bit elements; how exact they have to be, the bound alone decides.
No kernel may reach another device: no remote copies, remote signals or barrier semaphores. Data moves between devices by JAX's collectives and lax.ppermute only.
A program may use at most 64 MiB of HBM per device.

v0:
```python
import functools
import math

import jax
import jax.numpy as jnp
import numpy as np
from jax import lax
from jax.experimental import pallas as pl
from jax.experimental.pallas import tpu as pltpu
from jax.sharding import PartitionSpec as P


NTC = 128
NPC = 256
CORES = 2
REACH = 6.0
F32 = jnp.float32
BF16 = jnp.bfloat16
MIB = 1 << 20


VMEM = pl.BlockSpec(memory_space=pltpu.VMEM)
SMEM = pl.BlockSpec(memory_space=pltpu.SMEM)
HBM = pl.BlockSpec(memory_space=pltpu.HBM)


def theta_table(fine, coarse):
    t = math.pi * (np.arange(fine) + 0.5) / fine
    j = math.pi * (np.arange(coarse) + 0.5) / coarse
    m = np.arange(coarse)
    w = np.where(m > 0, 2.0, 1.0)
    return (np.cos(np.outer(j, m)) * w) @ np.cos(np.outer(t, m)).T / fine


def phi_table(fine, coarse):
    f = 2.0 * math.pi * np.arange(fine) / fine
    g = 2.0 * math.pi * np.arange(coarse) / coarse
    m = np.arange(coarse // 2 + 1)
    v = np.where((m > 0) & (m < coarse // 2), 2.0, 1.0)
    cos_part = (np.cos(np.outer(g, m)) * v) @ np.cos(np.outer(f, m)).T
    sin_part = (np.sin(np.outer(g, m)) * v) @ np.sin(np.outer(f, m)).T
    return (cos_part + sin_part) / fine


def split_const(a):
    hi = np.asarray(a, np.float32).astype(BF16)
    lo = (np.asarray(a) - hi.astype(np.float64)).astype(np.float32).astype(BF16)
    return jnp.asarray(hi), jnp.asarray(lo)


def split(x):
    hi = x.astype(BF16)
    return hi, (x - hi.astype(F32)).astype(BF16)


def dot(a, b):
    return jnp.dot(a, b, preferred_element_type=F32)


def dot3(a, b):
    return dot(a[0], b[0]) + (dot(a[0], b[1]) + dot(a[1], b[0]))


def phase_tables(member, theta_count, phase_ref):
    rows, lons = phase_ref.shape[2], phase_ref.shape[3]
    quarter = lons // 4
    row = lax.broadcasted_iota(jnp.int32, (rows, 2 * quarter), 0)
    lon = lax.broadcasted_iota(jnp.int32, (rows, 2 * quarter), 1)
    theta = math.pi * ((row + member * rows).astype(F32) + 0.5) / theta_count
    phi = 2.0 * math.pi * lon.astype(F32) / lons
    x_arg = REACH * (jnp.sin(theta) * jnp.cos(phi))
    cos_x, sin_x = jnp.cos(x_arg), jnp.sin(x_arg)
    z_arg = REACH * jnp.cos(theta[:, :quarter])
    cz, sz = jnp.cos(z_arg), jnp.sin(z_arg)
    c0, c1 = cos_x[:, :quarter], cos_x[:, quarter:]
    s0, s1 = sin_x[:, :quarter], sin_x[:, quarter:]
    x_parts = ((c0, s0), (c1, s1), (c0, -s0), (c1, -s1))
    for q in range(4):
        ca, sa = x_parts[q]
        cb, sb = x_parts[(q + 3) % 4]
        cc, ss, sc, cs = ca * cb, sa * sb, sa * cb, ca * sb
        lanes = pl.ds(q * quarter, quarter)
        for octant in range(8):
            sgx = 1 - 2 * (octant % 2)
            sgy = 1 - 2 * (octant // 2 % 2)
            sgz = 1 - 2 * (octant // 4)
            re = cc - ss if sgx * sgy > 0 else cc + ss
            im = (sc if sgx > 0 else -sc) + (cs if sgy > 0 else -cs)
            szz = sz if sgz > 0 else -sz
            phase_ref[octant, 0, :, lanes] = re * cz - im * szz
            phase_ref[octant, 1, :, lanes] = re * szz + im * cz


def own_kernel(
    theta_count, width, table, patterns, operators, out, edge_ops, phase,
    mine, held, sems, mine_sem,
):
    clusters, _, rows, _ = out.shape
    terms = table.shape[1]
    inner = clusters - 2 * width

    def slot(c):
        return jnp.where(c < width, c, c - inner) * terms

    def fetch_edge(c, p):
        e = slot(c) + p
        return pltpu.make_async_copy(
            operators.at[table[clusters + c, p]], edge_ops.at[e], sems.at[c * terms + p]
        )

    def fetch_inner(c, p):
        return pltpu.make_async_copy(
            operators.at[table[clusters + c, p]], held.at[(c - width) * terms + p],
            sems.at[c * terms + p],
        )

    def edge_cluster(n):
        return jnp.where(n < width, n, n + inner)

    @pl.loop(0, inner * terms)
    def _(e):
        fetch_inner(width + e // terms, e % terms).start()

    @pl.loop(0, 2 * width * terms)
    def _(e):
        fetch_edge(edge_cluster(e // terms), e % terms).start()

    whole = pltpu.make_async_copy(patterns, mine, mine_sem)
    whole.start()
    phase_tables(table[2 * clusters, 0], theta_count, phase)
    base = table[2 * clusters, 1] * clusters
    whole.wait()

    def translate(c, ops, first):
        for r in range(rows // 8):
            band = pl.ds(r * 8, 8)
            re, im = 0.0, 0.0
            for p in range(terms):
                q = table[c, p] - base
                keep = jnp.where((q >= 0) & (q < clusters), 1.0, 0.0).astype(F32)
                q = jnp.clip(q, 0, clusters - 1)
                ore, oim = ops[first + p, 0, band, :], ops[first + p, 1, band, :]
                pre, pim = mine[q, 0, band, :] * keep, mine[q, 1, band, :] * keep
                re = re + (ore * pre - oim * pim)
                im = im + (ore * pim + oim * pre)
            out[c, 0, band, :] = re
            out[c, 1, band, :] = im

    @pl.loop(width, clusters - width)
    def _(c):
        for p in range(terms):
            fetch_inner(c, p).wait()
        translate(c, held, (c - width) * terms)

    @pl.loop(0, 2 * width)
    def _(n):
        c = edge_cluster(n)
        for p in range(terms):
            fetch_edge(c, p).wait()
        translate(c, edge_ops, n * terms)


def halo_terms(table, own, edge_ops, below, above, total):
    clusters, _, rows, _ = own.shape
    terms = table.shape[1]
    width = below.shape[0]
    base = table[2 * clusters, 1] * clusters
    total[...] = own[...]

    @pl.loop(0, 2 * width * terms)
    def _(e):
        n = e // terms
        c = jnp.where(n < width, n, n + clusters - 2 * width)
        q = table[c, e % terms] - base

        def accumulate(halo, h):
            for r in range(rows // 8):
                band = pl.ds(r * 8, 8)
                ore, oim = edge_ops[e, 0, band, :], edge_ops[e, 1, band, :]
                pre, pim = halo[h, 0, band, :], halo[h, 1, band, :]
                total[c, 0, band, :] += ore * pre - oim * pim
                total[c, 1, band, :] += ore * pim + oim * pre

        @pl.when(q < 0)
        def _():
            accumulate(below, jnp.clip(q + width, 0, width - 1))

        @pl.when(q >= clusters)
        def _():
            accumulate(above, jnp.clip(q - clusters, 0, width - 1))


def shift_and_phi(
    start, per_chip, others, table, child_parent, child_octant, total, phase, phi_hi, phi_lo,
    outs, shifted,
):
    clusters, _, rows, _ = total.shape
    base, chip = table[2 * clusters, 1] * clusters, table[2 * clusters, 2]
    for s, out in zip(others, outs):
        first = (chip ^ s) * per_chip + start
        size = out.shape[0] * 2 * rows
        for i in range(out.shape[0]):
            q = child_parent[first + i] - base
            o = child_octant[first + i]
            for r in range(rows // 8):
                band = pl.ds(r * 8, 8)
                pre, pim = total[q, 0, band, :], total[q, 1, band, :]
                ere, eim = phase[o, 0, band, :], phase[o, 1, band, :]
                at = i * 2 * rows + r * 8
                shifted[pl.ds(at, 8), :] = pre * ere - pim * eim
                shifted[pl.ds(at + rows, 8), :] = pre * eim + pim * ere
        y = dot3(split(shifted[pl.ds(0, size), :]), (phi_hi[...], phi_lo[...]))
        out[...] = y.reshape(out.shape)


def first_kernel(
    per_chip, table, child_parent, child_octant, own, edge_ops, below, above, phase,
    phi_hi, phi_lo, *rest
):
    outs, (total, shifted) = rest[:-2], rest[-2:]
    halo_terms(table, own, edge_ops, below, above, total)
    shift_and_phi(
        0, per_chip, range(1, len(outs) + 1), table, child_parent, child_octant, total, phase,
        phi_hi, phi_lo, outs, shifted,
    )


def later_kernel(
    start, per_chip, table, child_parent, child_octant, total, phase, phi_hi, phi_lo, *rest
):
    (mine, *outs), shifted = rest[:-1], rest[-1]
    args = (table, child_parent, child_octant, total, phase, phi_hi, phi_lo)
    shift_and_phi(start, per_chip, range(1, len(outs) + 1), *args, outs, shifted)
    shift_and_phi(0, per_chip, [0], *args, [mine], shifted)


def theta_kernel(start, table, t_hi, t_lo, mine, *rest):
    others, (away, keep, lats) = rest[:-3], rest[-3:]
    last = table.shape[0] - 1
    chip, core = table[last, 2], table[last, 3]
    rows = mine.shape[2]
    for i in range(away.shape[0]):
        for part in range(2):
            at = pl.multiple_of(chip * rows, rows)
            lats[pl.ds(at, rows), :] = mine[start + i, part]
            for s, block in enumerate(others, 1):
                at = pl.multiple_of((chip ^ s) * rows, rows)
                lats[pl.ds(at, rows), :] = block[i, part]
            x = split(lats[...])
            for out, which in ((away, 1 - core), (keep, core)):
                t = core * CORES + which
                out[i, part] = dot3((t_hi[t], t_lo[t]), x)


def sum_kernel(*refs):
    *halves, out = refs
    parts = len(halves) // 2
    chips, _, _, rows, _ = out.shape
    first = 0
    for keep, arrived in zip(halves[:parts], halves[parts:]):
        per = keep.shape[0]
        for chip in range(chips):
            band = pl.ds(chip * rows, rows)
            out[chip, pl.ds(first, per)] = keep[:, :, band, :] + arrived[:, :, band, :]
        first += per


def in_hbm(x):
    return pltpu.with_memory_space_constraint(x, pltpu.HBM)


def shape(*dims):
    return jax.ShapeDtypeStruct(dims, F32)


def params(limit):
    return pltpu.CompilerParams(vmem_limit_bytes=limit * MIB)


def call(*args, **kwargs):
    return pl.pallas_call(*args, **kwargs)


def cost(us):
    return pl.CostEstimate(flops=us * 2_000_000, bytes_accessed=0, transcendentals=0)


def on_device(patterns, operators, partners, operator_index, child_parent, child_octant):
    clusters, _, rows, lons = patterns.shape
    members = lax.axis_size("member")
    groups = lax.axis_size("group")
    theta_count = rows * members
    chips = members // CORES
    children = child_parent.shape[0]
    per_chip = children // chips
    out_rows = NTC // members
    width = clusters // 4
    member = lax.axis_index("member")
    group = lax.axis_index("group")
    chip, core = member // CORES, member % CORES
    terms = partners.shape[1]
    here = jnp.stack([member, group, chip, core]).astype(jnp.int32)
    table = jnp.concatenate(
        [partners, operator_index, jnp.pad(here, (0, terms - 4))[None, :]]
    )

    up = [(i, i + 1) for i in range(groups - 1)]
    down = [(i + 1, i) for i in range(groups - 1)]
    below = lax.ppermute(patterns[clusters - width:], "group", up)
    above = lax.ppermute(patterns[:width], "group", down)

    edge = 2 * width * terms
    total_shape = shape(clusters, 2, rows, lons)
    own, edge_ops, phase = pl.pallas_call(
        functools.partial(own_kernel, theta_count, width),
        out_shape=(
            total_shape, shape(edge, 2, rows, lons), shape(8, 2, rows, lons),
        ),
        in_specs=[SMEM, HBM, HBM],
        out_specs=(VMEM, VMEM, VMEM),
        scratch_shapes=[
            pltpu.VMEM((clusters, 2, rows, lons), F32),
            pltpu.VMEM((clusters * terms - edge, 2, rows, lons), F32),
            pltpu.SemaphoreType.DMA((clusters * terms,)),
            pltpu.SemaphoreType.DMA,
        ],
        compiler_params=params(20),
        cost_estimate=cost(8),
    )(table, in_hbm(patterns), in_hbm(operators))

    phi = split_const(phi_table(lons, NPC).T)
    lead = max(per_chip // 2, 1)
    sizes = [lead, per_chip - lead]

    def blocks_of(count):
        return (shape(count, 2, rows, NPC),) * (chips - 1)

    shifted = pltpu.VMEM((per_chip * 2 * rows, lons), F32)
    *blocks0, total = call(
        functools.partial(first_kernel, per_chip),
        out_shape=blocks_of(sizes[0]) + (total_shape,),
        in_specs=[SMEM] * 3 + [VMEM] * 7,
        out_specs=(VMEM,) * chips,
        scratch_shapes=[shifted],
        compiler_params=params(20),
        cost_estimate=cost(2),
    )(table, child_parent, child_octant, own, edge_ops, below, above, phase, *phi)
    mine, *blocks1 = call(
        functools.partial(later_kernel, sizes[0], per_chip),
        out_shape=(shape(per_chip, 2, rows, NPC),) + blocks_of(sizes[1]),
        in_specs=[SMEM] * 3 + [VMEM] * 4,
        out_specs=(VMEM,) * chips,
        scratch_shapes=[shifted],
        compiler_params=params(20),
        cost_estimate=cost(1),
    )(table, child_parent, child_octant, total, phase, *phi)

    def between_chips(blocks):
        moved = []
        for s, block in enumerate(blocks, 1):
            pairs = [(i, i ^ (CORES * s)) for i in range(members)]
            moved.append(lax.ppermute(block, "member", pairs))
        return moved

    arrived = [between_chips(blocks0), between_chips(blocks1)]

    theta = theta_table(theta_count, NTC).reshape(chips, CORES, out_rows, chips, CORES, rows)
    theta = theta.transpose(4, 1, 0, 2, 3, 5).reshape(
        CORES * CORES, chips * out_rows, chips * rows
    )
    swap = [(i, i ^ 1) for i in range(members)]
    if out_rows % 8 == 0:
        t_hi, t_lo = split_const(theta)
        keeps, swapped = [], []
        for h, first in enumerate((0, sizes[0])):
            half = shape(sizes[h], 2, chips * out_rows, NPC)
            away, keep = call(
                functools.partial(theta_kernel, first),
                out_shape=(half, half),
                in_specs=[SMEM] + [VMEM] * (2 + chips),
                out_specs=(VMEM, VMEM),
                scratch_shapes=[pltpu.VMEM((chips * rows, NPC), F32)],
                compiler_params=params(12),
                cost_estimate=cost(1),
            )(table, t_hi, t_lo, mine, *arrived[h])
            keeps.append(keep)
            swapped.append(lax.ppermute(away, "member", swap))
        pieces = call(
            sum_kernel,
            out_shape=shape(chips, per_chip, 2, out_rows, NPC),
            in_specs=[VMEM] * 4,
            out_specs=VMEM,
            compiler_params=params(12),
            cost_estimate=cost(1),
        )(*keeps, *swapped)
    else:
        lats = jnp.stack([jnp.concatenate(pair) for pair in zip(*arrived)])
        lats = jnp.concatenate([mine[None], lats])
        lats = jnp.take(lats, chip ^ jnp.arange(chips), axis=0)
        lats = lats.transpose(1, 2, 0, 3, 4).reshape(per_chip, 2, chips * rows, NPC)
        both = jnp.take(
            jnp.asarray(theta, F32).reshape(CORES, CORES, chips * out_rows, chips * rows),
            core, axis=0,
        )
        sums = jnp.einsum(
            "wjt,kptg->wkpjg", both, lats, precision=lax.Precision.HIGHEST
        )
        moved = lax.ppermute(jnp.take(sums, 1 - core, axis=0), "member", swap)
        pieces = jnp.take(sums, core, axis=0) + moved
        pieces = pieces.reshape(per_chip, 2, chips, out_rows, NPC).transpose(2, 0, 1, 3, 4)

    same_core = [list(range(c, members, CORES)) for c in range(CORES)]
    out = lax.all_to_all(
        pieces, "member", 0, 0, tiled=True, axis_index_groups=same_core
    )
    return out.reshape(children, 2, out_rows, NPC)


def solution(mesh):
    return jax.shard_map(
        on_device,
        mesh=mesh,
        in_specs=(
            P("group", None, "member", None),
            P(None, None, "member", None),
            P("group", None),
            P("group", None),
            P("group"),
            P("group"),
        ),
        out_specs=P("group", None, "member", None),
        check_vma=False,
    )
```

profile of v0, /device:TPU:0, one launch (start us, length us, event | category | flops | bytes accessed | tf_op | source)
XLA Modules:
  0.0 49.1 jit_solution(2865106237809974937)
XLA Ops:
  0.0 0.0 copy-start
  0.0 0.0 copy-start.1
  0.0 0.0 copy-start.2
  0.0 0.0 copy-start.3
  0.0 0.0 copy-start.5
  0.0 0.0 copy-start.4
  0.0 1.1 %fusion = (f32[2,2,32,512]{3,2,1,0:T(8,128)S(1)}, f32[2,2,32,512]{3,2,1,0:T(8,128)S(1)}) fusion(f32[8,2,32,512]{3,2,1,0:T(8,128)} %patterns.1), kind=kLoop, calls=%fused_computation.3 | loop fusion | bytes 1048576 | tf_op jit(solution)/shard_map/slice | solution.py:310
  1.2 1.3 %collective-permute-start.1 = (f32[2,2,32,512]{3,2,1,0:T(8,128)S(1)}, f32[2,2,32,512]{3,2,1,0:T(8,128)S(1)}, u32[]{:S(2)}, u32[]{:S(2)}) collective-permute-start(f32[2,2,32,512]{3,2,1,0:T(8,128)S(1)} %get-tuple-element.35), channel_id=1, source_target_pairs={{8,0},{16,8},{24,16},{9,1},{17,9},{25,17},{10,2},{18,10},{26,18},{... | collective-permute-start | bytes 786440 | tf_op jit(solution)/shard_map/ppermute | solution.py:310
  2.5 5.6 %collective-permute-start = (f32[2,2,32,512]{3,2,1,0:T(8,128)S(1)}, f32[2,2,32,512]{3,2,1,0:T(8,128)S(1)}, u32[]{:S(2)}, u32[]{:S(2)}) collective-permute-start(f32[2,2,32,512]{3,2,1,0:T(8,128)S(1)} %get-tuple-element.36), channel_id=1, source_target_pairs={{0,8},{8,16},{16,24},{1,9},{9,17},{17,25},{2,10},{10,18},{18,26},{... | collective-permute-start | bytes 786440 | tf_op jit(solution)/shard_map/ppermute | solution.py:309
  8.1 0.1 pad_add_fusion.1
  8.2 0.7 %pad_add_fusion.table = s32[17,8]{1,0:T(8,128)S(1)} fusion(s32[1,8]{1,0:T(1,128)S(1)} %pad_bitcast_fusion, s32[8,8]{1,0:T(8,128)} %param.13, s32[8,8]{1,0:T(8,128)} %param.12), kind=kLoop, calls=%fused_computation | loop fusion | flops 272 | bytes 1088 | tf_op jit(solution)/shard_map/concatenate | solution.py:303
  8.9 7.3 %shard_map.100 = (f32[8,2,32,512]{3,2,1,0:T(8,128)S(1)}, f32[32,2,32,512]{3,2,1,0:T(8,128)S(1)}, f32[8,2,32,512]{3,2,1,0:T(8,128)S(1)}) custom-call(s32[17,8]{1,0:T(8,128)S(1)} %pad_add_fusion.table, f32[8,2,32,512]{3,2,1,0:T(8,128)} %patterns.1, f32[100,2,32,512]{3,2,1,0:T(8,128)} %operators.1), custom_call_target="tpu_custom_call" | custom-call | flops 16000000 | tf_op jit(solution)/shard_map/pallas_call | solution.py:314
  16.2 0.0 collective-permute-done.1.above
  16.2 0.0 collective-permute-done.below
  16.2 0.0 copy-done
  16.2 0.0 copy-done.1
  16.2 0.0 copy-done.5
  16.2 0.0 copy-done.4
  16.2 2.4 %shard_map.101 = (f32[2,2,32,256]{3,2,1,0:T(8,128)S(1)}, f32[2,2,32,256]{3,2,1,0:T(8,128)S(1)}, f32[2,2,32,256]{3,2,1,0:T(8,128)S(1)}, f32[8,2,32,512]{3,2,1,0:T(8,128)S(1)}) custom-call(s32[17,8]{1,0:T(8,128)S(1)} %pad_add_fusion.table, s32[16]{0:T(128)S(1)} %copy-done.4, s32[16]{0:T(128)S(1)} %copy-done.5, f32[8,2,32,512]{3,2,1,0:T(8,128)S(1)} %get-tuple-element.20.own, ...), custom_call_target="tpu_custom_call" | custom-call | flops 4000000 | tf_op jit(solution)/shard_map/pallas_call | solution.py:339
  18.6 2.0 %collective-permute-start.2 = (f32[2,2,32,256]{3,2,1,0:T(8,128)S(1)}, f32[2,2,32,256]{3,2,1,0:T(8,128)S(1)}, u32[]{:S(2)}, u32[]{:S(2)}) collective-permute-start(f32[2,2,32,256]{3,2,1,0:T(8,128)S(1)} %get-tuple-element.25), channel_id=1, source_target_pairs={{0,2},{1,3},{2,0},{3,1},{4,6},{5,7},{6,4},{7,5},{8,10},{9,11},{10,... | collective-permute-start | bytes 393224 | tf_op jit(solution)/shard_map/ppermute | solution.py:362
  20.6 1.5 %collective-permute-start.3 = (f32[2,2,32,256]{3,2,1,0:T(8,128)S(1)}, f32[2,2,32,256]{3,2,1,0:T(8,128)S(1)}, u32[]{:S(2)}, u32[]{:S(2)}) collective-permute-start(f32[2,2,32,256]{3,2,1,0:T(8,128)S(1)} %get-tuple-element.26), channel_id=1, source_target_pairs={{0,4},{1,5},{2,6},{3,7},{4,0},{5,1},{6,2},{7,3},{8,12},{9,13},{10,... | collective-permute-start | bytes 393224 | tf_op jit(solution)/shard_map/ppermute | solution.py:362
  22.2 0.0 collective-permute-start.4
  22.2 1.6 %shard_map.102 = (f32[4,2,32,256]{3,2,1,0:T(8,128)S(1)}, f32[2,2,32,256]{3,2,1,0:T(8,128)S(1)}, f32[2,2,32,256]{3,2,1,0:T(8,128)S(1)}, f32[2,2,32,256]{3,2,1,0:T(8,128)S(1)}) custom-call(s32[17,8]{1,0:T(8,128)S(1)} %pad_add_fusion.table, s32[16]{0:T(128)S(1)} %copy-done.4, s32[16]{0:T(128)S(1)} %copy-done.5, f32[8,2,32,512]{3,2,1,0:T(8,128)S(1)} %get-tuple-element.23.total, ...), custom_call_target="tpu_custom_call" | custom-call | flops 2000000 | tf_op jit(solution)/shard_map/pallas_call | solution.py:348
  23.8 2.0 %collective-permute-start.5 = (f32[2,2,32,256]{3,2,1,0:T(8,128)S(1)}, f32[2,2,32,256]{3,2,1,0:T(8,128)S(1)}, u32[]{:S(2)}, u32[]{:S(2)}) collective-permute-start(f32[2,2,32,256]{3,2,1,0:T(8,128)S(1)} %get-tuple-element.29), channel_id=1, source_target_pairs={{0,2},{1,3},{2,0},{3,1},{4,6},{5,7},{6,4},{7,5},{8,10},{9,11},{10,... | collective-permute-start | bytes 393224 | tf_op jit(solution)/shard_map/ppermute | solution.py:362
  25.8 1.5 %collective-permute-start.6 = (f32[2,2,32,256]{3,2,1,0:T(8,128)S(1)}, f32[2,2,32,256]{3,2,1,0:T(8,128)S(1)}, u32[]{:S(2)}, u32[]{:S(2)}) collective-permute-start(f32[2,2,32,256]{3,2,1,0:T(8,128)S(1)} %get-tuple-element.30), channel_id=1, source_target_pairs={{0,4},{1,5},{2,6},{3,7},{4,0},{5,1},{6,2},{7,3},{8,12},{9,13},{10,... | collective-permute-start | bytes 393224 | tf_op jit(solution)/shard_map/ppermute | solution.py:362
  27.3 0.0 collective-permute-done.2.rest_0_
  27.3 0.4 collective-permute-start.7
  27.7 0.6 %collective-permute-done.3.rest_1_ = f32[2,2,32,256]{3,2,1,0:T(8,128)S(1)} collective-permute-done((f32[2,2,32,256]{3,2,1,0:T(8,128)S(1)}, f32[2,2,32,256]{3,2,1,0:T(8,128)S(1)}, u32[]{:S(2)}, u32[]{:S(2)}) %collective-permute-start.3) | collective-permute-done | bytes 131104 | tf_op jit(solution)/shard_map/ppermute | solution.py:362
  28.3 1.2 %collective-permute-done.4.rest_2_ = f32[2,2,32,256]{3,2,1,0:T(8,128)S(1)} collective-permute-done((f32[2,2,32,256]{3,2,1,0:T(8,128)S(1)}, f32[2,2,32,256]{3,2,1,0:T(8,128)S(1)}, u32[]{:S(2)}, u32[]{:S(2)}) %collective-permute-start.4) | collective-permute-done | bytes 131104 | tf_op jit(solution)/shard_map/ppermute | solution.py:362
  29.4 0.0 copy-done.2
  29.4 0.0 copy-done.3
  29.4 1.1 %shard_map.103 = (f32[2,2,64,256]{3,2,1,0:T(8,128)S(1)}, f32[2,2,64,256]{3,2,1,0:T(8,128)S(1)}) custom-call(s32[17,8]{1,0:T(8,128)S(1)} %pad_add_fusion.table, bf16[4,64,128]{2,1,0:T(8,128)(2,1)S(1)} %copy-done.3, bf16[4,64,128]{2,1,0:T(8,128)(2,1)S(1)} %copy-done.2, f32[4,2,32,256]{3,2,1,0:T(8,128)S(1)} %get-tuple-element.24.mine, ...), custom_call_target="tpu_custom_call" | custom-call | flops 2000000 | tf_op jit(solution)/shard_map/pallas_call | solution.py:377
  30.6 0.1 collective-permute-start.8
  30.6 0.1 collective-permute-done.5.rest_0_
  30.8 3.3 %collective-permute-done.6.rest_1_ = f32[2,2,32,256]{3,2,1,0:T(8,128)S(1)} collective-permute-done((f32[2,2,32,256]{3,2,1,0:T(8,128)S(1)}, f32[2,2,32,256]{3,2,1,0:T(8,128)S(1)}, u32[]{:S(2)}, u32[]{:S(2)}) %collective-permute-start.6) | collective-permute-done | bytes 131104 | tf_op jit(solution)/shard_map/ppermute | solution.py:362
  34.0 0.0 collective-permute-done.7.rest_2_
  34.0 1.1 %shard_map.104 = (f32[2,2,64,256]{3,2,1,0:T(8,128)S(1)}, f32[2,2,64,256]{3,2,1,0:T(8,128)S(1)}) custom-call(s32[17,8]{1,0:T(8,128)S(1)} %pad_add_fusion.table, bf16[4,64,128]{2,1,0:T(8,128)(2,1)S(1)} %copy-done.3, bf16[4,64,128]{2,1,0:T(8,128)(2,1)S(1)} %copy-done.2, f32[4,2,32,256]{3,2,1,0:T(8,128)S(1)} %get-tuple-element.24.mine, ...), custom_call_target="tpu_custom_call" | custom-call | flops 2000000 | tf_op jit(solution)/shard_map/pallas_call | solution.py:377
  35.1 0.1 collective-permute-start.9
  35.2 0.0 collective-permute-done.8.refs_2_
  35.2 1.5 %collective-permute-done.9.refs_3_ = f32[2,2,64,256]{3,2,1,0:T(8,128)S(1)} collective-permute-done((f32[2,2,64,256]{3,2,1,0:T(8,128)S(1)}, f32[2,2,64,256]{3,2,1,0:T(8,128)S(1)}, u32[]{:S(2)}, u32[]{:S(2)}) %collective-permute-start.9) | collective-permute-done | bytes 262176 | tf_op jit(solution)/shard_map/ppermute | solution.py:387
  36.8 0.1 shard_map.105
  36.8 11.5 %all_to_all.5 = f32[4,4,2,16,256]{4,3,2,1,0:T(8,128)S(1)} all-to-all(f32[4,4,2,16,256]{4,3,2,1,0:T(8,128)S(1)} %shard_map.105), channel_id=1, replica_groups={{0,2,4,6},{1,3,5,7},{8,10,12,14},{9,11,13,15},{16,18,20,22},{17,19,21,2..., dimensions={0} | all-to-all | bytes 1048576 | tf_op jit(solution)/shard_map/all_to_all | solution.py:413
  48.3 0.8 %copy.20 = f32[16,2,16,256]{3,2,1,0:T(8,128)} copy(f32[16,2,16,256]{3,2,1,0:T(8,128)S(1)} %bitcast.7) | data formatting | bytes 1048576
  (1 shorter events, 0.0 us)
Async XLA Ops:
  0.0 16.2 %copy-start = (bf16[512,256]{1,0:T(8,128)(2,1)S(1)}, bf16[512,256]{1,0:T(8,128)(2,1)}, u32[]{:S(2)}) copy-start(bf16[512,256]{1,0:T(8,128)(2,1)} %constant.42.clone.phi_lo) | copy-start | bytes 786436
  0.0 16.2 %copy-start.1 = (bf16[512,256]{1,0:T(8,128)(2,1)S(1)}, bf16[512,256]{1,0:T(8,128)(2,1)}, u32[]{:S(2)}) copy-start(bf16[512,256]{1,0:T(8,128)(2,1)} %constant.41.clone.phi_hi) | copy-start | bytes 786436
  0.0 29.4 %copy-start.2 = (bf16[4,64,128]{2,1,0:T(8,128)(2,1)S(1)}, bf16[4,64,128]{2,1,0:T(8,128)(2,1)}, u32[]{:S(2)}) copy-start(bf16[4,64,128]{2,1,0:T(8,128)(2,1)} %constant.44.clone.t_lo) | copy-start | bytes 196612
  0.0 29.4 %copy-start.3 = (bf16[4,64,128]{2,1,0:T(8,128)(2,1)S(1)}, bf16[4,64,128]{2,1,0:T(8,128)(2,1)}, u32[]{:S(2)}) copy-start(bf16[4,64,128]{2,1,0:T(8,128)(2,1)} %constant.43.clone.t_hi) | copy-start | bytes 196612
  0.0 16.2 %copy-start.5 = (s32[16]{0:T(128)S(1)}, s32[16]{0:T(128)}, u32[]{:S(2)}) copy-start(s32[16]{0:T(128)} %child_octant.3) | copy-start | bytes 196
  0.0 16.2 %copy-start.4 = (s32[16]{0:T(128)S(1)}, s32[16]{0:T(128)}, u32[]{:S(2)}) copy-start(s32[16]{0:T(128)} %child_parent.3) | copy-start | bytes 196
  1.2 15.0 %collective-permute-start.1 = (f32[2,2,32,512]{3,2,1,0:T(8,128)S(1)}, f32[2,2,32,512]{3,2,1,0:T(8,128)S(1)}, u32[]{:S(2)}, u32[]{:S(2)}) collective-permute-start(f32[2,2,32,512]{3,2,1,0:T(8,128)S(1)} %get-tuple-element.35), channel_id=1, source_target_pairs={{8,0},{16,8},{24,16},{9,1},{17,9},{25,17},{10,2},{18,10},{26,18},{... | collective-permute-start | bytes 786440 | tf_op jit(solution)/shard_map/ppermute | solution.py:310
  2.5 13.7 %collective-permute-start = (f32[2,2,32,512]{3,2,1,0:T(8,128)S(1)}, f32[2,2,32,512]{3,2,1,0:T(8,128)S(1)}, u32[]{:S(2)}, u32[]{:S(2)}) collective-permute-start(f32[2,2,32,512]{3,2,1,0:T(8,128)S(1)} %get-tuple-element.36), channel_id=1, source_target_pairs={{0,8},{8,16},{16,24},{1,9},{9,17},{17,25},{2,10},{10,18},{18,26},{... | collective-permute-start | bytes 786440 | tf_op jit(solution)/shard_map/ppermute | solution.py:309
  18.6 8.7 %collective-permute-start.2 = (f32[2,2,32,256]{3,2,1,0:T(8,128)S(1)}, f32[2,2,32,256]{3,2,1,0:T(8,128)S(1)}, u32[]{:S(2)}, u32[]{:S(2)}) collective-permute-start(f32[2,2,32,256]{3,2,1,0:T(8,128)S(1)} %get-tuple-element.25), channel_id=1, source_target_pairs={{0,2},{1,3},{2,0},{3,1},{4,6},{5,7},{6,4},{7,5},{8,10},{9,11},{10,... | collective-permute-start | bytes 393224 | tf_op jit(solution)/shard_map/ppermute | solution.py:362
  20.6 7.6 %collective-permute-start.3 = (f32[2,2,32,256]{3,2,1,0:T(8,128)S(1)}, f32[2,2,32,256]{3,2,1,0:T(8,128)S(1)}, u32[]{:S(2)}, u32[]{:S(2)}) collective-permute-start(f32[2,2,32,256]{3,2,1,0:T(8,128)S(1)} %get-tuple-element.26), channel_id=1, source_target_pairs={{0,4},{1,5},{2,6},{3,7},{4,0},{5,1},{6,2},{7,3},{8,12},{9,13},{10,... | collective-permute-start | bytes 393224 | tf_op jit(solution)/shard_map/ppermute | solution.py:362
  22.2 7.3 %collective-permute-start.4 = (f32[2,2,32,256]{3,2,1,0:T(8,128)S(1)}, f32[2,2,32,256]{3,2,1,0:T(8,128)S(1)}, u32[]{:S(2)}, u32[]{:S(2)}) collective-permute-start(f32[2,2,32,256]{3,2,1,0:T(8,128)S(1)} %get-tuple-element.27), channel_id=1, source_target_pairs={{0,6},{1,7},{2,4},{3,5},{4,2},{5,3},{6,0},{7,1},{8,14},{9,15},{10,... | collective-permute-start | bytes 393224 | tf_op jit(solution)/shard_map/ppermute | solution.py:362
  23.8 7.0 %collective-permute-start.5 = (f32[2,2,32,256]{3,2,1,0:T(8,128)S(1)}, f32[2,2,32,256]{3,2,1,0:T(8,128)S(1)}, u32[]{:S(2)}, u32[]{:S(2)}) collective-permute-start(f32[2,2,32,256]{3,2,1,0:T(8,128)S(1)} %get-tuple-element.29), channel_id=1, source_target_pairs={{0,2},{1,3},{2,0},{3,1},{4,6},{5,7},{6,4},{7,5},{8,10},{9,11},{10,... | collective-permute-start | bytes 393224 | tf_op jit(solution)/shard_map/ppermute | solution.py:362
  25.8 8.2 %collective-permute-start.6 = (f32[2,2,32,256]{3,2,1,0:T(8,128)S(1)}, f32[2,2,32,256]{3,2,1,0:T(8,128)S(1)}, u32[]{:S(2)}, u32[]{:S(2)}) collective-permute-start(f32[2,2,32,256]{3,2,1,0:T(8,128)S(1)} %get-tuple-element.30), channel_id=1, source_target_pairs={{0,4},{1,5},{2,6},{3,7},{4,0},{5,1},{6,2},{7,3},{8,12},{9,13},{10,... | collective-permute-start | bytes 393224 | tf_op jit(solution)/shard_map/ppermute | solution.py:362
  27.3 6.7 %collective-permute-start.7 = (f32[2,2,32,256]{3,2,1,0:T(8,128)S(1)}, f32[2,2,32,256]{3,2,1,0:T(8,128)S(1)}, u32[]{:S(2)}, u32[]{:S(2)}) collective-permute-start(f32[2,2,32,256]{3,2,1,0:T(8,128)S(1)} %get-tuple-element.31), channel_id=1, source_target_pairs={{0,6},{1,7},{2,4},{3,5},{4,2},{5,3},{6,0},{7,1},{8,14},{9,15},{10,... | collective-permute-start | bytes 393224 | tf_op jit(solution)/shard_map/ppermute | solution.py:362
  30.6 4.7 %collective-permute-start.8 = (f32[2,2,64,256]{3,2,1,0:T(8,128)S(1)}, f32[2,2,64,256]{3,2,1,0:T(8,128)S(1)}, u32[]{:S(2)}, u32[]{:S(2)}) collective-permute-start(f32[2,2,64,256]{3,2,1,0:T(8,128)S(1)} %get-tuple-element.33), channel_id=1, source_target_pairs={{0,1},{1,0},{2,3},{3,2},{4,5},{5,4},{6,7},{7,6},{8,9},{9,8},{10,11... | collective-permute-start | bytes 786440 | tf_op jit(solution)/shard_map/ppermute | solution.py:387
  35.1 1.6 %collective-permute-start.9 = (f32[2,2,64,256]{3,2,1,0:T(8,128)S(1)}, f32[2,2,64,256]{3,2,1,0:T(8,128)S(1)}, u32[]{:S(2)}, u32[]{:S(2)}) collective-permute-start(f32[2,2,64,256]{3,2,1,0:T(8,128)S(1)} %get-tuple-element.34), channel_id=1, source_target_pairs={{0,1},{1,0},{2,3},{3,2},{4,5},{5,4},{6,7},{7,6},{8,9},{9,8},{10,11... | collective-permute-start | bytes 786440 | tf_op jit(solution)/shard_map/ppermute | solution.py:387
where the time goes:
time: 49.4 us; the launch traced here: 49.1 us
  starting transfers between devices  14.5 us (29%)
  Pallas kernels  13.5 us (27%)
  blocking collectives  11.5 us (23%)
  waiting for transfers between devices  6.64 us (13%)
  local copies, waits for them, and re-layouts  1.95 us (4%)
  other arithmetic  0.79 us (2%)
    all_to_all x1, blocking collectives, on_device(): lax.all_to_all(pieces, 'member', 0, 0, tiled=True, axis_index_groups=same...  11.5 us
    ppermute x6, starting transfers between devices, between_chips(): moved.append(lax.ppermute(block, 'member', pairs))  7.47 us
    pallas_call x1, Pallas kernels, on_device(): pl.pallas_call(functools.partial(own_kernel, theta_count, width), out_sha...  7.28 us
    ppermute x1, starting transfers between devices, on_device(): below = lax.ppermute(patterns[clusters - width:], 'group', up)  5.62 us
    ppermute x6, waiting for transfers between devices, between_chips(): moved.append(lax.ppermute(block, 'member', pairs))  5.12 us
    pallas_call x1, Pallas kernels, on_device(): call(functools.partial(first_kernel, per_chip), out_shape=blocks_of(sizes...  2.39 us
    pallas_call x2, Pallas kernels, on_device(): call(functools.partial(theta_kernel, first), out_shape=(half, half), in_s...  2.23 us
    pallas_call x1, Pallas kernels, on_device(): call(functools.partial(later_kernel, sizes[0], per_chip), out_shape=(shap...  1.58 us
  transfers between devices with their start and end apart: 10, of which 5 were waited for; matrix products, arithmetic and copies ran while one was open for 2% of the time, Pallas kernels for 23%

commit v1 on v0

--- a/solution.py
+++ b/solution.py
@@ -114,6 +114,9 @@
             sems.at[c * terms + p],
         )
 
+    whole = pltpu.make_async_copy(patterns, mine, mine_sem)
+    whole.start()
+
     def edge_cluster(n):
         return jnp.where(n < width, n, n + inner)
 
@@ -125,10 +128,8 @@
     def _(e):
         fetch_edge(edge_cluster(e // terms), e % terms).start()
 
-    whole = pltpu.make_async_copy(patterns, mine, mine_sem)
-    whole.start()
-    phase_tables(table[2 * clusters, 0], theta_count, phase)
-    base = table[2 * clusters, 1] * clusters
+    phase_tables(lax.axis_index("member"), theta_count, phase)
+    base = lax.axis_index("group") * clusters
     whole.wait()
 
     def translate(c, ops, first):
@@ -164,44 +165,43 @@
     clusters, _, rows, _ = own.shape
     terms = table.shape[1]
     width = below.shape[0]
-    base = table[2 * clusters, 1] * clusters
+    base = lax.axis_index("group") * clusters
     total[...] = own[...]
 
-    @pl.loop(0, 2 * width * terms)
-    def _(e):
-        n = e // terms
-        c = jnp.where(n < width, n, n + clusters - 2 * width)
-        q = table[c, e % terms] - base
-
-        def accumulate(halo, h):
-            for r in range(rows // 8):
-                band = pl.ds(r * 8, 8)
-                ore, oim = edge_ops[e, 0, band, :], edge_ops[e, 1, band, :]
-                pre, pim = halo[h, 0, band, :], halo[h, 1, band, :]
-                total[c, 0, band, :] += ore * pre - oim * pim
-                total[c, 1, band, :] += ore * pim + oim * pre
-
-        @pl.when(q < 0)
-        def _():
-            accumulate(below, jnp.clip(q + width, 0, width - 1))
-
-        @pl.when(q >= clusters)
-        def _():
-            accumulate(above, jnp.clip(q - clusters, 0, width - 1))
-
-
-def shift_and_phi(
-    start, per_chip, others, table, child_parent, child_octant, total, phase, phi_hi, phi_lo,
-    outs, shifted,
-):
+    for n in range(2 * width):
+        c = n if n < width else n + clusters - 2 * width
+        halo = below if n < width else above
+        shift = width - base if n < width else -base - clusters
+
+        @pl.loop(0, terms)
+        def _(p):
+            q = table[c, p] - base
+
+            @pl.when((q < 0) | (q >= clusters))
+            def _():
+                e = n * terms + p
+                h = jnp.clip(table[c, p] + shift, 0, width - 1)
+                for r in range(rows // 8):
+                    band = pl.ds(r * 8, 8)
+                    ore, oim = edge_ops[e, 0, band, :], edge_ops[e, 1, band, :]
+                    pre, pim = halo[h, 0, band, :], halo[h, 1, band, :]
+                    total[c, 0, band, :] += ore * pre - oim * pim
+                    total[c, 1, band, :] += ore * pim + oim * pre
+
+
+def shift_and_phi(order, table, total, phase, phi_hi, phi_lo, outs, shifted):
     clusters, _, rows, _ = total.shape
-    base, chip = table[2 * clusters, 1] * clusters, table[2 * clusters, 2]
-    for s, out in zip(others, outs):
-        first = (chip ^ s) * per_chip + start
-        size = out.shape[0] * 2 * rows
+    terms = table.shape[1]
+    base = lax.axis_index("group") * clusters
+    chip = lax.axis_index("member") // CORES
+    parents = 2 * clusters
+    octants = parents + (table.shape[0] - parents) // 2
+    for s, out in zip(order, outs):
+        first = (chip ^ s) * out.shape[0]
         for i in range(out.shape[0]):
-            q = child_parent[first + i] - base
-            o = child_octant[first + i]
+            row, column = (first + i) // terms, (first + i) % terms
+            q = table[parents + row, column] - base
+            o = table[octants + row, column]
             for r in range(rows // 8):
                 band = pl.ds(r * 8, 8)
                 pre, pim = total[q, 0, band, :], total[q, 1, band, :]
@@ -209,41 +209,30 @@
                 at = i * 2 * rows + r * 8
                 shifted[pl.ds(at, 8), :] = pre * ere - pim * eim
                 shifted[pl.ds(at + rows, 8), :] = pre * eim + pim * ere
-        y = dot3(split(shifted[pl.ds(0, size), :]), (phi_hi[...], phi_lo[...]))
+        y = dot3(split(shifted[...]), (phi_hi[...], phi_lo[...]))
         out[...] = y.reshape(out.shape)
 
 
 def first_kernel(
-    per_chip, table, child_parent, child_octant, own, edge_ops, below, above, phase,
-    phi_hi, phi_lo, *rest
+    order, table, own, edge_ops, below, above, phase, phi_hi, phi_lo, *rest
 ):
     outs, (total, shifted) = rest[:-2], rest[-2:]
     halo_terms(table, own, edge_ops, below, above, total)
-    shift_and_phi(
-        0, per_chip, range(1, len(outs) + 1), table, child_parent, child_octant, total, phase,
-        phi_hi, phi_lo, outs, shifted,
-    )
-
-
-def later_kernel(
-    start, per_chip, table, child_parent, child_octant, total, phase, phi_hi, phi_lo, *rest
-):
-    (mine, *outs), shifted = rest[:-1], rest[-1]
-    args = (table, child_parent, child_octant, total, phase, phi_hi, phi_lo)
-    shift_and_phi(start, per_chip, range(1, len(outs) + 1), *args, outs, shifted)
-    shift_and_phi(0, per_chip, [0], *args, [mine], shifted)
-
-
-def theta_kernel(start, table, t_hi, t_lo, mine, *rest):
-    others, (away, keep, lats) = rest[:-3], rest[-3:]
-    last = table.shape[0] - 1
-    chip, core = table[last, 2], table[last, 3]
-    rows = mine.shape[2]
-    for i in range(away.shape[0]):
+    shift_and_phi(order, table, total, phase, phi_hi, phi_lo, outs, shifted)
+
+
+def later_kernel(order, table, total, phase, phi_hi, phi_lo, *rest):
+    shift_and_phi(order, table, total, phase, phi_hi, phi_lo, rest[:-1], rest[-1])
+
+
+def theta_kernel(t_hi, t_lo, *rest):
+    blocks, (away, keep, lats) = rest[:-3], rest[-3:]
+    member = lax.axis_index("member")
+    chip, core = member // CORES, member % CORES
+    per_chip, _, rows, _ = blocks[0].shape
+    for i in range(per_chip):
         for part in range(2):
-            at = pl.multiple_of(chip * rows, rows)
-            lats[pl.ds(at, rows), :] = mine[start + i, part]
-            for s, block in enumerate(others, 1):
+            for s, block in enumerate(blocks):
                 at = pl.multiple_of((chip ^ s) * rows, rows)
                 lats[pl.ds(at, rows), :] = block[i, part]
             x = split(lats[...])
@@ -252,17 +241,26 @@
                 out[i, part] = dot3((t_hi[t], t_lo[t]), x)
 
 
-def sum_kernel(*refs):
-    *halves, out = refs
-    parts = len(halves) // 2
-    chips, _, _, rows, _ = out.shape
-    first = 0
-    for keep, arrived in zip(halves[:parts], halves[parts:]):
-        per = keep.shape[0]
-        for chip in range(chips):
-            band = pl.ds(chip * rows, rows)
-            out[chip, pl.ds(first, per)] = keep[:, :, band, :] + arrived[:, :, band, :]
-        first += per
+def sum_kernel(keep, arrived, *outs):
+    chip = lax.axis_index("member") // CORES
+    rows = outs[0].shape[2]
+    for s, out in enumerate(outs):
+        band = pl.ds(pl.multiple_of((chip ^ s) * rows, rows), rows)
+        out[...] = keep[:, :, band, :] + arrived[:, :, band, :]
+
+
+def place_kernel(*rest):
+    blocks, (out, sems) = rest[:-2], rest[-2:]
+    chip = lax.axis_index("member") // CORES
+    per_chip = blocks[0].shape[0]
+    copies = []
+    for s, block in enumerate(blocks):
+        first = (chip ^ s) * per_chip
+        copy = pltpu.make_async_copy(block, out.at[pl.ds(first, per_chip)], sems.at[s])
+        copy.start()
+        copies.append(copy)
+    for copy in copies:
+        copy.wait()
 
 
 def in_hbm(x):
@@ -296,12 +294,15 @@
     out_rows = NTC // members
     width = clusters // 4
     member = lax.axis_index("member")
-    group = lax.axis_index("group")
     chip, core = member // CORES, member % CORES
     terms = partners.shape[1]
-    here = jnp.stack([member, group, chip, core]).astype(jnp.int32)
     table = jnp.concatenate(
-        [partners, operator_index, jnp.pad(here, (0, terms - 4))[None, :]]
+        [
+            partners,
+            operator_index,
+            child_parent.reshape(-1, terms),
+            child_octant.reshape(-1, terms),
+        ]
     )
 
     up = [(i, i + 1) for i in range(groups - 1)]
@@ -329,40 +330,39 @@
     )(table, in_hbm(patterns), in_hbm(operators))
 
     phi = split_const(phi_table(lons, NPC).T)
-    lead = max(per_chip // 2, 1)
-    sizes = [lead, per_chip - lead]
-
-    def blocks_of(count):
-        return (shape(count, 2, rows, NPC),) * (chips - 1)
-
+    block = shape(per_chip, 2, rows, NPC)
     shifted = pltpu.VMEM((per_chip * 2 * rows, lons), F32)
-    *blocks0, total = call(
-        functools.partial(first_kernel, per_chip),
-        out_shape=blocks_of(sizes[0]) + (total_shape,),
-        in_specs=[SMEM] * 3 + [VMEM] * 7,
-        out_specs=(VMEM,) * chips,
+    far, near = [chips - 1], [*range(1, chips - 1), 0]
+    sent = dict.fromkeys(range(chips))
+    *outs, total = call(
+        functools.partial(first_kernel, far),
+        out_shape=(block,) * len(far) + (total_shape,),
+        in_specs=[SMEM] + [VMEM] * 7,
+        out_specs=(VMEM,) * (len(far) + 1),
         scratch_shapes=[shifted],
         compiler_params=params(20),
         cost_estimate=cost(2),
-    )(table, child_parent, child_octant, own, edge_ops, below, above, phase, *phi)
-    mine, *blocks1 = call(
-        functools.partial(later_kernel, sizes[0], per_chip),
-        out_shape=(shape(per_chip, 2, rows, NPC),) + blocks_of(sizes[1]),
-        in_specs=[SMEM] * 3 + [VMEM] * 4,
-        out_specs=(VMEM,) * chips,
+    )(table, own, edge_ops, below, above, phase, *phi)
+    sent.update(zip(far, outs))
+    outs = call(
+        functools.partial(later_kernel, near),
+        out_shape=(block,) * len(near),
+        in_specs=[SMEM] + [VMEM] * 4,
+        out_specs=(VMEM,) * len(near),
         scratch_shapes=[shifted],
         compiler_params=params(20),
         cost_estimate=cost(1),
-    )(table, child_parent, child_octant, total, phase, *phi)
+    )(table, total, phase, *phi)
+    sent.update(zip(near, outs))
 
     def between_chips(blocks):
-        moved = []
-        for s, block in enumerate(blocks, 1):
+        moved = dict(blocks)
+        for s in range(chips - 1, 0, -1):
             pairs = [(i, i ^ (CORES * s)) for i in range(members)]
-            moved.append(lax.ppermute(block, "member", pairs))
-        return moved
-
-    arrived = [between_chips(blocks0), between_chips(blocks1)]
+            moved[s] = lax.ppermute(blocks[s], "member", pairs)
+        return [moved[s] for s in range(chips)]
+
+    arrived = between_chips(sent)
 
     theta = theta_table(theta_count, NTC).reshape(chips, CORES, out_rows, chips, CORES, rows)
     theta = theta.transpose(4, 1, 0, 2, 3, 5).reshape(
@@ -370,33 +370,28 @@
     )
     swap = [(i, i ^ 1) for i in range(members)]
     if out_rows % 8 == 0:
-        t_hi, t_lo = split_const(theta)
-        keeps, swapped = [], []
-        for h, first in enumerate((0, sizes[0])):
-            half = shape(sizes[h], 2, chips * out_rows, NPC)
-            away, keep = call(
-                functools.partial(theta_kernel, first),
-                out_shape=(half, half),
-                in_specs=[SMEM] + [VMEM] * (2 + chips),
-                out_specs=(VMEM, VMEM),
-                scratch_shapes=[pltpu.VMEM((chips * rows, NPC), F32)],
-                compiler_params=params(12),
-                cost_estimate=cost(1),
-            )(table, t_hi, t_lo, mine, *arrived[h])
-            keeps.append(keep)
-            swapped.append(lax.ppermute(away, "member", swap))
+        half = shape(per_chip, 2, chips * out_rows, NPC)
+        away, keep = call(
+            theta_kernel,
+            out_shape=(half, half),
+            in_specs=[VMEM] * (2 + chips),
+            out_specs=(VMEM, VMEM),
+            scratch_shapes=[pltpu.VMEM((chips * rows, NPC), F32)],
+            compiler_params=params(12),
+            cost_estimate=cost(1),
+        )(*split_const(theta), *arrived)
+        swapped = lax.ppermute(away, "member", swap)
         pieces = call(
             sum_kernel,
-            out_shape=shape(chips, per_chip, 2, out_rows, NPC),
-            in_specs=[VMEM] * 4,
-            out_specs=VMEM,
+            out_shape=(shape(per_chip, 2, out_rows, NPC),) * chips,
+            in_specs=[VMEM] * 2,
+            out_specs=(VMEM,) * chips,
             compiler_params=params(12),
             cost_estimate=cost(1),
-        )(*keeps, *swapped)
+        )(keep, swapped)
     else:
-        lats = jnp.stack([jnp.concatenate(pair) for pair in zip(*arrived)])
-        lats = jnp.concatenate([mine[None], lats])
-        lats = jnp.take(lats, chip ^ jnp.arange(chips), axis=0)
+        order = chip ^ jnp.arange(chips)
+        lats = jnp.take(jnp.stack(arrived), order, axis=0)
         lats = lats.transpose(1, 2, 0, 3, 4).reshape(per_chip, 2, chips * rows, NPC)
         both = jnp.take(
             jnp.asarray(theta, F32).reshape(CORES, CORES, chips * out_rows, chips * rows),
@@ -407,13 +402,19 @@
         )
         moved = lax.ppermute(jnp.take(sums, 1 - core, axis=0), "member", swap)
         pieces = jnp.take(sums, core, axis=0) + moved
-        pieces = pieces.reshape(per_chip, 2, chips, out_rows, NPC).transpose(2, 0, 1, 3, 4)
-
-    same_core = [list(range(c, members, CORES)) for c in range(CORES)]
-    out = lax.all_to_all(
-        pieces, "member", 0, 0, tiled=True, axis_index_groups=same_core
-    )
-    return out.reshape(children, 2, out_rows, NPC)
+        pieces = pieces.reshape(per_chip, 2, chips, out_rows, NPC)
+        pieces = [jnp.take(pieces, order[s], axis=2) for s in range(chips)]
+
+    final = between_chips(dict(enumerate(pieces)))
+    return call(
+        place_kernel,
+        out_shape=shape(children, 2, out_rows, NPC),
+        in_specs=[VMEM] * chips,
+        out_specs=HBM,
+        scratch_shapes=[pltpu.SemaphoreType.DMA((chips,))],
+        compiler_params=params(12),
+        cost_estimate=cost(1),
+    )(*final)
 
 
 def solution(mesh):

time: 49.4 us -> 47.7 us (0.966)
  waiting for transfers between devices: 6.64 us -> 19 us
  blocking collectives: 11.5 us -> 0 us
  Pallas kernels: 13.5 us -> 10.9 us
  local copies, waits for them, and re-layouts: 1.95 us -> 2.62 us
    ppermute x8 -> x7, waiting for transfers between devices: 6.64 us -> 19 us  [the longest x6 17.1 us: between_chips(): moved[s] = lax.ppermute(blocks[s], 'member', pairs)]
    all_to_all x1 -> x0, blocking collectives: 11.5 us -> none  [on_device(): lax.all_to_all(pieces, 'member', 0, 0, tiled=True, axis_index_groups=same...]
    reshape x0 -> x2, local copies, waits for them, and re-layouts: none -> 1.47 us  [the longest x1 0.74 us: on_device(): child_parent.reshape(-1, terms)]
    pallas_call x5, Pallas kernels: 6.27 us -> 4.95 us  [the longest x1 1.82 us: on_device(): call(functools.partial(first_kernel, far), out_shape=(block,) * len(far)...]
    pallas_call x1, Pallas kernels: 7.28 us -> 5.99 us  [on_device(): pl.pallas_call(functools.partial(own_kernel, theta_count, width), out_sha...]
    unnamed x13 -> x8, local copies, waits for them, and re-layouts: 0.82 us -> 0.01 us
    ppermute x8 -> x7, starting transfers between devices: 7.61 us -> 7.18 us  [the longest x6 7.11 us: between_chips(): moved[s] = lax.ppermute(blocks[s], 'member', pairs)]
  transfers between devices with their start and end apart: 10 -> 9, of which waited for: 5 -> 6; matrix products, arithmetic and copies ran while one was open for 2% -> 5% of each run, Pallas kernels for 23% -> 13%
where the time goes in v1:
time: 47.7 us; the launch traced here: 47.5 us
  waiting for transfers between devices  19 us (40%)
  starting transfers between devices  14.1 us (30%)
  Pallas kernels  10.9 us (23%)
  local copies, waits for them, and re-layouts  2.62 us (5%)
  other arithmetic  0.71 us (1%)
    ppermute x6, waiting for transfers between devices, between_chips(): moved[s] = lax.ppermute(blocks[s], 'member', pairs)  17.1 us
    ppermute x6, starting transfers between devices, between_chips(): moved[s] = lax.ppermute(blocks[s], 'member', pairs)  7.11 us
    pallas_call x1, Pallas kernels, on_device(): pl.pallas_call(functools.partial(own_kernel, theta_count, width), out_sha...  5.99 us
    ppermute x1, starting transfers between devices, on_device(): below = lax.ppermute(patterns[clusters - width:], 'group', up)  5.61 us
    ppermute x1, waiting for transfers between devices, on_device(): swapped = lax.ppermute(away, 'member', swap)  1.9 us
    pallas_call x1, Pallas kernels, on_device(): call(functools.partial(first_kernel, far), out_shape=(block,) * len(far)...  1.82 us
    pallas_call x1, Pallas kernels, on_device(): call(functools.partial(later_kernel, near), out_shape=(block,) * len(near...  1.64 us
    ppermute x1, starting transfers between devices, on_device(): above = lax.ppermute(patterns[:width], 'group', down)  1.29 us
  transfers between devices with their start and end apart: 9, of which 6 were waited for; matrix products, arithmetic and copies ran while one was open for 5% of the time, Pallas kernels for 13%

profile of v1, /device:TPU:0, one launch (start us, length us, event | category | flops | bytes accessed | tf_op | source)
XLA Modules:
  0.0 47.5 jit_solution(13799691308184041055)
XLA Ops:
  0.0 0.0 copy-start
  0.0 0.0 copy-start.1
  0.0 0.0 copy-start.2
  0.0 0.0 copy-start.3
  0.0 1.1 %fusion = (f32[2,2,32,512]{3,2,1,0:T(8,128)S(1)}, f32[2,2,32,512]{3,2,1,0:T(8,128)S(1)}) fusion(f32[8,2,32,512]{3,2,1,0:T(8,128)} %patterns.1), kind=kLoop, calls=%fused_computation.1 | loop fusion | bytes 1048576 | tf_op jit(solution)/shard_map/slice | solution.py:311
  1.2 1.3 %collective-permute-start.1 = (f32[2,2,32,512]{3,2,1,0:T(8,128)S(1)}, f32[2,2,32,512]{3,2,1,0:T(8,128)S(1)}, u32[]{:S(2)}, u32[]{:S(2)}) collective-permute-start(f32[2,2,32,512]{3,2,1,0:T(8,128)S(1)} %get-tuple-element.33), channel_id=1, source_target_pairs={{8,0},{16,8},{24,16},{9,1},{17,9},{25,17},{10,2},{18,10},{26,18},{... | collective-permute-start | bytes 786440 | tf_op jit(solution)/shard_map/ppermute | solution.py:311
  2.5 5.6 %collective-permute-start = (f32[2,2,32,512]{3,2,1,0:T(8,128)S(1)}, f32[2,2,32,512]{3,2,1,0:T(8,128)S(1)}, u32[]{:S(2)}, u32[]{:S(2)}) collective-permute-start(f32[2,2,32,512]{3,2,1,0:T(8,128)S(1)} %get-tuple-element.34), channel_id=1, source_target_pairs={{0,8},{8,16},{16,24},{1,9},{9,17},{17,25},{2,10},{10,18},{18,26},{... | collective-permute-start | bytes 786440 | tf_op jit(solution)/shard_map/ppermute | solution.py:310
  8.1 0.7 %reshape.6 = s32[2,8]{1,0:T(2,128)S(1)} reshape(s32[16]{0:T(128)} %param.14) | data formatting | bytes 128 | tf_op jit(solution)/shard_map/reshape | solution.py:303
  8.8 0.7 %reshape.7 = s32[2,8]{1,0:T(2,128)S(1)} reshape(s32[16]{0:T(128)} %param.15) | data formatting | bytes 128 | tf_op jit(solution)/shard_map/reshape | solution.py:304
  9.5 0.7 %pad_add_fusion.table = s32[20,8]{1,0:T(8,128)S(1)} fusion(s32[2,8]{1,0:T(2,128)S(1)} %reshape.7, s32[2,8]{1,0:T(2,128)S(1)} %reshape.6, s32[8,8]{1,0:T(8,128)} %param.13, s32[8,8]{1,0:T(8,128)} %param.12), kind=kLoop, calls=%fused_computation | loop fusion | flops 480 | bytes 1280 | tf_op jit(solution)/shard_map/concatenate | solution.py:299
  10.3 6.0 %shard_map.100 = (f32[8,2,32,512]{3,2,1,0:T(8,128)S(1)}, f32[32,2,32,512]{3,2,1,0:T(8,128)S(1)}, f32[8,2,32,512]{3,2,1,0:T(8,128)S(1)}) custom-call(s32[20,8]{1,0:T(8,128)S(1)} %pad_add_fusion.table, f32[8,2,32,512]{3,2,1,0:T(8,128)} %patterns.1, f32[100,2,32,512]{3,2,1,0:T(8,128)} %operators.1), custom_call_target="tpu_custom_call" | custom-call | flops 16000000 | tf_op jit(solution)/shard_map/pallas_call | solution.py:315
  16.3 0.0 collective-permute-done.1.above
  16.3 0.0 collective-permute-done.below
  16.3 0.0 copy-done
  16.3 0.0 copy-done.1
  16.3 1.8 %shard_map.101 = (f32[4,2,32,256]{3,2,1,0:T(8,128)S(1)}, f32[8,2,32,512]{3,2,1,0:T(8,128)S(1)}) custom-call(s32[20,8]{1,0:T(8,128)S(1)} %pad_add_fusion.table, f32[8,2,32,512]{3,2,1,0:T(8,128)S(1)} %get-tuple-element.19.own, f32[32,2,32,512]{3,2,1,0:T(8,128)S(1)} %get-tuple-element.20.edge_ops, f32[2,2,32,512]{3,2,1,0:T(8,128)S(1)} %collective-permute-done.below, ...), custom_call_target="tpu_custom_call" | custom-call | flops 4000000 | tf_op jit(solution)/shard_map/pallas_call | solution.py:337
  18.1 1.6 %shard_map.102 = (f32[4,2,32,256]{3,2,1,0:T(8,128)S(1)}, f32[4,2,32,256]{3,2,1,0:T(8,128)S(1)}, f32[4,2,32,256]{3,2,1,0:T(8,128)S(1)}) custom-call(s32[20,8]{1,0:T(8,128)S(1)} %pad_add_fusion.table, f32[8,2,32,512]{3,2,1,0:T(8,128)S(1)} %get-tuple-element.22.total, f32[8,2,32,512]{3,2,1,0:T(8,128)S(1)} %get-tuple-element.21.phase, ...), custom_call_target="tpu_custom_call" | custom-call | flops 2000000 | tf_op jit(solution)/shard_map/pallas_call | solution.py:347
  19.8 2.0 %collective-permute-start.2 = (f32[4,2,32,256]{3,2,1,0:T(8,128)S(1)}, f32[4,2,32,256]{3,2,1,0:T(8,128)S(1)}, u32[]{:S(2)}, u32[]{:S(2)}) collective-permute-start(f32[4,2,32,256]{3,2,1,0:T(8,128)S(1)} %get-tuple-element.24), channel_id=1, source_target_pairs={{0,2},{1,3},{2,0},{3,1},{4,6},{5,7},{6,4},{7,5},{8,10},{9,11},{10,... | collective-permute-start | bytes 786440 | tf_op jit(solution)/shard_map/ppermute | solution.py:362
  21.8 1.5 %collective-permute-start.3 = (f32[4,2,32,256]{3,2,1,0:T(8,128)S(1)}, f32[4,2,32,256]{3,2,1,0:T(8,128)S(1)}, u32[]{:S(2)}, u32[]{:S(2)}) collective-permute-start(f32[4,2,32,256]{3,2,1,0:T(8,128)S(1)} %get-tuple-element.25), channel_id=1, source_target_pairs={{0,4},{1,5},{2,6},{3,7},{4,0},{5,1},{6,2},{7,3},{8,12},{9,13},{10,... | collective-permute-start | bytes 786440 | tf_op jit(solution)/shard_map/ppermute | solution.py:362
  23.3 0.0 collective-permute-start.4
  23.3 5.7 %collective-permute-done.2.rest_1_ = f32[4,2,32,256]{3,2,1,0:T(8,128)S(1)} collective-permute-done((f32[4,2,32,256]{3,2,1,0:T(8,128)S(1)}, f32[4,2,32,256]{3,2,1,0:T(8,128)S(1)}, u32[]{:S(2)}, u32[]{:S(2)}) %collective-permute-start.2) | collective-permute-done | bytes 262176 | tf_op jit(solution)/shard_map/ppermute | solution.py:362
  29.0 5.6 %collective-permute-done.3.rest_2_ = f32[4,2,32,256]{3,2,1,0:T(8,128)S(1)} collective-permute-done((f32[4,2,32,256]{3,2,1,0:T(8,128)S(1)}, f32[4,2,32,256]{3,2,1,0:T(8,128)S(1)}, u32[]{:S(2)}, u32[]{:S(2)}) %collective-permute-start.3) | collective-permute-done | bytes 262176 | tf_op jit(solution)/shard_map/ppermute | solution.py:362
  34.6 0.0 collective-permute-done.4.rest_3_
  34.6 0.0 copy-done.2
  34.6 0.0 copy-done.3
  34.6 0.6 %shard_map.103 = (f32[4,2,64,256]{3,2,1,0:T(8,128)S(1)}, f32[4,2,64,256]{3,2,1,0:T(8,128)S(1)}) custom-call(bf16[4,64,128]{2,1,0:T(8,128)(2,1)S(1)} %copy-done.3, bf16[4,64,128]{2,1,0:T(8,128)(2,1)S(1)} %copy-done.2, f32[4,2,32,256]{3,2,1,0:T(8,128)S(1)} %get-tuple-element.23.rest_0_, f32[4,2,32,256]{3,2,1,0:T(8,128)S(1)} %collective-permute-done.2.rest_1_, ...), custom_call_target="tpu_custom_call" | custom-call | flops 2000000 | tf_op jit(solution)/shard_map/pallas_call | solution.py:374
  35.2 0.1 collective-permute-start.5
  35.3 1.9 %collective-permute-done.5.arrived = f32[4,2,64,256]{3,2,1,0:T(8,128)S(1)} collective-permute-done((f32[4,2,64,256]{3,2,1,0:T(8,128)S(1)}, f32[4,2,64,256]{3,2,1,0:T(8,128)S(1)}, u32[]{:S(2)}, u32[]{:S(2)}) %collective-permute-start.5) | collective-permute-done | bytes 524320 | tf_op jit(solution)/shard_map/ppermute | solution.py:383
  37.2 0.1 shard_map.104
  37.3 1.3 %collective-permute-start.6 = (f32[4,2,16,256]{3,2,1,0:T(8,128)S(1)}, f32[4,2,16,256]{3,2,1,0:T(8,128)S(1)}, u32[]{:S(2)}, u32[]{:S(2)}) collective-permute-start(f32[4,2,16,256]{3,2,1,0:T(8,128)S(1)} %get-tuple-element.30), channel_id=1, source_target_pairs={{0,2},{1,3},{2,0},{3,1},{4,6},{5,7},{6,4},{7,5},{8,10},{9,11},{10,... | collective-permute-start | bytes 393224 | tf_op jit(solution)/shard_map/ppermute | solution.py:362
  38.6 0.8 %collective-permute-start.7 = (f32[4,2,16,256]{3,2,1,0:T(8,128)S(1)}, f32[4,2,16,256]{3,2,1,0:T(8,128)S(1)}, u32[]{:S(2)}, u32[]{:S(2)}) collective-permute-start(f32[4,2,16,256]{3,2,1,0:T(8,128)S(1)} %get-tuple-element.31), channel_id=1, source_target_pairs={{0,4},{1,5},{2,6},{3,7},{4,0},{5,1},{6,2},{7,3},{8,12},{9,13},{10,... | collective-permute-start | bytes 393224 | tf_op jit(solution)/shard_map/ppermute | solution.py:362
  39.4 1.4 %collective-permute-start.8 = (f32[4,2,16,256]{3,2,1,0:T(8,128)S(1)}, f32[4,2,16,256]{3,2,1,0:T(8,128)S(1)}, u32[]{:S(2)}, u32[]{:S(2)}) collective-permute-start(f32[4,2,16,256]{3,2,1,0:T(8,128)S(1)} %get-tuple-element.32), channel_id=1, source_target_pairs={{0,6},{1,7},{2,4},{3,5},{4,2},{5,3},{6,0},{7,1},{8,14},{9,15},{10,... | collective-permute-start | bytes 393224 | tf_op jit(solution)/shard_map/ppermute | solution.py:362
  40.8 2.7 %collective-permute-done.6.rest_1_ = f32[4,2,16,256]{3,2,1,0:T(8,128)S(1)} collective-permute-done((f32[4,2,16,256]{3,2,1,0:T(8,128)S(1)}, f32[4,2,16,256]{3,2,1,0:T(8,128)S(1)}, u32[]{:S(2)}, u32[]{:S(2)}) %collective-permute-start.6) | collective-permute-done | bytes 131104 | tf_op jit(solution)/shard_map/ppermute | solution.py:362
  43.6 1.5 %collective-permute-done.7.rest_2_ = f32[4,2,16,256]{3,2,1,0:T(8,128)S(1)} collective-permute-done((f32[4,2,16,256]{3,2,1,0:T(8,128)S(1)}, f32[4,2,16,256]{3,2,1,0:T(8,128)S(1)}, u32[]{:S(2)}, u32[]{:S(2)}) %collective-permute-start.7) | collective-permute-done | bytes 131104 | tf_op jit(solution)/shard_map/ppermute | solution.py:362
  45.0 1.6 %collective-permute-done.8.rest_3_ = f32[4,2,16,256]{3,2,1,0:T(8,128)S(1)} collective-permute-done((f32[4,2,16,256]{3,2,1,0:T(8,128)S(1)}, f32[4,2,16,256]{3,2,1,0:T(8,128)S(1)}, u32[]{:S(2)}, u32[]{:S(2)}) %collective-permute-start.8) | collective-permute-done | bytes 131104 | tf_op jit(solution)/shard_map/ppermute | solution.py:362
  46.6 0.8 %shard_map.105 = f32[16,2,16,256]{3,2,1,0:T(8,128)} custom-call(f32[4,2,16,256]{3,2,1,0:T(8,128)S(1)} %get-tuple-element.29.rest_0_, f32[4,2,16,256]{3,2,1,0:T(8,128)S(1)} %collective-permute-done.6.rest_1_, f32[4,2,16,256]{3,2,1,0:T(8,128)S(1)} %collective-permute-done.7.rest_2_, f32[4,2,16,256]{3,2,1,0:T(8,128)S(1)} %collective-permute-done.8.rest_3_), custom_call_target="tpu_custom_call" | custom-call | flops 2000000 | tf_op jit(solution)/shard_map/pallas_call | solution.py:409
Async XLA Ops:
  0.0 16.3 %copy-start = (bf16[512,256]{1,0:T(8,128)(2,1)S(1)}, bf16[512,256]{1,0:T(8,128)(2,1)}, u32[]{:S(2)}) copy-start(bf16[512,256]{1,0:T(8,128)(2,1)} %constant.9.clone.phi_lo) | copy-start | bytes 786436
  0.0 16.3 %copy-start.1 = (bf16[512,256]{1,0:T(8,128)(2,1)S(1)}, bf16[512,256]{1,0:T(8,128)(2,1)}, u32[]{:S(2)}) copy-start(bf16[512,256]{1,0:T(8,128)(2,1)} %constant.8.clone.phi_hi) | copy-start | bytes 786436
  0.0 34.6 %copy-start.2 = (bf16[4,64,128]{2,1,0:T(8,128)(2,1)S(1)}, bf16[4,64,128]{2,1,0:T(8,128)(2,1)}, u32[]{:S(2)}) copy-start(bf16[4,64,128]{2,1,0:T(8,128)(2,1)} %constant.11.clone.t_lo) | copy-start | bytes 196612
  0.0 34.6 %copy-start.3 = (bf16[4,64,128]{2,1,0:T(8,128)(2,1)S(1)}, bf16[4,64,128]{2,1,0:T(8,128)(2,1)}, u32[]{:S(2)}) copy-start(bf16[4,64,128]{2,1,0:T(8,128)(2,1)} %constant.10.clone.t_hi) | copy-start | bytes 196612
  1.2 15.1 %collective-permute-start.1 = (f32[2,2,32,512]{3,2,1,0:T(8,128)S(1)}, f32[2,2,32,512]{3,2,1,0:T(8,128)S(1)}, u32[]{:S(2)}, u32[]{:S(2)}) collective-permute-start(f32[2,2,32,512]{3,2,1,0:T(8,128)S(1)} %get-tuple-element.33), channel_id=1, source_target_pairs={{8,0},{16,8},{24,16},{9,1},{17,9},{25,17},{10,2},{18,10},{26,18},{... | collective-permute-start | bytes 786440 | tf_op jit(solution)/shard_map/ppermute | solution.py:311
  2.5 13.8 %collective-permute-start = (f32[2,2,32,512]{3,2,1,0:T(8,128)S(1)}, f32[2,2,32,512]{3,2,1,0:T(8,128)S(1)}, u32[]{:S(2)}, u32[]{:S(2)}) collective-permute-start(f32[2,2,32,512]{3,2,1,0:T(8,128)S(1)} %get-tuple-element.34), channel_id=1, source_target_pairs={{0,8},{8,16},{16,24},{1,9},{9,17},{17,25},{2,10},{10,18},{18,26},{... | collective-permute-start | bytes 786440 | tf_op jit(solution)/shard_map/ppermute | solution.py:310
  19.8 9.2 %collective-permute-start.2 = (f32[4,2,32,256]{3,2,1,0:T(8,128)S(1)}, f32[4,2,32,256]{3,2,1,0:T(8,128)S(1)}, u32[]{:S(2)}, u32[]{:S(2)}) collective-permute-start(f32[4,2,32,256]{3,2,1,0:T(8,128)S(1)} %get-tuple-element.24), channel_id=1, source_target_pairs={{0,2},{1,3},{2,0},{3,1},{4,6},{5,7},{6,4},{7,5},{8,10},{9,11},{10,... | collective-permute-start | bytes 786440 | tf_op jit(solution)/shard_map/ppermute | solution.py:362
  21.8 12.8 %collective-permute-start.3 = (f32[4,2,32,256]{3,2,1,0:T(8,128)S(1)}, f32[4,2,32,256]{3,2,1,0:T(8,128)S(1)}, u32[]{:S(2)}, u32[]{:S(2)}) collective-permute-start(f32[4,2,32,256]{3,2,1,0:T(8,128)S(1)} %get-tuple-element.25), channel_id=1, source_target_pairs={{0,4},{1,5},{2,6},{3,7},{4,0},{5,1},{6,2},{7,3},{8,12},{9,13},{10,... | collective-permute-start | bytes 786440 | tf_op jit(solution)/shard_map/ppermute | solution.py:362
  23.3 11.3 %collective-permute-start.4 = (f32[4,2,32,256]{3,2,1,0:T(8,128)S(1)}, f32[4,2,32,256]{3,2,1,0:T(8,128)S(1)}, u32[]{:S(2)}, u32[]{:S(2)}) collective-permute-start(f32[4,2,32,256]{3,2,1,0:T(8,128)S(1)} %get-tuple-element.26), channel_id=1, source_target_pairs={{0,6},{1,7},{2,4},{3,5},{4,2},{5,3},{6,0},{7,1},{8,14},{9,15},{10,... | collective-permute-start | bytes 786440 | tf_op jit(solution)/shard_map/ppermute | solution.py:362
  35.2 2.0 %collective-permute-start.5 = (f32[4,2,64,256]{3,2,1,0:T(8,128)S(1)}, f32[4,2,64,256]{3,2,1,0:T(8,128)S(1)}, u32[]{:S(2)}, u32[]{:S(2)}) collective-permute-start(f32[4,2,64,256]{3,2,1,0:T(8,128)S(1)} %get-tuple-element.28), channel_id=1, source_target_pairs={{0,1},{1,0},{2,3},{3,2},{4,5},{5,4},{6,7},{7,6},{8,9},{9,8},{10,11... | collective-permute-start | bytes 1572872 | tf_op jit(solution)/shard_map/ppermute | solution.py:383
  37.3 6.3 %collective-permute-start.6 = (f32[4,2,16,256]{3,2,1,0:T(8,128)S(1)}, f32[4,2,16,256]{3,2,1,0:T(8,128)S(1)}, u32[]{:S(2)}, u32[]{:S(2)}) collective-permute-start(f32[4,2,16,256]{3,2,1,0:T(8,128)S(1)} %get-tuple-element.30), channel_id=1, source_target_pairs={{0,2},{1,3},{2,0},{3,1},{4,6},{5,7},{6,4},{7,5},{8,10},{9,11},{10,... | collective-permute-start | bytes 393224 | tf_op jit(solution)/shard_map/ppermute | solution.py:362
  38.6 6.5 %collective-permute-start.7 = (f32[4,2,16,256]{3,2,1,0:T(8,128)S(1)}, f32[4,2,16,256]{3,2,1,0:T(8,128)S(1)}, u32[]{:S(2)}, u32[]{:S(2)}) collective-permute-start(f32[4,2,16,256]{3,2,1,0:T(8,128)S(1)} %get-tuple-element.31), channel_id=1, source_target_pairs={{0,4},{1,5},{2,6},{3,7},{4,0},{5,1},{6,2},{7,3},{8,12},{9,13},{10,... | collective-permute-start | bytes 393224 | tf_op jit(solution)/shard_map/ppermute | solution.py:362
  39.4 7.2 %collective-permute-start.8 = (f32[4,2,16,256]{3,2,1,0:T(8,128)S(1)}, f32[4,2,16,256]{3,2,1,0:T(8,128)S(1)}, u32[]{:S(2)}, u32[]{:S(2)}) collective-permute-start(f32[4,2,16,256]{3,2,1,0:T(8,128)S(1)} %get-tuple-element.32), channel_id=1, source_target_pairs={{0,6},{1,7},{2,4},{3,5},{4,2},{5,3},{6,0},{7,1},{8,14},{9,15},{10,... | collective-permute-start | bytes 393224 | tf_op jit(solution)/shard_map/ppermute | solution.py:362

commit v2 on v1

--- a/solution.py
+++ b/solution.py
@@ -92,11 +92,20 @@
 
 
 def own_kernel(
-    theta_count, width, table, patterns, operators, out, edge_ops, phase,
-    mine, held, sems, mine_sem,
+    theta_count, width, partners_hbm, op_index_hbm, patterns, operators, out, edge_ops, phase,
+    mine, held, partners, op_index, sems, more_sems,
 ):
-    clusters, _, rows, _ = out.shape
-    terms = table.shape[1]
+    clusters, terms = partners.shape
+    rows = out.shape[2]
+    tables = [
+        pltpu.make_async_copy(op_index_hbm, op_index, more_sems.at[0]),
+        pltpu.make_async_copy(partners_hbm, partners, more_sems.at[1]),
+        pltpu.make_async_copy(patterns, mine, more_sems.at[2]),
+    ]
+    for copy in tables:
+        copy.start()
+    phase_tables(lax.axis_index("member"), theta_count, phase)
+    tables[0].wait()
     inner = clusters - 2 * width
 
     def slot(c):
@@ -105,39 +114,38 @@
     def fetch_edge(c, p):
         e = slot(c) + p
         return pltpu.make_async_copy(
-            operators.at[table[clusters + c, p]], edge_ops.at[e], sems.at[c * terms + p]
+            operators.at[op_index[c, p]], edge_ops.at[e], sems.at[c * terms + p]
         )
 
     def fetch_inner(c, p):
         return pltpu.make_async_copy(
-            operators.at[table[clusters + c, p]], held.at[(c - width) * terms + p],
+            operators.at[op_index[c, p]], held.at[(c - width) * terms + p],
             sems.at[c * terms + p],
         )
 
-    whole = pltpu.make_async_copy(patterns, mine, mine_sem)
-    whole.start()
-
     def edge_cluster(n):
         return jnp.where(n < width, n, n + inner)
 
-    @pl.loop(0, inner * terms)
-    def _(e):
-        fetch_inner(width + e // terms, e % terms).start()
-
-    @pl.loop(0, 2 * width * terms)
-    def _(e):
-        fetch_edge(edge_cluster(e // terms), e % terms).start()
-
-    phase_tables(lax.axis_index("member"), theta_count, phase)
+    @pl.loop(width, clusters - width)
+    def _(c):
+        for p in range(terms):
+            fetch_inner(c, p).start()
+
+    @pl.loop(0, 2 * width)
+    def _(n):
+        for p in range(terms):
+            fetch_edge(edge_cluster(n), p).start()
+
     base = lax.axis_index("group") * clusters
-    whole.wait()
+    tables[1].wait()
+    tables[2].wait()
 
     def translate(c, ops, first):
         for r in range(rows // 8):
             band = pl.ds(r * 8, 8)
             re, im = 0.0, 0.0
             for p in range(terms):
-                q = table[c, p] - base
+                q = partners[c, p] - base
                 keep = jnp.where((q >= 0) & (q < clusters), 1.0, 0.0).astype(F32)
                 q = jnp.clip(q, 0, clusters - 1)
                 ore, oim = ops[first + p, 0, band, :], ops[first + p, 1, band, :]
@@ -161,9 +169,9 @@
         translate(c, edge_ops, n * terms)
 
 
-def halo_terms(table, own, edge_ops, below, above, total):
+def halo_terms(partners, own, edge_ops, below, above, total):
     clusters, _, rows, _ = own.shape
-    terms = table.shape[1]
+    terms = partners.shape[1]
     width = below.shape[0]
     base = lax.axis_index("group") * clusters
     total[...] = own[...]
@@ -175,12 +183,12 @@
 
         @pl.loop(0, terms)
         def _(p):
-            q = table[c, p] - base
+            q = partners[c, p] - base
 
             @pl.when((q < 0) | (q >= clusters))
             def _():
                 e = n * terms + p
-                h = jnp.clip(table[c, p] + shift, 0, width - 1)
+                h = jnp.clip(partners[c, p] + shift, 0, width - 1)
                 for r in range(rows // 8):
                     band = pl.ds(r * 8, 8)
                     ore, oim = edge_ops[e, 0, band, :], edge_ops[e, 1, band, :]
@@ -189,19 +197,17 @@
                     total[c, 1, band, :] += ore * pim + oim * pre
 
 
-def shift_and_phi(order, table, total, phase, phi_hi, phi_lo, outs, shifted):
+def shift_and_phi(
+    order, child_parent, child_octant, total, phase, phi_hi, phi_lo, outs, shifted
+):
     clusters, _, rows, _ = total.shape
-    terms = table.shape[1]
     base = lax.axis_index("group") * clusters
     chip = lax.axis_index("member") // CORES
-    parents = 2 * clusters
-    octants = parents + (table.shape[0] - parents) // 2
     for s, out in zip(order, outs):
         first = (chip ^ s) * out.shape[0]
         for i in range(out.shape[0]):
-            row, column = (first + i) // terms, (first + i) % terms
-            q = table[parents + row, column] - base
-            o = table[octants + row, column]
+            q = child_parent[first + i] - base
+            o = child_octant[first + i]
             for r in range(rows // 8):
                 band = pl.ds(r * 8, 8)
                 pre, pim = total[q, 0, band, :], total[q, 1, band, :]
@@ -214,31 +220,34 @@
 
 
 def first_kernel(
-    order, table, own, edge_ops, below, above, phase, phi_hi, phi_lo, *rest
+    order, partners, child_parent, child_octant, own, edge_ops, below, above, phase, phi_hi,
+    phi_lo, *rest
 ):
     outs, (total, shifted) = rest[:-2], rest[-2:]
-    halo_terms(table, own, edge_ops, below, above, total)
-    shift_and_phi(order, table, total, phase, phi_hi, phi_lo, outs, shifted)
-
-
-def later_kernel(order, table, total, phase, phi_hi, phi_lo, *rest):
-    shift_and_phi(order, table, total, phase, phi_hi, phi_lo, rest[:-1], rest[-1])
-
-
-def theta_kernel(t_hi, t_lo, *rest):
-    blocks, (away, keep, lats) = rest[:-3], rest[-3:]
+    halo_terms(partners, own, edge_ops, below, above, total)
+    shift_and_phi(
+        order, child_parent, child_octant, total, phase, phi_hi, phi_lo, outs, shifted
+    )
+
+
+def later_kernel(order, child_parent, child_octant, total, phase, phi_hi, phi_lo, *rest):
+    shift_and_phi(
+        order, child_parent, child_octant, total, phase, phi_hi, phi_lo, rest[:-1], rest[-1]
+    )
+
+
+def theta_kernel(away, t_hi, t_lo, *rest):
+    blocks, (out, lats) = rest[:-2], rest[-2:]
     member = lax.axis_index("member")
     chip, core = member // CORES, member % CORES
+    t = core * CORES + (1 - core if away else core)
     per_chip, _, rows, _ = blocks[0].shape
     for i in range(per_chip):
         for part in range(2):
             for s, block in enumerate(blocks):
                 at = pl.multiple_of((chip ^ s) * rows, rows)
                 lats[pl.ds(at, rows), :] = block[i, part]
-            x = split(lats[...])
-            for out, which in ((away, 1 - core), (keep, core)):
-                t = core * CORES + which
-                out[i, part] = dot3((t_hi[t], t_lo[t]), x)
+            out[i, part] = dot3((t_hi[t], t_lo[t]), split(lats[...]))
 
 
 def sum_kernel(keep, arrived, *outs):
@@ -296,15 +305,6 @@
     member = lax.axis_index("member")
     chip, core = member // CORES, member % CORES
     terms = partners.shape[1]
-    table = jnp.concatenate(
-        [
-            partners,
-            operator_index,
-            child_parent.reshape(-1, terms),
-            child_octant.reshape(-1, terms),
-        ]
-    )
-
     up = [(i, i + 1) for i in range(groups - 1)]
     down = [(i + 1, i) for i in range(groups - 1)]
     below = lax.ppermute(patterns[clusters - width:], "group", up)
@@ -317,17 +317,19 @@
         out_shape=(
             total_shape, shape(edge, 2, rows, lons), shape(8, 2, rows, lons),
         ),
-        in_specs=[SMEM, HBM, HBM],
+        in_specs=[HBM] * 4,
         out_specs=(VMEM, VMEM, VMEM),
         scratch_shapes=[
             pltpu.VMEM((clusters, 2, rows, lons), F32),
             pltpu.VMEM((clusters * terms - edge, 2, rows, lons), F32),
+            pltpu.SMEM((clusters, terms), jnp.int32),
+            pltpu.SMEM((clusters, terms), jnp.int32),
             pltpu.SemaphoreType.DMA((clusters * terms,)),
-            pltpu.SemaphoreType.DMA,
+            pltpu.SemaphoreType.DMA((3,)),
         ],
         compiler_params=params(20),
         cost_estimate=cost(8),
-    )(table, in_hbm(patterns), in_hbm(operators))
+    )(in_hbm(partners), in_hbm(operator_index), in_hbm(patterns), in_hbm(operators))
 
     phi = split_const(phi_table(lons, NPC).T)
     block = shape(per_chip, 2, rows, NPC)
@@ -337,22 +339,24 @@
     *outs, total = call(
         functools.partial(first_kernel, far),
         out_shape=(block,) * len(far) + (total_shape,),
-        in_specs=[SMEM] + [VMEM] * 7,
+        in_specs=[SMEM] * 3 + [VMEM] * 7,
         out_specs=(VMEM,) * (len(far) + 1),
         scratch_shapes=[shifted],
         compiler_params=params(20),
         cost_estimate=cost(2),
-    )(table, own, edge_ops, below, above, phase, *phi)
+    )(
+        partners, child_parent, child_octant, own, edge_ops, below, above, phase, *phi
+    )
     sent.update(zip(far, outs))
     outs = call(
         functools.partial(later_kernel, near),
         out_shape=(block,) * len(near),
-        in_specs=[SMEM] + [VMEM] * 4,
+        in_specs=[SMEM] * 2 + [VMEM] * 4,
         out_specs=(VMEM,) * len(near),
         scratch_shapes=[shifted],
         compiler_params=params(20),
         cost_estimate=cost(1),
-    )(table, total, phase, *phi)
+    )(child_parent, child_octant, total, phase, *phi)
     sent.update(zip(near, outs))
 
     def between_chips(blocks):
@@ -371,15 +375,18 @@
     swap = [(i, i ^ 1) for i in range(members)]
     if out_rows % 8 == 0:
         half = shape(per_chip, 2, chips * out_rows, NPC)
-        away, keep = call(
-            theta_kernel,
-            out_shape=(half, half),
-            in_specs=[VMEM] * (2 + chips),
-            out_specs=(VMEM, VMEM),
-            scratch_shapes=[pltpu.VMEM((chips * rows, NPC), F32)],
-            compiler_params=params(12),
-            cost_estimate=cost(1),
-        )(*split_const(theta), *arrived)
+        away, keep = (
+            call(
+                functools.partial(theta_kernel, name == "away"),
+                out_shape=half,
+                in_specs=[VMEM] * (2 + chips),
+                out_specs=VMEM,
+                scratch_shapes=[pltpu.VMEM((chips * rows, NPC), F32)],
+                compiler_params=params(12),
+                cost_estimate=cost(1),
+            )(*split_const(theta), *arrived)
+            for name in ("away", "keep")
+        )
         swapped = lax.ppermute(away, "member", swap)
         pieces = call(
             sum_kernel,

time: 47.7 us -> 44.8 us (0.939)
  local copies, waits for them, and re-layouts: 2.62 us -> 1.16 us
  other arithmetic: 0.71 us -> 0 us
  waiting for transfers between devices: 19 us -> 18.5 us
    reshape x2 -> x0, local copies, waits for them, and re-layouts: 1.47 us -> none  [the longest x1 0.74 us: on_device(): child_parent.reshape(-1, terms)]
    concatenate x1 -> x0, other arithmetic: 0.71 us -> none  [on_device(): jnp.concatenate([partners, operator_index, child_parent.reshape(-1, terms...]
  transfers between devices with their start and end apart: 9 -> 9, of which waited for: 6 -> 6; matrix products, arithmetic and copies ran while one was open for 5% -> 0% of each run, Pallas kernels for 13% -> 14%
where the time goes in v2:
time: 44.8 us; the launch traced here: 44.6 us
  waiting for transfers between devices  18.5 us (41%)
  starting transfers between devices  14.1 us (31%)
  Pallas kernels  10.7 us (24%)
  local copies, waits for them, and re-layouts  1.16 us (3%)
    ppermute x6, waiting for transfers between devices, between_chips(): moved[s] = lax.ppermute(blocks[s], 'member', pairs)  17.1 us
    ppermute x6, starting transfers between devices, between_chips(): moved[s] = lax.ppermute(blocks[s], 'member', pairs)  7.11 us
    pallas_call x1, Pallas kernels, on_device(): pl.pallas_call(functools.partial(own_kernel, theta_count, width), out_sha...  5.7 us
    ppermute x1, starting transfers between devices, on_device(): below = lax.ppermute(patterns[clusters - width:], 'group', up)  5.61 us
    pallas_call x1, Pallas kernels, on_device(): call(functools.partial(first_kernel, far), out_shape=(block,) * len(far)...  1.71 us
    pallas_call x1, Pallas kernels, on_device(): call(functools.partial(later_kernel, near), out_shape=(block,) * len(near...  1.5 us
    ppermute x1, waiting for transfers between devices, on_device(): swapped = lax.ppermute(away, 'member', swap)  1.43 us
    ppermute x1, starting transfers between devices, on_device(): above = lax.ppermute(patterns[:width], 'group', down)  1.29 us
  transfers between devices with their start and end apart: 9, of which 6 were waited for; matrix products, arithmetic and copies ran while one was open for 0% of the time, Pallas kernels for 14%

profile of v2, /device:TPU:0, one launch (start us, length us, event | category | flops | bytes accessed | tf_op | source)
XLA Modules:
  0.0 44.6 jit_solution(2297783299844752544)
XLA Ops:
  0.0 0.0 copy-start
  0.0 0.0 copy-start.1
  0.0 0.0 copy-start.2
  0.0 0.0 copy-start.3
  0.0 0.0 copy-start.4
  0.0 0.0 copy-start.6
  0.0 0.0 copy-start.5
  0.0 1.1 %fusion = (f32[2,2,32,512]{3,2,1,0:T(8,128)S(1)}, f32[2,2,32,512]{3,2,1,0:T(8,128)S(1)}) fusion(f32[8,2,32,512]{3,2,1,0:T(8,128)} %patterns.1), kind=kLoop, calls=%fused_computation | loop fusion | bytes 1048576 | tf_op jit(solution)/shard_map/slice | solution.py:311
  1.2 1.3 %collective-permute-start.1 = (f32[2,2,32,512]{3,2,1,0:T(8,128)S(1)}, f32[2,2,32,512]{3,2,1,0:T(8,128)S(1)}, u32[]{:S(2)}, u32[]{:S(2)}) collective-permute-start(f32[2,2,32,512]{3,2,1,0:T(8,128)S(1)} %get-tuple-element.29), channel_id=1, source_target_pairs={{8,0},{16,8},{24,16},{9,1},{17,9},{25,17},{10,2},{18,10},{26,18},{... | collective-permute-start | bytes 786440 | tf_op jit(solution)/shard_map/ppermute | solution.py:311
  2.5 5.6 %collective-permute-start = (f32[2,2,32,512]{3,2,1,0:T(8,128)S(1)}, f32[2,2,32,512]{3,2,1,0:T(8,128)S(1)}, u32[]{:S(2)}, u32[]{:S(2)}) collective-permute-start(f32[2,2,32,512]{3,2,1,0:T(8,128)S(1)} %get-tuple-element.30), channel_id=1, source_target_pairs={{0,8},{8,16},{16,24},{1,9},{9,17},{17,25},{2,10},{10,18},{18,26},{... | collective-permute-start | bytes 786440 | tf_op jit(solution)/shard_map/ppermute | solution.py:310
  8.1 5.7 %shard_map.118 = (f32[8,2,32,512]{3,2,1,0:T(8,128)S(1)}, f32[32,2,32,512]{3,2,1,0:T(8,128)S(1)}, f32[8,2,32,512]{3,2,1,0:T(8,128)S(1)}) custom-call(s32[8,8]{1,0:T(8,128)} %partners.1, s32[8,8]{1,0:T(8,128)} %op_index_hbm.1, f32[8,2,32,512]{3,2,1,0:T(8,128)} %patterns.1, f32[100,2,32,512]{3,2,1,0:T(8,128)} %operators.1), custom_call_target="tpu_custom_call" | custom-call | flops 16000000 | tf_op jit(solution)/shard_map/pallas_call | solution.py:315
  13.8 0.0 collective-permute-done.1.above
  13.8 0.0 collective-permute-done.below
  13.8 0.0 copy-done
  13.8 0.0 copy-done.1
  13.9 0.0 copy-done.4
  13.9 0.0 copy-done.6
  13.9 0.0 copy-done.5
  13.9 1.7 %shard_map.119 = (f32[4,2,32,256]{3,2,1,0:T(8,128)S(1)}, f32[8,2,32,512]{3,2,1,0:T(8,128)S(1)}) custom-call(s32[8,8]{1,0:T(8,128)S(1)} %copy-done.4, s32[16]{0:T(128)S(1)} %copy-done.5, s32[16]{0:T(128)S(1)} %copy-done.6, f32[8,2,32,512]{3,2,1,0:T(8,128)S(1)} %get-tuple-element.17.own, f32[32,2,32,512]{3,2,1,0:T(8,128)S(1)} %get-tuple-element.18.edge_ops, ...), custom_call_target="tpu_custom_call" | custom-call | flops 4000000 | tf_op jit(solution)/shard_map/pallas_call | solution.py:339
  15.6 1.5 %shard_map.120 = (f32[4,2,32,256]{3,2,1,0:T(8,128)S(1)}, f32[4,2,32,256]{3,2,1,0:T(8,128)S(1)}, f32[4,2,32,256]{3,2,1,0:T(8,128)S(1)}) custom-call(s32[16]{0:T(128)S(1)} %copy-done.5, s32[16]{0:T(128)S(1)} %copy-done.6, f32[8,2,32,512]{3,2,1,0:T(8,128)S(1)} %get-tuple-element.20.total, f32[8,2,32,512]{3,2,1,0:T(8,128)S(1)} %get-tuple-element.19.phase, ...), custom_call_target="tpu_custom_call" | custom-call | flops 2000000 | tf_op jit(solution)/shard_map/pallas_call | solution.py:351
  17.1 2.0 %collective-permute-start.2 = (f32[4,2,32,256]{3,2,1,0:T(8,128)S(1)}, f32[4,2,32,256]{3,2,1,0:T(8,128)S(1)}, u32[]{:S(2)}, u32[]{:S(2)}) collective-permute-start(f32[4,2,32,256]{3,2,1,0:T(8,128)S(1)} %get-tuple-element.22), channel_id=1, source_target_pairs={{0,2},{1,3},{2,0},{3,1},{4,6},{5,7},{6,4},{7,5},{8,10},{9,11},{10,... | collective-permute-start | bytes 786440 | tf_op jit(solution)/shard_map/ppermute | solution.py:366
  19.1 1.5 %collective-permute-start.3 = (f32[4,2,32,256]{3,2,1,0:T(8,128)S(1)}, f32[4,2,32,256]{3,2,1,0:T(8,128)S(1)}, u32[]{:S(2)}, u32[]{:S(2)}) collective-permute-start(f32[4,2,32,256]{3,2,1,0:T(8,128)S(1)} %get-tuple-element.23), channel_id=1, source_target_pairs={{0,4},{1,5},{2,6},{3,7},{4,0},{5,1},{6,2},{7,3},{8,12},{9,13},{10,... | collective-permute-start | bytes 786440 | tf_op jit(solution)/shard_map/ppermute | solution.py:366
  20.6 0.0 collective-permute-start.4
  20.7 5.7 %collective-permute-done.2.rest_1_ = f32[4,2,32,256]{3,2,1,0:T(8,128)S(1)} collective-permute-done((f32[4,2,32,256]{3,2,1,0:T(8,128)S(1)}, f32[4,2,32,256]{3,2,1,0:T(8,128)S(1)}, u32[]{:S(2)}, u32[]{:S(2)}) %collective-permute-start.2) | collective-permute-done | bytes 262176 | tf_op jit(solution)/shard_map/ppermute | solution.py:366
  26.3 5.6 %collective-permute-done.3.rest_2_ = f32[4,2,32,256]{3,2,1,0:T(8,128)S(1)} collective-permute-done((f32[4,2,32,256]{3,2,1,0:T(8,128)S(1)}, f32[4,2,32,256]{3,2,1,0:T(8,128)S(1)}, u32[]{:S(2)}, u32[]{:S(2)}) %collective-permute-start.3) | collective-permute-done | bytes 262176 | tf_op jit(solution)/shard_map/ppermute | solution.py:366
  31.9 0.0 collective-permute-done.4.rest_3_
  31.9 0.0 copy-done.2
  31.9 0.0 copy-done.3
  31.9 0.5 %shard_map.122 = f32[4,2,64,256]{3,2,1,0:T(8,128)S(1)} custom-call(bf16[4,64,128]{2,1,0:T(8,128)(2,1)S(1)} %copy-done.3, bf16[4,64,128]{2,1,0:T(8,128)(2,1)S(1)} %copy-done.2, f32[4,2,32,256]{3,2,1,0:T(8,128)S(1)} %get-tuple-element.21.rest_0_, f32[4,2,32,256]{3,2,1,0:T(8,128)S(1)} %collective-permute-done.2.rest_1_, ...), custom_call_target="tpu_custom_call" | custom-call | flops 2000000 | tf_op jit(solution)/shard_map/pallas_call | solution.py:379
  32.4 0.1 collective-permute-start.5
  32.5 0.5 %shard_map.121.keep = f32[4,2,64,256]{3,2,1,0:T(8,128)S(1)} custom-call(bf16[4,64,128]{2,1,0:T(8,128)(2,1)S(1)} %copy-done.3, bf16[4,64,128]{2,1,0:T(8,128)(2,1)S(1)} %copy-done.2, f32[4,2,32,256]{3,2,1,0:T(8,128)S(1)} %get-tuple-element.21.rest_0_, f32[4,2,32,256]{3,2,1,0:T(8,128)S(1)} %collective-permute-done.2.rest_1_, ...), custom_call_target="tpu_custom_call" | custom-call | flops 2000000 | tf_op jit(solution)/shard_map/pallas_call | solution.py:379
  33.0 1.4 %collective-permute-done.5.arrived = f32[4,2,64,256]{3,2,1,0:T(8,128)S(1)} collective-permute-done((f32[4,2,64,256]{3,2,1,0:T(8,128)S(1)}, f32[4,2,64,256]{3,2,1,0:T(8,128)S(1)}, u32[]{:S(2)}, u32[]{:S(2)}) %collective-permute-start.5) | collective-permute-done | bytes 524320 | tf_op jit(solution)/shard_map/ppermute | solution.py:390
  34.4 0.1 shard_map.123
  34.4 1.3 %collective-permute-start.6 = (f32[4,2,16,256]{3,2,1,0:T(8,128)S(1)}, f32[4,2,16,256]{3,2,1,0:T(8,128)S(1)}, u32[]{:S(2)}, u32[]{:S(2)}) collective-permute-start(f32[4,2,16,256]{3,2,1,0:T(8,128)S(1)} %get-tuple-element.26), channel_id=1, source_target_pairs={{0,2},{1,3},{2,0},{3,1},{4,6},{5,7},{6,4},{7,5},{8,10},{9,11},{10,... | collective-permute-start | bytes 393224 | tf_op jit(solution)/shard_map/ppermute | solution.py:366
  35.7 0.8 %collective-permute-start.7 = (f32[4,2,16,256]{3,2,1,0:T(8,128)S(1)}, f32[4,2,16,256]{3,2,1,0:T(8,128)S(1)}, u32[]{:S(2)}, u32[]{:S(2)}) collective-permute-start(f32[4,2,16,256]{3,2,1,0:T(8,128)S(1)} %get-tuple-element.27), channel_id=1, source_target_pairs={{0,4},{1,5},{2,6},{3,7},{4,0},{5,1},{6,2},{7,3},{8,12},{9,13},{10,... | collective-permute-start | bytes 393224 | tf_op jit(solution)/shard_map/ppermute | solution.py:366
  36.6 1.4 %collective-permute-start.8 = (f32[4,2,16,256]{3,2,1,0:T(8,128)S(1)}, f32[4,2,16,256]{3,2,1,0:T(8,128)S(1)}, u32[]{:S(2)}, u32[]{:S(2)}) collective-permute-start(f32[4,2,16,256]{3,2,1,0:T(8,128)S(1)} %get-tuple-element.28), channel_id=1, source_target_pairs={{0,6},{1,7},{2,4},{3,5},{4,2},{5,3},{6,0},{7,1},{8,14},{9,15},{10,... | collective-permute-start | bytes 393224 | tf_op jit(solution)/shard_map/ppermute | solution.py:366
  38.0 2.7 %collective-permute-done.6.rest_1_ = f32[4,2,16,256]{3,2,1,0:T(8,128)S(1)} collective-permute-done((f32[4,2,16,256]{3,2,1,0:T(8,128)S(1)}, f32[4,2,16,256]{3,2,1,0:T(8,128)S(1)}, u32[]{:S(2)}, u32[]{:S(2)}) %collective-permute-start.6) | collective-permute-done | bytes 131104 | tf_op jit(solution)/shard_map/ppermute | solution.py:366
  40.7 1.5 %collective-permute-done.7.rest_2_ = f32[4,2,16,256]{3,2,1,0:T(8,128)S(1)} collective-permute-done((f32[4,2,16,256]{3,2,1,0:T(8,128)S(1)}, f32[4,2,16,256]{3,2,1,0:T(8,128)S(1)}, u32[]{:S(2)}, u32[]{:S(2)}) %collective-permute-start.7) | collective-permute-done | bytes 131104 | tf_op jit(solution)/shard_map/ppermute | solution.py:366
  42.2 1.6 %collective-permute-done.8.rest_3_ = f32[4,2,16,256]{3,2,1,0:T(8,128)S(1)} collective-permute-done((f32[4,2,16,256]{3,2,1,0:T(8,128)S(1)}, f32[4,2,16,256]{3,2,1,0:T(8,128)S(1)}, u32[]{:S(2)}, u32[]{:S(2)}) %collective-permute-start.8) | collective-permute-done | bytes 131104 | tf_op jit(solution)/shard_map/ppermute | solution.py:366
  43.8 0.8 %shard_map.124 = f32[16,2,16,256]{3,2,1,0:T(8,128)} custom-call(f32[4,2,16,256]{3,2,1,0:T(8,128)S(1)} %get-tuple-element.25.rest_0_, f32[4,2,16,256]{3,2,1,0:T(8,128)S(1)} %collective-permute-done.6.rest_1_, f32[4,2,16,256]{3,2,1,0:T(8,128)S(1)} %collective-permute-done.7.rest_2_, f32[4,2,16,256]{3,2,1,0:T(8,128)S(1)} %collective-permute-done.8.rest_3_), custom_call_target="tpu_custom_call" | custom-call | flops 2000000 | tf_op jit(solution)/shard_map/pallas_call | solution.py:416
Async XLA Ops:
  0.0 13.8 %copy-start = (bf16[512,256]{1,0:T(8,128)(2,1)S(1)}, bf16[512,256]{1,0:T(8,128)(2,1)}, u32[]{:S(2)}) copy-start(bf16[512,256]{1,0:T(8,128)(2,1)} %constant.9.clone.phi_lo) | copy-start | bytes 786436
  0.0 13.8 %copy-start.1 = (bf16[512,256]{1,0:T(8,128)(2,1)S(1)}, bf16[512,256]{1,0:T(8,128)(2,1)}, u32[]{:S(2)}) copy-start(bf16[512,256]{1,0:T(8,128)(2,1)} %constant.8.clone.phi_hi) | copy-start | bytes 786436
  0.0 31.9 %copy-start.2 = (bf16[4,64,128]{2,1,0:T(8,128)(2,1)S(1)}, bf16[4,64,128]{2,1,0:T(8,128)(2,1)}, u32[]{:S(2)}) copy-start(bf16[4,64,128]{2,1,0:T(8,128)(2,1)} %constant.11.clone.t_lo) | copy-start | bytes 196612
  0.0 31.9 %copy-start.3 = (bf16[4,64,128]{2,1,0:T(8,128)(2,1)S(1)}, bf16[4,64,128]{2,1,0:T(8,128)(2,1)}, u32[]{:S(2)}) copy-start(bf16[4,64,128]{2,1,0:T(8,128)(2,1)} %constant.10.clone.t_hi) | copy-start | bytes 196612
  0.0 13.8 %copy-start.4 = (s32[8,8]{1,0:T(8,128)S(1)}, s32[8,8]{1,0:T(8,128)}, u32[]{:S(2)}) copy-start(s32[8,8]{1,0:T(8,128)} %partners.1) | copy-start | bytes 772
  0.0 13.8 %copy-start.6 = (s32[16]{0:T(128)S(1)}, s32[16]{0:T(128)}, u32[]{:S(2)}) copy-start(s32[16]{0:T(128)} %child_octant.3) | copy-start | bytes 196
  0.0 13.8 %copy-start.5 = (s32[16]{0:T(128)S(1)}, s32[16]{0:T(128)}, u32[]{:S(2)}) copy-start(s32[16]{0:T(128)} %child_parent.3) | copy-start | bytes 196
  1.2 12.6 %collective-permute-start.1 = (f32[2,2,32,512]{3,2,1,0:T(8,128)S(1)}, f32[2,2,32,512]{3,2,1,0:T(8,128)S(1)}, u32[]{:S(2)}, u32[]{:S(2)}) collective-permute-start(f32[2,2,32,512]{3,2,1,0:T(8,128)S(1)} %get-tuple-element.29), channel_id=1, source_target_pairs={{8,0},{16,8},{24,16},{9,1},{17,9},{25,17},{10,2},{18,10},{26,18},{... | collective-permute-start | bytes 786440 | tf_op jit(solution)/shard_map/ppermute | solution.py:311
  2.5 11.3 %collective-permute-start = (f32[2,2,32,512]{3,2,1,0:T(8,128)S(1)}, f32[2,2,32,512]{3,2,1,0:T(8,128)S(1)}, u32[]{:S(2)}, u32[]{:S(2)}) collective-permute-start(f32[2,2,32,512]{3,2,1,0:T(8,128)S(1)} %get-tuple-element.30), channel_id=1, source_target_pairs={{0,8},{8,16},{16,24},{1,9},{9,17},{17,25},{2,10},{10,18},{18,26},{... | collective-permute-start | bytes 786440 | tf_op jit(solution)/shard_map/ppermute | solution.py:310
  17.1 9.2 %collective-permute-start.2 = (f32[4,2,32,256]{3,2,1,0:T(8,128)S(1)}, f32[4,2,32,256]{3,2,1,0:T(8,128)S(1)}, u32[]{:S(2)}, u32[]{:S(2)}) collective-permute-start(f32[4,2,32,256]{3,2,1,0:T(8,128)S(1)} %get-tuple-element.22), channel_id=1, source_target_pairs={{0,2},{1,3},{2,0},{3,1},{4,6},{5,7},{6,4},{7,5},{8,10},{9,11},{10,... | collective-permute-start | bytes 786440 | tf_op jit(solution)/shard_map/ppermute | solution.py:366
  19.1 12.8 %collective-permute-start.3 = (f32[4,2,32,256]{3,2,1,0:T(8,128)S(1)}, f32[4,2,32,256]{3,2,1,0:T(8,128)S(1)}, u32[]{:S(2)}, u32[]{:S(2)}) collective-permute-start(f32[4,2,32,256]{3,2,1,0:T(8,128)S(1)} %get-tuple-element.23), channel_id=1, source_target_pairs={{0,4},{1,5},{2,6},{3,7},{4,0},{5,1},{6,2},{7,3},{8,12},{9,13},{10,... | collective-permute-start | bytes 786440 | tf_op jit(solution)/shard_map/ppermute | solution.py:366
  20.6 11.3 %collective-permute-start.4 = (f32[4,2,32,256]{3,2,1,0:T(8,128)S(1)}, f32[4,2,32,256]{3,2,1,0:T(8,128)S(1)}, u32[]{:S(2)}, u32[]{:S(2)}) collective-permute-start(f32[4,2,32,256]{3,2,1,0:T(8,128)S(1)} %get-tuple-element.24), channel_id=1, source_target_pairs={{0,6},{1,7},{2,4},{3,5},{4,2},{5,3},{6,0},{7,1},{8,14},{9,15},{10,... | collective-permute-start | bytes 786440 | tf_op jit(solution)/shard_map/ppermute | solution.py:366
  32.4 2.0 %collective-permute-start.5 = (f32[4,2,64,256]{3,2,1,0:T(8,128)S(1)}, f32[4,2,64,256]{3,2,1,0:T(8,128)S(1)}, u32[]{:S(2)}, u32[]{:S(2)}) collective-permute-start(f32[4,2,64,256]{3,2,1,0:T(8,128)S(1)} %shard_map.122), channel_id=1, source_target_pairs={{0,1},{1,0},{2,3},{3,2},{4,5},{5,4},{6,7},{7,6},{8,9},{9,8},{10,11... | collective-permute-start | bytes 1572872 | tf_op jit(solution)/shard_map/ppermute | solution.py:390
  34.4 6.3 %collective-permute-start.6 = (f32[4,2,16,256]{3,2,1,0:T(8,128)S(1)}, f32[4,2,16,256]{3,2,1,0:T(8,128)S(1)}, u32[]{:S(2)}, u32[]{:S(2)}) collective-permute-start(f32[4,2,16,256]{3,2,1,0:T(8,128)S(1)} %get-tuple-element.26), channel_id=1, source_target_pairs={{0,2},{1,3},{2,0},{3,1},{4,6},{5,7},{6,4},{7,5},{8,10},{9,11},{10,... | collective-permute-start | bytes 393224 | tf_op jit(solution)/shard_map/ppermute | solution.py:366
  35.7 6.5 %collective-permute-start.7 = (f32[4,2,16,256]{3,2,1,0:T(8,128)S(1)}, f32[4,2,16,256]{3,2,1,0:T(8,128)S(1)}, u32[]{:S(2)}, u32[]{:S(2)}) collective-permute-start(f32[4,2,16,256]{3,2,1,0:T(8,128)S(1)} %get-tuple-element.27), channel_id=1, source_target_pairs={{0,4},{1,5},{2,6},{3,7},{4,0},{5,1},{6,2},{7,3},{8,12},{9,13},{10,... | collective-permute-start | bytes 393224 | tf_op jit(solution)/shard_map/ppermute | solution.py:366
  36.6 7.2 %collective-permute-start.8 = (f32[4,2,16,256]{3,2,1,0:T(8,128)S(1)}, f32[4,2,16,256]{3,2,1,0:T(8,128)S(1)}, u32[]{:S(2)}, u32[]{:S(2)}) collective-permute-start(f32[4,2,16,256]{3,2,1,0:T(8,128)S(1)} %get-tuple-element.28), channel_id=1, source_target_pairs={{0,6},{1,7},{2,4},{3,5},{4,2},{5,3},{6,0},{7,1},{8,14},{9,15},{10,... | collective-permute-start | bytes 393224 | tf_op jit(solution)/shard_map/ppermute | solution.py:366

commit v3 on v2

--- a/solution.py
+++ b/solution.py
@@ -91,56 +91,42 @@
             phase_ref[octant, 1, :, lanes] = re * szz + im * cz
 
 
+def copy_all(pairs, sems):
+    copies = [
+        pltpu.make_async_copy(source, target, sems.at[n])
+        for n, (source, target) in enumerate(pairs)
+    ]
+    for copy in copies:
+        copy.start()
+    return copies
+
+
+def ends_kernel(patterns, partners, op_index, operators, low, high, partners_out, op_out, sems):
+    width = low.shape[0]
+    last = patterns.shape[0] - width
+    pairs = [
+        (patterns.at[pl.ds(0, width)], low),
+        (patterns.at[pl.ds(last, width)], high),
+        (partners, partners_out),
+        (op_index, op_out),
+    ]
+    for copy in copy_all(pairs, sems):
+        copy.wait()
+
+
 def own_kernel(
-    theta_count, width, partners_hbm, op_index_hbm, patterns, operators, out, edge_ops, phase,
-    mine, held, partners, op_index, sems, more_sems,
+    theta_count, partners_in, op_in, patterns, operators, out, phase, partners, op_index, sems
 ):
     clusters, terms = partners.shape
     rows = out.shape[2]
-    tables = [
-        pltpu.make_async_copy(op_index_hbm, op_index, more_sems.at[0]),
-        pltpu.make_async_copy(partners_hbm, partners, more_sems.at[1]),
-        pltpu.make_async_copy(patterns, mine, more_sems.at[2]),
-    ]
-    for copy in tables:
-        copy.start()
+    copies = copy_all([(partners_in, partners), (op_in, op_index)], sems)
     phase_tables(lax.axis_index("member"), theta_count, phase)
-    tables[0].wait()
-    inner = clusters - 2 * width
-
-    def slot(c):
-        return jnp.where(c < width, c, c - inner) * terms
-
-    def fetch_edge(c, p):
-        e = slot(c) + p
-        return pltpu.make_async_copy(
-            operators.at[op_index[c, p]], edge_ops.at[e], sems.at[c * terms + p]
-        )
-
-    def fetch_inner(c, p):
-        return pltpu.make_async_copy(
-            operators.at[op_index[c, p]], held.at[(c - width) * terms + p],
-            sems.at[c * terms + p],
-        )
-
-    def edge_cluster(n):
-        return jnp.where(n < width, n, n + inner)
-
-    @pl.loop(width, clusters - width)
+    base = lax.axis_index("group") * clusters
+    for copy in copies:
+        copy.wait()
+
+    @pl.loop(0, clusters)
     def _(c):
-        for p in range(terms):
-            fetch_inner(c, p).start()
-
-    @pl.loop(0, 2 * width)
-    def _(n):
-        for p in range(terms):
-            fetch_edge(edge_cluster(n), p).start()
-
-    base = lax.axis_index("group") * clusters
-    tables[1].wait()
-    tables[2].wait()
-
-    def translate(c, ops, first):
         for r in range(rows // 8):
             band = pl.ds(r * 8, 8)
             re, im = 0.0, 0.0
@@ -148,28 +134,16 @@
                 q = partners[c, p] - base
                 keep = jnp.where((q >= 0) & (q < clusters), 1.0, 0.0).astype(F32)
                 q = jnp.clip(q, 0, clusters - 1)
-                ore, oim = ops[first + p, 0, band, :], ops[first + p, 1, band, :]
-                pre, pim = mine[q, 0, band, :] * keep, mine[q, 1, band, :] * keep
+                e = op_index[c, p]
+                ore, oim = operators[e, 0, band, :], operators[e, 1, band, :]
+                pre, pim = patterns[q, 0, band, :] * keep, patterns[q, 1, band, :] * keep
                 re = re + (ore * pre - oim * pim)
                 im = im + (ore * pim + oim * pre)
             out[c, 0, band, :] = re
             out[c, 1, band, :] = im
 
-    @pl.loop(width, clusters - width)
-    def _(c):
-        for p in range(terms):
-            fetch_inner(c, p).wait()
-        translate(c, held, (c - width) * terms)
-
-    @pl.loop(0, 2 * width)
-    def _(n):
-        c = edge_cluster(n)
-        for p in range(terms):
-            fetch_edge(c, p).wait()
-        translate(c, edge_ops, n * terms)
-
-
-def halo_terms(partners, own, edge_ops, below, above, total):
+
+def halo_terms(partners, op_index, own, operators, below, above, total):
     clusters, _, rows, _ = own.shape
     terms = partners.shape[1]
     width = below.shape[0]
@@ -187,11 +161,11 @@
 
             @pl.when((q < 0) | (q >= clusters))
             def _():
-                e = n * terms + p
+                e = op_index[c, p]
                 h = jnp.clip(partners[c, p] + shift, 0, width - 1)
                 for r in range(rows // 8):
                     band = pl.ds(r * 8, 8)
-                    ore, oim = edge_ops[e, 0, band, :], edge_ops[e, 1, band, :]
+                    ore, oim = operators[e, 0, band, :], operators[e, 1, band, :]
                     pre, pim = halo[h, 0, band, :], halo[h, 1, band, :]
                     total[c, 0, band, :] += ore * pre - oim * pim
                     total[c, 1, band, :] += ore * pim + oim * pre
@@ -220,11 +194,11 @@
 
 
 def first_kernel(
-    order, partners, child_parent, child_octant, own, edge_ops, below, above, phase, phi_hi,
-    phi_lo, *rest
+    order, partners, op_index, child_parent, child_octant, own, operators, below, above, phase,
+    phi_hi, phi_lo, *rest
 ):
     outs, (total, shifted) = rest[:-2], rest[-2:]
-    halo_terms(partners, own, edge_ops, below, above, total)
+    halo_terms(partners, op_index, own, operators, below, above, total)
     shift_and_phi(
         order, child_parent, child_octant, total, phase, phi_hi, phi_lo, outs, shifted
     )
@@ -289,7 +263,7 @@
 
 
 def cost(us):
-    return pl.CostEstimate(flops=us * 2_000_000, bytes_accessed=0, transcendentals=0)
+    return pl.CostEstimate(flops=us * 2_000_000, bytes_accessed=us * 3_000_000, transcendentals=0)
 
 
 def on_device(patterns, operators, partners, operator_index, child_parent, child_octant):
@@ -304,32 +278,35 @@
     width = clusters // 4
     member = lax.axis_index("member")
     chip, core = member // CORES, member % CORES
-    terms = partners.shape[1]
     up = [(i, i + 1) for i in range(groups - 1)]
     down = [(i + 1, i) for i in range(groups - 1)]
-    below = lax.ppermute(patterns[clusters - width:], "group", up)
-    above = lax.ppermute(patterns[:width], "group", down)
-
-    edge = 2 * width * terms
+    end = shape(width, 2, rows, lons)
+    index = jax.ShapeDtypeStruct(partners.shape, jnp.int32)
+    low, high, partners, operator_index = pl.pallas_call(
+        ends_kernel,
+        out_shape=(end, end, index, index),
+        in_specs=[HBM] * 4,
+        out_specs=(VMEM,) * 4,
+        scratch_shapes=[pltpu.SemaphoreType.DMA((4,))],
+        compiler_params=params(4),
+    )(*map(in_hbm, (patterns, partners, operator_index, operators)))
+    below = lax.ppermute(high, "group", up)
+    above = lax.ppermute(low, "group", down)
+
     total_shape = shape(clusters, 2, rows, lons)
-    own, edge_ops, phase = pl.pallas_call(
-        functools.partial(own_kernel, theta_count, width),
-        out_shape=(
-            total_shape, shape(edge, 2, rows, lons), shape(8, 2, rows, lons),
-        ),
-        in_specs=[HBM] * 4,
-        out_specs=(VMEM, VMEM, VMEM),
+    own, phase = pl.pallas_call(
+        functools.partial(own_kernel, theta_count),
+        out_shape=(total_shape, shape(8, 2, rows, lons)),
+        in_specs=[VMEM] * 4,
+        out_specs=(VMEM, VMEM),
         scratch_shapes=[
-            pltpu.VMEM((clusters, 2, rows, lons), F32),
-            pltpu.VMEM((clusters * terms - edge, 2, rows, lons), F32),
-            pltpu.SMEM((clusters, terms), jnp.int32),
-            pltpu.SMEM((clusters, terms), jnp.int32),
-            pltpu.SemaphoreType.DMA((clusters * terms,)),
-            pltpu.SemaphoreType.DMA((3,)),
+            pltpu.SMEM(partners.shape, jnp.int32),
+            pltpu.SMEM(partners.shape, jnp.int32),
+            pltpu.SemaphoreType.DMA((2,)),
         ],
         compiler_params=params(20),
         cost_estimate=cost(8),
-    )(in_hbm(partners), in_hbm(operator_index), in_hbm(patterns), in_hbm(operators))
+    )(partners, operator_index, patterns, operators)
 
     phi = split_const(phi_table(lons, NPC).T)
     block = shape(per_chip, 2, rows, NPC)
@@ -339,13 +316,14 @@
     *outs, total = call(
         functools.partial(first_kernel, far),
         out_shape=(block,) * len(far) + (total_shape,),
-        in_specs=[SMEM] * 3 + [VMEM] * 7,
+        in_specs=[SMEM] * 4 + [VMEM] * 7,
         out_specs=(VMEM,) * (len(far) + 1),
         scratch_shapes=[shifted],
         compiler_params=params(20),
         cost_estimate=cost(2),
     )(
-        partners, child_parent, child_octant, own, edge_ops, below, above, phase, *phi
+        partners, operator_index, child_parent, child_octant, own, operators, below, above,
+        phase, *phi,
     )
     sent.update(zip(far, outs))
     outs = call(

time: 44.8 us -> 46.4 us (1.036)
  waiting for transfers between devices: 18.5 us -> 23.7 us
  Pallas kernels: 10.7 us -> 8.68 us
  local copies, waits for them, and re-layouts: 1.16 us -> 0.04 us
    ppermute x2, waiting for transfers between devices: 0.01 us -> 5.89 us  [the longest x1 4.13 us: on_device(): above = lax.ppermute(low, 'group', down)]
    pallas_call x1 -> x2, Pallas kernels: 5.7 us -> 3.64 us  [the longest x1 2.42 us: on_device(): pl.pallas_call(functools.partial(own_kernel, theta_count), out_shape=(tot...]
    slice x1 -> x0, local copies, waits for them, and re-layouts: 1.13 us -> none  [on_device(): above = lax.ppermute(patterns[:width], 'group', down)]
    ppermute x6, waiting for transfers between devices: 17.1 us -> 16.3 us  [between_chips(): moved[s] = lax.ppermute(blocks[s], 'member', pairs)]
  transfers between devices with their start and end apart: 9 -> 9, of which waited for: 6 -> 8; matrix products, arithmetic and copies ran while one was open for 0% -> 0% of each run, Pallas kernels for 14% -> 6%
where the time goes in v3:
time: 46.4 us; the launch traced here: 46.2 us
  waiting for transfers between devices  23.7 us (51%)
  starting transfers between devices  13.7 us (30%)
  Pallas kernels  8.68 us (19%)
    ppermute x6, waiting for transfers between devices, between_chips(): moved[s] = lax.ppermute(blocks[s], 'member', pairs)  16.3 us
    ppermute x6, starting transfers between devices, between_chips(): moved[s] = lax.ppermute(blocks[s], 'member', pairs)  7.11 us
    ppermute x1, starting transfers between devices, on_device(): below = lax.ppermute(high, 'group', up)  5.25 us
    ppermute x1, waiting for transfers between devices, on_device(): above = lax.ppermute(low, 'group', down)  4.13 us
    pallas_call x1, Pallas kernels, on_device(): pl.pallas_call(functools.partial(own_kernel, theta_count), out_shape=(tot...  2.42 us
    pallas_call x1, Pallas kernels, on_device(): call(functools.partial(first_kernel, far), out_shape=(block,) * len(far)...  1.78 us
    ppermute x1, waiting for transfers between devices, on_device(): below = lax.ppermute(high, 'group', up)  1.76 us
    pallas_call x1, Pallas kernels, on_device(): call(functools.partial(later_kernel, near), out_shape=(block,) * len(near...  1.48 us
  transfers between devices with their start and end apart: 9, of which 8 were waited for; matrix products, arithmetic and copies ran while one was open for 0% of the time, Pallas kernels for 6%

profile of v3, /device:TPU:0, one launch (start us, length us, event | category | flops | bytes accessed | tf_op | source)
XLA Modules:
  0.0 46.2 jit_solution(2591724883888798043)
XLA Ops:
  0.0 0.0 copy-start
  0.0 0.0 copy-start.1
  0.0 0.0 copy-start.2
  0.0 0.0 copy-start.3
  0.0 0.0 copy-start.7
  0.0 0.0 copy-start.6
  0.0 1.2 %shard_map.118 = (f32[2,2,32,512]{3,2,1,0:T(8,128)S(1)}, f32[2,2,32,512]{3,2,1,0:T(8,128)S(1)}, s32[8,8]{1,0:T(8,128)S(1)}, s32[8,8]{1,0:T(8,128)S(1)}) custom-call(f32[8,2,32,512]{3,2,1,0:T(8,128)} %patterns.3, s32[8,8]{1,0:T(8,128)} %partners.1, s32[8,8]{1,0:T(8,128)} %op_index.1, f32[100,2,32,512]{3,2,1,0:T(8,128)} %operators.5), custom_call_target="tpu_custom_call" | custom-call | tf_op jit(solution)/shard_map/pallas_call | solution.py:285
  1.3 5.3 %collective-permute-start = (f32[2,2,32,512]{3,2,1,0:T(8,128)S(1)}, f32[2,2,32,512]{3,2,1,0:T(8,128)S(1)}, u32[]{:S(2)}, u32[]{:S(2)}) collective-permute-start(f32[2,2,32,512]{3,2,1,0:T(8,128)S(1)} %get-tuple-element.23), channel_id=1, source_target_pairs={{0,8},{8,16},{16,24},{1,9},{9,17},{17,25},{2,10},{10,18},{18,26},{... | collective-permute-start | bytes 786440 | tf_op jit(solution)/shard_map/ppermute | solution.py:293
  6.5 1.3 %collective-permute-start.1 = (f32[2,2,32,512]{3,2,1,0:T(8,128)S(1)}, f32[2,2,32,512]{3,2,1,0:T(8,128)S(1)}, u32[]{:S(2)}, u32[]{:S(2)}) collective-permute-start(f32[2,2,32,512]{3,2,1,0:T(8,128)S(1)} %get-tuple-element.24), channel_id=1, source_target_pairs={{8,0},{16,8},{24,16},{9,1},{17,9},{25,17},{10,2},{18,10},{26,18},{... | collective-permute-start | bytes 786440 | tf_op jit(solution)/shard_map/ppermute | solution.py:294
  7.8 0.0 copy-done
  7.8 0.0 copy-done.1
  7.8 0.0 copy-start.4
  7.8 0.0 copy-start.5
  7.9 2.4 %shard_map.119 = (f32[8,2,32,512]{3,2,1,0:T(8,128)S(1)}, f32[8,2,32,512]{3,2,1,0:T(8,128)S(1)}) custom-call(s32[8,8]{1,0:T(8,128)S(1)} %get-tuple-element.20.partners_in.partners, s32[8,8]{1,0:T(8,128)S(1)} %get-tuple-element.21.op_in.op_index, f32[8,2,32,512]{3,2,1,0:T(8,128)S(1)} %copy-done.1, f32[100,2,32,512]{3,2,1,0:T(8,128)S(1)} %copy-done), custom_call_target="tpu_custom_call" | custom-call | flops 16000000 | bytes 24000000 | tf_op jit(solution)/shard_map/pallas_call | solution.py:297
  10.3 1.8 %collective-permute-done.below = f32[2,2,32,512]{3,2,1,0:T(8,128)S(1)} collective-permute-done((f32[2,2,32,512]{3,2,1,0:T(8,128)S(1)}, f32[2,2,32,512]{3,2,1,0:T(8,128)S(1)}, u32[]{:S(2)}, u32[]{:S(2)}) %collective-permute-start) | collective-permute-done | bytes 262176 | tf_op jit(solution)/shard_map/ppermute | solution.py:293
  12.0 4.1 %collective-permute-done.1.above = f32[2,2,32,512]{3,2,1,0:T(8,128)S(1)} collective-permute-done((f32[2,2,32,512]{3,2,1,0:T(8,128)S(1)}, f32[2,2,32,512]{3,2,1,0:T(8,128)S(1)}, u32[]{:S(2)}, u32[]{:S(2)}) %collective-permute-start.1) | collective-permute-done | bytes 262176 | tf_op jit(solution)/shard_map/ppermute | solution.py:294
  16.2 0.0 copy-done.2
  16.2 0.0 copy-done.3
  16.2 0.0 copy-done.7
  16.2 0.0 copy-done.6
  16.2 1.8 %shard_map.120 = (f32[4,2,32,256]{3,2,1,0:T(8,128)S(1)}, f32[8,2,32,512]{3,2,1,0:T(8,128)S(1)}) custom-call(s32[8,8]{1,0:T(8,128)S(1)} %get-tuple-element.20.partners_in.partners, s32[8,8]{1,0:T(8,128)S(1)} %get-tuple-element.21.op_in.op_index, s32[16]{0:T(128)S(1)} %copy-done.6, s32[16]{0:T(128)S(1)} %copy-done.7, ...), custom_call_target="tpu_custom_call" | custom-call | flops 4000000 | bytes 6000000 | tf_op jit(solution)/shard_map/pallas_call | solution.py:316
  18.0 1.5 %shard_map.121 = (f32[4,2,32,256]{3,2,1,0:T(8,128)S(1)}, f32[4,2,32,256]{3,2,1,0:T(8,128)S(1)}, f32[4,2,32,256]{3,2,1,0:T(8,128)S(1)}) custom-call(s32[16]{0:T(128)S(1)} %copy-done.6, s32[16]{0:T(128)S(1)} %copy-done.7, f32[8,2,32,512]{3,2,1,0:T(8,128)S(1)} %get-tuple-element.26.total, f32[8,2,32,512]{3,2,1,0:T(8,128)S(1)} %get-tuple-element.25.phase, ...), custom_call_target="tpu_custom_call" | custom-call | flops 2000000 | bytes 3000000 | tf_op jit(solution)/shard_map/pallas_call | solution.py:329
  19.5 1.7 %collective-permute-start.2 = (f32[4,2,32,256]{3,2,1,0:T(8,128)S(1)}, f32[4,2,32,256]{3,2,1,0:T(8,128)S(1)}, u32[]{:S(2)}, u32[]{:S(2)}) collective-permute-start(f32[4,2,32,256]{3,2,1,0:T(8,128)S(1)} %get-tuple-element.28), channel_id=1, source_target_pairs={{0,2},{1,3},{2,0},{3,1},{4,6},{5,7},{6,4},{7,5},{8,10},{9,11},{10,... | collective-permute-start | bytes 786440 | tf_op jit(solution)/shard_map/ppermute | solution.py:344
  21.2 1.5 %collective-permute-start.3 = (f32[4,2,32,256]{3,2,1,0:T(8,128)S(1)}, f32[4,2,32,256]{3,2,1,0:T(8,128)S(1)}, u32[]{:S(2)}, u32[]{:S(2)}) collective-permute-start(f32[4,2,32,256]{3,2,1,0:T(8,128)S(1)} %get-tuple-element.29), channel_id=1, source_target_pairs={{0,4},{1,5},{2,6},{3,7},{4,0},{5,1},{6,2},{7,3},{8,12},{9,13},{10,... | collective-permute-start | bytes 786440 | tf_op jit(solution)/shard_map/ppermute | solution.py:344
  22.7 0.3 collective-permute-start.4
  23.0 5.7 %collective-permute-done.2.rest_1_ = f32[4,2,32,256]{3,2,1,0:T(8,128)S(1)} collective-permute-done((f32[4,2,32,256]{3,2,1,0:T(8,128)S(1)}, f32[4,2,32,256]{3,2,1,0:T(8,128)S(1)}, u32[]{:S(2)}, u32[]{:S(2)}) %collective-permute-start.2) | collective-permute-done | bytes 262176 | tf_op jit(solution)/shard_map/ppermute | solution.py:344
  28.7 4.8 %collective-permute-done.3.rest_2_ = f32[4,2,32,256]{3,2,1,0:T(8,128)S(1)} collective-permute-done((f32[4,2,32,256]{3,2,1,0:T(8,128)S(1)}, f32[4,2,32,256]{3,2,1,0:T(8,128)S(1)}, u32[]{:S(2)}, u32[]{:S(2)}) %collective-permute-start.3) | collective-permute-done | bytes 262176 | tf_op jit(solution)/shard_map/ppermute | solution.py:344
  33.5 0.0 collective-permute-done.4.rest_3_
  33.5 0.0 copy-done.4
  33.5 0.0 copy-done.5
  33.5 0.5 shard_map.123
  34.0 0.1 collective-permute-start.5
  34.1 0.5 shard_map.122.keep
  34.6 1.4 %collective-permute-done.5.arrived = f32[4,2,64,256]{3,2,1,0:T(8,128)S(1)} collective-permute-done((f32[4,2,64,256]{3,2,1,0:T(8,128)S(1)}, f32[4,2,64,256]{3,2,1,0:T(8,128)S(1)}, u32[]{:S(2)}, u32[]{:S(2)}) %collective-permute-start.5) | collective-permute-done | bytes 524320 | tf_op jit(solution)/shard_map/ppermute | solution.py:368
  36.0 0.1 shard_map.124
  36.0 1.3 %collective-permute-start.6 = (f32[4,2,16,256]{3,2,1,0:T(8,128)S(1)}, f32[4,2,16,256]{3,2,1,0:T(8,128)S(1)}, u32[]{:S(2)}, u32[]{:S(2)}) collective-permute-start(f32[4,2,16,256]{3,2,1,0:T(8,128)S(1)} %get-tuple-element.32), channel_id=1, source_target_pairs={{0,2},{1,3},{2,0},{3,1},{4,6},{5,7},{6,4},{7,5},{8,10},{9,11},{10,... | collective-permute-start | bytes 393224 | tf_op jit(solution)/shard_map/ppermute | solution.py:344
  37.3 0.8 %collective-permute-start.7 = (f32[4,2,16,256]{3,2,1,0:T(8,128)S(1)}, f32[4,2,16,256]{3,2,1,0:T(8,128)S(1)}, u32[]{:S(2)}, u32[]{:S(2)}) collective-permute-start(f32[4,2,16,256]{3,2,1,0:T(8,128)S(1)} %get-tuple-element.33), channel_id=1, source_target_pairs={{0,4},{1,5},{2,6},{3,7},{4,0},{5,1},{6,2},{7,3},{8,12},{9,13},{10,... | collective-permute-start | bytes 393224 | tf_op jit(solution)/shard_map/ppermute | solution.py:344
  38.2 1.4 %collective-permute-start.8 = (f32[4,2,16,256]{3,2,1,0:T(8,128)S(1)}, f32[4,2,16,256]{3,2,1,0:T(8,128)S(1)}, u32[]{:S(2)}, u32[]{:S(2)}) collective-permute-start(f32[4,2,16,256]{3,2,1,0:T(8,128)S(1)} %get-tuple-element.34), channel_id=1, source_target_pairs={{0,6},{1,7},{2,4},{3,5},{4,2},{5,3},{6,0},{7,1},{8,14},{9,15},{10,... | collective-permute-start | bytes 393224 | tf_op jit(solution)/shard_map/ppermute | solution.py:344
  39.6 2.7 %collective-permute-done.6.rest_1_ = f32[4,2,16,256]{3,2,1,0:T(8,128)S(1)} collective-permute-done((f32[4,2,16,256]{3,2,1,0:T(8,128)S(1)}, f32[4,2,16,256]{3,2,1,0:T(8,128)S(1)}, u32[]{:S(2)}, u32[]{:S(2)}) %collective-permute-start.6) | collective-permute-done | bytes 131104 | tf_op jit(solution)/shard_map/ppermute | solution.py:344
  42.3 1.5 %collective-permute-done.7.rest_2_ = f32[4,2,16,256]{3,2,1,0:T(8,128)S(1)} collective-permute-done((f32[4,2,16,256]{3,2,1,0:T(8,128)S(1)}, f32[4,2,16,256]{3,2,1,0:T(8,128)S(1)}, u32[]{:S(2)}, u32[]{:S(2)}) %collective-permute-start.7) | collective-permute-done | bytes 131104 | tf_op jit(solution)/shard_map/ppermute | solution.py:344
  43.8 1.6 %collective-permute-done.8.rest_3_ = f32[4,2,16,256]{3,2,1,0:T(8,128)S(1)} collective-permute-done((f32[4,2,16,256]{3,2,1,0:T(8,128)S(1)}, f32[4,2,16,256]{3,2,1,0:T(8,128)S(1)}, u32[]{:S(2)}, u32[]{:S(2)}) %collective-permute-start.8) | collective-permute-done | bytes 131104 | tf_op jit(solution)/shard_map/ppermute | solution.py:344
  45.4 0.8 %shard_map.125 = f32[16,2,16,256]{3,2,1,0:T(8,128)} custom-call(f32[4,2,16,256]{3,2,1,0:T(8,128)S(1)} %get-tuple-element.31.rest_0_, f32[4,2,16,256]{3,2,1,0:T(8,128)S(1)} %collective-permute-done.6.rest_1_, f32[4,2,16,256]{3,2,1,0:T(8,128)S(1)} %collective-permute-done.7.rest_2_, f32[4,2,16,256]{3,2,1,0:T(8,128)S(1)} %collective-permute-done.8.rest_3_), custom_call_target="tpu_custom_call" | custom-call | flops 2000000 | bytes 3000000 | tf_op jit(solution)/shard_map/pallas_call | solution.py:394
Async XLA Ops:
  0.0 7.8 %copy-start = (f32[100,2,32,512]{3,2,1,0:T(8,128)S(1)}, f32[100,2,32,512]{3,2,1,0:T(8,128)}, u32[]{:S(2)}) copy-start(f32[100,2,32,512]{3,2,1,0:T(8,128)} %operators.5) | copy-start | bytes 39321604
  0.0 7.8 %copy-start.1 = (f32[8,2,32,512]{3,2,1,0:T(8,128)S(1)}, f32[8,2,32,512]{3,2,1,0:T(8,128)}, u32[]{:S(2)}) copy-start(f32[8,2,32,512]{3,2,1,0:T(8,128)} %patterns.3) | copy-start | bytes 3145732
  0.0 16.2 %copy-start.2 = (bf16[512,256]{1,0:T(8,128)(2,1)S(1)}, bf16[512,256]{1,0:T(8,128)(2,1)}, u32[]{:S(2)}) copy-start(bf16[512,256]{1,0:T(8,128)(2,1)} %constant.9.clone.phi_lo) | copy-start | bytes 786436
  0.0 16.2 %copy-start.3 = (bf16[512,256]{1,0:T(8,128)(2,1)S(1)}, bf16[512,256]{1,0:T(8,128)(2,1)}, u32[]{:S(2)}) copy-start(bf16[512,256]{1,0:T(8,128)(2,1)} %constant.8.clone.phi_hi) | copy-start | bytes 786436
  0.0 16.2 %copy-start.7 = (s32[16]{0:T(128)S(1)}, s32[16]{0:T(128)}, u32[]{:S(2)}) copy-start(s32[16]{0:T(128)} %child_octant.3) | copy-start | bytes 196
  0.0 16.2 %copy-start.6 = (s32[16]{0:T(128)S(1)}, s32[16]{0:T(128)}, u32[]{:S(2)}) copy-start(s32[16]{0:T(128)} %child_parent.3) | copy-start | bytes 196
  1.3 10.8 %collective-permute-start = (f32[2,2,32,512]{3,2,1,0:T(8,128)S(1)}, f32[2,2,32,512]{3,2,1,0:T(8,128)S(1)}, u32[]{:S(2)}, u32[]{:S(2)}) collective-permute-start(f32[2,2,32,512]{3,2,1,0:T(8,128)S(1)} %get-tuple-element.23), channel_id=1, source_target_pairs={{0,8},{8,16},{16,24},{1,9},{9,17},{17,25},{2,10},{10,18},{18,26},{... | collective-permute-start | bytes 786440 | tf_op jit(solution)/shard_map/ppermute | solution.py:293
  6.5 9.7 %collective-permute-start.1 = (f32[2,2,32,512]{3,2,1,0:T(8,128)S(1)}, f32[2,2,32,512]{3,2,1,0:T(8,128)S(1)}, u32[]{:S(2)}, u32[]{:S(2)}) collective-permute-start(f32[2,2,32,512]{3,2,1,0:T(8,128)S(1)} %get-tuple-element.24), channel_id=1, source_target_pairs={{8,0},{16,8},{24,16},{9,1},{17,9},{25,17},{10,2},{18,10},{26,18},{... | collective-permute-start | bytes 786440 | tf_op jit(solution)/shard_map/ppermute | solution.py:294
  7.8 25.7 %copy-start.4 = (bf16[4,64,128]{2,1,0:T(8,128)(2,1)S(1)}, bf16[4,64,128]{2,1,0:T(8,128)(2,1)}, u32[]{:S(2)}) copy-start(bf16[4,64,128]{2,1,0:T(8,128)(2,1)} %constant.11.clone.t_lo) | copy-start | bytes 196612
  7.8 25.7 %copy-start.5 = (bf16[4,64,128]{2,1,0:T(8,128)(2,1)S(1)}, bf16[4,64,128]{2,1,0:T(8,128)(2,1)}, u32[]{:S(2)}) copy-start(bf16[4,64,128]{2,1,0:T(8,128)(2,1)} %constant.10.clone.t_hi) | copy-start | bytes 196612
  19.5 9.2 %collective-permute-start.2 = (f32[4,2,32,256]{3,2,1,0:T(8,128)S(1)}, f32[4,2,32,256]{3,2,1,0:T(8,128)S(1)}, u32[]{:S(2)}, u32[]{:S(2)}) collective-permute-start(f32[4,2,32,256]{3,2,1,0:T(8,128)S(1)} %get-tuple-element.28), channel_id=1, source_target_pairs={{0,2},{1,3},{2,0},{3,1},{4,6},{5,7},{6,4},{7,5},{8,10},{9,11},{10,... | collective-permute-start | bytes 786440 | tf_op jit(solution)/shard_map/ppermute | solution.py:344
  21.2 12.4 %collective-permute-start.3 = (f32[4,2,32,256]{3,2,1,0:T(8,128)S(1)}, f32[4,2,32,256]{3,2,1,0:T(8,128)S(1)}, u32[]{:S(2)}, u32[]{:S(2)}) collective-permute-start(f32[4,2,32,256]{3,2,1,0:T(8,128)S(1)} %get-tuple-element.29), channel_id=1, source_target_pairs={{0,4},{1,5},{2,6},{3,7},{4,0},{5,1},{6,2},{7,3},{8,12},{9,13},{10,... | collective-permute-start | bytes 786440 | tf_op jit(solution)/shard_map/ppermute | solution.py:344
  22.7 10.9 %collective-permute-start.4 = (f32[4,2,32,256]{3,2,1,0:T(8,128)S(1)}, f32[4,2,32,256]{3,2,1,0:T(8,128)S(1)}, u32[]{:S(2)}, u32[]{:S(2)}) collective-permute-start(f32[4,2,32,256]{3,2,1,0:T(8,128)S(1)} %get-tuple-element.30), channel_id=1, source_target_pairs={{0,6},{1,7},{2,4},{3,5},{4,2},{5,3},{6,0},{7,1},{8,14},{9,15},{10,... | collective-permute-start | bytes 786440 | tf_op jit(solution)/shard_map/ppermute | solution.py:344
  34.0 2.0 %collective-permute-start.5 = (f32[4,2,64,256]{3,2,1,0:T(8,128)S(1)}, f32[4,2,64,256]{3,2,1,0:T(8,128)S(1)}, u32[]{:S(2)}, u32[]{:S(2)}) collective-permute-start(f32[4,2,64,256]{3,2,1,0:T(8,128)S(1)} %shard_map.123), channel_id=1, source_target_pairs={{0,1},{1,0},{2,3},{3,2},{4,5},{5,4},{6,7},{7,6},{8,9},{9,8},{10,11... | collective-permute-start | bytes 1572872 | tf_op jit(solution)/shard_map/ppermute | solution.py:368
  36.0 6.3 %collective-permute-start.6 = (f32[4,2,16,256]{3,2,1,0:T(8,128)S(1)}, f32[4,2,16,256]{3,2,1,0:T(8,128)S(1)}, u32[]{:S(2)}, u32[]{:S(2)}) collective-permute-start(f32[4,2,16,256]{3,2,1,0:T(8,128)S(1)} %get-tuple-element.32), channel_id=1, source_target_pairs={{0,2},{1,3},{2,0},{3,1},{4,6},{5,7},{6,4},{7,5},{8,10},{9,11},{10,... | collective-permute-start | bytes 393224 | tf_op jit(solution)/shard_map/ppermute | solution.py:344
  37.3 6.5 %collective-permute-start.7 = (f32[4,2,16,256]{3,2,1,0:T(8,128)S(1)}, f32[4,2,16,256]{3,2,1,0:T(8,128)S(1)}, u32[]{:S(2)}, u32[]{:S(2)}) collective-permute-start(f32[4,2,16,256]{3,2,1,0:T(8,128)S(1)} %get-tuple-element.33), channel_id=1, source_target_pairs={{0,4},{1,5},{2,6},{3,7},{4,0},{5,1},{6,2},{7,3},{8,12},{9,13},{10,... | collective-permute-start | bytes 393224 | tf_op jit(solution)/shard_map/ppermute | solution.py:344
  38.2 7.2 %collective-permute-start.8 = (f32[4,2,16,256]{3,2,1,0:T(8,128)S(1)}, f32[4,2,16,256]{3,2,1,0:T(8,128)S(1)}, u32[]{:S(2)}, u32[]{:S(2)}) collective-permute-start(f32[4,2,16,256]{3,2,1,0:T(8,128)S(1)} %get-tuple-element.34), channel_id=1, source_target_pairs={{0,6},{1,7},{2,4},{3,5},{4,2},{5,3},{6,0},{7,1},{8,14},{9,15},{10,... | collective-permute-start | bytes 393224 | tf_op jit(solution)/shard_map/ppermute | solution.py:344

commit v4 on v3

--- a/solution.py
+++ b/solution.py
@@ -101,12 +101,15 @@
     return copies
 
 
-def ends_kernel(patterns, partners, op_index, operators, low, high, partners_out, op_out, sems):
-    width = low.shape[0]
+def ends_kernel(
+    patterns, partners, op_index, operators, first, second, partners_out, op_out, sems
+):
+    width = first.shape[0]
     last = patterns.shape[0] - width
+    odd = lax.axis_index("group") % 2
     pairs = [
-        (patterns.at[pl.ds(0, width)], low),
-        (patterns.at[pl.ds(last, width)], high),
+        (patterns.at[pl.ds((1 - odd) * last, width)], first),
+        (patterns.at[pl.ds(odd * last, width)], second),
         (partners, partners_out),
         (op_index, op_out),
     ]
@@ -143,17 +146,16 @@
             out[c, 1, band, :] = im
 
 
-def halo_terms(partners, op_index, own, operators, below, above, total):
+def halo_terms(partners, op_index, own, operators, first, second, total):
     clusters, _, rows, _ = own.shape
     terms = partners.shape[1]
-    width = below.shape[0]
-    base = lax.axis_index("group") * clusters
+    width = first.shape[0]
+    group = lax.axis_index("group")
+    base = group * clusters
     total[...] = own[...]
 
-    for n in range(2 * width):
+    def add(n, halo, shift):
         c = n if n < width else n + clusters - 2 * width
-        halo = below if n < width else above
-        shift = width - base if n < width else -base - clusters
 
         @pl.loop(0, terms)
         def _(p):
@@ -162,13 +164,23 @@
             @pl.when((q < 0) | (q >= clusters))
             def _():
                 e = op_index[c, p]
-                h = jnp.clip(partners[c, p] + shift, 0, width - 1)
+                h = jnp.clip(q + shift, 0, width - 1)
                 for r in range(rows // 8):
                     band = pl.ds(r * 8, 8)
                     ore, oim = operators[e, 0, band, :], operators[e, 1, band, :]
                     pre, pim = halo[h, 0, band, :], halo[h, 1, band, :]
                     total[c, 0, band, :] += ore * pre - oim * pim
                     total[c, 1, band, :] += ore * pim + oim * pre
+
+    for odd, below, above in ((0, second, first), (1, first, second)):
+
+        @pl.when(group % 2 == odd)
+        def _():
+            for n in range(2 * width):
+                if n < width:
+                    add(n, below, width)
+                else:
+                    add(n, above, -clusters)
 
 
 def shift_and_phi(
@@ -194,11 +206,11 @@
 
 
 def first_kernel(
-    order, partners, op_index, child_parent, child_octant, own, operators, below, above, phase,
+    order, partners, op_index, child_parent, child_octant, own, operators, first, second, phase,
     phi_hi, phi_lo, *rest
 ):
     outs, (total, shifted) = rest[:-2], rest[-2:]
-    halo_terms(partners, op_index, own, operators, below, above, total)
+    halo_terms(partners, op_index, own, operators, first, second, total)
     shift_and_phi(
         order, child_parent, child_octant, total, phase, phi_hi, phi_lo, outs, shifted
     )
@@ -278,11 +290,9 @@
     width = clusters // 4
     member = lax.axis_index("member")
     chip, core = member // CORES, member % CORES
-    up = [(i, i + 1) for i in range(groups - 1)]
-    down = [(i + 1, i) for i in range(groups - 1)]
     end = shape(width, 2, rows, lons)
     index = jax.ShapeDtypeStruct(partners.shape, jnp.int32)
-    low, high, partners, operator_index = pl.pallas_call(
+    first, second, partners, operator_index = pl.pallas_call(
         ends_kernel,
         out_shape=(end, end, index, index),
         in_specs=[HBM] * 4,
@@ -290,8 +300,10 @@
         scratch_shapes=[pltpu.SemaphoreType.DMA((4,))],
         compiler_params=params(4),
     )(*map(in_hbm, (patterns, partners, operator_index, operators)))
-    below = lax.ppermute(high, "group", up)
-    above = lax.ppermute(low, "group", down)
+    pairs = [[(i, i + 1) for i in range(start, groups - 1, 2)] for start in range(2)]
+    pairs = [both + [(j, i) for i, j in both] for both in pairs]
+    first = lax.ppermute(first, "group", pairs[0])
+    second = lax.ppermute(second, "group", pairs[1])
 
     total_shape = shape(clusters, 2, rows, lons)
     own, phase = pl.pallas_call(
@@ -322,7 +334,7 @@
         compiler_params=params(20),
         cost_estimate=cost(2),
     )(
-        partners, operator_index, child_parent, child_octant, own, operators, below, above,
+        partners, operator_index, child_parent, child_octant, own, operators, first, second,
         phase, *phi,
     )
     sent.update(zip(far, outs))

time: 46.4 us -> 43.3 us (0.933)
  the two profiles are of different devices: /device:TPU:0 before, /device:TPU:8 now
where the time goes in v4:
time: 43.3 us; the launch traced here: 43.2 us
  waiting for transfers between devices  21.6 us (50%)
  starting transfers between devices  12.5 us (29%)
  Pallas kernels  8.87 us (20%)
    ppermute x6, waiting for transfers between devices, between_chips(): moved[s] = lax.ppermute(blocks[s], 'member', pairs)  16.5 us
    ppermute x6, starting transfers between devices, between_chips(): moved[s] = lax.ppermute(blocks[s], 'member', pairs)  7.11 us
    ppermute x1, starting transfers between devices, on_device(): second = lax.ppermute(second, 'group', pairs[1])  5.3 us
    ppermute x1, waiting for transfers between devices, on_device(): second = lax.ppermute(second, 'group', pairs[1])  3.42 us
    pallas_call x1, Pallas kernels, on_device(): pl.pallas_call(functools.partial(own_kernel, theta_count), out_shape=(tot...  2.42 us
    pallas_call x1, Pallas kernels, on_device(): call(functools.partial(first_kernel, far), out_shape=(block,) * len(far)...  1.95 us
    pallas_call x1, Pallas kernels, on_device(): call(functools.partial(later_kernel, near), out_shape=(block,) * len(near...  1.48 us
    ppermute x1, waiting for transfers between devices, on_device(): swapped = lax.ppermute(away, 'member', swap)  1.43 us
  transfers between devices with their start and end apart: 9, of which 8 were waited for; matrix products, arithmetic and copies ran while one was open for 0% of the time, Pallas kernels for 7%

profile of v4, /device:TPU:8, one launch (start us, length us, event | category | flops | bytes accessed | tf_op | source)
XLA Modules:
  0.0 43.2 jit_solution(2623579870799405509)
XLA Ops:
  0.0 0.0 copy-start
  0.0 0.0 copy-start.1
  0.0 0.0 copy-start.2
  0.0 0.0 copy-start.3
  0.0 0.0 copy-start.7
  0.0 0.0 copy-start.6
  0.0 1.2 %shard_map.118 = (f32[2,2,32,512]{3,2,1,0:T(8,128)S(1)}, f32[2,2,32,512]{3,2,1,0:T(8,128)S(1)}, s32[8,8]{1,0:T(8,128)S(1)}, s32[8,8]{1,0:T(8,128)S(1)}) custom-call(f32[8,2,32,512]{3,2,1,0:T(8,128)} %patterns.3, s32[8,8]{1,0:T(8,128)} %partners.1, s32[8,8]{1,0:T(8,128)} %op_index.1, f32[100,2,32,512]{3,2,1,0:T(8,128)} %operators.5), custom_call_target="tpu_custom_call" | custom-call | tf_op jit(solution)/shard_map/pallas_call | solution.py:295
  1.3 0.1 collective-permute-start
  1.4 5.3 %collective-permute-start.1 = (f32[2,2,32,512]{3,2,1,0:T(8,128)S(1)}, f32[2,2,32,512]{3,2,1,0:T(8,128)S(1)}, u32[]{:S(2)}, u32[]{:S(2)}) collective-permute-start(f32[2,2,32,512]{3,2,1,0:T(8,128)S(1)} %get-tuple-element.24), channel_id=1, source_target_pairs={{8,16},{16,8},{9,17},{17,9},{10,18},{18,10},{11,19},{19,11},{12,20... | collective-permute-start | bytes 786440 | tf_op jit(solution)/shard_map/ppermute | solution.py:306
  6.7 0.0 copy-done
  6.7 0.0 copy-done.1
  6.7 0.0 copy-start.4
  6.7 0.0 copy-start.5
  6.7 2.4 %shard_map.119 = (f32[8,2,32,512]{3,2,1,0:T(8,128)S(1)}, f32[8,2,32,512]{3,2,1,0:T(8,128)S(1)}) custom-call(s32[8,8]{1,0:T(8,128)S(1)} %get-tuple-element.20.partners_in.partners, s32[8,8]{1,0:T(8,128)S(1)} %get-tuple-element.21.op_in.op_index, f32[8,2,32,512]{3,2,1,0:T(8,128)S(1)} %copy-done.1, f32[100,2,32,512]{3,2,1,0:T(8,128)S(1)} %copy-done), custom_call_target="tpu_custom_call" | custom-call | flops 16000000 | bytes 24000000 | tf_op jit(solution)/shard_map/pallas_call | solution.py:309
  9.1 0.3 collective-permute-done.first
  9.4 3.4 %collective-permute-done.1.second = f32[2,2,32,512]{3,2,1,0:T(8,128)S(1)} collective-permute-done((f32[2,2,32,512]{3,2,1,0:T(8,128)S(1)}, f32[2,2,32,512]{3,2,1,0:T(8,128)S(1)}, u32[]{:S(2)}, u32[]{:S(2)}) %collective-permute-start.1) | collective-permute-done | bytes 262176 | tf_op jit(solution)/shard_map/ppermute | solution.py:306
  12.8 0.0 copy-done.2
  12.8 0.0 copy-done.3
  12.8 0.0 copy-done.7
  12.8 0.0 copy-done.6
  12.8 2.0 %shard_map.120 = (f32[4,2,32,256]{3,2,1,0:T(8,128)S(1)}, f32[8,2,32,512]{3,2,1,0:T(8,128)S(1)}) custom-call(s32[8,8]{1,0:T(8,128)S(1)} %get-tuple-element.20.partners_in.partners, s32[8,8]{1,0:T(8,128)S(1)} %get-tuple-element.21.op_in.op_index, s32[16]{0:T(128)S(1)} %copy-done.6, s32[16]{0:T(128)S(1)} %copy-done.7, ...), custom_call_target="tpu_custom_call" | custom-call | flops 4000000 | bytes 6000000 | tf_op jit(solution)/shard_map/pallas_call | solution.py:328
  14.8 1.5 %shard_map.121 = (f32[4,2,32,256]{3,2,1,0:T(8,128)S(1)}, f32[4,2,32,256]{3,2,1,0:T(8,128)S(1)}, f32[4,2,32,256]{3,2,1,0:T(8,128)S(1)}) custom-call(s32[16]{0:T(128)S(1)} %copy-done.6, s32[16]{0:T(128)S(1)} %copy-done.7, f32[8,2,32,512]{3,2,1,0:T(8,128)S(1)} %get-tuple-element.26.total, f32[8,2,32,512]{3,2,1,0:T(8,128)S(1)} %get-tuple-element.25.phase, ...), custom_call_target="tpu_custom_call" | custom-call | flops 2000000 | bytes 3000000 | tf_op jit(solution)/shard_map/pallas_call | solution.py:341
  16.3 1.6 %collective-permute-start.2 = (f32[4,2,32,256]{3,2,1,0:T(8,128)S(1)}, f32[4,2,32,256]{3,2,1,0:T(8,128)S(1)}, u32[]{:S(2)}, u32[]{:S(2)}) collective-permute-start(f32[4,2,32,256]{3,2,1,0:T(8,128)S(1)} %get-tuple-element.28), channel_id=1, source_target_pairs={{0,2},{1,3},{2,0},{3,1},{4,6},{5,7},{6,4},{7,5},{8,10},{9,11},{10,... | collective-permute-start | bytes 786440 | tf_op jit(solution)/shard_map/ppermute | solution.py:356
  17.8 1.5 %collective-permute-start.3 = (f32[4,2,32,256]{3,2,1,0:T(8,128)S(1)}, f32[4,2,32,256]{3,2,1,0:T(8,128)S(1)}, u32[]{:S(2)}, u32[]{:S(2)}) collective-permute-start(f32[4,2,32,256]{3,2,1,0:T(8,128)S(1)} %get-tuple-element.29), channel_id=1, source_target_pairs={{0,4},{1,5},{2,6},{3,7},{4,0},{5,1},{6,2},{7,3},{8,12},{9,13},{10,... | collective-permute-start | bytes 786440 | tf_op jit(solution)/shard_map/ppermute | solution.py:356
  19.4 0.5 %collective-permute-start.4 = (f32[4,2,32,256]{3,2,1,0:T(8,128)S(1)}, f32[4,2,32,256]{3,2,1,0:T(8,128)S(1)}, u32[]{:S(2)}, u32[]{:S(2)}) collective-permute-start(f32[4,2,32,256]{3,2,1,0:T(8,128)S(1)} %get-tuple-element.30), channel_id=1, source_target_pairs={{0,6},{1,7},{2,4},{3,5},{4,2},{5,3},{6,0},{7,1},{8,14},{9,15},{10,... | collective-permute-start | bytes 786440 | tf_op jit(solution)/shard_map/ppermute | solution.py:356
  19.8 5.7 %collective-permute-done.2.rest_1_ = f32[4,2,32,256]{3,2,1,0:T(8,128)S(1)} collective-permute-done((f32[4,2,32,256]{3,2,1,0:T(8,128)S(1)}, f32[4,2,32,256]{3,2,1,0:T(8,128)S(1)}, u32[]{:S(2)}, u32[]{:S(2)}) %collective-permute-start.2) | collective-permute-done | bytes 262176 | tf_op jit(solution)/shard_map/ppermute | solution.py:356
  25.5 5.0 %collective-permute-done.3.rest_2_ = f32[4,2,32,256]{3,2,1,0:T(8,128)S(1)} collective-permute-done((f32[4,2,32,256]{3,2,1,0:T(8,128)S(1)}, f32[4,2,32,256]{3,2,1,0:T(8,128)S(1)}, u32[]{:S(2)}, u32[]{:S(2)}) %collective-permute-start.3) | collective-permute-done | bytes 262176 | tf_op jit(solution)/shard_map/ppermute | solution.py:356
  30.5 0.0 collective-permute-done.4.rest_3_
  30.5 0.0 copy-done.4
  30.5 0.0 copy-done.5
  30.5 0.5 %shard_map.123 = f32[4,2,64,256]{3,2,1,0:T(8,128)S(1)} custom-call(bf16[4,64,128]{2,1,0:T(8,128)(2,1)S(1)} %copy-done.5, bf16[4,64,128]{2,1,0:T(8,128)(2,1)S(1)} %copy-done.4, f32[4,2,32,256]{3,2,1,0:T(8,128)S(1)} %get-tuple-element.27.rest_0_, f32[4,2,32,256]{3,2,1,0:T(8,128)S(1)} %collective-permute-done.2.rest_1_, ...), custom_call_target="tpu_custom_call" | custom-call | flops 2000000 | bytes 3000000 | tf_op jit(solution)/shard_map/pallas_call | solution.py:369
  31.0 0.1 collective-permute-start.5
  31.0 0.5 %shard_map.122.keep = f32[4,2,64,256]{3,2,1,0:T(8,128)S(1)} custom-call(bf16[4,64,128]{2,1,0:T(8,128)(2,1)S(1)} %copy-done.5, bf16[4,64,128]{2,1,0:T(8,128)(2,1)S(1)} %copy-done.4, f32[4,2,32,256]{3,2,1,0:T(8,128)S(1)} %get-tuple-element.27.rest_0_, f32[4,2,32,256]{3,2,1,0:T(8,128)S(1)} %collective-permute-done.2.rest_1_, ...), custom_call_target="tpu_custom_call" | custom-call | flops 2000000 | bytes 3000000 | tf_op jit(solution)/shard_map/pallas_call | solution.py:369
  31.5 1.4 %collective-permute-done.5.arrived = f32[4,2,64,256]{3,2,1,0:T(8,128)S(1)} collective-permute-done((f32[4,2,64,256]{3,2,1,0:T(8,128)S(1)}, f32[4,2,64,256]{3,2,1,0:T(8,128)S(1)}, u32[]{:S(2)}, u32[]{:S(2)}) %collective-permute-start.5) | collective-permute-done | bytes 524320 | tf_op jit(solution)/shard_map/ppermute | solution.py:380
  32.9 0.1 shard_map.124
  33.0 1.3 %collective-permute-start.6 = (f32[4,2,16,256]{3,2,1,0:T(8,128)S(1)}, f32[4,2,16,256]{3,2,1,0:T(8,128)S(1)}, u32[]{:S(2)}, u32[]{:S(2)}) collective-permute-start(f32[4,2,16,256]{3,2,1,0:T(8,128)S(1)} %get-tuple-element.32), channel_id=1, source_target_pairs={{0,2},{1,3},{2,0},{3,1},{4,6},{5,7},{6,4},{7,5},{8,10},{9,11},{10,... | collective-permute-start | bytes 393224 | tf_op jit(solution)/shard_map/ppermute | solution.py:356
  34.3 0.8 %collective-permute-start.7 = (f32[4,2,16,256]{3,2,1,0:T(8,128)S(1)}, f32[4,2,16,256]{3,2,1,0:T(8,128)S(1)}, u32[]{:S(2)}, u32[]{:S(2)}) collective-permute-start(f32[4,2,16,256]{3,2,1,0:T(8,128)S(1)} %get-tuple-element.33), channel_id=1, source_target_pairs={{0,4},{1,5},{2,6},{3,7},{4,0},{5,1},{6,2},{7,3},{8,12},{9,13},{10,... | collective-permute-start | bytes 393224 | tf_op jit(solution)/shard_map/ppermute | solution.py:356
  35.1 1.4 %collective-permute-start.8 = (f32[4,2,16,256]{3,2,1,0:T(8,128)S(1)}, f32[4,2,16,256]{3,2,1,0:T(8,128)S(1)}, u32[]{:S(2)}, u32[]{:S(2)}) collective-permute-start(f32[4,2,16,256]{3,2,1,0:T(8,128)S(1)} %get-tuple-element.34), channel_id=1, source_target_pairs={{0,6},{1,7},{2,4},{3,5},{4,2},{5,3},{6,0},{7,1},{8,14},{9,15},{10,... | collective-permute-start | bytes 393224 | tf_op jit(solution)/shard_map/ppermute | solution.py:356
  36.6 2.7 %collective-permute-done.6.rest_1_ = f32[4,2,16,256]{3,2,1,0:T(8,128)S(1)} collective-permute-done((f32[4,2,16,256]{3,2,1,0:T(8,128)S(1)}, f32[4,2,16,256]{3,2,1,0:T(8,128)S(1)}, u32[]{:S(2)}, u32[]{:S(2)}) %collective-permute-start.6) | collective-permute-done | bytes 131104 | tf_op jit(solution)/shard_map/ppermute | solution.py:356
  39.3 1.5 %collective-permute-done.7.rest_2_ = f32[4,2,16,256]{3,2,1,0:T(8,128)S(1)} collective-permute-done((f32[4,2,16,256]{3,2,1,0:T(8,128)S(1)}, f32[4,2,16,256]{3,2,1,0:T(8,128)S(1)}, u32[]{:S(2)}, u32[]{:S(2)}) %collective-permute-start.7) | collective-permute-done | bytes 131104 | tf_op jit(solution)/shard_map/ppermute | solution.py:356
  40.7 1.6 %collective-permute-done.8.rest_3_ = f32[4,2,16,256]{3,2,1,0:T(8,128)S(1)} collective-permute-done((f32[4,2,16,256]{3,2,1,0:T(8,128)S(1)}, f32[4,2,16,256]{3,2,1,0:T(8,128)S(1)}, u32[]{:S(2)}, u32[]{:S(2)}) %collective-permute-start.8) | collective-permute-done | bytes 131104 | tf_op jit(solution)/shard_map/ppermute | solution.py:356
  42.4 0.8 %shard_map.125 = f32[16,2,16,256]{3,2,1,0:T(8,128)} custom-call(f32[4,2,16,256]{3,2,1,0:T(8,128)S(1)} %get-tuple-element.31.rest_0_, f32[4,2,16,256]{3,2,1,0:T(8,128)S(1)} %collective-permute-done.6.rest_1_, f32[4,2,16,256]{3,2,1,0:T(8,128)S(1)} %collective-permute-done.7.rest_2_, f32[4,2,16,256]{3,2,1,0:T(8,128)S(1)} %collective-permute-done.8.rest_3_), custom_call_target="tpu_custom_call" | custom-call | flops 2000000 | bytes 3000000 | tf_op jit(solution)/shard_map/pallas_call | solution.py:406
Async XLA Ops:
  0.0 6.7 %copy-start = (f32[100,2,32,512]{3,2,1,0:T(8,128)S(1)}, f32[100,2,32,512]{3,2,1,0:T(8,128)}, u32[]{:S(2)}) copy-start(f32[100,2,32,512]{3,2,1,0:T(8,128)} %operators.5) | copy-start | bytes 39321604
  0.0 6.7 %copy-start.1 = (f32[8,2,32,512]{3,2,1,0:T(8,128)S(1)}, f32[8,2,32,512]{3,2,1,0:T(8,128)}, u32[]{:S(2)}) copy-start(f32[8,2,32,512]{3,2,1,0:T(8,128)} %patterns.3) | copy-start | bytes 3145732
  0.0 12.8 %copy-start.2 = (bf16[512,256]{1,0:T(8,128)(2,1)S(1)}, bf16[512,256]{1,0:T(8,128)(2,1)}, u32[]{:S(2)}) copy-start(bf16[512,256]{1,0:T(8,128)(2,1)} %constant.9.clone.phi_lo) | copy-start | bytes 786436
  0.0 12.8 %copy-start.3 = (bf16[512,256]{1,0:T(8,128)(2,1)S(1)}, bf16[512,256]{1,0:T(8,128)(2,1)}, u32[]{:S(2)}) copy-start(bf16[512,256]{1,0:T(8,128)(2,1)} %constant.8.clone.phi_hi) | copy-start | bytes 786436
  0.0 12.8 %copy-start.7 = (s32[16]{0:T(128)S(1)}, s32[16]{0:T(128)}, u32[]{:S(2)}) copy-start(s32[16]{0:T(128)} %child_octant.3) | copy-start | bytes 196
  0.0 12.8 %copy-start.6 = (s32[16]{0:T(128)S(1)}, s32[16]{0:T(128)}, u32[]{:S(2)}) copy-start(s32[16]{0:T(128)} %child_parent.3) | copy-start | bytes 196
  1.3 8.1 %collective-permute-start = (f32[2,2,32,512]{3,2,1,0:T(8,128)S(1)}, f32[2,2,32,512]{3,2,1,0:T(8,128)S(1)}, u32[]{:S(2)}, u32[]{:S(2)}) collective-permute-start(f32[2,2,32,512]{3,2,1,0:T(8,128)S(1)} %get-tuple-element.23), channel_id=1, source_target_pairs={{0,8},{16,24},{8,0},{24,16},{1,9},{17,25},{9,1},{25,17},{2,10},{18... | collective-permute-start | bytes 786440 | tf_op jit(solution)/shard_map/ppermute | solution.py:305
  1.4 11.4 %collective-permute-start.1 = (f32[2,2,32,512]{3,2,1,0:T(8,128)S(1)}, f32[2,2,32,512]{3,2,1,0:T(8,128)S(1)}, u32[]{:S(2)}, u32[]{:S(2)}) collective-permute-start(f32[2,2,32,512]{3,2,1,0:T(8,128)S(1)} %get-tuple-element.24), channel_id=1, source_target_pairs={{8,16},{16,8},{9,17},{17,9},{10,18},{18,10},{11,19},{19,11},{12,20... | collective-permute-start | bytes 786440 | tf_op jit(solution)/shard_map/ppermute | solution.py:306
  6.7 23.8 %copy-start.4 = (bf16[4,64,128]{2,1,0:T(8,128)(2,1)S(1)}, bf16[4,64,128]{2,1,0:T(8,128)(2,1)}, u32[]{:S(2)}) copy-start(bf16[4,64,128]{2,1,0:T(8,128)(2,1)} %constant.11.clone.t_lo) | copy-start | bytes 196612
  6.7 23.8 %copy-start.5 = (bf16[4,64,128]{2,1,0:T(8,128)(2,1)S(1)}, bf16[4,64,128]{2,1,0:T(8,128)(2,1)}, u32[]{:S(2)}) copy-start(bf16[4,64,128]{2,1,0:T(8,128)(2,1)} %constant.10.clone.t_hi) | copy-start | bytes 196612
  16.3 9.2 %collective-permute-start.2 = (f32[4,2,32,256]{3,2,1,0:T(8,128)S(1)}, f32[4,2,32,256]{3,2,1,0:T(8,128)S(1)}, u32[]{:S(2)}, u32[]{:S(2)}) collective-permute-start(f32[4,2,32,256]{3,2,1,0:T(8,128)S(1)} %get-tuple-element.28), channel_id=1, source_target_pairs={{0,2},{1,3},{2,0},{3,1},{4,6},{5,7},{6,4},{7,5},{8,10},{9,11},{10,... | collective-permute-start | bytes 786440 | tf_op jit(solution)/shard_map/ppermute | solution.py:356
  17.8 12.7 %collective-permute-start.3 = (f32[4,2,32,256]{3,2,1,0:T(8,128)S(1)}, f32[4,2,32,256]{3,2,1,0:T(8,128)S(1)}, u32[]{:S(2)}, u32[]{:S(2)}) collective-permute-start(f32[4,2,32,256]{3,2,1,0:T(8,128)S(1)} %get-tuple-element.29), channel_id=1, source_target_pairs={{0,4},{1,5},{2,6},{3,7},{4,0},{5,1},{6,2},{7,3},{8,12},{9,13},{10,... | collective-permute-start | bytes 786440 | tf_op jit(solution)/shard_map/ppermute | solution.py:356
  19.4 11.1 %collective-permute-start.4 = (f32[4,2,32,256]{3,2,1,0:T(8,128)S(1)}, f32[4,2,32,256]{3,2,1,0:T(8,128)S(1)}, u32[]{:S(2)}, u32[]{:S(2)}) collective-permute-start(f32[4,2,32,256]{3,2,1,0:T(8,128)S(1)} %get-tuple-element.30), channel_id=1, source_target_pairs={{0,6},{1,7},{2,4},{3,5},{4,2},{5,3},{6,0},{7,1},{8,14},{9,15},{10,... | collective-permute-start | bytes 786440 | tf_op jit(solution)/shard_map/ppermute | solution.py:356
  31.0 2.0 %collective-permute-start.5 = (f32[4,2,64,256]{3,2,1,0:T(8,128)S(1)}, f32[4,2,64,256]{3,2,1,0:T(8,128)S(1)}, u32[]{:S(2)}, u32[]{:S(2)}) collective-permute-start(f32[4,2,64,256]{3,2,1,0:T(8,128)S(1)} %shard_map.123), channel_id=1, source_target_pairs={{0,1},{1,0},{2,3},{3,2},{4,5},{5,4},{6,7},{7,6},{8,9},{9,8},{10,11... | collective-permute-start | bytes 1572872 | tf_op jit(solution)/shard_map/ppermute | solution.py:380
  33.0 6.3 %collective-permute-start.6 = (f32[4,2,16,256]{3,2,1,0:T(8,128)S(1)}, f32[4,2,16,256]{3,2,1,0:T(8,128)S(1)}, u32[]{:S(2)}, u32[]{:S(2)}) collective-permute-start(f32[4,2,16,256]{3,2,1,0:T(8,128)S(1)} %get-tuple-element.32), channel_id=1, source_target_pairs={{0,2},{1,3},{2,0},{3,1},{4,6},{5,7},{6,4},{7,5},{8,10},{9,11},{10,... | collective-permute-start | bytes 393224 | tf_op jit(solution)/shard_map/ppermute | solution.py:356
  34.3 6.5 %collective-permute-start.7 = (f32[4,2,16,256]{3,2,1,0:T(8,128)S(1)}, f32[4,2,16,256]{3,2,1,0:T(8,128)S(1)}, u32[]{:S(2)}, u32[]{:S(2)}) collective-permute-start(f32[4,2,16,256]{3,2,1,0:T(8,128)S(1)} %get-tuple-element.33), channel_id=1, source_target_pairs={{0,4},{1,5},{2,6},{3,7},{4,0},{5,1},{6,2},{7,3},{8,12},{9,13},{10,... | collective-permute-start | bytes 393224 | tf_op jit(solution)/shard_map/ppermute | solution.py:356
  35.1 7.2 %collective-permute-start.8 = (f32[4,2,16,256]{3,2,1,0:T(8,128)S(1)}, f32[4,2,16,256]{3,2,1,0:T(8,128)S(1)}, u32[]{:S(2)}, u32[]{:S(2)}) collective-permute-start(f32[4,2,16,256]{3,2,1,0:T(8,128)S(1)} %get-tuple-element.34), channel_id=1, source_target_pairs={{0,6},{1,7},{2,4},{3,5},{4,2},{5,3},{6,0},{7,1},{8,14},{9,15},{10,... | collective-permute-start | bytes 393224 | tf_op jit(solution)/shard_map/ppermute | solution.py:356

commit v5 on v4

--- a/solution.py
+++ b/solution.py
@@ -13,6 +13,7 @@
 NTC = 128
 NPC = 256
 CORES = 2
+ROUNDS = 3
 REACH = 6.0
 F32 = jnp.float32
 BF16 = jnp.bfloat16
@@ -101,18 +102,14 @@
     return copies
 
 
-def ends_kernel(
-    patterns, partners, op_index, operators, first, second, partners_out, op_out, sems
-):
-    width = first.shape[0]
+def ends_kernel(patterns, partners, op_index, operators, *rest):
+    *ends, partners_out, op_out, sems = rest
+    width = ends[0].shape[0]
     last = patterns.shape[0] - width
-    odd = lax.axis_index("group") % 2
-    pairs = [
-        (patterns.at[pl.ds((1 - odd) * last, width)], first),
-        (patterns.at[pl.ds(odd * last, width)], second),
-        (partners, partners_out),
-        (op_index, op_out),
-    ]
+    upper = lax.axis_index("group") % ROUNDS
+    pairs = [(partners, partners_out), (op_index, op_out)]
+    for n, end in enumerate(ends):
+        pairs.append((patterns.at[pl.ds(jnp.where(upper == n, last, 0), width)], end))
     for copy in copy_all(pairs, sems):
         copy.wait()
 
@@ -146,10 +143,10 @@
             out[c, 1, band, :] = im
 
 
-def halo_terms(partners, op_index, own, operators, first, second, total):
+def halo_terms(partners, op_index, own, operators, halos, total):
     clusters, _, rows, _ = own.shape
     terms = partners.shape[1]
-    width = first.shape[0]
+    width = halos[0].shape[0]
     group = lax.axis_index("group")
     base = group * clusters
     total[...] = own[...]
@@ -172,9 +169,10 @@
                     total[c, 0, band, :] += ore * pre - oim * pim
                     total[c, 1, band, :] += ore * pim + oim * pre
 
-    for odd, below, above in ((0, second, first), (1, first, second)):
-
-        @pl.when(group % 2 == odd)
+    for turn in range(ROUNDS):
+        below, above = halos[turn - 1], halos[turn]
+
+        @pl.when(group % ROUNDS == turn)
         def _():
             for n in range(2 * width):
                 if n < width:
@@ -206,11 +204,10 @@
 
 
 def first_kernel(
-    order, partners, op_index, child_parent, child_octant, own, operators, first, second, phase,
-    phi_hi, phi_lo, *rest
+    order, partners, op_index, child_parent, child_octant, own, operators, phase, phi_hi, phi_lo, *rest
 ):
-    outs, (total, shifted) = rest[:-2], rest[-2:]
-    halo_terms(partners, op_index, own, operators, first, second, total)
+    halos, outs, (total, shifted) = rest[:ROUNDS], rest[ROUNDS:-2], rest[-2:]
+    halo_terms(partners, op_index, own, operators, halos, total)
     shift_and_phi(
         order, child_parent, child_octant, total, phase, phi_hi, phi_lo, outs, shifted
     )
@@ -292,18 +289,17 @@
     chip, core = member // CORES, member % CORES
     end = shape(width, 2, rows, lons)
     index = jax.ShapeDtypeStruct(partners.shape, jnp.int32)
-    first, second, partners, operator_index = pl.pallas_call(
+    *halos, partners, operator_index = pl.pallas_call(
         ends_kernel,
-        out_shape=(end, end, index, index),
+        out_shape=(end,) * ROUNDS + (index, index),
         in_specs=[HBM] * 4,
-        out_specs=(VMEM,) * 4,
-        scratch_shapes=[pltpu.SemaphoreType.DMA((4,))],
+        out_specs=(VMEM,) * (ROUNDS + 2),
+        scratch_shapes=[pltpu.SemaphoreType.DMA((ROUNDS + 2,))],
         compiler_params=params(4),
     )(*map(in_hbm, (patterns, partners, operator_index, operators)))
-    pairs = [[(i, i + 1) for i in range(start, groups - 1, 2)] for start in range(2)]
-    pairs = [both + [(j, i) for i, j in both] for both in pairs]
-    first = lax.ppermute(first, "group", pairs[0])
-    second = lax.ppermute(second, "group", pairs[1])
+    for n in range(ROUNDS):
+        both = [(i, i + 1) for i in range(n, groups - 1, ROUNDS)]
+        halos[n] = lax.ppermute(halos[n], "group", both + [(j, i) for i, j in both])
 
     total_shape = shape(clusters, 2, rows, lons)
     own, phase = pl.pallas_call(
@@ -328,14 +324,14 @@
     *outs, total = call(
         functools.partial(first_kernel, far),
         out_shape=(block,) * len(far) + (total_shape,),
-        in_specs=[SMEM] * 4 + [VMEM] * 7,
+        in_specs=[SMEM] * 4 + [VMEM] * (5 + ROUNDS),
         out_specs=(VMEM,) * (len(far) + 1),
         scratch_shapes=[shifted],
         compiler_params=params(20),
         cost_estimate=cost(2),
     )(
-        partners, operator_index, child_parent, child_octant, own, operators, first, second,
-        phase, *phi,
+        partners, operator_index, child_parent, child_octant, own, operators,
+        phase, *phi, *halos,
     )
     sent.update(zip(far, outs))
     outs = call(

time: 43.3 us -> 45.9 us (1.060)
  the two profiles are of different devices: /device:TPU:8 before, /device:TPU:16 now
where the time goes in v5:
time: 45.9 us; the launch traced here: 45.7 us
  waiting for transfers between devices  22.6 us (49%)
  starting transfers between devices  13.9 us (30%)
  Pallas kernels  8.93 us (19%)
    ppermute x6, waiting for transfers between devices, between_chips(): moved[s] = lax.ppermute(blocks[s], 'member', pairs)  15.9 us
    ppermute x6, starting transfers between devices, between_chips(): moved[s] = lax.ppermute(blocks[s], 'member', pairs)  7.11 us
    ppermute x3, starting transfers between devices, on_device(): halos[n] = lax.ppermute(halos[n], 'group', both + [(j, i) for i, j in both])  6.73 us
    ppermute x3, waiting for transfers between devices, on_device(): halos[n] = lax.ppermute(halos[n], 'group', both + [(j, i) for i, j in both])  5.25 us
    pallas_call x1, Pallas kernels, on_device(): pl.pallas_call(functools.partial(own_kernel, theta_count), out_shape=(tot...  2.42 us
    pallas_call x1, Pallas kernels, on_device(): call(functools.partial(first_kernel, far), out_shape=(block,) * len(far)...  1.9 us
    pallas_call x1, Pallas kernels, on_device(): call(functools.partial(later_kernel, near), out_shape=(block,) * len(near...  1.48 us
    ppermute x1, waiting for transfers between devices, on_device(): swapped = lax.ppermute(away, 'member', swap)  1.43 us
  transfers between devices with their start and end apart: 10, of which 8 were waited for; matrix products, arithmetic and copies ran while one was open for 0% of the time, Pallas kernels for 6%

profile of v5, /device:TPU:16, one launch (start us, length us, event | category | flops | bytes accessed | tf_op | source)
XLA Modules:
  0.0 45.7 jit_solution(17822609142854616880)
XLA Ops:
  0.0 0.0 copy-start
  0.0 0.0 copy-start.1
  0.0 0.0 copy-start.2
  0.0 0.0 copy-start.3
  0.0 0.0 copy-start.7
  0.0 0.0 copy-start.6
  0.0 1.3 %shard_map.118 = (f32[2,2,32,512]{3,2,1,0:T(8,128)S(1)}, f32[2,2,32,512]{3,2,1,0:T(8,128)S(1)}, f32[2,2,32,512]{3,2,1,0:T(8,128)S(1)}, s32[8,8]{1,0:T(8,128)S(1)}, s32[8,8]{1,0:T(8,128)S(1)}) custom-call(f32[8,2,32,512]{3,2,1,0:T(8,128)} %patterns.3, s32[8,8]{1,0:T(8,128)} %partners.1, s32[8,8]{1,0:T(8,128)} %op_index.1, f32[100,2,32,512]{3,2,1,0:T(8,128)} %operators.5), custom_call_target="tpu_custom_call" | custom-call | tf_op jit(solution)/shard_map/pallas_call | solution.py:292
  1.4 0.8 %collective-permute-start = (f32[2,2,32,512]{3,2,1,0:T(8,128)S(1)}, f32[2,2,32,512]{3,2,1,0:T(8,128)S(1)}, u32[]{:S(2)}, u32[]{:S(2)}) collective-permute-start(f32[2,2,32,512]{3,2,1,0:T(8,128)S(1)} %get-tuple-element.25), channel_id=1, source_target_pairs={{0,8},{8,0},{1,9},{9,1},{2,10},{10,2},{3,11},{11,3},{4,12},{12,4},... | collective-permute-start | bytes 786440 | tf_op jit(solution)/shard_map/ppermute | solution.py:302
  2.2 4.0 %collective-permute-start.1 = (f32[2,2,32,512]{3,2,1,0:T(8,128)S(1)}, f32[2,2,32,512]{3,2,1,0:T(8,128)S(1)}, u32[]{:S(2)}, u32[]{:S(2)}) collective-permute-start(f32[2,2,32,512]{3,2,1,0:T(8,128)S(1)} %get-tuple-element.26), channel_id=1, source_target_pairs={{8,16},{16,8},{9,17},{17,9},{10,18},{18,10},{11,19},{19,11},{12,20... | collective-permute-start | bytes 786440 | tf_op jit(solution)/shard_map/ppermute | solution.py:302
  6.2 1.9 %collective-permute-start.2 = (f32[2,2,32,512]{3,2,1,0:T(8,128)S(1)}, f32[2,2,32,512]{3,2,1,0:T(8,128)S(1)}, u32[]{:S(2)}, u32[]{:S(2)}) collective-permute-start(f32[2,2,32,512]{3,2,1,0:T(8,128)S(1)} %get-tuple-element.27), channel_id=1, source_target_pairs={{16,24},{24,16},{17,25},{25,17},{18,26},{26,18},{19,27},{27,19},{2... | collective-permute-start | bytes 786440 | tf_op jit(solution)/shard_map/ppermute | solution.py:302
  8.1 0.0 copy-done
  8.1 0.0 copy-done.1
  8.2 2.4 %shard_map.119 = (f32[8,2,32,512]{3,2,1,0:T(8,128)S(1)}, f32[8,2,32,512]{3,2,1,0:T(8,128)S(1)}) custom-call(s32[8,8]{1,0:T(8,128)S(1)} %get-tuple-element.21.partners_in.partners, s32[8,8]{1,0:T(8,128)S(1)} %get-tuple-element.22.op_in.op_index, f32[8,2,32,512]{3,2,1,0:T(8,128)S(1)} %copy-done.1, f32[100,2,32,512]{3,2,1,0:T(8,128)S(1)} %copy-done), custom_call_target="tpu_custom_call" | custom-call | flops 16000000 | bytes 24000000 | tf_op jit(solution)/shard_map/pallas_call | solution.py:305
  10.6 0.0 copy-start.4
  10.6 0.0 copy-start.5
  10.6 0.0 collective-permute-done.rest_0_
  10.6 1.9 %collective-permute-done.1.rest_1_ = f32[2,2,32,512]{3,2,1,0:T(8,128)S(1)} collective-permute-done((f32[2,2,32,512]{3,2,1,0:T(8,128)S(1)}, f32[2,2,32,512]{3,2,1,0:T(8,128)S(1)}, u32[]{:S(2)}, u32[]{:S(2)}) %collective-permute-start.1) | collective-permute-done | bytes 262176 | tf_op jit(solution)/shard_map/ppermute | solution.py:302
  12.5 3.4 %collective-permute-done.2.rest_2_ = f32[2,2,32,512]{3,2,1,0:T(8,128)S(1)} collective-permute-done((f32[2,2,32,512]{3,2,1,0:T(8,128)S(1)}, f32[2,2,32,512]{3,2,1,0:T(8,128)S(1)}, u32[]{:S(2)}, u32[]{:S(2)}) %collective-permute-start.2) | collective-permute-done | bytes 262176 | tf_op jit(solution)/shard_map/ppermute | solution.py:302
  15.9 0.0 copy-done.2
  15.9 0.0 copy-done.3
  15.9 0.0 copy-done.7
  15.9 0.0 copy-done.6
  15.9 1.9 %shard_map.120 = (f32[4,2,32,256]{3,2,1,0:T(8,128)S(1)}, f32[8,2,32,512]{3,2,1,0:T(8,128)S(1)}) custom-call(s32[8,8]{1,0:T(8,128)S(1)} %get-tuple-element.21.partners_in.partners, s32[8,8]{1,0:T(8,128)S(1)} %get-tuple-element.22.op_in.op_index, s32[16]{0:T(128)S(1)} %copy-done.6, s32[16]{0:T(128)S(1)} %copy-done.7, ...), custom_call_target="tpu_custom_call" | custom-call | flops 4000000 | bytes 6000000 | tf_op jit(solution)/shard_map/pallas_call | solution.py:324
  17.8 1.5 %shard_map.121 = (f32[4,2,32,256]{3,2,1,0:T(8,128)S(1)}, f32[4,2,32,256]{3,2,1,0:T(8,128)S(1)}, f32[4,2,32,256]{3,2,1,0:T(8,128)S(1)}) custom-call(s32[16]{0:T(128)S(1)} %copy-done.6, s32[16]{0:T(128)S(1)} %copy-done.7, f32[8,2,32,512]{3,2,1,0:T(8,128)S(1)} %get-tuple-element.28.total, f32[8,2,32,512]{3,2,1,0:T(8,128)S(1)} %get-tuple-element.24.phase, ...), custom_call_target="tpu_custom_call" | custom-call | flops 2000000 | bytes 3000000 | tf_op jit(solution)/shard_map/pallas_call | solution.py:337
  19.3 1.7 %collective-permute-start.3 = (f32[4,2,32,256]{3,2,1,0:T(8,128)S(1)}, f32[4,2,32,256]{3,2,1,0:T(8,128)S(1)}, u32[]{:S(2)}, u32[]{:S(2)}) collective-permute-start(f32[4,2,32,256]{3,2,1,0:T(8,128)S(1)} %get-tuple-element.30), channel_id=1, source_target_pairs={{0,2},{1,3},{2,0},{3,1},{4,6},{5,7},{6,4},{7,5},{8,10},{9,11},{10,... | collective-permute-start | bytes 786440 | tf_op jit(solution)/shard_map/ppermute | solution.py:352
  21.0 1.5 %collective-permute-start.4 = (f32[4,2,32,256]{3,2,1,0:T(8,128)S(1)}, f32[4,2,32,256]{3,2,1,0:T(8,128)S(1)}, u32[]{:S(2)}, u32[]{:S(2)}) collective-permute-start(f32[4,2,32,256]{3,2,1,0:T(8,128)S(1)} %get-tuple-element.31), channel_id=1, source_target_pairs={{0,4},{1,5},{2,6},{3,7},{4,0},{5,1},{6,2},{7,3},{8,12},{9,13},{10,... | collective-permute-start | bytes 786440 | tf_op jit(solution)/shard_map/ppermute | solution.py:352
  22.5 0.3 collective-permute-start.5
  22.8 5.7 %collective-permute-done.3.rest_1_ = f32[4,2,32,256]{3,2,1,0:T(8,128)S(1)} collective-permute-done((f32[4,2,32,256]{3,2,1,0:T(8,128)S(1)}, f32[4,2,32,256]{3,2,1,0:T(8,128)S(1)}, u32[]{:S(2)}, u32[]{:S(2)}) %collective-permute-start.3) | collective-permute-done | bytes 262176 | tf_op jit(solution)/shard_map/ppermute | solution.py:352
  28.5 4.4 %collective-permute-done.4.rest_2_ = f32[4,2,32,256]{3,2,1,0:T(8,128)S(1)} collective-permute-done((f32[4,2,32,256]{3,2,1,0:T(8,128)S(1)}, f32[4,2,32,256]{3,2,1,0:T(8,128)S(1)}, u32[]{:S(2)}, u32[]{:S(2)}) %collective-permute-start.4) | collective-permute-done | bytes 262176 | tf_op jit(solution)/shard_map/ppermute | solution.py:352
  33.0 0.0 collective-permute-done.5.rest_3_
  33.0 0.0 copy-done.4
  33.0 0.0 copy-done.5
  33.0 0.5 %shard_map.123 = f32[4,2,64,256]{3,2,1,0:T(8,128)S(1)} custom-call(bf16[4,64,128]{2,1,0:T(8,128)(2,1)S(1)} %copy-done.5, bf16[4,64,128]{2,1,0:T(8,128)(2,1)S(1)} %copy-done.4, f32[4,2,32,256]{3,2,1,0:T(8,128)S(1)} %get-tuple-element.29.rest_0_, f32[4,2,32,256]{3,2,1,0:T(8,128)S(1)} %collective-permute-done.3.rest_1_, ...), custom_call_target="tpu_custom_call" | custom-call | flops 2000000 | bytes 3000000 | tf_op jit(solution)/shard_map/pallas_call | solution.py:365
  33.5 0.1 collective-permute-start.6
  33.5 0.5 %shard_map.122.keep = f32[4,2,64,256]{3,2,1,0:T(8,128)S(1)} custom-call(bf16[4,64,128]{2,1,0:T(8,128)(2,1)S(1)} %copy-done.5, bf16[4,64,128]{2,1,0:T(8,128)(2,1)S(1)} %copy-done.4, f32[4,2,32,256]{3,2,1,0:T(8,128)S(1)} %get-tuple-element.29.rest_0_, f32[4,2,32,256]{3,2,1,0:T(8,128)S(1)} %collective-permute-done.3.rest_1_, ...), custom_call_target="tpu_custom_call" | custom-call | flops 2000000 | bytes 3000000 | tf_op jit(solution)/shard_map/pallas_call | solution.py:365
  34.0 1.4 %collective-permute-done.6.arrived = f32[4,2,64,256]{3,2,1,0:T(8,128)S(1)} collective-permute-done((f32[4,2,64,256]{3,2,1,0:T(8,128)S(1)}, f32[4,2,64,256]{3,2,1,0:T(8,128)S(1)}, u32[]{:S(2)}, u32[]{:S(2)}) %collective-permute-start.6) | collective-permute-done | bytes 524320 | tf_op jit(solution)/shard_map/ppermute | solution.py:376
  35.4 0.1 shard_map.124
  35.5 1.3 %collective-permute-start.7 = (f32[4,2,16,256]{3,2,1,0:T(8,128)S(1)}, f32[4,2,16,256]{3,2,1,0:T(8,128)S(1)}, u32[]{:S(2)}, u32[]{:S(2)}) collective-permute-start(f32[4,2,16,256]{3,2,1,0:T(8,128)S(1)} %get-tuple-element.34), channel_id=1, source_target_pairs={{0,2},{1,3},{2,0},{3,1},{4,6},{5,7},{6,4},{7,5},{8,10},{9,11},{10,... | collective-permute-start | bytes 393224 | tf_op jit(solution)/shard_map/ppermute | solution.py:352
  36.8 0.8 %collective-permute-start.8 = (f32[4,2,16,256]{3,2,1,0:T(8,128)S(1)}, f32[4,2,16,256]{3,2,1,0:T(8,128)S(1)}, u32[]{:S(2)}, u32[]{:S(2)}) collective-permute-start(f32[4,2,16,256]{3,2,1,0:T(8,128)S(1)} %get-tuple-element.35), channel_id=1, source_target_pairs={{0,4},{1,5},{2,6},{3,7},{4,0},{5,1},{6,2},{7,3},{8,12},{9,13},{10,... | collective-permute-start | bytes 393224 | tf_op jit(solution)/shard_map/ppermute | solution.py:352
  37.6 1.4 %collective-permute-start.9 = (f32[4,2,16,256]{3,2,1,0:T(8,128)S(1)}, f32[4,2,16,256]{3,2,1,0:T(8,128)S(1)}, u32[]{:S(2)}, u32[]{:S(2)}) collective-permute-start(f32[4,2,16,256]{3,2,1,0:T(8,128)S(1)} %get-tuple-element.36), channel_id=1, source_target_pairs={{0,6},{1,7},{2,4},{3,5},{4,2},{5,3},{6,0},{7,1},{8,14},{9,15},{10,... | collective-permute-start | bytes 393224 | tf_op jit(solution)/shard_map/ppermute | solution.py:352
  39.0 2.7 %collective-permute-done.7.rest_1_ = f32[4,2,16,256]{3,2,1,0:T(8,128)S(1)} collective-permute-done((f32[4,2,16,256]{3,2,1,0:T(8,128)S(1)}, f32[4,2,16,256]{3,2,1,0:T(8,128)S(1)}, u32[]{:S(2)}, u32[]{:S(2)}) %collective-permute-start.7) | collective-permute-done | bytes 131104 | tf_op jit(solution)/shard_map/ppermute | solution.py:352
  41.8 1.4 %collective-permute-done.8.rest_2_ = f32[4,2,16,256]{3,2,1,0:T(8,128)S(1)} collective-permute-done((f32[4,2,16,256]{3,2,1,0:T(8,128)S(1)}, f32[4,2,16,256]{3,2,1,0:T(8,128)S(1)}, u32[]{:S(2)}, u32[]{:S(2)}) %collective-permute-start.8) | collective-permute-done | bytes 131104 | tf_op jit(solution)/shard_map/ppermute | solution.py:352
  43.2 1.6 %collective-permute-done.9.rest_3_ = f32[4,2,16,256]{3,2,1,0:T(8,128)S(1)} collective-permute-done((f32[4,2,16,256]{3,2,1,0:T(8,128)S(1)}, f32[4,2,16,256]{3,2,1,0:T(8,128)S(1)}, u32[]{:S(2)}, u32[]{:S(2)}) %collective-permute-start.9) | collective-permute-done | bytes 131104 | tf_op jit(solution)/shard_map/ppermute | solution.py:352
  44.8 0.8 %shard_map.125 = f32[16,2,16,256]{3,2,1,0:T(8,128)} custom-call(f32[4,2,16,256]{3,2,1,0:T(8,128)S(1)} %get-tuple-element.33.rest_0_, f32[4,2,16,256]{3,2,1,0:T(8,128)S(1)} %collective-permute-done.7.rest_1_, f32[4,2,16,256]{3,2,1,0:T(8,128)S(1)} %collective-permute-done.8.rest_2_, f32[4,2,16,256]{3,2,1,0:T(8,128)S(1)} %collective-permute-done.9.rest_3_), custom_call_target="tpu_custom_call" | custom-call | flops 2000000 | bytes 3000000 | tf_op jit(solution)/shard_map/pallas_call | solution.py:402
Async XLA Ops:
  0.0 8.1 %copy-start = (f32[100,2,32,512]{3,2,1,0:T(8,128)S(1)}, f32[100,2,32,512]{3,2,1,0:T(8,128)}, u32[]{:S(2)}) copy-start(f32[100,2,32,512]{3,2,1,0:T(8,128)} %operators.5) | copy-start | bytes 39321604
  0.0 8.1 %copy-start.1 = (f32[8,2,32,512]{3,2,1,0:T(8,128)S(1)}, f32[8,2,32,512]{3,2,1,0:T(8,128)}, u32[]{:S(2)}) copy-start(f32[8,2,32,512]{3,2,1,0:T(8,128)} %patterns.3) | copy-start | bytes 3145732
  0.0 15.9 %copy-start.2 = (bf16[512,256]{1,0:T(8,128)(2,1)S(1)}, bf16[512,256]{1,0:T(8,128)(2,1)}, u32[]{:S(2)}) copy-start(bf16[512,256]{1,0:T(8,128)(2,1)} %constant.9.clone.phi_lo) | copy-start | bytes 786436
  0.0 15.9 %copy-start.3 = (bf16[512,256]{1,0:T(8,128)(2,1)S(1)}, bf16[512,256]{1,0:T(8,128)(2,1)}, u32[]{:S(2)}) copy-start(bf16[512,256]{1,0:T(8,128)(2,1)} %constant.8.clone.phi_hi) | copy-start | bytes 786436
  0.0 15.9 %copy-start.7 = (s32[16]{0:T(128)S(1)}, s32[16]{0:T(128)}, u32[]{:S(2)}) copy-start(s32[16]{0:T(128)} %child_octant.3) | copy-start | bytes 196
  0.0 15.8 %copy-start.6 = (s32[16]{0:T(128)S(1)}, s32[16]{0:T(128)}, u32[]{:S(2)}) copy-start(s32[16]{0:T(128)} %child_parent.3) | copy-start | bytes 196
  1.4 9.2 %collective-permute-start = (f32[2,2,32,512]{3,2,1,0:T(8,128)S(1)}, f32[2,2,32,512]{3,2,1,0:T(8,128)S(1)}, u32[]{:S(2)}, u32[]{:S(2)}) collective-permute-start(f32[2,2,32,512]{3,2,1,0:T(8,128)S(1)} %get-tuple-element.25), channel_id=1, source_target_pairs={{0,8},{8,0},{1,9},{9,1},{2,10},{10,2},{3,11},{11,3},{4,12},{12,4},... | collective-permute-start | bytes 786440 | tf_op jit(solution)/shard_map/ppermute | solution.py:302
  2.2 10.3 %collective-permute-start.1 = (f32[2,2,32,512]{3,2,1,0:T(8,128)S(1)}, f32[2,2,32,512]{3,2,1,0:T(8,128)S(1)}, u32[]{:S(2)}, u32[]{:S(2)}) collective-permute-start(f32[2,2,32,512]{3,2,1,0:T(8,128)S(1)} %get-tuple-element.26), channel_id=1, source_target_pairs={{8,16},{16,8},{9,17},{17,9},{10,18},{18,10},{11,19},{19,11},{12,20... | collective-permute-start | bytes 786440 | tf_op jit(solution)/shard_map/ppermute | solution.py:302
  6.2 9.7 %collective-permute-start.2 = (f32[2,2,32,512]{3,2,1,0:T(8,128)S(1)}, f32[2,2,32,512]{3,2,1,0:T(8,128)S(1)}, u32[]{:S(2)}, u32[]{:S(2)}) collective-permute-start(f32[2,2,32,512]{3,2,1,0:T(8,128)S(1)} %get-tuple-element.27), channel_id=1, source_target_pairs={{16,24},{24,16},{17,25},{25,17},{18,26},{26,18},{19,27},{27,19},{2... | collective-permute-start | bytes 786440 | tf_op jit(solution)/shard_map/ppermute | solution.py:302
  10.6 22.4 %copy-start.4 = (bf16[4,64,128]{2,1,0:T(8,128)(2,1)S(1)}, bf16[4,64,128]{2,1,0:T(8,128)(2,1)}, u32[]{:S(2)}) copy-start(bf16[4,64,128]{2,1,0:T(8,128)(2,1)} %constant.11.clone.t_lo) | copy-start | bytes 196612
  10.6 22.4 %copy-start.5 = (bf16[4,64,128]{2,1,0:T(8,128)(2,1)S(1)}, bf16[4,64,128]{2,1,0:T(8,128)(2,1)}, u32[]{:S(2)}) copy-start(bf16[4,64,128]{2,1,0:T(8,128)(2,1)} %constant.10.clone.t_hi) | copy-start | bytes 196612
  19.3 9.2 %collective-permute-start.3 = (f32[4,2,32,256]{3,2,1,0:T(8,128)S(1)}, f32[4,2,32,256]{3,2,1,0:T(8,128)S(1)}, u32[]{:S(2)}, u32[]{:S(2)}) collective-permute-start(f32[4,2,32,256]{3,2,1,0:T(8,128)S(1)} %get-tuple-element.30), channel_id=1, source_target_pairs={{0,2},{1,3},{2,0},{3,1},{4,6},{5,7},{6,4},{7,5},{8,10},{9,11},{10,... | collective-permute-start | bytes 786440 | tf_op jit(solution)/shard_map/ppermute | solution.py:352
  21.0 12.0 %collective-permute-start.4 = (f32[4,2,32,256]{3,2,1,0:T(8,128)S(1)}, f32[4,2,32,256]{3,2,1,0:T(8,128)S(1)}, u32[]{:S(2)}, u32[]{:S(2)}) collective-permute-start(f32[4,2,32,256]{3,2,1,0:T(8,128)S(1)} %get-tuple-element.31), channel_id=1, source_target_pairs={{0,4},{1,5},{2,6},{3,7},{4,0},{5,1},{6,2},{7,3},{8,12},{9,13},{10,... | collective-permute-start | bytes 786440 | tf_op jit(solution)/shard_map/ppermute | solution.py:352
  22.5 10.5 %collective-permute-start.5 = (f32[4,2,32,256]{3,2,1,0:T(8,128)S(1)}, f32[4,2,32,256]{3,2,1,0:T(8,128)S(1)}, u32[]{:S(2)}, u32[]{:S(2)}) collective-permute-start(f32[4,2,32,256]{3,2,1,0:T(8,128)S(1)} %get-tuple-element.32), channel_id=1, source_target_pairs={{0,6},{1,7},{2,4},{3,5},{4,2},{5,3},{6,0},{7,1},{8,14},{9,15},{10,... | collective-permute-start | bytes 786440 | tf_op jit(solution)/shard_map/ppermute | solution.py:352
  33.5 2.0 %collective-permute-start.6 = (f32[4,2,64,256]{3,2,1,0:T(8,128)S(1)}, f32[4,2,64,256]{3,2,1,0:T(8,128)S(1)}, u32[]{:S(2)}, u32[]{:S(2)}) collective-permute-start(f32[4,2,64,256]{3,2,1,0:T(8,128)S(1)} %shard_map.123), channel_id=1, source_target_pairs={{0,1},{1,0},{2,3},{3,2},{4,5},{5,4},{6,7},{7,6},{8,9},{9,8},{10,11... | collective-permute-start | bytes 1572872 | tf_op jit(solution)/shard_map/ppermute | solution.py:376
  35.5 6.3 %collective-permute-start.7 = (f32[4,2,16,256]{3,2,1,0:T(8,128)S(1)}, f32[4,2,16,256]{3,2,1,0:T(8,128)S(1)}, u32[]{:S(2)}, u32[]{:S(2)}) collective-permute-start(f32[4,2,16,256]{3,2,1,0:T(8,128)S(1)} %get-tuple-element.34), channel_id=1, source_target_pairs={{0,2},{1,3},{2,0},{3,1},{4,6},{5,7},{6,4},{7,5},{8,10},{9,11},{10,... | collective-permute-start | bytes 393224 | tf_op jit(solution)/shard_map/ppermute | solution.py:352
  36.8 6.5 %collective-permute-start.8 = (f32[4,2,16,256]{3,2,1,0:T(8,128)S(1)}, f32[4,2,16,256]{3,2,1,0:T(8,128)S(1)}, u32[]{:S(2)}, u32[]{:S(2)}) collective-permute-start(f32[4,2,16,256]{3,2,1,0:T(8,128)S(1)} %get-tuple-element.35), channel_id=1, source_target_pairs={{0,4},{1,5},{2,6},{3,7},{4,0},{5,1},{6,2},{7,3},{8,12},{9,13},{10,... | collective-permute-start | bytes 393224 | tf_op jit(solution)/shard_map/ppermute | solution.py:352
  37.6 7.2 %collective-permute-start.9 = (f32[4,2,16,256]{3,2,1,0:T(8,128)S(1)}, f32[4,2,16,256]{3,2,1,0:T(8,128)S(1)}, u32[]{:S(2)}, u32[]{:S(2)}) collective-permute-start(f32[4,2,16,256]{3,2,1,0:T(8,128)S(1)} %get-tuple-element.36), channel_id=1, source_target_pairs={{0,6},{1,7},{2,4},{3,5},{4,2},{5,3},{6,0},{7,1},{8,14},{9,15},{10,... | collective-permute-start | bytes 393224 | tf_op jit(solution)/shard_map/ppermute | solution.py:352

commit v6 on v4

--- a/solution.py
+++ b/solution.py
@@ -183,56 +183,100 @@
                     add(n, above, -clusters)
 
 
+def fill_slots(child_parent, slots, clusters, width, chips):
+    base = lax.axis_index("group") * clusters
+
+    def place_child(k, counts):
+        early, late = counts
+        q = child_parent[k] - base
+        inner = (q >= width) & (q < clusters - width) & (early < chips)
+        slots[jnp.where(inner, early, late)] = k
+        step = jnp.where(inner, 1, 0)
+        return early + step, late + 1 - step
+
+    lax.fori_loop(0, slots.shape[0], place_child, (jnp.int32(0), jnp.int32(chips)))
+
+
+def slot_of(chip, i, chips, per_chip):
+    return jnp.where(i == 0, chip, chips + chip * (per_chip - 1) + i - 1)
+
+
 def shift_and_phi(
-    order, child_parent, child_octant, total, phase, phi_hi, phi_lo, outs, shifted
+    order, first, slots, child_parent, child_octant, total, phase, phi_hi, phi_lo, outs, shifted
 ):
     clusters, _, rows, _ = total.shape
+    chips = lax.axis_size("member") // CORES
+    per_chip = slots.shape[0] // chips
     base = lax.axis_index("group") * clusters
     chip = lax.axis_index("member") // CORES
-    for s, out in zip(order, outs):
-        first = (chip ^ s) * out.shape[0]
-        for i in range(out.shape[0]):
-            q = child_parent[first + i] - base
-            o = child_octant[first + i]
-            for r in range(rows // 8):
-                band = pl.ds(r * 8, 8)
-                pre, pim = total[q, 0, band, :], total[q, 1, band, :]
-                ere, eim = phase[o, 0, band, :], phase[o, 1, band, :]
-                at = i * 2 * rows + r * 8
-                shifted[pl.ds(at, 8), :] = pre * ere - pim * eim
-                shifted[pl.ds(at + rows, 8), :] = pre * eim + pim * ere
+    count = outs[0].shape[0]
+    size = count * 2 * rows
+    group = shifted.shape[0] // size
+    for start in range(0, len(order), group):
+        part = list(zip(order, outs))[start:start + group]
+        for m, (s, _) in enumerate(part):
+            for i in range(count):
+                k = slots[slot_of(chip ^ s, first + i, chips, per_chip)]
+                q = child_parent[k] - base
+                o = child_octant[k]
+                for r in range(rows // 8):
+                    band = pl.ds(r * 8, 8)
+                    pre, pim = total[q, 0, band, :], total[q, 1, band, :]
+                    ere, eim = phase[o, 0, band, :], phase[o, 1, band, :]
+                    at = m * size + i * 2 * rows + r * 8
+                    shifted[pl.ds(at, 8), :] = pre * ere - pim * eim
+                    shifted[pl.ds(at + rows, 8), :] = pre * eim + pim * ere
         y = dot3(split(shifted[...]), (phi_hi[...], phi_lo[...]))
-        out[...] = y.reshape(out.shape)
+        for m, (_, out) in enumerate(part):
+            out[...] = y[m * size:(m + 1) * size].reshape(out.shape)
+
+
+def early_kernel(width, child_parent, child_octant, own, phase, phi_hi, phi_lo, *rest):
+    *outs, slots, shifted = rest
+    fill_slots(child_parent, slots, own.shape[0], width, len(outs))
+    shift_and_phi(
+        range(len(outs)), 0, slots, child_parent, child_octant, own, phase, phi_hi, phi_lo,
+        outs, shifted,
+    )
 
 
 def first_kernel(
     order, partners, op_index, child_parent, child_octant, own, operators, first, second, phase,
     phi_hi, phi_lo, *rest
 ):
-    outs, (total, shifted) = rest[:-2], rest[-2:]
+    *outs, total, slots, shifted = rest
+    chips = lax.axis_size("member") // CORES
+    fill_slots(child_parent, slots, own.shape[0], first.shape[0], chips)
     halo_terms(partners, op_index, own, operators, first, second, total)
     shift_and_phi(
-        order, child_parent, child_octant, total, phase, phi_hi, phi_lo, outs, shifted
-    )
-
-
-def later_kernel(order, child_parent, child_octant, total, phase, phi_hi, phi_lo, *rest):
+        order, 1, slots, child_parent, child_octant, total, phase, phi_hi, phi_lo, outs, shifted
+    )
+
+
+def later_kernel(
+    order, width, child_parent, child_octant, total, phase, phi_hi, phi_lo, *rest
+):
+    *outs, slots, shifted = rest
+    fill_slots(child_parent, slots, total.shape[0], width, len(outs) + 1)
     shift_and_phi(
-        order, child_parent, child_octant, total, phase, phi_hi, phi_lo, rest[:-1], rest[-1]
+        order, 1, slots, child_parent, child_octant, total, phase, phi_hi, phi_lo, outs, shifted
     )
 
 
 def theta_kernel(away, t_hi, t_lo, *rest):
-    blocks, (out, lats) = rest[:-2], rest[-2:]
+    *blocks, out, lats = rest
+    chips = len(blocks) // 2
+    early, late = blocks[:chips], blocks[chips:]
     member = lax.axis_index("member")
     chip, core = member // CORES, member % CORES
     t = core * CORES + (1 - core if away else core)
-    per_chip, _, rows, _ = blocks[0].shape
-    for i in range(per_chip):
+    rows = early[0].shape[2]
+    for i in range(out.shape[0]):
         for part in range(2):
-            for s, block in enumerate(blocks):
+            for s in range(chips):
                 at = pl.multiple_of((chip ^ s) * rows, rows)
-                lats[pl.ds(at, rows), :] = block[i, part]
+                block = early[s][0, part] if i == 0 else late[s][i - 1, part]
+                lats[pl.ds(at, rows), :] = block
             out[i, part] = dot3((t_hi[t], t_lo[t]), split(lats[...]))
 
 
@@ -244,17 +288,17 @@
         out[...] = keep[:, :, band, :] + arrived[:, :, band, :]
 
 
-def place_kernel(*rest):
-    blocks, (out, sems) = rest[:-2], rest[-2:]
+def place_kernel(clusters, width, child_parent, *rest):
+    *blocks, out, slots, sems = rest
+    chips, per_chip = len(blocks), blocks[0].shape[0]
     chip = lax.axis_index("member") // CORES
-    per_chip = blocks[0].shape[0]
-    copies = []
-    for s, block in enumerate(blocks):
-        first = (chip ^ s) * per_chip
-        copy = pltpu.make_async_copy(block, out.at[pl.ds(first, per_chip)], sems.at[s])
-        copy.start()
-        copies.append(copy)
-    for copy in copies:
+    fill_slots(child_parent, slots, clusters, width, chips)
+    pairs = [
+        (block.at[i], out.at[slots[slot_of(chip ^ s, i, chips, per_chip)]])
+        for s, block in enumerate(blocks)
+        for i in range(per_chip)
+    ]
+    for copy in copy_all(pairs, sems):
         copy.wait()
 
 
@@ -321,33 +365,14 @@
     )(partners, operator_index, patterns, operators)
 
     phi = split_const(phi_table(lons, NPC).T)
-    block = shape(per_chip, 2, rows, NPC)
-    shifted = pltpu.VMEM((per_chip * 2 * rows, lons), F32)
-    far, near = [chips - 1], [*range(1, chips - 1), 0]
-    sent = dict.fromkeys(range(chips))
-    *outs, total = call(
-        functools.partial(first_kernel, far),
-        out_shape=(block,) * len(far) + (total_shape,),
-        in_specs=[SMEM] * 4 + [VMEM] * 7,
-        out_specs=(VMEM,) * (len(far) + 1),
-        scratch_shapes=[shifted],
-        compiler_params=params(20),
-        cost_estimate=cost(2),
-    )(
-        partners, operator_index, child_parent, child_octant, own, operators, first, second,
-        phase, *phi,
-    )
-    sent.update(zip(far, outs))
-    outs = call(
-        functools.partial(later_kernel, near),
-        out_shape=(block,) * len(near),
-        in_specs=[SMEM] * 2 + [VMEM] * 4,
-        out_specs=(VMEM,) * len(near),
-        scratch_shapes=[shifted],
-        compiler_params=params(20),
-        cost_estimate=cost(1),
-    )(child_parent, child_octant, total, phase, *phi)
-    sent.update(zip(near, outs))
+    assert per_chip > 1 and clusters - 2 * width >= chips
+    slots = pltpu.SMEM((children,), jnp.int32)
+
+    def blocks_of(count, number):
+        return (shape(count, 2, rows, NPC),) * number
+
+    def rows_of(count):
+        return pltpu.VMEM((count * 2 * rows, lons), F32)
 
     def between_chips(blocks):
         moved = dict(blocks)
@@ -356,7 +381,44 @@
             moved[s] = lax.ppermute(blocks[s], "member", pairs)
         return [moved[s] for s in range(chips)]
 
-    arrived = between_chips(sent)
+    early = call(
+        functools.partial(early_kernel, width),
+        out_shape=blocks_of(1, chips),
+        in_specs=[SMEM] * 2 + [VMEM] * 4,
+        out_specs=(VMEM,) * chips,
+        scratch_shapes=[slots, rows_of(chips)],
+        compiler_params=params(20),
+        cost_estimate=cost(1),
+    )(child_parent, child_octant, own, phase, *phi)
+    early = between_chips(dict(enumerate(early)))
+
+    count = per_chip - 1
+    far, near = [chips - 1], [*range(1, chips - 1), 0]
+    late = {}
+    *outs, total = call(
+        functools.partial(first_kernel, far),
+        out_shape=blocks_of(count, len(far)) + (total_shape,),
+        in_specs=[SMEM] * 4 + [VMEM] * 7,
+        out_specs=(VMEM,) * (len(far) + 1),
+        scratch_shapes=[slots, rows_of(count)],
+        compiler_params=params(20),
+        cost_estimate=cost(2),
+    )(
+        partners, operator_index, child_parent, child_octant, own, operators, first, second,
+        phase, *phi,
+    )
+    late.update(zip(far, outs))
+    outs = call(
+        functools.partial(later_kernel, near, width),
+        out_shape=blocks_of(count, len(near)),
+        in_specs=[SMEM] * 2 + [VMEM] * 4,
+        out_specs=(VMEM,) * len(near),
+        scratch_shapes=[slots, rows_of(count)],
+        compiler_params=params(20),
+        cost_estimate=cost(1),
+    )(child_parent, child_octant, total, phase, *phi)
+    late.update(zip(near, outs))
+    late = between_chips(late)
 
     theta = theta_table(theta_count, NTC).reshape(chips, CORES, out_rows, chips, CORES, rows)
     theta = theta.transpose(4, 1, 0, 2, 3, 5).reshape(
@@ -369,12 +431,12 @@
             call(
                 functools.partial(theta_kernel, name == "away"),
                 out_shape=half,
-                in_specs=[VMEM] * (2 + chips),
+                in_specs=[VMEM] * (2 + 2 * chips),
                 out_specs=VMEM,
                 scratch_shapes=[pltpu.VMEM((chips * rows, NPC), F32)],
                 compiler_params=params(12),
                 cost_estimate=cost(1),
-            )(*split_const(theta), *arrived)
+            )(*split_const(theta), *early, *late)
             for name in ("away", "keep")
         )
         swapped = lax.ppermute(away, "member", swap)
@@ -388,7 +450,8 @@
         )(keep, swapped)
     else:
         order = chip ^ jnp.arange(chips)
-        lats = jnp.take(jnp.stack(arrived), order, axis=0)
+        lats = jnp.stack([jnp.concatenate(pair) for pair in zip(early, late)])
+        lats = jnp.take(lats, order, axis=0)
         lats = lats.transpose(1, 2, 0, 3, 4).reshape(per_chip, 2, chips * rows, NPC)
         both = jnp.take(
             jnp.asarray(theta, F32).reshape(CORES, CORES, chips * out_rows, chips * rows),
@@ -404,14 +467,14 @@
 
     final = between_chips(dict(enumerate(pieces)))
     return call(
-        place_kernel,
+        functools.partial(place_kernel, clusters, width),
         out_shape=shape(children, 2, out_rows, NPC),
-        in_specs=[VMEM] * chips,
+        in_specs=[SMEM] + [VMEM] * chips,
         out_specs=HBM,
-        scratch_shapes=[pltpu.SemaphoreType.DMA((chips,))],
+        scratch_shapes=[slots, pltpu.SemaphoreType.DMA((children,))],
         compiler_params=params(12),
         cost_estimate=cost(1),
-    )(*final)
+    )(child_parent, *final)
 
 
 def solution(mesh):

time: 43.3 us -> 47.3 us (1.092)
  the two profiles are of different devices: /device:TPU:8 before, /device:TPU:14 now
where the time goes in v6:
time: 47.3 us; the launch traced here: 47.2 us
  waiting for transfers between devices  21.6 us (46%)
  starting transfers between devices  14.1 us (30%)
  Pallas kernels  11.2 us (24%)
    ppermute x9, waiting for transfers between devices, between_chips(): moved[s] = lax.ppermute(blocks[s], 'member', pairs)  16.5 us
    ppermute x9, starting transfers between devices, between_chips(): moved[s] = lax.ppermute(blocks[s], 'member', pairs)  8.69 us
    ppermute x1, starting transfers between devices, on_device(): second = lax.ppermute(second, 'group', pairs[1])  4.86 us
    ppermute x1, waiting for transfers between devices, on_device(): second = lax.ppermute(second, 'group', pairs[1])  3.42 us
    pallas_call x1, Pallas kernels, on_device(): pl.pallas_call(functools.partial(own_kernel, theta_count), out_shape=(tot...  2.42 us
    pallas_call x1, Pallas kernels, on_device(): call(functools.partial(first_kernel, far), out_shape=blocks_of(count, len...  2.13 us
    pallas_call x1, Pallas kernels, on_device(): call(functools.partial(place_kernel, clusters, width), out_shape=shape(ch...  1.69 us
    pallas_call x1, Pallas kernels, on_device(): call(functools.partial(later_kernel, near, width), out_shape=blocks_of(co...  1.54 us
  transfers between devices with their start and end apart: 12, of which 7 were waited for; matrix products, arithmetic and copies ran while one was open for 0% of the time, Pallas kernels for 9%

profile of v6, /device:TPU:14, one launch (start us, length us, event | category | flops | bytes accessed | tf_op | source)
XLA Modules:
  0.0 47.2 jit_solution(3331489795857900113)
XLA Ops:
  0.0 0.0 copy-start.1
  0.0 0.0 copy-start
  0.0 0.0 copy-start.3
  0.0 0.0 copy-start.6
  0.0 0.0 copy-start.7
  0.0 1.2 %shard_map.118 = (f32[2,2,32,512]{3,2,1,0:T(8,128)S(1)}, f32[2,2,32,512]{3,2,1,0:T(8,128)S(1)}, s32[8,8]{1,0:T(8,128)S(1)}, s32[8,8]{1,0:T(8,128)S(1)}) custom-call(f32[8,2,32,512]{3,2,1,0:T(8,128)} %patterns.3, s32[8,8]{1,0:T(8,128)} %partners.1, s32[8,8]{1,0:T(8,128)} %op_index.1, f32[100,2,32,512]{3,2,1,0:T(8,128)} %operators.5), custom_call_target="tpu_custom_call" | custom-call | tf_op jit(solution)/shard_map/pallas_call | solution.py:339
  1.3 0.5 %collective-permute-start.3 = (f32[2,2,32,512]{3,2,1,0:T(8,128)S(1)}, f32[2,2,32,512]{3,2,1,0:T(8,128)S(1)}, u32[]{:S(2)}, u32[]{:S(2)}) collective-permute-start(f32[2,2,32,512]{3,2,1,0:T(8,128)S(1)} %get-tuple-element.32), channel_id=1, source_target_pairs={{0,8},{16,24},{8,0},{24,16},{1,9},{17,25},{9,1},{25,17},{2,10},{18... | collective-permute-start | bytes 786440 | tf_op jit(solution)/shard_map/ppermute | solution.py:349
  1.8 4.9 %collective-permute-start.4 = (f32[2,2,32,512]{3,2,1,0:T(8,128)S(1)}, f32[2,2,32,512]{3,2,1,0:T(8,128)S(1)}, u32[]{:S(2)}, u32[]{:S(2)}) collective-permute-start(f32[2,2,32,512]{3,2,1,0:T(8,128)S(1)} %get-tuple-element.33), channel_id=1, source_target_pairs={{8,16},{16,8},{9,17},{17,9},{10,18},{18,10},{11,19},{19,11},{12,20... | collective-permute-start | bytes 786440 | tf_op jit(solution)/shard_map/ppermute | solution.py:350
  6.7 0.0 copy-done.1
  6.7 0.0 copy-done
  6.7 2.4 %shard_map.119 = (f32[8,2,32,512]{3,2,1,0:T(8,128)S(1)}, f32[8,2,32,512]{3,2,1,0:T(8,128)S(1)}) custom-call(s32[8,8]{1,0:T(8,128)S(1)} %get-tuple-element.24.partners_in.partners, s32[8,8]{1,0:T(8,128)S(1)} %get-tuple-element.25.op_in.op_index, f32[8,2,32,512]{3,2,1,0:T(8,128)S(1)} %copy-done.1, f32[100,2,32,512]{3,2,1,0:T(8,128)S(1)} %copy-done), custom_call_target="tpu_custom_call" | custom-call | flops 16000000 | bytes 24000000 | tf_op jit(solution)/shard_map/pallas_call | solution.py:353
  9.1 0.0 copy-start.4
  9.1 0.0 copy-start.5
  9.1 0.3 collective-permute-done.3.first
  9.4 3.4 %collective-permute-done.4.second = f32[2,2,32,512]{3,2,1,0:T(8,128)S(1)} collective-permute-done((f32[2,2,32,512]{3,2,1,0:T(8,128)S(1)}, f32[2,2,32,512]{3,2,1,0:T(8,128)S(1)}, u32[]{:S(2)}, u32[]{:S(2)}) %collective-permute-start.4) | collective-permute-done | bytes 262176 | tf_op jit(solution)/shard_map/ppermute | solution.py:350
  12.8 0.0 copy-done.2
  12.8 0.0 copy-done.3
  12.8 0.0 copy-done.6
  12.8 0.0 copy-done.7
  12.8 2.1 %shard_map.121 = (f32[3,2,32,256]{3,2,1,0:T(8,128)S(1)}, f32[8,2,32,512]{3,2,1,0:T(8,128)S(1)}) custom-call(s32[8,8]{1,0:T(8,128)S(1)} %get-tuple-element.24.partners_in.partners, s32[8,8]{1,0:T(8,128)S(1)} %get-tuple-element.25.op_in.op_index, s32[16]{0:T(128)S(1)} %copy-done.6, s32[16]{0:T(128)S(1)} %copy-done.7, ...), custom_call_target="tpu_custom_call" | custom-call | flops 4000000 | bytes 6000000 | tf_op jit(solution)/shard_map/pallas_call | solution.py:398
  15.0 1.5 %shard_map.122 = (f32[3,2,32,256]{3,2,1,0:T(8,128)S(1)}, f32[3,2,32,256]{3,2,1,0:T(8,128)S(1)}, f32[3,2,32,256]{3,2,1,0:T(8,128)S(1)}) custom-call(s32[16]{0:T(128)S(1)} %copy-done.6, s32[16]{0:T(128)S(1)} %copy-done.7, f32[8,2,32,512]{3,2,1,0:T(8,128)S(1)} %get-tuple-element.34.total, f32[8,2,32,512]{3,2,1,0:T(8,128)S(1)} %get-tuple-element.27.phase, ...), custom_call_target="tpu_custom_call" | custom-call | flops 2000000 | bytes 3000000 | tf_op jit(solution)/shard_map/pallas_call | solution.py:411
  16.5 0.6 %collective-permute-start.5 = (f32[3,2,32,256]{3,2,1,0:T(8,128)S(1)}, f32[3,2,32,256]{3,2,1,0:T(8,128)S(1)}, u32[]{:S(2)}, u32[]{:S(2)}) collective-permute-start(f32[3,2,32,256]{3,2,1,0:T(8,128)S(1)} %get-tuple-element.36), channel_id=1, source_target_pairs={{0,2},{1,3},{2,0},{3,1},{4,6},{5,7},{6,4},{7,5},{8,10},{9,11},{10,... | collective-permute-start | bytes 589832 | tf_op jit(solution)/shard_map/ppermute | solution.py:381
  17.1 0.5 %collective-permute-start.6 = (f32[3,2,32,256]{3,2,1,0:T(8,128)S(1)}, f32[3,2,32,256]{3,2,1,0:T(8,128)S(1)}, u32[]{:S(2)}, u32[]{:S(2)}) collective-permute-start(f32[3,2,32,256]{3,2,1,0:T(8,128)S(1)} %get-tuple-element.37), channel_id=1, source_target_pairs={{0,4},{1,5},{2,6},{3,7},{4,0},{5,1},{6,2},{7,3},{8,12},{9,13},{10,... | collective-permute-start | bytes 589832 | tf_op jit(solution)/shard_map/ppermute | solution.py:381
  17.6 2.4 %collective-permute-start.7 = (f32[3,2,32,256]{3,2,1,0:T(8,128)S(1)}, f32[3,2,32,256]{3,2,1,0:T(8,128)S(1)}, u32[]{:S(2)}, u32[]{:S(2)}) collective-permute-start(f32[3,2,32,256]{3,2,1,0:T(8,128)S(1)} %get-tuple-element.38), channel_id=1, source_target_pairs={{0,6},{1,7},{2,4},{3,5},{4,2},{5,3},{6,0},{7,1},{8,14},{9,15},{10,... | collective-permute-start | bytes 589832 | tf_op jit(solution)/shard_map/ppermute | solution.py:381
  20.1 1.2 %shard_map.120 = (f32[1,2,32,256]{3,2,1,0:T(8,128)S(1)}, f32[1,2,32,256]{3,2,1,0:T(8,128)S(1)}, f32[1,2,32,256]{3,2,1,0:T(8,128)S(1)}, f32[1,2,32,256]{3,2,1,0:T(8,128)S(1)}) custom-call(s32[16]{0:T(128)S(1)} %copy-done.6, s32[16]{0:T(128)S(1)} %copy-done.7, f32[8,2,32,512]{3,2,1,0:T(8,128)S(1)} %get-tuple-element.26.own, ...), custom_call_target="tpu_custom_call" | custom-call | flops 2000000 | bytes 3000000 | tf_op jit(solution)/shard_map/pallas_call | solution.py:384
  21.3 0.6 %collective-permute-start = (f32[1,2,32,256]{3,2,1,0:T(8,128)S(1)}, f32[1,2,32,256]{3,2,1,0:T(8,128)S(1)}, u32[]{:S(2)}, u32[]{:S(2)}) collective-permute-start(f32[1,2,32,256]{3,2,1,0:T(8,128)S(1)} %get-tuple-element.29), channel_id=1, source_target_pairs={{0,2},{1,3},{2,0},{3,1},{4,6},{5,7},{6,4},{7,5},{8,10},{9,11},{10,... | collective-permute-start | bytes 196616 | tf_op jit(solution)/shard_map/ppermute | solution.py:381
  21.9 0.5 %collective-permute-start.1 = (f32[1,2,32,256]{3,2,1,0:T(8,128)S(1)}, f32[1,2,32,256]{3,2,1,0:T(8,128)S(1)}, u32[]{:S(2)}, u32[]{:S(2)}) collective-permute-start(f32[1,2,32,256]{3,2,1,0:T(8,128)S(1)} %get-tuple-element.30), channel_id=1, source_target_pairs={{0,4},{1,5},{2,6},{3,7},{4,0},{5,1},{6,2},{7,3},{8,12},{9,13},{10,... | collective-permute-start | bytes 196616 | tf_op jit(solution)/shard_map/ppermute | solution.py:381
  22.4 5.8 %collective-permute-done.rest_1_ = f32[1,2,32,256]{3,2,1,0:T(8,128)S(1)} collective-permute-done((f32[1,2,32,256]{3,2,1,0:T(8,128)S(1)}, f32[1,2,32,256]{3,2,1,0:T(8,128)S(1)}, u32[]{:S(2)}, u32[]{:S(2)}) %collective-permute-start) | collective-permute-done | bytes 65568 | tf_op jit(solution)/shard_map/ppermute | solution.py:381
  28.1 0.5 %collective-permute-start.2 = (f32[1,2,32,256]{3,2,1,0:T(8,128)S(1)}, f32[1,2,32,256]{3,2,1,0:T(8,128)S(1)}, u32[]{:S(2)}, u32[]{:S(2)}) collective-permute-start(f32[1,2,32,256]{3,2,1,0:T(8,128)S(1)} %get-tuple-element.31), channel_id=1, source_target_pairs={{0,6},{1,7},{2,4},{3,5},{4,2},{5,3},{6,0},{7,1},{8,14},{9,15},{10,... | collective-permute-start | bytes 196616 | tf_op jit(solution)/shard_map/ppermute | solution.py:381
  28.6 0.0 collective-permute-done.1.rest_2_
  28.6 4.7 %collective-permute-done.2.rest_3_ = f32[1,2,32,256]{3,2,1,0:T(8,128)S(1)} collective-permute-done((f32[1,2,32,256]{3,2,1,0:T(8,128)S(1)}, f32[1,2,32,256]{3,2,1,0:T(8,128)S(1)}, u32[]{:S(2)}, u32[]{:S(2)}) %collective-permute-start.2) | collective-permute-done | bytes 65568 | tf_op jit(solution)/shard_map/ppermute | solution.py:381
  33.3 0.0 collective-permute-done.5.rest_5_
  33.3 0.0 collective-permute-done.6.rest_6_
  33.3 0.0 collective-permute-done.7.rest_7_
  33.3 0.0 copy-done.4
  33.3 0.0 copy-done.5
  33.3 0.5 %shard_map.124 = f32[4,2,64,256]{3,2,1,0:T(8,128)S(1)} custom-call(bf16[4,64,128]{2,1,0:T(8,128)(2,1)S(1)} %copy-done.4, bf16[4,64,128]{2,1,0:T(8,128)(2,1)S(1)} %copy-done.5, f32[1,2,32,256]{3,2,1,0:T(8,128)S(1)} %get-tuple-element.28.rest_0_, f32[1,2,32,256]{3,2,1,0:T(8,128)S(1)} %collective-permute-done.rest_1_, ...), custom_call_target="tpu_custom_call" | custom-call | flops 2000000 | bytes 3000000 | tf_op jit(solution)/shard_map/pallas_call | solution.py:431
  33.8 0.1 collective-permute-start.8
  33.9 0.5 %shard_map.123.keep = f32[4,2,64,256]{3,2,1,0:T(8,128)S(1)} custom-call(bf16[4,64,128]{2,1,0:T(8,128)(2,1)S(1)} %copy-done.4, bf16[4,64,128]{2,1,0:T(8,128)(2,1)S(1)} %copy-done.5, f32[1,2,32,256]{3,2,1,0:T(8,128)S(1)} %get-tuple-element.28.rest_0_, f32[1,2,32,256]{3,2,1,0:T(8,128)S(1)} %collective-permute-done.rest_1_, ...), custom_call_target="tpu_custom_call" | custom-call | flops 2000000 | bytes 3000000 | tf_op jit(solution)/shard_map/pallas_call | solution.py:431
  34.4 1.4 %collective-permute-done.8.arrived = f32[4,2,64,256]{3,2,1,0:T(8,128)S(1)} collective-permute-done((f32[4,2,64,256]{3,2,1,0:T(8,128)S(1)}, f32[4,2,64,256]{3,2,1,0:T(8,128)S(1)}, u32[]{:S(2)}, u32[]{:S(2)}) %collective-permute-start.8) | collective-permute-done | bytes 524320 | tf_op jit(solution)/shard_map/ppermute | solution.py:442
  35.8 0.1 shard_map.125
  35.9 0.6 %collective-permute-start.10 = (f32[4,2,16,256]{3,2,1,0:T(8,128)S(1)}, f32[4,2,16,256]{3,2,1,0:T(8,128)S(1)}, u32[]{:S(2)}, u32[]{:S(2)}) collective-permute-start(f32[4,2,16,256]{3,2,1,0:T(8,128)S(1)} %get-tuple-element.41), channel_id=1, source_target_pairs={{0,4},{1,5},{2,6},{3,7},{4,0},{5,1},{6,2},{7,3},{8,12},{9,13},{10,... | collective-permute-start | bytes 393224 | tf_op jit(solution)/shard_map/ppermute | solution.py:381
  36.4 1.5 %collective-permute-start.11 = (f32[4,2,16,256]{3,2,1,0:T(8,128)S(1)}, f32[4,2,16,256]{3,2,1,0:T(8,128)S(1)}, u32[]{:S(2)}, u32[]{:S(2)}) collective-permute-start(f32[4,2,16,256]{3,2,1,0:T(8,128)S(1)} %get-tuple-element.42), channel_id=1, source_target_pairs={{0,6},{1,7},{2,4},{3,5},{4,2},{5,3},{6,0},{7,1},{8,14},{9,15},{10,... | collective-permute-start | bytes 393224 | tf_op jit(solution)/shard_map/ppermute | solution.py:381
  37.9 1.5 %collective-permute-start.9 = (f32[4,2,16,256]{3,2,1,0:T(8,128)S(1)}, f32[4,2,16,256]{3,2,1,0:T(8,128)S(1)}, u32[]{:S(2)}, u32[]{:S(2)}) collective-permute-start(f32[4,2,16,256]{3,2,1,0:T(8,128)S(1)} %get-tuple-element.40), channel_id=1, source_target_pairs={{0,2},{1,3},{2,0},{3,1},{4,6},{5,7},{6,4},{7,5},{8,10},{9,11},{10,... | collective-permute-start | bytes 393224 | tf_op jit(solution)/shard_map/ppermute | solution.py:381
  39.4 4.9 %collective-permute-done.10.rest_2_ = f32[4,2,16,256]{3,2,1,0:T(8,128)S(1)} collective-permute-done((f32[4,2,16,256]{3,2,1,0:T(8,128)S(1)}, f32[4,2,16,256]{3,2,1,0:T(8,128)S(1)}, u32[]{:S(2)}, u32[]{:S(2)}) %collective-permute-start.10) | collective-permute-done | bytes 131104 | tf_op jit(solution)/shard_map/ppermute | solution.py:381
  44.3 0.0 collective-permute-done.11.rest_3_
  44.3 1.2 %collective-permute-done.9.rest_1_ = f32[4,2,16,256]{3,2,1,0:T(8,128)S(1)} collective-permute-done((f32[4,2,16,256]{3,2,1,0:T(8,128)S(1)}, f32[4,2,16,256]{3,2,1,0:T(8,128)S(1)}, u32[]{:S(2)}, u32[]{:S(2)}) %collective-permute-start.9) | collective-permute-done | bytes 131104 | tf_op jit(solution)/shard_map/ppermute | solution.py:381
  45.5 1.7 %shard_map.126 = f32[16,2,16,256]{3,2,1,0:T(8,128)} custom-call(s32[16]{0:T(128)S(1)} %copy-done.6, f32[4,2,16,256]{3,2,1,0:T(8,128)S(1)} %get-tuple-element.39.rest_0_, f32[4,2,16,256]{3,2,1,0:T(8,128)S(1)} %collective-permute-done.9.rest_1_, f32[4,2,16,256]{3,2,1,0:T(8,128)S(1)} %collective-permute-done.10.rest_2_, ...), custom_call_target="tpu_custom_call" | custom-call | flops 2000000 | bytes 3000000 | tf_op jit(solution)/shard_map/pallas_call | solution.py:469
  (1 shorter events, 0.0 us)
Async XLA Ops:
  0.0 6.7 %copy-start.1 = (f32[8,2,32,512]{3,2,1,0:T(8,128)S(1)}, f32[8,2,32,512]{3,2,1,0:T(8,128)}, u32[]{:S(2)}) copy-start(f32[8,2,32,512]{3,2,1,0:T(8,128)} %patterns.3) | copy-start | bytes 3145732
  0.0 6.7 %copy-start = (f32[100,2,32,512]{3,2,1,0:T(8,128)S(1)}, f32[100,2,32,512]{3,2,1,0:T(8,128)}, u32[]{:S(2)}) copy-start(f32[100,2,32,512]{3,2,1,0:T(8,128)} %operators.5) | copy-start | bytes 39321604
  0.0 12.8 %copy-start.2 = (bf16[512,256]{1,0:T(8,128)(2,1)S(1)}, bf16[512,256]{1,0:T(8,128)(2,1)}, u32[]{:S(2)}) copy-start(bf16[512,256]{1,0:T(8,128)(2,1)} %constant.8.clone.phi_hi) | copy-start | bytes 786436
  0.0 12.8 %copy-start.3 = (bf16[512,256]{1,0:T(8,128)(2,1)S(1)}, bf16[512,256]{1,0:T(8,128)(2,1)}, u32[]{:S(2)}) copy-start(bf16[512,256]{1,0:T(8,128)(2,1)} %constant.9.clone.phi_lo) | copy-start | bytes 786436
  0.0 12.8 %copy-start.6 = (s32[16]{0:T(128)S(1)}, s32[16]{0:T(128)}, u32[]{:S(2)}) copy-start(s32[16]{0:T(128)} %child_parent.7) | copy-start | bytes 196
  0.0 12.8 %copy-start.7 = (s32[16]{0:T(128)S(1)}, s32[16]{0:T(128)}, u32[]{:S(2)}) copy-start(s32[16]{0:T(128)} %child_octant.5) | copy-start | bytes 196
  1.3 8.1 %collective-permute-start.3 = (f32[2,2,32,512]{3,2,1,0:T(8,128)S(1)}, f32[2,2,32,512]{3,2,1,0:T(8,128)S(1)}, u32[]{:S(2)}, u32[]{:S(2)}) collective-permute-start(f32[2,2,32,512]{3,2,1,0:T(8,128)S(1)} %get-tuple-element.32), channel_id=1, source_target_pairs={{0,8},{16,24},{8,0},{24,16},{1,9},{17,25},{9,1},{25,17},{2,10},{18... | collective-permute-start | bytes 786440 | tf_op jit(solution)/shard_map/ppermute | solution.py:349
  1.8 11.0 %collective-permute-start.4 = (f32[2,2,32,512]{3,2,1,0:T(8,128)S(1)}, f32[2,2,32,512]{3,2,1,0:T(8,128)S(1)}, u32[]{:S(2)}, u32[]{:S(2)}) collective-permute-start(f32[2,2,32,512]{3,2,1,0:T(8,128)S(1)} %get-tuple-element.33), channel_id=1, source_target_pairs={{8,16},{16,8},{9,17},{17,9},{10,18},{18,10},{11,19},{19,11},{12,20... | collective-permute-start | bytes 786440 | tf_op jit(solution)/shard_map/ppermute | solution.py:350
  9.1 24.2 %copy-start.4 = (bf16[4,64,128]{2,1,0:T(8,128)(2,1)S(1)}, bf16[4,64,128]{2,1,0:T(8,128)(2,1)}, u32[]{:S(2)}) copy-start(bf16[4,64,128]{2,1,0:T(8,128)(2,1)} %constant.10.clone.t_hi) | copy-start | bytes 196612
  9.1 24.2 %copy-start.5 = (bf16[4,64,128]{2,1,0:T(8,128)(2,1)S(1)}, bf16[4,64,128]{2,1,0:T(8,128)(2,1)}, u32[]{:S(2)}) copy-start(bf16[4,64,128]{2,1,0:T(8,128)(2,1)} %constant.11.clone.t_lo) | copy-start | bytes 196612
  16.5 16.8 %collective-permute-start.5 = (f32[3,2,32,256]{3,2,1,0:T(8,128)S(1)}, f32[3,2,32,256]{3,2,1,0:T(8,128)S(1)}, u32[]{:S(2)}, u32[]{:S(2)}) collective-permute-start(f32[3,2,32,256]{3,2,1,0:T(8,128)S(1)} %get-tuple-element.36), channel_id=1, source_target_pairs={{0,2},{1,3},{2,0},{3,1},{4,6},{5,7},{6,4},{7,5},{8,10},{9,11},{10,... | collective-permute-start | bytes 589832 | tf_op jit(solution)/shard_map/ppermute | solution.py:381
  17.1 16.2 %collective-permute-start.6 = (f32[3,2,32,256]{3,2,1,0:T(8,128)S(1)}, f32[3,2,32,256]{3,2,1,0:T(8,128)S(1)}, u32[]{:S(2)}, u32[]{:S(2)}) collective-permute-start(f32[3,2,32,256]{3,2,1,0:T(8,128)S(1)} %get-tuple-element.37), channel_id=1, source_target_pairs={{0,4},{1,5},{2,6},{3,7},{4,0},{5,1},{6,2},{7,3},{8,12},{9,13},{10,... | collective-permute-start | bytes 589832 | tf_op jit(solution)/shard_map/ppermute | solution.py:381
  17.6 15.7 %collective-permute-start.7 = (f32[3,2,32,256]{3,2,1,0:T(8,128)S(1)}, f32[3,2,32,256]{3,2,1,0:T(8,128)S(1)}, u32[]{:S(2)}, u32[]{:S(2)}) collective-permute-start(f32[3,2,32,256]{3,2,1,0:T(8,128)S(1)} %get-tuple-element.38), channel_id=1, source_target_pairs={{0,6},{1,7},{2,4},{3,5},{4,2},{5,3},{6,0},{7,1},{8,14},{9,15},{10,... | collective-permute-start | bytes 589832 | tf_op jit(solution)/shard_map/ppermute | solution.py:381
  21.3 6.9 %collective-permute-start = (f32[1,2,32,256]{3,2,1,0:T(8,128)S(1)}, f32[1,2,32,256]{3,2,1,0:T(8,128)S(1)}, u32[]{:S(2)}, u32[]{:S(2)}) collective-permute-start(f32[1,2,32,256]{3,2,1,0:T(8,128)S(1)} %get-tuple-element.29), channel_id=1, source_target_pairs={{0,2},{1,3},{2,0},{3,1},{4,6},{5,7},{6,4},{7,5},{8,10},{9,11},{10,... | collective-permute-start | bytes 196616 | tf_op jit(solution)/shard_map/ppermute | solution.py:381
  21.9 6.7 %collective-permute-start.1 = (f32[1,2,32,256]{3,2,1,0:T(8,128)S(1)}, f32[1,2,32,256]{3,2,1,0:T(8,128)S(1)}, u32[]{:S(2)}, u32[]{:S(2)}) collective-permute-start(f32[1,2,32,256]{3,2,1,0:T(8,128)S(1)} %get-tuple-element.30), channel_id=1, source_target_pairs={{0,4},{1,5},{2,6},{3,7},{4,0},{5,1},{6,2},{7,3},{8,12},{9,13},{10,... | collective-permute-start | bytes 196616 | tf_op jit(solution)/shard_map/ppermute | solution.py:381
  28.1 5.2 %collective-permute-start.2 = (f32[1,2,32,256]{3,2,1,0:T(8,128)S(1)}, f32[1,2,32,256]{3,2,1,0:T(8,128)S(1)}, u32[]{:S(2)}, u32[]{:S(2)}) collective-permute-start(f32[1,2,32,256]{3,2,1,0:T(8,128)S(1)} %get-tuple-element.31), channel_id=1, source_target_pairs={{0,6},{1,7},{2,4},{3,5},{4,2},{5,3},{6,0},{7,1},{8,14},{9,15},{10,... | collective-permute-start | bytes 196616 | tf_op jit(solution)/shard_map/ppermute | solution.py:381
  33.8 2.0 %collective-permute-start.8 = (f32[4,2,64,256]{3,2,1,0:T(8,128)S(1)}, f32[4,2,64,256]{3,2,1,0:T(8,128)S(1)}, u32[]{:S(2)}, u32[]{:S(2)}) collective-permute-start(f32[4,2,64,256]{3,2,1,0:T(8,128)S(1)} %shard_map.124), channel_id=1, source_target_pairs={{0,1},{1,0},{2,3},{3,2},{4,5},{5,4},{6,7},{7,6},{8,9},{9,8},{10,11... | collective-permute-start | bytes 1572872 | tf_op jit(solution)/shard_map/ppermute | solution.py:442
  35.9 8.4 %collective-permute-start.10 = (f32[4,2,16,256]{3,2,1,0:T(8,128)S(1)}, f32[4,2,16,256]{3,2,1,0:T(8,128)S(1)}, u32[]{:S(2)}, u32[]{:S(2)}) collective-permute-start(f32[4,2,16,256]{3,2,1,0:T(8,128)S(1)} %get-tuple-element.41), channel_id=1, source_target_pairs={{0,4},{1,5},{2,6},{3,7},{4,0},{5,1},{6,2},{7,3},{8,12},{9,13},{10,... | collective-permute-start | bytes 393224 | tf_op jit(solution)/shard_map/ppermute | solution.py:381
  36.4 7.8 %collective-permute-start.11 = (f32[4,2,16,256]{3,2,1,0:T(8,128)S(1)}, f32[4,2,16,256]{3,2,1,0:T(8,128)S(1)}, u32[]{:S(2)}, u32[]{:S(2)}) collective-permute-start(f32[4,2,16,256]{3,2,1,0:T(8,128)S(1)} %get-tuple-element.42), channel_id=1, source_target_pairs={{0,6},{1,7},{2,4},{3,5},{4,2},{5,3},{6,0},{7,1},{8,14},{9,15},{10,... | collective-permute-start | bytes 393224 | tf_op jit(solution)/shard_map/ppermute | solution.py:381
  37.9 7.6 %collective-permute-start.9 = (f32[4,2,16,256]{3,2,1,0:T(8,128)S(1)}, f32[4,2,16,256]{3,2,1,0:T(8,128)S(1)}, u32[]{:S(2)}, u32[]{:S(2)}) collective-permute-start(f32[4,2,16,256]{3,2,1,0:T(8,128)S(1)} %get-tuple-element.40), channel_id=1, source_target_pairs={{0,2},{1,3},{2,0},{3,1},{4,6},{5,7},{6,4},{7,5},{8,10},{9,11},{10,... | collective-permute-start | bytes 393224 | tf_op jit(solution)/shard_map/ppermute | solution.py:381

commit v7 on v6

--- a/solution.py
+++ b/solution.py
@@ -117,35 +117,6 @@
         copy.wait()
 
 
-def own_kernel(
-    theta_count, partners_in, op_in, patterns, operators, out, phase, partners, op_index, sems
-):
-    clusters, terms = partners.shape
-    rows = out.shape[2]
-    copies = copy_all([(partners_in, partners), (op_in, op_index)], sems)
-    phase_tables(lax.axis_index("member"), theta_count, phase)
-    base = lax.axis_index("group") * clusters
-    for copy in copies:
-        copy.wait()
-
-    @pl.loop(0, clusters)
-    def _(c):
-        for r in range(rows // 8):
-            band = pl.ds(r * 8, 8)
-            re, im = 0.0, 0.0
-            for p in range(terms):
-                q = partners[c, p] - base
-                keep = jnp.where((q >= 0) & (q < clusters), 1.0, 0.0).astype(F32)
-                q = jnp.clip(q, 0, clusters - 1)
-                e = op_index[c, p]
-                ore, oim = operators[e, 0, band, :], operators[e, 1, band, :]
-                pre, pim = patterns[q, 0, band, :] * keep, patterns[q, 1, band, :] * keep
-                re = re + (ore * pre - oim * pim)
-                im = im + (ore * pim + oim * pre)
-            out[c, 0, band, :] = re
-            out[c, 1, band, :] = im
-
-
 def halo_terms(partners, op_index, own, operators, first, second, total):
     clusters, _, rows, _ = own.shape
     terms = partners.shape[1]
@@ -186,19 +157,17 @@
 def fill_slots(child_parent, slots, clusters, width, chips):
     base = lax.axis_index("group") * clusters
 
-    def place_child(k, counts):
-        early, late = counts
+    early, late = jnp.int32(0), jnp.int32(chips)
+    for k in range(slots.shape[0]):
         q = child_parent[k] - base
         inner = (q >= width) & (q < clusters - width) & (early < chips)
         slots[jnp.where(inner, early, late)] = k
         step = jnp.where(inner, 1, 0)
-        return early + step, late + 1 - step
-
-    lax.fori_loop(0, slots.shape[0], place_child, (jnp.int32(0), jnp.int32(chips)))
+        early, late = early + step, late + 1 - step
 
 
 def slot_of(chip, i, chips, per_chip):
-    return jnp.where(i == 0, chip, chips + chip * (per_chip - 1) + i - 1)
+    return chip if i == 0 else chips + chip * (per_chip - 1) + i - 1
 
 
 def shift_and_phi(
@@ -226,18 +195,10 @@
                     at = m * size + i * 2 * rows + r * 8
                     shifted[pl.ds(at, 8), :] = pre * ere - pim * eim
                     shifted[pl.ds(at + rows, 8), :] = pre * eim + pim * ere
-        y = dot3(split(shifted[...]), (phi_hi[...], phi_lo[...]))
+        used = pl.ds(0, len(part) * size)
+        y = dot3(split(shifted[used, :]), (phi_hi[...], phi_lo[...]))
         for m, (_, out) in enumerate(part):
             out[...] = y[m * size:(m + 1) * size].reshape(out.shape)
-
-
-def early_kernel(width, child_parent, child_octant, own, phase, phi_hi, phi_lo, *rest):
-    *outs, slots, shifted = rest
-    fill_slots(child_parent, slots, own.shape[0], width, len(outs))
-    shift_and_phi(
-        range(len(outs)), 0, slots, child_parent, child_octant, own, phase, phi_hi, phi_lo,
-        outs, shifted,
-    )
 
 
 def first_kernel(
@@ -254,28 +215,79 @@
 
 
 def later_kernel(
-    order, width, child_parent, child_octant, total, phase, phi_hi, phi_lo, *rest
+    order, first, width, child_parent, child_octant, total, phase, phi_hi, phi_lo, *rest
 ):
     *outs, slots, shifted = rest
-    fill_slots(child_parent, slots, total.shape[0], width, len(outs) + 1)
+    chips = lax.axis_size("member") // CORES
+    fill_slots(child_parent, slots, total.shape[0], width, chips)
     shift_and_phi(
-        order, 1, slots, child_parent, child_octant, total, phase, phi_hi, phi_lo, outs, shifted
+        order, first, slots, child_parent, child_octant, total, phase, phi_hi, phi_lo, outs,
+        shifted,
+    )
+
+
+def own_kernel(
+    theta_count, width, partners_in, op_in, parent_in, octant_in, patterns, operators, phi_hi,
+    phi_lo, out, phase, *rest
+):
+    *early, partners, op_index, child_parent, child_octant, slots, shifted, sems = rest
+    clusters, terms = partners.shape
+    rows = out.shape[2]
+    copies = copy_all(
+        [
+            (partners_in, partners),
+            (op_in, op_index),
+            (parent_in, child_parent),
+            (octant_in, child_octant),
+        ],
+        sems,
+    )
+    phase_tables(lax.axis_index("member"), theta_count, phase)
+    base = lax.axis_index("group") * clusters
+    for copy in copies:
+        copy.wait()
+
+    @pl.loop(0, clusters)
+    def _(c):
+        for r in range(rows // 8):
+            band = pl.ds(r * 8, 8)
+            re, im = 0.0, 0.0
+            for p in range(terms):
+                q = partners[c, p] - base
+                keep = jnp.where((q >= 0) & (q < clusters), 1.0, 0.0).astype(F32)
+                q = jnp.clip(q, 0, clusters - 1)
+                e = op_index[c, p]
+                ore, oim = operators[e, 0, band, :], operators[e, 1, band, :]
+                pre, pim = patterns[q, 0, band, :] * keep, patterns[q, 1, band, :] * keep
+                re = re + (ore * pre - oim * pim)
+                im = im + (ore * pim + oim * pre)
+            out[c, 0, band, :] = re
+            out[c, 1, band, :] = im
+
+    chips = len(early) + 1
+    fill_slots(child_parent, slots, clusters, width, chips)
+    shift_and_phi(
+        range(1, chips), 0, slots, child_parent, child_octant, out, phase, phi_hi, phi_lo,
+        early, shifted,
     )
 
 
 def theta_kernel(away, t_hi, t_lo, *rest):
-    *blocks, out, lats = rest
-    chips = len(blocks) // 2
-    early, late = blocks[:chips], blocks[chips:]
+    mine, *blocks, out, lats = rest
+    chips = len(blocks) // 2 + 1
+    early, late = blocks[:chips - 1], blocks[chips - 1:]
     member = lax.axis_index("member")
     chip, core = member // CORES, member % CORES
     t = core * CORES + (1 - core if away else core)
-    rows = early[0].shape[2]
+    rows = mine.shape[2]
     for i in range(out.shape[0]):
         for part in range(2):
             for s in range(chips):
                 at = pl.multiple_of((chip ^ s) * rows, rows)
-                block = early[s][0, part] if i == 0 else late[s][i - 1, part]
+                if s == 0:
+                    block = mine[i, part]
+                else:
+                    block = early[s - 1][0, part] if i == 0 else late[s - 1][i - 1, part]
                 lats[pl.ds(at, rows), :] = block
             out[i, part] = dot3((t_hi[t], t_lo[t]), split(lats[...]))
 
@@ -349,51 +361,45 @@
     first = lax.ppermute(first, "group", pairs[0])
     second = lax.ppermute(second, "group", pairs[1])
 
+    phi = split_const(phi_table(lons, NPC).T)
+    assert per_chip > 1 and clusters - 2 * width >= chips
+    slots = pltpu.SMEM((children,), jnp.int32)
     total_shape = shape(clusters, 2, rows, lons)
-    own, phase = pl.pallas_call(
-        functools.partial(own_kernel, theta_count),
-        out_shape=(total_shape, shape(8, 2, rows, lons)),
-        in_specs=[VMEM] * 4,
-        out_specs=(VMEM, VMEM),
+
+    def blocks_of(count, number):
+        return (shape(count, 2, rows, NPC),) * number
+
+    def rows_of(count):
+        return pltpu.VMEM((count * 2 * rows, lons), F32)
+
+    def between_chips(blocks):
+        moved = []
+        for s in range(chips - 1, 0, -1):
+            pairs = [(i, i ^ (CORES * s)) for i in range(members)]
+            moved.append(lax.ppermute(blocks[s], "member", pairs))
+        return moved[::-1]
+
+    own, phase, *early = call(
+        functools.partial(own_kernel, theta_count, width),
+        out_shape=(total_shape, shape(8, 2, rows, lons)) + blocks_of(1, chips - 1),
+        in_specs=[VMEM] * 8,
+        out_specs=(VMEM,) * (chips + 1),
         scratch_shapes=[
             pltpu.SMEM(partners.shape, jnp.int32),
             pltpu.SMEM(partners.shape, jnp.int32),
-            pltpu.SemaphoreType.DMA((2,)),
+            slots,
+            slots,
+            slots,
+            rows_of(chips - 1),
+            pltpu.SemaphoreType.DMA((4,)),
         ],
         compiler_params=params(20),
         cost_estimate=cost(8),
-    )(partners, operator_index, patterns, operators)
-
-    phi = split_const(phi_table(lons, NPC).T)
-    assert per_chip > 1 and clusters - 2 * width >= chips
-    slots = pltpu.SMEM((children,), jnp.int32)
-
-    def blocks_of(count, number):
-        return (shape(count, 2, rows, NPC),) * number
-
-    def rows_of(count):
-        return pltpu.VMEM((count * 2 * rows, lons), F32)
-
-    def between_chips(blocks):
-        moved = dict(blocks)
-        for s in range(chips - 1, 0, -1):
-            pairs = [(i, i ^ (CORES * s)) for i in range(members)]
-            moved[s] = lax.ppermute(blocks[s], "member", pairs)
-        return [moved[s] for s in range(chips)]
-
-    early = call(
-        functools.partial(early_kernel, width),
-        out_shape=blocks_of(1, chips),
-        in_specs=[SMEM] * 2 + [VMEM] * 4,
-        out_specs=(VMEM,) * chips,
-        scratch_shapes=[slots, rows_of(chips)],
-        compiler_params=params(20),
-        cost_estimate=cost(1),
-    )(child_parent, child_octant, own, phase, *phi)
-    early = between_chips(dict(enumerate(early)))
+    )(partners, operator_index, child_parent, child_octant, patterns, operators, *phi)
+    early = between_chips(dict(enumerate(early, 1)))
 
     count = per_chip - 1
-    far, near = [chips - 1], [*range(1, chips - 1), 0]
+    far, near = [chips - 1], list(range(1, chips - 1))
     late = {}
     *outs, total = call(
         functools.partial(first_kernel, far),
@@ -408,17 +414,21 @@
         phase, *phi,
     )
     late.update(zip(far, outs))
-    outs = call(
-        functools.partial(later_kernel, near, width),
-        out_shape=blocks_of(count, len(near)),
-        in_specs=[SMEM] * 2 + [VMEM] * 4,
-        out_specs=(VMEM,) * len(near),
-        scratch_shapes=[slots, rows_of(count)],
-        compiler_params=params(20),
-        cost_estimate=cost(1),
-    )(child_parent, child_octant, total, phase, *phi)
-    late.update(zip(near, outs))
+
+    def later(order, first_child, number):
+        return call(
+            functools.partial(later_kernel, order, first_child, width),
+            out_shape=blocks_of(number, len(order)),
+            in_specs=[SMEM] * 2 + [VMEM] * 4,
+            out_specs=(VMEM,) * len(order),
+            scratch_shapes=[slots, rows_of(number * len(order))],
+            compiler_params=params(20),
+            cost_estimate=cost(1),
+        )(child_parent, child_octant, total, phase, *phi)
+
+    late.update(zip(near, later(near, 1, count)))
     late = between_chips(late)
+    (mine,) = later([0], 0, per_chip)
 
     theta = theta_table(theta_count, NTC).reshape(chips, CORES, out_rows, chips, CORES, rows)
     theta = theta.transpose(4, 1, 0, 2, 3, 5).reshape(
@@ -431,12 +441,12 @@
             call(
                 functools.partial(theta_kernel, name == "away"),
                 out_shape=half,
-                in_specs=[VMEM] * (2 + 2 * chips),
+                in_specs=[VMEM] * (1 + 2 * chips),
                 out_specs=VMEM,
                 scratch_shapes=[pltpu.VMEM((chips * rows, NPC), F32)],
                 compiler_params=params(12),
                 cost_estimate=cost(1),
-            )(*split_const(theta), *early, *late)
+            )(*split_const(theta), mine, *early, *late)
             for name in ("away", "keep")
         )
         swapped = lax.ppermute(away, "member", swap)
@@ -450,7 +460,7 @@
         )(keep, swapped)
     else:
         order = chip ^ jnp.arange(chips)
-        lats = jnp.stack([jnp.concatenate(pair) for pair in zip(early, late)])
+        lats = jnp.stack([mine] + [jnp.concatenate(pair) for pair in zip(early, late)])
         lats = jnp.take(lats, order, axis=0)
         lats = lats.transpose(1, 2, 0, 3, 4).reshape(per_chip, 2, chips * rows, NPC)
         both = jnp.take(
@@ -465,7 +475,7 @@
         pieces = pieces.reshape(per_chip, 2, chips, out_rows, NPC)
         pieces = [jnp.take(pieces, order[s], axis=2) for s in range(chips)]
 
-    final = between_chips(dict(enumerate(pieces)))
+    final = [pieces[0], *between_chips(dict(enumerate(pieces)))]
     return call(
         functools.partial(place_kernel, clusters, width),
         out_shape=shape(children, 2, out_rows, NPC),

time: 47.3 us -> 46.3 us (0.979)
  the two profiles are of different devices: /device:TPU:14 before, /device:TPU:8 now
where the time goes in v7:
time: 46.3 us; the launch traced here: 46.2 us
  starting transfers between devices  17.1 us (37%)
  waiting for transfers between devices  16.5 us (36%)
  Pallas kernels  10.5 us (23%)
  local copies, waits for them, and re-layouts  1.93 us (4%)
    ppermute x9, waiting for transfers between devices, between_chips(): moved.append(lax.ppermute(blocks[s], 'member', pairs))  13.6 us
    ppermute x9, starting transfers between devices, between_chips(): moved.append(lax.ppermute(blocks[s], 'member', pairs))  11.6 us
    ppermute x1, starting transfers between devices, on_device(): second = lax.ppermute(second, 'group', pairs[1])  5.3 us
    pallas_call x1, Pallas kernels, on_device(): call(functools.partial(own_kernel, theta_count, width), out_shape=(total_...  2.68 us
    pallas_call x2, Pallas kernels, later(): call(functools.partial(later_kernel, order, first_child, width), out_shap...  2.13 us
    unnamed x20, local copies, waits for them, and re-layouts  1.93 us
    pallas_call x1, Pallas kernels, on_device(): call(functools.partial(first_kernel, far), out_shape=blocks_of(count, len...  1.9 us
    pallas_call x1, Pallas kernels, on_device(): call(functools.partial(place_kernel, clusters, width), out_shape=shape(ch...  1.54 us
  transfers between devices with their start and end apart: 12, of which 6 were waited for; matrix products, arithmetic and copies ran while one was open for 0% of the time, Pallas kernels for 11%

profile of v7, /device:TPU:8, one launch (start us, length us, event | category | flops | bytes accessed | tf_op | source)
XLA Modules:
  0.0 46.2 jit_solution(13432664251811417172)
XLA Ops:
  0.0 0.0 copy-start
  0.0 0.0 copy-start.9
  0.0 1.2 %shard_map.118 = (f32[2,2,32,512]{3,2,1,0:T(8,128)S(1)}, f32[2,2,32,512]{3,2,1,0:T(8,128)S(1)}, s32[8,8]{1,0:T(8,128)S(1)}, s32[8,8]{1,0:T(8,128)S(1)}) custom-call(f32[8,2,32,512]{3,2,1,0:T(8,128)} %patterns.3, s32[8,8]{1,0:T(8,128)} %partners.1, s32[8,8]{1,0:T(8,128)} %op_index.1, f32[100,2,32,512]{3,2,1,0:T(8,128)} %operators.5), custom_call_target="tpu_custom_call" | custom-call | tf_op jit(solution)/shard_map/pallas_call | solution.py:351
  1.3 0.1 collective-permute-start
  1.3 5.3 %collective-permute-start.1 = (f32[2,2,32,512]{3,2,1,0:T(8,128)S(1)}, f32[2,2,32,512]{3,2,1,0:T(8,128)S(1)}, u32[]{:S(2)}, u32[]{:S(2)}) collective-permute-start(f32[2,2,32,512]{3,2,1,0:T(8,128)S(1)} %get-tuple-element.26), channel_id=1, source_target_pairs={{8,16},{16,8},{9,17},{17,9},{10,18},{18,10},{11,19},{19,11},{12,20... | collective-permute-start | bytes 786440 | tf_op jit(solution)/shard_map/ppermute | solution.py:362
  6.6 0.0 copy-done
  6.7 0.0 copy-done.1
  6.7 0.0 copy-done.8
  6.7 0.0 copy-done.9
  6.7 0.0 copy-start.2
  6.7 0.9 %copy-done.2 = bf16[512,256]{1,0:T(8,128)(2,1)S(1)} copy-done((bf16[512,256]{1,0:T(8,128)(2,1)S(1)}, bf16[512,256]{1,0:T(8,128)(2,1)}, u32[]{:S(2)}) %copy-start.2) | copy-done | bytes 262168
  7.6 0.9 %copy-done.4 = bf16[512,256]{1,0:T(8,128)(2,1)S(1)} copy-done((bf16[512,256]{1,0:T(8,128)(2,1)S(1)}, bf16[512,256]{1,0:T(8,128)(2,1)}, u32[]{:S(2)}) %copy-start.4) | copy-done | bytes 262168
  8.6 2.7 %shard_map.119 = (f32[8,2,32,512]{3,2,1,0:T(8,128)S(1)}, f32[8,2,32,512]{3,2,1,0:T(8,128)S(1)}, f32[1,2,32,256]{3,2,1,0:T(8,128)S(1)}, f32[1,2,32,256]{3,2,1,0:T(8,128)S(1)}, f32[1,2,32,256]{3,2,1,0:T(8,128)S(1)}) custom-call(s32[8,8]{1,0:T(8,128)S(1)} %get-tuple-element.22.partners_in.partners, s32[8,8]{1,0:T(8,128)S(1)} %get-tuple-element.23.op_in.op_index, ...), custom_call_target="tpu_custom_call" | custom-call | flops 16000000 | bytes 24000000 | tf_op jit(solution)/shard_map/pallas_call | solution.py:382
  11.3 0.0 copy-start.6
  11.3 0.0 copy-start.7
  11.3 0.0 collective-permute-done.first
  11.3 1.5 %collective-permute-done.1.second = f32[2,2,32,512]{3,2,1,0:T(8,128)S(1)} collective-permute-done((f32[2,2,32,512]{3,2,1,0:T(8,128)S(1)}, f32[2,2,32,512]{3,2,1,0:T(8,128)S(1)}, u32[]{:S(2)}, u32[]{:S(2)}) %collective-permute-start.1) | collective-permute-done | bytes 262176 | tf_op jit(solution)/shard_map/ppermute | solution.py:362
  12.8 0.0 copy-done.3
  12.8 0.0 copy-done.5
  12.8 1.9 %shard_map.120 = (f32[3,2,32,256]{3,2,1,0:T(8,128)S(1)}, f32[8,2,32,512]{3,2,1,0:T(8,128)S(1)}) custom-call(s32[8,8]{1,0:T(8,128)S(1)} %get-tuple-element.22.partners_in.partners, s32[8,8]{1,0:T(8,128)S(1)} %get-tuple-element.23.op_in.op_index, s32[16]{0:T(128)S(1)} %copy-done.8, s32[16]{0:T(128)S(1)} %copy-done.9, ...), custom_call_target="tpu_custom_call" | custom-call | flops 4000000 | bytes 6000000 | tf_op jit(solution)/shard_map/pallas_call | solution.py:404
  14.7 2.5 %collective-permute-start.7 = (f32[3,2,32,256]{3,2,1,0:T(8,128)S(1)}, f32[3,2,32,256]{3,2,1,0:T(8,128)S(1)}, u32[]{:S(2)}, u32[]{:S(2)}) collective-permute-start(f32[3,2,32,256]{3,2,1,0:T(8,128)S(1)} %get-tuple-element.34), channel_id=1, source_target_pairs={{0,6},{1,7},{2,4},{3,5},{4,2},{5,3},{6,0},{7,1},{8,14},{9,15},{10,... | collective-permute-start | bytes 589832 | tf_op jit(solution)/shard_map/ppermute | solution.py:379
  17.2 1.1 %shard_map.122 = (f32[3,2,32,256]{3,2,1,0:T(8,128)S(1)}, f32[3,2,32,256]{3,2,1,0:T(8,128)S(1)}) custom-call(s32[16]{0:T(128)S(1)} %copy-done.8, s32[16]{0:T(128)S(1)} %copy-done.9, f32[8,2,32,512]{3,2,1,0:T(8,128)S(1)} %get-tuple-element.28.total, f32[8,2,32,512]{3,2,1,0:T(8,128)S(1)} %get-tuple-element.27.phase, bf16[512,256]{1,0:T(8,128)(2,1)S(1)} %copy-done.5, ...), custom_call_target="tpu_custom_call" | custom-call | flops 2000000 | bytes 3000000 | tf_op jit(solution)/shard_map/pallas_call | solution.py:419
  18.3 0.6 %collective-permute-start.5 = (f32[3,2,32,256]{3,2,1,0:T(8,128)S(1)}, f32[3,2,32,256]{3,2,1,0:T(8,128)S(1)}, u32[]{:S(2)}, u32[]{:S(2)}) collective-permute-start(f32[3,2,32,256]{3,2,1,0:T(8,128)S(1)} %get-tuple-element.32), channel_id=1, source_target_pairs={{0,2},{1,3},{2,0},{3,1},{4,6},{5,7},{6,4},{7,5},{8,10},{9,11},{10,... | collective-permute-start | bytes 589832 | tf_op jit(solution)/shard_map/ppermute | solution.py:379
  18.9 0.5 %collective-permute-start.6 = (f32[3,2,32,256]{3,2,1,0:T(8,128)S(1)}, f32[3,2,32,256]{3,2,1,0:T(8,128)S(1)}, u32[]{:S(2)}, u32[]{:S(2)}) collective-permute-start(f32[3,2,32,256]{3,2,1,0:T(8,128)S(1)} %get-tuple-element.33), channel_id=1, source_target_pairs={{0,4},{1,5},{2,6},{3,7},{4,0},{5,1},{6,2},{7,3},{8,12},{9,13},{10,... | collective-permute-start | bytes 589832 | tf_op jit(solution)/shard_map/ppermute | solution.py:379
  19.4 1.5 %collective-permute-start.2 = (f32[1,2,32,256]{3,2,1,0:T(8,128)S(1)}, f32[1,2,32,256]{3,2,1,0:T(8,128)S(1)}, u32[]{:S(2)}, u32[]{:S(2)}) collective-permute-start(f32[1,2,32,256]{3,2,1,0:T(8,128)S(1)} %get-tuple-element.29), channel_id=1, source_target_pairs={{0,2},{1,3},{2,0},{3,1},{4,6},{5,7},{6,4},{7,5},{8,10},{9,11},{10,... | collective-permute-start | bytes 196616 | tf_op jit(solution)/shard_map/ppermute | solution.py:379
  20.9 1.5 %collective-permute-start.3 = (f32[1,2,32,256]{3,2,1,0:T(8,128)S(1)}, f32[1,2,32,256]{3,2,1,0:T(8,128)S(1)}, u32[]{:S(2)}, u32[]{:S(2)}) collective-permute-start(f32[1,2,32,256]{3,2,1,0:T(8,128)S(1)} %get-tuple-element.30), channel_id=1, source_target_pairs={{0,4},{1,5},{2,6},{3,7},{4,0},{5,1},{6,2},{7,3},{8,12},{9,13},{10,... | collective-permute-start | bytes 196616 | tf_op jit(solution)/shard_map/ppermute | solution.py:379
  22.5 4.8 %collective-permute-done.2.rest_1_ = f32[1,2,32,256]{3,2,1,0:T(8,128)S(1)} collective-permute-done((f32[1,2,32,256]{3,2,1,0:T(8,128)S(1)}, f32[1,2,32,256]{3,2,1,0:T(8,128)S(1)}, u32[]{:S(2)}, u32[]{:S(2)}) %collective-permute-start.2) | collective-permute-done | bytes 65568 | tf_op jit(solution)/shard_map/ppermute | solution.py:379
  27.3 1.4 %collective-permute-start.4 = (f32[1,2,32,256]{3,2,1,0:T(8,128)S(1)}, f32[1,2,32,256]{3,2,1,0:T(8,128)S(1)}, u32[]{:S(2)}, u32[]{:S(2)}) collective-permute-start(f32[1,2,32,256]{3,2,1,0:T(8,128)S(1)} %get-tuple-element.31), channel_id=1, source_target_pairs={{0,6},{1,7},{2,4},{3,5},{4,2},{5,3},{6,0},{7,1},{8,14},{9,15},{10,... | collective-permute-start | bytes 196616 | tf_op jit(solution)/shard_map/ppermute | solution.py:379
  28.7 1.0 %shard_map.121.rest_0_ = f32[4,2,32,256]{3,2,1,0:T(8,128)S(1)} custom-call(s32[16]{0:T(128)S(1)} %copy-done.8, s32[16]{0:T(128)S(1)} %copy-done.9, f32[8,2,32,512]{3,2,1,0:T(8,128)S(1)} %get-tuple-element.28.total, f32[8,2,32,512]{3,2,1,0:T(8,128)S(1)} %get-tuple-element.27.phase, bf16[512,256]{1,0:T(8,128)(2,1)S(1)} %copy-done.5, bf16[512,256]{1,0:T(8,128)(2,1)S(1)} %copy-done.3), custom_call_target="tpu_custom_call" | custom-call | flops 2000000 | bytes 3000000 | tf_op jit(solution)/shard_map/pallas_call | solution.py:419
  29.7 0.0 collective-permute-done.3.rest_2_
  29.7 2.7 %collective-permute-done.4.rest_3_ = f32[1,2,32,256]{3,2,1,0:T(8,128)S(1)} collective-permute-done((f32[1,2,32,256]{3,2,1,0:T(8,128)S(1)}, f32[1,2,32,256]{3,2,1,0:T(8,128)S(1)}, u32[]{:S(2)}, u32[]{:S(2)}) %collective-permute-start.4) | collective-permute-done | bytes 65568 | tf_op jit(solution)/shard_map/ppermute | solution.py:379
  32.4 0.0 collective-permute-done.7.rest_6_
  32.4 0.0 collective-permute-done.5.rest_4_
  32.4 0.0 collective-permute-done.6.rest_5_
  32.4 0.0 copy-done.6
  32.4 0.0 copy-done.7
  32.5 0.5 %shard_map.124 = f32[4,2,64,256]{3,2,1,0:T(8,128)S(1)} custom-call(bf16[4,64,128]{2,1,0:T(8,128)(2,1)S(1)} %copy-done.7, bf16[4,64,128]{2,1,0:T(8,128)(2,1)S(1)} %copy-done.6, f32[4,2,32,256]{3,2,1,0:T(8,128)S(1)} %shard_map.121.rest_0_, f32[1,2,32,256]{3,2,1,0:T(8,128)S(1)} %collective-permute-done.2.rest_1_, ...), custom_call_target="tpu_custom_call" | custom-call | flops 2000000 | bytes 3000000 | tf_op jit(solution)/shard_map/pallas_call | solution.py:441
  32.9 0.1 collective-permute-start.8
  33.0 0.5 %shard_map.123.keep = f32[4,2,64,256]{3,2,1,0:T(8,128)S(1)} custom-call(bf16[4,64,128]{2,1,0:T(8,128)(2,1)S(1)} %copy-done.7, bf16[4,64,128]{2,1,0:T(8,128)(2,1)S(1)} %copy-done.6, f32[4,2,32,256]{3,2,1,0:T(8,128)S(1)} %shard_map.121.rest_0_, f32[1,2,32,256]{3,2,1,0:T(8,128)S(1)} %collective-permute-done.2.rest_1_, ...), custom_call_target="tpu_custom_call" | custom-call | flops 2000000 | bytes 3000000 | tf_op jit(solution)/shard_map/pallas_call | solution.py:441
  33.5 1.4 %collective-permute-done.8.arrived = f32[4,2,64,256]{3,2,1,0:T(8,128)S(1)} collective-permute-done((f32[4,2,64,256]{3,2,1,0:T(8,128)S(1)}, f32[4,2,64,256]{3,2,1,0:T(8,128)S(1)}, u32[]{:S(2)}, u32[]{:S(2)}) %collective-permute-start.8) | collective-permute-done | bytes 524320 | tf_op jit(solution)/shard_map/ppermute | solution.py:452
  34.9 0.1 shard_map.125
  35.0 1.6 %collective-permute-start.9 = (f32[4,2,16,256]{3,2,1,0:T(8,128)S(1)}, f32[4,2,16,256]{3,2,1,0:T(8,128)S(1)}, u32[]{:S(2)}, u32[]{:S(2)}) collective-permute-start(f32[4,2,16,256]{3,2,1,0:T(8,128)S(1)} %get-tuple-element.36), channel_id=1, source_target_pairs={{0,2},{1,3},{2,0},{3,1},{4,6},{5,7},{6,4},{7,5},{8,10},{9,11},{10,... | collective-permute-start | bytes 393224 | tf_op jit(solution)/shard_map/ppermute | solution.py:379
  36.5 0.5 %collective-permute-start.10 = (f32[4,2,16,256]{3,2,1,0:T(8,128)S(1)}, f32[4,2,16,256]{3,2,1,0:T(8,128)S(1)}, u32[]{:S(2)}, u32[]{:S(2)}) collective-permute-start(f32[4,2,16,256]{3,2,1,0:T(8,128)S(1)} %get-tuple-element.37), channel_id=1, source_target_pairs={{0,4},{1,5},{2,6},{3,7},{4,0},{5,1},{6,2},{7,3},{8,12},{9,13},{10,... | collective-permute-start | bytes 393224 | tf_op jit(solution)/shard_map/ppermute | solution.py:379
  37.1 1.5 %collective-permute-start.11 = (f32[4,2,16,256]{3,2,1,0:T(8,128)S(1)}, f32[4,2,16,256]{3,2,1,0:T(8,128)S(1)}, u32[]{:S(2)}, u32[]{:S(2)}) collective-permute-start(f32[4,2,16,256]{3,2,1,0:T(8,128)S(1)} %get-tuple-element.38), channel_id=1, source_target_pairs={{0,6},{1,7},{2,4},{3,5},{4,2},{5,3},{6,0},{7,1},{8,14},{9,15},{10,... | collective-permute-start | bytes 393224 | tf_op jit(solution)/shard_map/ppermute | solution.py:379
  38.5 2.5 %collective-permute-done.9.rest_1_ = f32[4,2,16,256]{3,2,1,0:T(8,128)S(1)} collective-permute-done((f32[4,2,16,256]{3,2,1,0:T(8,128)S(1)}, f32[4,2,16,256]{3,2,1,0:T(8,128)S(1)}, u32[]{:S(2)}, u32[]{:S(2)}) %collective-permute-start.9) | collective-permute-done | bytes 131104 | tf_op jit(solution)/shard_map/ppermute | solution.py:379
  41.0 3.6 %collective-permute-done.10.rest_2_ = f32[4,2,16,256]{3,2,1,0:T(8,128)S(1)} collective-permute-done((f32[4,2,16,256]{3,2,1,0:T(8,128)S(1)}, f32[4,2,16,256]{3,2,1,0:T(8,128)S(1)}, u32[]{:S(2)}, u32[]{:S(2)}) %collective-permute-start.10) | collective-permute-done | bytes 131104 | tf_op jit(solution)/shard_map/ppermute | solution.py:379
  44.6 0.0 collective-permute-done.11.rest_3_
  44.6 1.5 %shard_map.126 = f32[16,2,16,256]{3,2,1,0:T(8,128)} custom-call(s32[16]{0:T(128)S(1)} %copy-done.8, f32[4,2,16,256]{3,2,1,0:T(8,128)S(1)} %get-tuple-element.35.rest_0_, f32[4,2,16,256]{3,2,1,0:T(8,128)S(1)} %collective-permute-done.9.rest_1_, f32[4,2,16,256]{3,2,1,0:T(8,128)S(1)} %collective-permute-done.10.rest_2_, ...), custom_call_target="tpu_custom_call" | custom-call | flops 2000000 | bytes 3000000 | tf_op jit(solution)/shard_map/pallas_call | solution.py:479
  (5 shorter events, 0.0 us)
Async XLA Ops:
  0.0 6.6 %copy-start = (f32[100,2,32,512]{3,2,1,0:T(8,128)S(1)}, f32[100,2,32,512]{3,2,1,0:T(8,128)}, u32[]{:S(2)}) copy-start(f32[100,2,32,512]{3,2,1,0:T(8,128)} %operators.5) | copy-start | bytes 39321604
  0.0 6.7 %copy-start.1 = (f32[8,2,32,512]{3,2,1,0:T(8,128)S(1)}, f32[8,2,32,512]{3,2,1,0:T(8,128)}, u32[]{:S(2)}) copy-start(f32[8,2,32,512]{3,2,1,0:T(8,128)} %patterns.3) | copy-start | bytes 3145732
  0.0 6.7 %copy-start.8 = (s32[16]{0:T(128)S(1)}, s32[16]{0:T(128)}, u32[]{:S(2)}) copy-start(s32[16]{0:T(128)} %child_parent.7) | copy-start | bytes 196
  0.0 6.7 %copy-start.9 = (s32[16]{0:T(128)S(1)}, s32[16]{0:T(128)}, u32[]{:S(2)}) copy-start(s32[16]{0:T(128)} %child_octant.5) | copy-start | bytes 196
  1.3 10.1 %collective-permute-start = (f32[2,2,32,512]{3,2,1,0:T(8,128)S(1)}, f32[2,2,32,512]{3,2,1,0:T(8,128)S(1)}, u32[]{:S(2)}, u32[]{:S(2)}) collective-permute-start(f32[2,2,32,512]{3,2,1,0:T(8,128)S(1)} %get-tuple-element.25), channel_id=1, source_target_pairs={{0,8},{16,24},{8,0},{24,16},{1,9},{17,25},{9,1},{25,17},{2,10},{18... | collective-permute-start | bytes 786440 | tf_op jit(solution)/shard_map/ppermute | solution.py:361
  1.3 11.4 %collective-permute-start.1 = (f32[2,2,32,512]{3,2,1,0:T(8,128)S(1)}, f32[2,2,32,512]{3,2,1,0:T(8,128)S(1)}, u32[]{:S(2)}, u32[]{:S(2)}) collective-permute-start(f32[2,2,32,512]{3,2,1,0:T(8,128)S(1)} %get-tuple-element.26), channel_id=1, source_target_pairs={{8,16},{16,8},{9,17},{17,9},{10,18},{18,10},{11,19},{19,11},{12,20... | collective-permute-start | bytes 786440 | tf_op jit(solution)/shard_map/ppermute | solution.py:362
  6.7 1.0 %copy-start.2 = (bf16[512,256]{1,0:T(8,128)(2,1)S(1)}, bf16[512,256]{1,0:T(8,128)(2,1)}, u32[]{:S(2)}) copy-start(bf16[512,256]{1,0:T(8,128)(2,1)} %constant.9.clone.phi_lo) | copy-start | bytes 786436
  7.6 0.9 %copy-start.4 = (bf16[512,256]{1,0:T(8,128)(2,1)S(1)}, bf16[512,256]{1,0:T(8,128)(2,1)}, u32[]{:S(2)}) copy-start(bf16[512,256]{1,0:T(8,128)(2,1)} %constant.8.clone.phi_hi) | copy-start | bytes 786436
  8.6 4.2 %copy-start.3 = (bf16[512,256]{1,0:T(8,128)(2,1)S(1)}, bf16[512,256]{1,0:T(8,128)(2,1)}, u32[]{:S(2)}) copy-start(bf16[512,256]{1,0:T(8,128)(2,1)} %constant.9.clone.phi_lo) | copy-start | bytes 786436
  8.6 4.2 %copy-start.5 = (bf16[512,256]{1,0:T(8,128)(2,1)S(1)}, bf16[512,256]{1,0:T(8,128)(2,1)}, u32[]{:S(2)}) copy-start(bf16[512,256]{1,0:T(8,128)(2,1)} %constant.8.clone.phi_hi) | copy-start | bytes 786436
  11.3 21.2 %copy-start.6 = (bf16[4,64,128]{2,1,0:T(8,128)(2,1)S(1)}, bf16[4,64,128]{2,1,0:T(8,128)(2,1)}, u32[]{:S(2)}) copy-start(bf16[4,64,128]{2,1,0:T(8,128)(2,1)} %constant.11.clone.t_lo) | copy-start | bytes 196612
  11.3 21.2 %copy-start.7 = (bf16[4,64,128]{2,1,0:T(8,128)(2,1)S(1)}, bf16[4,64,128]{2,1,0:T(8,128)(2,1)}, u32[]{:S(2)}) copy-start(bf16[4,64,128]{2,1,0:T(8,128)(2,1)} %constant.10.clone.t_hi) | copy-start | bytes 196612
  14.7 17.7 %collective-permute-start.7 = (f32[3,2,32,256]{3,2,1,0:T(8,128)S(1)}, f32[3,2,32,256]{3,2,1,0:T(8,128)S(1)}, u32[]{:S(2)}, u32[]{:S(2)}) collective-permute-start(f32[3,2,32,256]{3,2,1,0:T(8,128)S(1)} %get-tuple-element.34), channel_id=1, source_target_pairs={{0,6},{1,7},{2,4},{3,5},{4,2},{5,3},{6,0},{7,1},{8,14},{9,15},{10,... | collective-permute-start | bytes 589832 | tf_op jit(solution)/shard_map/ppermute | solution.py:379
  18.3 14.1 %collective-permute-start.5 = (f32[3,2,32,256]{3,2,1,0:T(8,128)S(1)}, f32[3,2,32,256]{3,2,1,0:T(8,128)S(1)}, u32[]{:S(2)}, u32[]{:S(2)}) collective-permute-start(f32[3,2,32,256]{3,2,1,0:T(8,128)S(1)} %get-tuple-element.32), channel_id=1, source_target_pairs={{0,2},{1,3},{2,0},{3,1},{4,6},{5,7},{6,4},{7,5},{8,10},{9,11},{10,... | collective-permute-start | bytes 589832 | tf_op jit(solution)/shard_map/ppermute | solution.py:379
  18.9 13.5 %collective-permute-start.6 = (f32[3,2,32,256]{3,2,1,0:T(8,128)S(1)}, f32[3,2,32,256]{3,2,1,0:T(8,128)S(1)}, u32[]{:S(2)}, u32[]{:S(2)}) collective-permute-start(f32[3,2,32,256]{3,2,1,0:T(8,128)S(1)} %get-tuple-element.33), channel_id=1, source_target_pairs={{0,4},{1,5},{2,6},{3,7},{4,0},{5,1},{6,2},{7,3},{8,12},{9,13},{10,... | collective-permute-start | bytes 589832 | tf_op jit(solution)/shard_map/ppermute | solution.py:379
  19.4 7.8 %collective-permute-start.2 = (f32[1,2,32,256]{3,2,1,0:T(8,128)S(1)}, f32[1,2,32,256]{3,2,1,0:T(8,128)S(1)}, u32[]{:S(2)}, u32[]{:S(2)}) collective-permute-start(f32[1,2,32,256]{3,2,1,0:T(8,128)S(1)} %get-tuple-element.29), channel_id=1, source_target_pairs={{0,2},{1,3},{2,0},{3,1},{4,6},{5,7},{6,4},{7,5},{8,10},{9,11},{10,... | collective-permute-start | bytes 196616 | tf_op jit(solution)/shard_map/ppermute | solution.py:379
  20.9 8.8 %collective-permute-start.3 = (f32[1,2,32,256]{3,2,1,0:T(8,128)S(1)}, f32[1,2,32,256]{3,2,1,0:T(8,128)S(1)}, u32[]{:S(2)}, u32[]{:S(2)}) collective-permute-start(f32[1,2,32,256]{3,2,1,0:T(8,128)S(1)} %get-tuple-element.30), channel_id=1, source_target_pairs={{0,4},{1,5},{2,6},{3,7},{4,0},{5,1},{6,2},{7,3},{8,12},{9,13},{10,... | collective-permute-start | bytes 196616 | tf_op jit(solution)/shard_map/ppermute | solution.py:379
  27.3 5.2 %collective-permute-start.4 = (f32[1,2,32,256]{3,2,1,0:T(8,128)S(1)}, f32[1,2,32,256]{3,2,1,0:T(8,128)S(1)}, u32[]{:S(2)}, u32[]{:S(2)}) collective-permute-start(f32[1,2,32,256]{3,2,1,0:T(8,128)S(1)} %get-tuple-element.31), channel_id=1, source_target_pairs={{0,6},{1,7},{2,4},{3,5},{4,2},{5,3},{6,0},{7,1},{8,14},{9,15},{10,... | collective-permute-start | bytes 196616 | tf_op jit(solution)/shard_map/ppermute | solution.py:379
  32.9 2.0 %collective-permute-start.8 = (f32[4,2,64,256]{3,2,1,0:T(8,128)S(1)}, f32[4,2,64,256]{3,2,1,0:T(8,128)S(1)}, u32[]{:S(2)}, u32[]{:S(2)}) collective-permute-start(f32[4,2,64,256]{3,2,1,0:T(8,128)S(1)} %shard_map.124), channel_id=1, source_target_pairs={{0,1},{1,0},{2,3},{3,2},{4,5},{5,4},{6,7},{7,6},{8,9},{9,8},{10,11... | collective-permute-start | bytes 1572872 | tf_op jit(solution)/shard_map/ppermute | solution.py:452
  35.0 6.0 %collective-permute-start.9 = (f32[4,2,16,256]{3,2,1,0:T(8,128)S(1)}, f32[4,2,16,256]{3,2,1,0:T(8,128)S(1)}, u32[]{:S(2)}, u32[]{:S(2)}) collective-permute-start(f32[4,2,16,256]{3,2,1,0:T(8,128)S(1)} %get-tuple-element.36), channel_id=1, source_target_pairs={{0,2},{1,3},{2,0},{3,1},{4,6},{5,7},{6,4},{7,5},{8,10},{9,11},{10,... | collective-permute-start | bytes 393224 | tf_op jit(solution)/shard_map/ppermute | solution.py:379
  36.5 8.1 %collective-permute-start.10 = (f32[4,2,16,256]{3,2,1,0:T(8,128)S(1)}, f32[4,2,16,256]{3,2,1,0:T(8,128)S(1)}, u32[]{:S(2)}, u32[]{:S(2)}) collective-permute-start(f32[4,2,16,256]{3,2,1,0:T(8,128)S(1)} %get-tuple-element.37), channel_id=1, source_target_pairs={{0,4},{1,5},{2,6},{3,7},{4,0},{5,1},{6,2},{7,3},{8,12},{9,13},{10,... | collective-permute-start | bytes 393224 | tf_op jit(solution)/shard_map/ppermute | solution.py:379
  37.1 7.6 %collective-permute-start.11 = (f32[4,2,16,256]{3,2,1,0:T(8,128)S(1)}, f32[4,2,16,256]{3,2,1,0:T(8,128)S(1)}, u32[]{:S(2)}, u32[]{:S(2)}) collective-permute-start(f32[4,2,16,256]{3,2,1,0:T(8,128)S(1)} %get-tuple-element.38), channel_id=1, source_target_pairs={{0,6},{1,7},{2,4},{3,5},{4,2},{5,3},{6,0},{7,1},{8,14},{9,15},{10,... | collective-permute-start | bytes 393224 | tf_op jit(solution)/shard_map/ppermute | solution.py:379

commit v8 on v7

--- a/solution.py
+++ b/solution.py
@@ -101,17 +101,16 @@
     return copies
 
 
-def ends_kernel(
-    patterns, partners, op_index, operators, first, second, partners_out, op_out, sems
-):
+def ends_kernel(patterns, operators, *rest):
+    *rest, first, second, sems = rest
+    tables = len(rest) // 2
     width = first.shape[0]
     last = patterns.shape[0] - width
     odd = lax.axis_index("group") % 2
     pairs = [
         (patterns.at[pl.ds((1 - odd) * last, width)], first),
         (patterns.at[pl.ds(odd * last, width)], second),
-        (partners, partners_out),
-        (op_index, op_out),
+        *zip(rest[:tables], rest[tables:]),
     ]
     for copy in copy_all(pairs, sems):
         copy.wait()
@@ -227,10 +226,12 @@
 
 
 def own_kernel(
-    theta_count, width, partners_in, op_in, parent_in, octant_in, patterns, operators, phi_hi,
-    phi_lo, out, phase, *rest
+    theta_count, width, partners_in, op_in, parent_in, octant_in, patterns, operators, hi_in,
+    lo_in, out, phase, *rest
 ):
-    *early, partners, op_index, child_parent, child_octant, slots, shifted, sems = rest
+    *early, partners, op_index, child_parent, child_octant, slots, shifted, phi_hi, phi_lo, sems = (
+        rest
+    )
     clusters, terms = partners.shape
     rows = out.shape[2]
     copies = copy_all(
@@ -239,30 +240,43 @@
             (op_in, op_index),
             (parent_in, child_parent),
             (octant_in, child_octant),
+            (hi_in, phi_hi),
+            (lo_in, phi_lo),
         ],
         sems,
     )
     phase_tables(lax.axis_index("member"), theta_count, phase)
     base = lax.axis_index("group") * clusters
-    for copy in copies:
+    for copy in copies[:4]:
         copy.wait()
 
-    @pl.loop(0, clusters)
-    def _(c):
+    def translate(c, edge):
         for r in range(rows // 8):
             band = pl.ds(r * 8, 8)
             re, im = 0.0, 0.0
             for p in range(terms):
-                q = partners[c, p] - base
-                keep = jnp.where((q >= 0) & (q < clusters), 1.0, 0.0).astype(F32)
-                q = jnp.clip(q, 0, clusters - 1)
-                e = op_index[c, p]
+                q, e = partners[c, p] - base, op_index[c, p]
                 ore, oim = operators[e, 0, band, :], operators[e, 1, band, :]
-                pre, pim = patterns[q, 0, band, :] * keep, patterns[q, 1, band, :] * keep
+                if edge:
+                    keep = jnp.where((q >= 0) & (q < clusters), 1.0, 0.0).astype(F32)
+                    q = jnp.clip(q, 0, clusters - 1)
+                    ore, oim = ore * keep, oim * keep
+                pre, pim = patterns[q, 0, band, :], patterns[q, 1, band, :]
                 re = re + (ore * pre - oim * pim)
                 im = im + (ore * pim + oim * pre)
             out[c, 0, band, :] = re
             out[c, 1, band, :] = im
+
+    @pl.loop(width, clusters - width)
+    def _(c):
+        translate(c, False)
+
+    @pl.loop(0, 2 * width)
+    def _(n):
+        translate(jnp.where(n < width, n, n + clusters - 2 * width), True)
+
+    for copy in copies[4:]:
+        copy.wait()
 
     chips = len(early) + 1
     fill_slots(child_parent, slots, clusters, width, chips)
@@ -347,15 +361,16 @@
     member = lax.axis_index("member")
     chip, core = member // CORES, member % CORES
     end = shape(width, 2, rows, lons)
-    index = jax.ShapeDtypeStruct(partners.shape, jnp.int32)
-    first, second, partners, operator_index = pl.pallas_call(
+    tables = (partners, operator_index, child_parent, child_octant)
+    *tables, first, second = pl.pallas_call(
         ends_kernel,
-        out_shape=(end, end, index, index),
-        in_specs=[HBM] * 4,
-        out_specs=(VMEM,) * 4,
-        scratch_shapes=[pltpu.SemaphoreType.DMA((4,))],
+        out_shape=tuple(jax.ShapeDtypeStruct(x.shape, x.dtype) for x in tables) + (end, end),
+        in_specs=[HBM] * (2 + len(tables)),
+        out_specs=(VMEM,) * (2 + len(tables)),
+        scratch_shapes=[pltpu.SemaphoreType.DMA((2 + len(tables),))],
         compiler_params=params(4),
-    )(*map(in_hbm, (patterns, partners, operator_index, operators)))
+    )(*map(in_hbm, (patterns, operators, *tables)))
+    partners, operator_index, child_parent, child_octant = tables
     pairs = [[(i, i + 1) for i in range(start, groups - 1, 2)] for start in range(2)]
     pairs = [both + [(j, i) for i, j in both] for both in pairs]
     first = lax.ppermute(first, "group", pairs[0])
@@ -382,7 +397,7 @@
     own, phase, *early = call(
         functools.partial(own_kernel, theta_count, width),
         out_shape=(total_shape, shape(8, 2, rows, lons)) + blocks_of(1, chips - 1),
-        in_specs=[VMEM] * 8,
+        in_specs=[VMEM] * 6 + [HBM] * 2,
         out_specs=(VMEM,) * (chips + 1),
         scratch_shapes=[
             pltpu.SMEM(partners.shape, jnp.int32),
@@ -391,11 +406,16 @@
             slots,
             slots,
             rows_of(chips - 1),
-            pltpu.SemaphoreType.DMA((4,)),
+            pltpu.VMEM(phi[0].shape, BF16),
+            pltpu.VMEM(phi[1].shape, BF16),
+            pltpu.SemaphoreType.DMA((6,)),
         ],
         compiler_params=params(20),
         cost_estimate=cost(8),
-    )(partners, operator_index, child_parent, child_octant, patterns, operators, *phi)
+    )(
+        partners, operator_index, child_parent, child_octant, patterns, operators,
+        *map(in_hbm, phi),
+    )
     early = between_chips(dict(enumerate(early, 1)))
 
     count = per_chip - 1

time: 46.3 us -> 46.3 us (level)
  local copies, waits for them, and re-layouts: 1.93 us -> 0.03 us
  waiting for transfers between devices: 16.5 us -> 18.3 us
    unnamed x20 -> x12, local copies, waits for them, and re-layouts: 1.93 us -> 0.03 us
    ppermute x1, waiting for transfers between devices: 1.47 us -> 3.29 us  [on_device(): second = lax.ppermute(second, 'group', pairs[1])]
  transfers between devices with their start and end apart: 12 -> 12, of which waited for: 6 -> 6; matrix products, arithmetic and copies ran while one was open for 0% -> 0% of each run, Pallas kernels for 11% -> 12%
where the time goes in v8:
time: 46.3 us; the launch traced here: 46.2 us
  waiting for transfers between devices  18.3 us (40%)
  starting transfers between devices  17.1 us (37%)
  Pallas kernels  10.6 us (23%)
    ppermute x9, waiting for transfers between devices, between_chips(): moved.append(lax.ppermute(blocks[s], 'member', pairs))  13.6 us
    ppermute x9, starting transfers between devices, between_chips(): moved.append(lax.ppermute(blocks[s], 'member', pairs))  11.6 us
    ppermute x1, starting transfers between devices, on_device(): second = lax.ppermute(second, 'group', pairs[1])  5.3 us
    ppermute x1, waiting for transfers between devices, on_device(): second = lax.ppermute(second, 'group', pairs[1])  3.29 us
    pallas_call x1, Pallas kernels, on_device(): call(functools.partial(own_kernel, theta_count, width), out_shape=(total_...  2.79 us
    pallas_call x2, Pallas kernels, later(): call(functools.partial(later_kernel, order, first_child, width), out_shap...  2.13 us
    pallas_call x1, Pallas kernels, on_device(): call(functools.partial(first_kernel, far), out_shape=blocks_of(count, len...  1.9 us
    pallas_call x1, Pallas kernels, on_device(): call(functools.partial(place_kernel, clusters, width), out_shape=shape(ch...  1.54 us
  transfers between devices with their start and end apart: 12, of which 6 were waited for; matrix products, arithmetic and copies ran while one was open for 0% of the time, Pallas kernels for 12%

profile of v8, /device:TPU:8, one launch (start us, length us, event | category | flops | bytes accessed | tf_op | source)
XLA Modules:
  0.0 46.2 jit_solution(1835899837553621679)
XLA Ops:
  0.0 0.0 copy-start
  0.0 0.0 copy-start.1
  0.0 0.0 copy-start.2
  0.0 0.0 copy-start.3
  0.0 1.3 %shard_map.118 = (s32[8,8]{1,0:T(8,128)S(1)}, s32[8,8]{1,0:T(8,128)S(1)}, s32[16]{0:T(128)S(1)}, s32[16]{0:T(128)S(1)}, f32[2,2,32,512]{3,2,1,0:T(8,128)S(1)}, /*index=5*/f32[2,2,32,512]{3,2,1,0:T(8,128)S(1)}) custom-call(f32[8,2,32,512]{3,2,1,0:T(8,128)} %patterns.3, f32[100,2,32,512]{3,2,1,0:T(8,128)} %operators.5, s32[8,8]{1,0:T(8,128)} %rest_0_.1, ...), custom_call_target="tpu_custom_call" | custom-call | tf_op jit(solution)/shard_map/pallas_call | solution.py:365
  1.3 0.1 collective-permute-start
  1.4 5.3 %collective-permute-start.1 = (f32[2,2,32,512]{3,2,1,0:T(8,128)S(1)}, f32[2,2,32,512]{3,2,1,0:T(8,128)S(1)}, u32[]{:S(2)}, u32[]{:S(2)}) collective-permute-start(f32[2,2,32,512]{3,2,1,0:T(8,128)S(1)} %get-tuple-element.30), channel_id=1, source_target_pairs={{8,16},{16,8},{9,17},{17,9},{10,18},{18,10},{11,19},{19,11},{12,20... | collective-permute-start | bytes 786440 | tf_op jit(solution)/shard_map/ppermute | solution.py:377
  6.7 0.0 copy-done
  6.7 0.0 copy-done.1
  6.7 2.8 %shard_map.119 = (f32[8,2,32,512]{3,2,1,0:T(8,128)S(1)}, f32[8,2,32,512]{3,2,1,0:T(8,128)S(1)}, f32[1,2,32,256]{3,2,1,0:T(8,128)S(1)}, f32[1,2,32,256]{3,2,1,0:T(8,128)S(1)}, f32[1,2,32,256]{3,2,1,0:T(8,128)S(1)}) custom-call(s32[8,8]{1,0:T(8,128)S(1)} %get-tuple-element.26.partners_in.partners, s32[8,8]{1,0:T(8,128)S(1)} %get-tuple-element.27.op_in.op_index, ...), custom_call_target="tpu_custom_call" | custom-call | flops 16000000 | bytes 24000000 | tf_op jit(solution)/shard_map/pallas_call | solution.py:397
  9.5 0.0 copy-start.4
  9.5 0.0 copy-start.5
  9.5 0.0 collective-permute-done.first
  9.5 3.3 %collective-permute-done.1.second = f32[2,2,32,512]{3,2,1,0:T(8,128)S(1)} collective-permute-done((f32[2,2,32,512]{3,2,1,0:T(8,128)S(1)}, f32[2,2,32,512]{3,2,1,0:T(8,128)S(1)}, u32[]{:S(2)}, u32[]{:S(2)}) %collective-permute-start.1) | collective-permute-done | bytes 262176 | tf_op jit(solution)/shard_map/ppermute | solution.py:377
  12.8 0.0 copy-done.2
  12.8 0.0 copy-done.3
  12.8 1.9 %shard_map.120 = (f32[3,2,32,256]{3,2,1,0:T(8,128)S(1)}, f32[8,2,32,512]{3,2,1,0:T(8,128)S(1)}) custom-call(s32[8,8]{1,0:T(8,128)S(1)} %get-tuple-element.26.partners_in.partners, s32[8,8]{1,0:T(8,128)S(1)} %get-tuple-element.27.op_in.op_index, s32[16]{0:T(128)S(1)} %get-tuple-element.24.parent_in.child_parent, ...), custom_call_target="tpu_custom_call" | custom-call | flops 4000000 | bytes 6000000 | tf_op jit(solution)/shard_map/pallas_call | solution.py:424
  14.7 2.5 %collective-permute-start.7 = (f32[3,2,32,256]{3,2,1,0:T(8,128)S(1)}, f32[3,2,32,256]{3,2,1,0:T(8,128)S(1)}, u32[]{:S(2)}, u32[]{:S(2)}) collective-permute-start(f32[3,2,32,256]{3,2,1,0:T(8,128)S(1)} %get-tuple-element.38), channel_id=1, source_target_pairs={{0,6},{1,7},{2,4},{3,5},{4,2},{5,3},{6,0},{7,1},{8,14},{9,15},{10,... | collective-permute-start | bytes 589832 | tf_op jit(solution)/shard_map/ppermute | solution.py:394
  17.2 1.1 %shard_map.122 = (f32[3,2,32,256]{3,2,1,0:T(8,128)S(1)}, f32[3,2,32,256]{3,2,1,0:T(8,128)S(1)}) custom-call(s32[16]{0:T(128)S(1)} %get-tuple-element.24.parent_in.child_parent, s32[16]{0:T(128)S(1)} %get-tuple-element.25.octant_in.child_octant, f32[8,2,32,512]{3,2,1,0:T(8,128)S(1)} %get-tuple-element.32.total, ...), custom_call_target="tpu_custom_call" | custom-call | flops 2000000 | bytes 3000000 | tf_op jit(solution)/shard_map/pallas_call | solution.py:439
  18.4 0.6 %collective-permute-start.5 = (f32[3,2,32,256]{3,2,1,0:T(8,128)S(1)}, f32[3,2,32,256]{3,2,1,0:T(8,128)S(1)}, u32[]{:S(2)}, u32[]{:S(2)}) collective-permute-start(f32[3,2,32,256]{3,2,1,0:T(8,128)S(1)} %get-tuple-element.36), channel_id=1, source_target_pairs={{0,2},{1,3},{2,0},{3,1},{4,6},{5,7},{6,4},{7,5},{8,10},{9,11},{10,... | collective-permute-start | bytes 589832 | tf_op jit(solution)/shard_map/ppermute | solution.py:394
  19.0 0.5 %collective-permute-start.6 = (f32[3,2,32,256]{3,2,1,0:T(8,128)S(1)}, f32[3,2,32,256]{3,2,1,0:T(8,128)S(1)}, u32[]{:S(2)}, u32[]{:S(2)}) collective-permute-start(f32[3,2,32,256]{3,2,1,0:T(8,128)S(1)} %get-tuple-element.37), channel_id=1, source_target_pairs={{0,4},{1,5},{2,6},{3,7},{4,0},{5,1},{6,2},{7,3},{8,12},{9,13},{10,... | collective-permute-start | bytes 589832 | tf_op jit(solution)/shard_map/ppermute | solution.py:394
  19.5 1.5 %collective-permute-start.2 = (f32[1,2,32,256]{3,2,1,0:T(8,128)S(1)}, f32[1,2,32,256]{3,2,1,0:T(8,128)S(1)}, u32[]{:S(2)}, u32[]{:S(2)}) collective-permute-start(f32[1,2,32,256]{3,2,1,0:T(8,128)S(1)} %get-tuple-element.33), channel_id=1, source_target_pairs={{0,2},{1,3},{2,0},{3,1},{4,6},{5,7},{6,4},{7,5},{8,10},{9,11},{10,... | collective-permute-start | bytes 196616 | tf_op jit(solution)/shard_map/ppermute | solution.py:394
  21.0 1.5 %collective-permute-start.3 = (f32[1,2,32,256]{3,2,1,0:T(8,128)S(1)}, f32[1,2,32,256]{3,2,1,0:T(8,128)S(1)}, u32[]{:S(2)}, u32[]{:S(2)}) collective-permute-start(f32[1,2,32,256]{3,2,1,0:T(8,128)S(1)} %get-tuple-element.34), channel_id=1, source_target_pairs={{0,4},{1,5},{2,6},{3,7},{4,0},{5,1},{6,2},{7,3},{8,12},{9,13},{10,... | collective-permute-start | bytes 196616 | tf_op jit(solution)/shard_map/ppermute | solution.py:394
  22.5 4.8 %collective-permute-done.2.rest_1_ = f32[1,2,32,256]{3,2,1,0:T(8,128)S(1)} collective-permute-done((f32[1,2,32,256]{3,2,1,0:T(8,128)S(1)}, f32[1,2,32,256]{3,2,1,0:T(8,128)S(1)}, u32[]{:S(2)}, u32[]{:S(2)}) %collective-permute-start.2) | collective-permute-done | bytes 65568 | tf_op jit(solution)/shard_map/ppermute | solution.py:394
  27.3 1.4 %collective-permute-start.4 = (f32[1,2,32,256]{3,2,1,0:T(8,128)S(1)}, f32[1,2,32,256]{3,2,1,0:T(8,128)S(1)}, u32[]{:S(2)}, u32[]{:S(2)}) collective-permute-start(f32[1,2,32,256]{3,2,1,0:T(8,128)S(1)} %get-tuple-element.35), channel_id=1, source_target_pairs={{0,6},{1,7},{2,4},{3,5},{4,2},{5,3},{6,0},{7,1},{8,14},{9,15},{10,... | collective-permute-start | bytes 196616 | tf_op jit(solution)/shard_map/ppermute | solution.py:394
  28.7 1.0 %shard_map.121.rest_0_ = f32[4,2,32,256]{3,2,1,0:T(8,128)S(1)} custom-call(s32[16]{0:T(128)S(1)} %get-tuple-element.24.parent_in.child_parent, s32[16]{0:T(128)S(1)} %get-tuple-element.25.octant_in.child_octant, f32[8,2,32,512]{3,2,1,0:T(8,128)S(1)} %get-tuple-element.32.total, f32[8,2,32,512]{3,2,1,0:T(8,128)S(1)} %get-tuple-element.31.phase, ...), custom_call_target="tpu_custom_call" | custom-call | flops 2000000 | bytes 3000000 | tf_op jit(solution)/shard_map/pallas_call | solution.py:439
  29.7 0.0 collective-permute-done.3.rest_2_
  29.7 2.7 %collective-permute-done.4.rest_3_ = f32[1,2,32,256]{3,2,1,0:T(8,128)S(1)} collective-permute-done((f32[1,2,32,256]{3,2,1,0:T(8,128)S(1)}, f32[1,2,32,256]{3,2,1,0:T(8,128)S(1)}, u32[]{:S(2)}, u32[]{:S(2)}) %collective-permute-start.4) | collective-permute-done | bytes 65568 | tf_op jit(solution)/shard_map/ppermute | solution.py:394
  32.4 0.0 collective-permute-done.7.rest_6_
  32.4 0.0 collective-permute-done.5.rest_4_
  32.5 0.0 collective-permute-done.6.rest_5_
  32.5 0.0 copy-done.4
  32.5 0.0 copy-done.5
  32.5 0.5 %shard_map.124 = f32[4,2,64,256]{3,2,1,0:T(8,128)S(1)} custom-call(bf16[4,64,128]{2,1,0:T(8,128)(2,1)S(1)} %copy-done.5, bf16[4,64,128]{2,1,0:T(8,128)(2,1)S(1)} %copy-done.4, f32[4,2,32,256]{3,2,1,0:T(8,128)S(1)} %shard_map.121.rest_0_, f32[1,2,32,256]{3,2,1,0:T(8,128)S(1)} %collective-permute-done.2.rest_1_, ...), custom_call_target="tpu_custom_call" | custom-call | flops 2000000 | bytes 3000000 | tf_op jit(solution)/shard_map/pallas_call | solution.py:461
  33.0 0.1 collective-permute-start.8
  33.0 0.5 %shard_map.123.keep = f32[4,2,64,256]{3,2,1,0:T(8,128)S(1)} custom-call(bf16[4,64,128]{2,1,0:T(8,128)(2,1)S(1)} %copy-done.5, bf16[4,64,128]{2,1,0:T(8,128)(2,1)S(1)} %copy-done.4, f32[4,2,32,256]{3,2,1,0:T(8,128)S(1)} %shard_map.121.rest_0_, f32[1,2,32,256]{3,2,1,0:T(8,128)S(1)} %collective-permute-done.2.rest_1_, ...), custom_call_target="tpu_custom_call" | custom-call | flops 2000000 | bytes 3000000 | tf_op jit(solution)/shard_map/pallas_call | solution.py:461
  33.5 1.4 %collective-permute-done.8.arrived = f32[4,2,64,256]{3,2,1,0:T(8,128)S(1)} collective-permute-done((f32[4,2,64,256]{3,2,1,0:T(8,128)S(1)}, f32[4,2,64,256]{3,2,1,0:T(8,128)S(1)}, u32[]{:S(2)}, u32[]{:S(2)}) %collective-permute-start.8) | collective-permute-done | bytes 524320 | tf_op jit(solution)/shard_map/ppermute | solution.py:472
  34.9 0.1 shard_map.125
  35.0 1.6 %collective-permute-start.9 = (f32[4,2,16,256]{3,2,1,0:T(8,128)S(1)}, f32[4,2,16,256]{3,2,1,0:T(8,128)S(1)}, u32[]{:S(2)}, u32[]{:S(2)}) collective-permute-start(f32[4,2,16,256]{3,2,1,0:T(8,128)S(1)} %get-tuple-element.40), channel_id=1, source_target_pairs={{0,2},{1,3},{2,0},{3,1},{4,6},{5,7},{6,4},{7,5},{8,10},{9,11},{10,... | collective-permute-start | bytes 393224 | tf_op jit(solution)/shard_map/ppermute | solution.py:394
  36.6 0.5 %collective-permute-start.10 = (f32[4,2,16,256]{3,2,1,0:T(8,128)S(1)}, f32[4,2,16,256]{3,2,1,0:T(8,128)S(1)}, u32[]{:S(2)}, u32[]{:S(2)}) collective-permute-start(f32[4,2,16,256]{3,2,1,0:T(8,128)S(1)} %get-tuple-element.41), channel_id=1, source_target_pairs={{0,4},{1,5},{2,6},{3,7},{4,0},{5,1},{6,2},{7,3},{8,12},{9,13},{10,... | collective-permute-start | bytes 393224 | tf_op jit(solution)/shard_map/ppermute | solution.py:394
  37.1 1.5 %collective-permute-start.11 = (f32[4,2,16,256]{3,2,1,0:T(8,128)S(1)}, f32[4,2,16,256]{3,2,1,0:T(8,128)S(1)}, u32[]{:S(2)}, u32[]{:S(2)}) collective-permute-start(f32[4,2,16,256]{3,2,1,0:T(8,128)S(1)} %get-tuple-element.42), channel_id=1, source_target_pairs={{0,6},{1,7},{2,4},{3,5},{4,2},{5,3},{6,0},{7,1},{8,14},{9,15},{10,... | collective-permute-start | bytes 393224 | tf_op jit(solution)/shard_map/ppermute | solution.py:394
  38.6 2.5 %collective-permute-done.9.rest_1_ = f32[4,2,16,256]{3,2,1,0:T(8,128)S(1)} collective-permute-done((f32[4,2,16,256]{3,2,1,0:T(8,128)S(1)}, f32[4,2,16,256]{3,2,1,0:T(8,128)S(1)}, u32[]{:S(2)}, u32[]{:S(2)}) %collective-permute-start.9) | collective-permute-done | bytes 131104 | tf_op jit(solution)/shard_map/ppermute | solution.py:394
  41.0 3.6 %collective-permute-done.10.rest_2_ = f32[4,2,16,256]{3,2,1,0:T(8,128)S(1)} collective-permute-done((f32[4,2,16,256]{3,2,1,0:T(8,128)S(1)}, f32[4,2,16,256]{3,2,1,0:T(8,128)S(1)}, u32[]{:S(2)}, u32[]{:S(2)}) %collective-permute-start.10) | collective-permute-done | bytes 131104 | tf_op jit(solution)/shard_map/ppermute | solution.py:394
  44.6 0.0 collective-permute-done.11.rest_3_
  44.6 1.5 %shard_map.126 = f32[16,2,16,256]{3,2,1,0:T(8,128)} custom-call(s32[16]{0:T(128)S(1)} %get-tuple-element.24.parent_in.child_parent, f32[4,2,16,256]{3,2,1,0:T(8,128)S(1)} %get-tuple-element.39.rest_0_, f32[4,2,16,256]{3,2,1,0:T(8,128)S(1)} %collective-permute-done.9.rest_1_, f32[4,2,16,256]{3,2,1,0:T(8,128)S(1)} %collective-permute-done.10.rest_2_, ...), custom_call_target="tpu_custom_call" | custom-call | flops 2000000 | bytes 3000000 | tf_op jit(solution)/shard_map/pallas_call | solution.py:499
Async XLA Ops:
  0.0 6.7 %copy-start = (f32[100,2,32,512]{3,2,1,0:T(8,128)S(1)}, f32[100,2,32,512]{3,2,1,0:T(8,128)}, u32[]{:S(2)}) copy-start(f32[100,2,32,512]{3,2,1,0:T(8,128)} %operators.5) | copy-start | bytes 39321604
  0.0 6.7 %copy-start.1 = (f32[8,2,32,512]{3,2,1,0:T(8,128)S(1)}, f32[8,2,32,512]{3,2,1,0:T(8,128)}, u32[]{:S(2)}) copy-start(f32[8,2,32,512]{3,2,1,0:T(8,128)} %patterns.3) | copy-start | bytes 3145732
  0.0 12.8 %copy-start.2 = (bf16[512,256]{1,0:T(8,128)(2,1)S(1)}, bf16[512,256]{1,0:T(8,128)(2,1)}, u32[]{:S(2)}) copy-start(bf16[512,256]{1,0:T(8,128)(2,1)} %constant.9.clone.lo_in.phi_lo) | copy-start | bytes 786436
  0.0 12.8 %copy-start.3 = (bf16[512,256]{1,0:T(8,128)(2,1)S(1)}, bf16[512,256]{1,0:T(8,128)(2,1)}, u32[]{:S(2)}) copy-start(bf16[512,256]{1,0:T(8,128)(2,1)} %constant.8.clone.hi_in.phi_hi) | copy-start | bytes 786436
  1.3 8.2 %collective-permute-start = (f32[2,2,32,512]{3,2,1,0:T(8,128)S(1)}, f32[2,2,32,512]{3,2,1,0:T(8,128)S(1)}, u32[]{:S(2)}, u32[]{:S(2)}) collective-permute-start(f32[2,2,32,512]{3,2,1,0:T(8,128)S(1)} %get-tuple-element.29), channel_id=1, source_target_pairs={{0,8},{16,24},{8,0},{24,16},{1,9},{17,25},{9,1},{25,17},{2,10},{18... | collective-permute-start | bytes 786440 | tf_op jit(solution)/shard_map/ppermute | solution.py:376
  1.4 11.4 %collective-permute-start.1 = (f32[2,2,32,512]{3,2,1,0:T(8,128)S(1)}, f32[2,2,32,512]{3,2,1,0:T(8,128)S(1)}, u32[]{:S(2)}, u32[]{:S(2)}) collective-permute-start(f32[2,2,32,512]{3,2,1,0:T(8,128)S(1)} %get-tuple-element.30), channel_id=1, source_target_pairs={{8,16},{16,8},{9,17},{17,9},{10,18},{18,10},{11,19},{19,11},{12,20... | collective-permute-start | bytes 786440 | tf_op jit(solution)/shard_map/ppermute | solution.py:377
  9.5 23.0 %copy-start.4 = (bf16[4,64,128]{2,1,0:T(8,128)(2,1)S(1)}, bf16[4,64,128]{2,1,0:T(8,128)(2,1)}, u32[]{:S(2)}) copy-start(bf16[4,64,128]{2,1,0:T(8,128)(2,1)} %constant.11.clone.t_lo) | copy-start | bytes 196612
  9.5 23.0 %copy-start.5 = (bf16[4,64,128]{2,1,0:T(8,128)(2,1)S(1)}, bf16[4,64,128]{2,1,0:T(8,128)(2,1)}, u32[]{:S(2)}) copy-start(bf16[4,64,128]{2,1,0:T(8,128)(2,1)} %constant.10.clone.t_hi) | copy-start | bytes 196612
  14.7 17.7 %collective-permute-start.7 = (f32[3,2,32,256]{3,2,1,0:T(8,128)S(1)}, f32[3,2,32,256]{3,2,1,0:T(8,128)S(1)}, u32[]{:S(2)}, u32[]{:S(2)}) collective-permute-start(f32[3,2,32,256]{3,2,1,0:T(8,128)S(1)} %get-tuple-element.38), channel_id=1, source_target_pairs={{0,6},{1,7},{2,4},{3,5},{4,2},{5,3},{6,0},{7,1},{8,14},{9,15},{10,... | collective-permute-start | bytes 589832 | tf_op jit(solution)/shard_map/ppermute | solution.py:394
  18.4 14.1 %collective-permute-start.5 = (f32[3,2,32,256]{3,2,1,0:T(8,128)S(1)}, f32[3,2,32,256]{3,2,1,0:T(8,128)S(1)}, u32[]{:S(2)}, u32[]{:S(2)}) collective-permute-start(f32[3,2,32,256]{3,2,1,0:T(8,128)S(1)} %get-tuple-element.36), channel_id=1, source_target_pairs={{0,2},{1,3},{2,0},{3,1},{4,6},{5,7},{6,4},{7,5},{8,10},{9,11},{10,... | collective-permute-start | bytes 589832 | tf_op jit(solution)/shard_map/ppermute | solution.py:394
  19.0 13.5 %collective-permute-start.6 = (f32[3,2,32,256]{3,2,1,0:T(8,128)S(1)}, f32[3,2,32,256]{3,2,1,0:T(8,128)S(1)}, u32[]{:S(2)}, u32[]{:S(2)}) collective-permute-start(f32[3,2,32,256]{3,2,1,0:T(8,128)S(1)} %get-tuple-element.37), channel_id=1, source_target_pairs={{0,4},{1,5},{2,6},{3,7},{4,0},{5,1},{6,2},{7,3},{8,12},{9,13},{10,... | collective-permute-start | bytes 589832 | tf_op jit(solution)/shard_map/ppermute | solution.py:394
  19.5 7.8 %collective-permute-start.2 = (f32[1,2,32,256]{3,2,1,0:T(8,128)S(1)}, f32[1,2,32,256]{3,2,1,0:T(8,128)S(1)}, u32[]{:S(2)}, u32[]{:S(2)}) collective-permute-start(f32[1,2,32,256]{3,2,1,0:T(8,128)S(1)} %get-tuple-element.33), channel_id=1, source_target_pairs={{0,2},{1,3},{2,0},{3,1},{4,6},{5,7},{6,4},{7,5},{8,10},{9,11},{10,... | collective-permute-start | bytes 196616 | tf_op jit(solution)/shard_map/ppermute | solution.py:394
  21.0 8.8 %collective-permute-start.3 = (f32[1,2,32,256]{3,2,1,0:T(8,128)S(1)}, f32[1,2,32,256]{3,2,1,0:T(8,128)S(1)}, u32[]{:S(2)}, u32[]{:S(2)}) collective-permute-start(f32[1,2,32,256]{3,2,1,0:T(8,128)S(1)} %get-tuple-element.34), channel_id=1, source_target_pairs={{0,4},{1,5},{2,6},{3,7},{4,0},{5,1},{6,2},{7,3},{8,12},{9,13},{10,... | collective-permute-start | bytes 196616 | tf_op jit(solution)/shard_map/ppermute | solution.py:394
  27.3 5.2 %collective-permute-start.4 = (f32[1,2,32,256]{3,2,1,0:T(8,128)S(1)}, f32[1,2,32,256]{3,2,1,0:T(8,128)S(1)}, u32[]{:S(2)}, u32[]{:S(2)}) collective-permute-start(f32[1,2,32,256]{3,2,1,0:T(8,128)S(1)} %get-tuple-element.35), channel_id=1, source_target_pairs={{0,6},{1,7},{2,4},{3,5},{4,2},{5,3},{6,0},{7,1},{8,14},{9,15},{10,... | collective-permute-start | bytes 196616 | tf_op jit(solution)/shard_map/ppermute | solution.py:394
  33.0 2.0 %collective-permute-start.8 = (f32[4,2,64,256]{3,2,1,0:T(8,128)S(1)}, f32[4,2,64,256]{3,2,1,0:T(8,128)S(1)}, u32[]{:S(2)}, u32[]{:S(2)}) collective-permute-start(f32[4,2,64,256]{3,2,1,0:T(8,128)S(1)} %shard_map.124), channel_id=1, source_target_pairs={{0,1},{1,0},{2,3},{3,2},{4,5},{5,4},{6,7},{7,6},{8,9},{9,8},{10,11... | collective-permute-start | bytes 1572872 | tf_op jit(solution)/shard_map/ppermute | solution.py:472
  35.0 6.0 %collective-permute-start.9 = (f32[4,2,16,256]{3,2,1,0:T(8,128)S(1)}, f32[4,2,16,256]{3,2,1,0:T(8,128)S(1)}, u32[]{:S(2)}, u32[]{:S(2)}) collective-permute-start(f32[4,2,16,256]{3,2,1,0:T(8,128)S(1)} %get-tuple-element.40), channel_id=1, source_target_pairs={{0,2},{1,3},{2,0},{3,1},{4,6},{5,7},{6,4},{7,5},{8,10},{9,11},{10,... | collective-permute-start | bytes 393224 | tf_op jit(solution)/shard_map/ppermute | solution.py:394
  36.6 8.1 %collective-permute-start.10 = (f32[4,2,16,256]{3,2,1,0:T(8,128)S(1)}, f32[4,2,16,256]{3,2,1,0:T(8,128)S(1)}, u32[]{:S(2)}, u32[]{:S(2)}) collective-permute-start(f32[4,2,16,256]{3,2,1,0:T(8,128)S(1)} %get-tuple-element.41), channel_id=1, source_target_pairs={{0,4},{1,5},{2,6},{3,7},{4,0},{5,1},{6,2},{7,3},{8,12},{9,13},{10,... | collective-permute-start | bytes 393224 | tf_op jit(solution)/shard_map/ppermute | solution.py:394
  37.1 7.6 %collective-permute-start.11 = (f32[4,2,16,256]{3,2,1,0:T(8,128)S(1)}, f32[4,2,16,256]{3,2,1,0:T(8,128)S(1)}, u32[]{:S(2)}, u32[]{:S(2)}) collective-permute-start(f32[4,2,16,256]{3,2,1,0:T(8,128)S(1)} %get-tuple-element.42), channel_id=1, source_target_pairs={{0,6},{1,7},{2,4},{3,5},{4,2},{5,3},{6,0},{7,1},{8,14},{9,15},{10,... | collective-permute-start | bytes 393224 | tf_op jit(solution)/shard_map/ppermute | solution.py:394

commit v9 on v8

--- a/solution.py
+++ b/solution.py
@@ -286,6 +286,19 @@
     )
 
 
+def last_kernel(width, child_parent, child_octant, total, phase, phi_hi, phi_lo, *rest):
+    out, child_of, slots, shifted = rest
+    chips = lax.axis_size("member") // CORES
+    chip = lax.axis_index("member") // CORES
+    per_chip = out.shape[0]
+    args = (child_parent, child_octant, total, phase, phi_hi, phi_lo, out, slots, shifted)
+    later_kernel([0], 0, width, *args)
+    for s in range(chips):
+        for i in range(per_chip):
+            k = slots[slot_of(chip ^ s, i, chips, per_chip)]
+            child_of[s * per_chip + i] = jnp.full(child_of.shape[1:], k, jnp.int32)
+
+
 def theta_kernel(away, t_hi, t_lo, *rest):
     mine, *blocks, out, lats = rest
     chips = len(blocks) // 2 + 1
@@ -314,13 +327,11 @@
         out[...] = keep[:, :, band, :] + arrived[:, :, band, :]
 
 
-def place_kernel(clusters, width, child_parent, *rest):
-    *blocks, out, slots, sems = rest
-    chips, per_chip = len(blocks), blocks[0].shape[0]
-    chip = lax.axis_index("member") // CORES
-    fill_slots(child_parent, slots, clusters, width, chips)
+def place_kernel(child_of, *rest):
+    *blocks, out, sems = rest
+    per_chip = blocks[0].shape[0]
     pairs = [
-        (block.at[i], out.at[slots[slot_of(chip ^ s, i, chips, per_chip)]])
+        (block.at[i], out.at[child_of[s * per_chip + i][0, 0]])
         for s, block in enumerate(blocks)
         for i in range(per_chip)
     ]
@@ -435,20 +446,28 @@
     )
     late.update(zip(far, outs))
 
-    def later(order, first_child, number):
+    def later(kernel, out_shape, number):
         return call(
-            functools.partial(later_kernel, order, first_child, width),
-            out_shape=blocks_of(number, len(order)),
+            kernel,
+            out_shape=out_shape,
             in_specs=[SMEM] * 2 + [VMEM] * 4,
-            out_specs=(VMEM,) * len(order),
-            scratch_shapes=[slots, rows_of(number * len(order))],
+            out_specs=(VMEM,) * len(out_shape),
+            scratch_shapes=[slots, rows_of(number)],
             compiler_params=params(20),
             cost_estimate=cost(1),
         )(child_parent, child_octant, total, phase, *phi)
 
-    late.update(zip(near, later(near, 1, count)))
+    outs = later(
+        functools.partial(later_kernel, near, 1, width),
+        blocks_of(count, len(near)), count * len(near),
+    )
+    late.update(zip(near, outs))
     late = between_chips(late)
-    (mine,) = later([0], 0, per_chip)
+    tiles = jax.ShapeDtypeStruct((children, 8, 128), jnp.int32)
+    mine, child_of = later(
+        functools.partial(last_kernel, width),
+        blocks_of(per_chip, 1) + (tiles,), per_chip,
+    )
 
     theta = theta_table(theta_count, NTC).reshape(chips, CORES, out_rows, chips, CORES, rows)
     theta = theta.transpose(4, 1, 0, 2, 3, 5).reshape(
@@ -497,14 +516,14 @@
 
     final = [pieces[0], *between_chips(dict(enumerate(pieces)))]
     return call(
-        functools.partial(place_kernel, clusters, width),
+        place_kernel,
         out_shape=shape(children, 2, out_rows, NPC),
-        in_specs=[SMEM] + [VMEM] * chips,
+        in_specs=[VMEM] * (1 + chips),
         out_specs=HBM,
-        scratch_shapes=[slots, pltpu.SemaphoreType.DMA((children,))],
+        scratch_shapes=[pltpu.SemaphoreType.DMA((children,))],
         compiler_params=params(12),
         cost_estimate=cost(1),
-    )(child_parent, *final)
+    )(child_of, *final)
 
 
 def solution(mesh):

time: 46.3 us -> 45.7 us (0.987)
  Pallas kernels: 10.6 us -> 10.1 us
    pallas_call x3, Pallas kernels: 3.67 us -> 3.09 us  [the longest x2 2.13 us: later(): call(kernel, out_shape=out_shape, in_specs=[SMEM] * 2 + [VMEM] * 4, out_s...]
where the time goes in v9:
time: 45.7 us; the launch traced here: 45.6 us
  waiting for transfers between devices  18.3 us (40%)
  starting transfers between devices  17.1 us (37%)
  Pallas kernels  10.1 us (22%)
    ppermute x9, waiting for transfers between devices, between_chips(): moved.append(lax.ppermute(blocks[s], 'member', pairs))  13.6 us
    ppermute x9, starting transfers between devices, between_chips(): moved.append(lax.ppermute(blocks[s], 'member', pairs))  11.6 us
    ppermute x1, starting transfers between devices, on_device(): second = lax.ppermute(second, 'group', pairs[1])  5.3 us
    ppermute x1, waiting for transfers between devices, on_device(): second = lax.ppermute(second, 'group', pairs[1])  3.29 us
    pallas_call x1, Pallas kernels, on_device(): call(functools.partial(own_kernel, theta_count, width), out_shape=(total_...  2.79 us
    pallas_call x2, Pallas kernels, later(): call(kernel, out_shape=out_shape, in_specs=[SMEM] * 2 + [VMEM] * 4, out_s...  2.13 us
    pallas_call x1, Pallas kernels, on_device(): call(functools.partial(first_kernel, far), out_shape=blocks_of(count, len...  1.9 us
    ppermute x1, waiting for transfers between devices, on_device(): swapped = lax.ppermute(away, 'member', swap)  1.41 us
  transfers between devices with their start and end apart: 12, of which 6 were waited for; matrix products, arithmetic and copies ran while one was open for 0% of the time, Pallas kernels for 12%

profile of v9, /device:TPU:8, one launch (start us, length us, event | category | flops | bytes accessed | tf_op | source)
XLA Modules:
  0.0 45.6 jit_solution(7610499476759039383)
XLA Ops:
  0.0 0.0 copy-start
  0.0 0.0 copy-start.1
  0.0 0.0 copy-start.2
  0.0 0.0 copy-start.3
  0.0 1.3 %shard_map.118 = (s32[8,8]{1,0:T(8,128)S(1)}, s32[8,8]{1,0:T(8,128)S(1)}, s32[16]{0:T(128)S(1)}, s32[16]{0:T(128)S(1)}, f32[2,2,32,512]{3,2,1,0:T(8,128)S(1)}, /*index=5*/f32[2,2,32,512]{3,2,1,0:T(8,128)S(1)}) custom-call(f32[8,2,32,512]{3,2,1,0:T(8,128)} %patterns.3, f32[100,2,32,512]{3,2,1,0:T(8,128)} %operators.5, s32[8,8]{1,0:T(8,128)} %rest_0_.1, ...), custom_call_target="tpu_custom_call" | custom-call | tf_op jit(solution)/shard_map/pallas_call | solution.py:376
  1.3 0.1 collective-permute-start
  1.4 5.3 %collective-permute-start.1 = (f32[2,2,32,512]{3,2,1,0:T(8,128)S(1)}, f32[2,2,32,512]{3,2,1,0:T(8,128)S(1)}, u32[]{:S(2)}, u32[]{:S(2)}) collective-permute-start(f32[2,2,32,512]{3,2,1,0:T(8,128)S(1)} %get-tuple-element.32), channel_id=1, source_target_pairs={{8,16},{16,8},{9,17},{17,9},{10,18},{18,10},{11,19},{19,11},{12,20... | collective-permute-start | bytes 786440 | tf_op jit(solution)/shard_map/ppermute | solution.py:388
  6.7 0.0 copy-done
  6.7 0.0 copy-done.1
  6.7 2.8 %shard_map.119 = (f32[8,2,32,512]{3,2,1,0:T(8,128)S(1)}, f32[8,2,32,512]{3,2,1,0:T(8,128)S(1)}, f32[1,2,32,256]{3,2,1,0:T(8,128)S(1)}, f32[1,2,32,256]{3,2,1,0:T(8,128)S(1)}, f32[1,2,32,256]{3,2,1,0:T(8,128)S(1)}) custom-call(s32[8,8]{1,0:T(8,128)S(1)} %get-tuple-element.28.partners_in.partners, s32[8,8]{1,0:T(8,128)S(1)} %get-tuple-element.29.op_in.op_index, ...), custom_call_target="tpu_custom_call" | custom-call | flops 16000000 | bytes 24000000 | tf_op jit(solution)/shard_map/pallas_call | solution.py:408
  9.5 0.0 copy-start.4
  9.5 0.0 copy-start.5
  9.5 0.0 collective-permute-done.first
  9.5 3.3 %collective-permute-done.1.second = f32[2,2,32,512]{3,2,1,0:T(8,128)S(1)} collective-permute-done((f32[2,2,32,512]{3,2,1,0:T(8,128)S(1)}, f32[2,2,32,512]{3,2,1,0:T(8,128)S(1)}, u32[]{:S(2)}, u32[]{:S(2)}) %collective-permute-start.1) | collective-permute-done | bytes 262176 | tf_op jit(solution)/shard_map/ppermute | solution.py:388
  12.8 0.0 copy-done.2
  12.8 0.0 copy-done.3
  12.8 1.9 %shard_map.120 = (f32[3,2,32,256]{3,2,1,0:T(8,128)S(1)}, f32[8,2,32,512]{3,2,1,0:T(8,128)S(1)}) custom-call(s32[8,8]{1,0:T(8,128)S(1)} %get-tuple-element.28.partners_in.partners, s32[8,8]{1,0:T(8,128)S(1)} %get-tuple-element.29.op_in.op_index, s32[16]{0:T(128)S(1)} %get-tuple-element.26.parent_in.child_parent, ...), custom_call_target="tpu_custom_call" | custom-call | flops 4000000 | bytes 6000000 | tf_op jit(solution)/shard_map/pallas_call | solution.py:435
  14.7 2.5 %collective-permute-start.7 = (f32[3,2,32,256]{3,2,1,0:T(8,128)S(1)}, f32[3,2,32,256]{3,2,1,0:T(8,128)S(1)}, u32[]{:S(2)}, u32[]{:S(2)}) collective-permute-start(f32[3,2,32,256]{3,2,1,0:T(8,128)S(1)} %get-tuple-element.42), channel_id=1, source_target_pairs={{0,6},{1,7},{2,4},{3,5},{4,2},{5,3},{6,0},{7,1},{8,14},{9,15},{10,... | collective-permute-start | bytes 589832 | tf_op jit(solution)/shard_map/ppermute | solution.py:405
  17.2 1.1 %shard_map.122 = (f32[3,2,32,256]{3,2,1,0:T(8,128)S(1)}, f32[3,2,32,256]{3,2,1,0:T(8,128)S(1)}) custom-call(s32[16]{0:T(128)S(1)} %get-tuple-element.26.parent_in.child_parent, s32[16]{0:T(128)S(1)} %get-tuple-element.27.octant_in.child_octant, f32[8,2,32,512]{3,2,1,0:T(8,128)S(1)} %get-tuple-element.34.total, ...), custom_call_target="tpu_custom_call" | custom-call | flops 2000000 | bytes 3000000 | tf_op jit(solution)/shard_map/pallas_call | solution.py:450
  18.4 0.6 %collective-permute-start.5 = (f32[3,2,32,256]{3,2,1,0:T(8,128)S(1)}, f32[3,2,32,256]{3,2,1,0:T(8,128)S(1)}, u32[]{:S(2)}, u32[]{:S(2)}) collective-permute-start(f32[3,2,32,256]{3,2,1,0:T(8,128)S(1)} %get-tuple-element.40), channel_id=1, source_target_pairs={{0,2},{1,3},{2,0},{3,1},{4,6},{5,7},{6,4},{7,5},{8,10},{9,11},{10,... | collective-permute-start | bytes 589832 | tf_op jit(solution)/shard_map/ppermute | solution.py:405
  19.0 0.5 %collective-permute-start.6 = (f32[3,2,32,256]{3,2,1,0:T(8,128)S(1)}, f32[3,2,32,256]{3,2,1,0:T(8,128)S(1)}, u32[]{:S(2)}, u32[]{:S(2)}) collective-permute-start(f32[3,2,32,256]{3,2,1,0:T(8,128)S(1)} %get-tuple-element.41), channel_id=1, source_target_pairs={{0,4},{1,5},{2,6},{3,7},{4,0},{5,1},{6,2},{7,3},{8,12},{9,13},{10,... | collective-permute-start | bytes 589832 | tf_op jit(solution)/shard_map/ppermute | solution.py:405
  19.5 1.5 %collective-permute-start.2 = (f32[1,2,32,256]{3,2,1,0:T(8,128)S(1)}, f32[1,2,32,256]{3,2,1,0:T(8,128)S(1)}, u32[]{:S(2)}, u32[]{:S(2)}) collective-permute-start(f32[1,2,32,256]{3,2,1,0:T(8,128)S(1)} %get-tuple-element.37), channel_id=1, source_target_pairs={{0,2},{1,3},{2,0},{3,1},{4,6},{5,7},{6,4},{7,5},{8,10},{9,11},{10,... | collective-permute-start | bytes 196616 | tf_op jit(solution)/shard_map/ppermute | solution.py:405
  21.0 1.5 %collective-permute-start.3 = (f32[1,2,32,256]{3,2,1,0:T(8,128)S(1)}, f32[1,2,32,256]{3,2,1,0:T(8,128)S(1)}, u32[]{:S(2)}, u32[]{:S(2)}) collective-permute-start(f32[1,2,32,256]{3,2,1,0:T(8,128)S(1)} %get-tuple-element.38), channel_id=1, source_target_pairs={{0,4},{1,5},{2,6},{3,7},{4,0},{5,1},{6,2},{7,3},{8,12},{9,13},{10,... | collective-permute-start | bytes 196616 | tf_op jit(solution)/shard_map/ppermute | solution.py:405
  22.5 4.8 %collective-permute-done.2.rest_1_ = f32[1,2,32,256]{3,2,1,0:T(8,128)S(1)} collective-permute-done((f32[1,2,32,256]{3,2,1,0:T(8,128)S(1)}, f32[1,2,32,256]{3,2,1,0:T(8,128)S(1)}, u32[]{:S(2)}, u32[]{:S(2)}) %collective-permute-start.2) | collective-permute-done | bytes 65568 | tf_op jit(solution)/shard_map/ppermute | solution.py:405
  27.3 1.4 %collective-permute-start.4 = (f32[1,2,32,256]{3,2,1,0:T(8,128)S(1)}, f32[1,2,32,256]{3,2,1,0:T(8,128)S(1)}, u32[]{:S(2)}, u32[]{:S(2)}) collective-permute-start(f32[1,2,32,256]{3,2,1,0:T(8,128)S(1)} %get-tuple-element.39), channel_id=1, source_target_pairs={{0,6},{1,7},{2,4},{3,5},{4,2},{5,3},{6,0},{7,1},{8,14},{9,15},{10,... | collective-permute-start | bytes 196616 | tf_op jit(solution)/shard_map/ppermute | solution.py:405
  28.7 1.0 %shard_map.121 = (f32[4,2,32,256]{3,2,1,0:T(8,128)S(1)}, s32[16,8,128]{2,1,0:T(8,128)S(1)}) custom-call(s32[16]{0:T(128)S(1)} %get-tuple-element.26.parent_in.child_parent, s32[16]{0:T(128)S(1)} %get-tuple-element.27.octant_in.child_octant, f32[8,2,32,512]{3,2,1,0:T(8,128)S(1)} %get-tuple-element.34.total, f32[8,2,32,512]{3,2,1,0:T(8,128)S(1)} %get-tuple-element.33.phase, ...), custom_call_target="tpu_custom_call" | custom-call | flops 2000000 | bytes 3000000 | tf_op jit(solution)/shard_map/pallas_call | solution.py:450
  29.7 0.0 collective-permute-done.3.rest_2_
  29.7 2.7 %collective-permute-done.4.rest_3_ = f32[1,2,32,256]{3,2,1,0:T(8,128)S(1)} collective-permute-done((f32[1,2,32,256]{3,2,1,0:T(8,128)S(1)}, f32[1,2,32,256]{3,2,1,0:T(8,128)S(1)}, u32[]{:S(2)}, u32[]{:S(2)}) %collective-permute-start.4) | collective-permute-done | bytes 65568 | tf_op jit(solution)/shard_map/ppermute | solution.py:405
  32.4 0.0 collective-permute-done.7.rest_6_
  32.4 0.0 collective-permute-done.5.rest_4_
  32.5 0.0 collective-permute-done.6.rest_5_
  32.5 0.0 copy-done.4
  32.5 0.0 copy-done.5
  32.5 0.5 %shard_map.124 = f32[4,2,64,256]{3,2,1,0:T(8,128)S(1)} custom-call(bf16[4,64,128]{2,1,0:T(8,128)(2,1)S(1)} %copy-done.5, bf16[4,64,128]{2,1,0:T(8,128)(2,1)S(1)} %copy-done.4, f32[4,2,32,256]{3,2,1,0:T(8,128)S(1)} %get-tuple-element.36.rest_0_, f32[1,2,32,256]{3,2,1,0:T(8,128)S(1)} %collective-permute-done.2.rest_1_, ...), custom_call_target="tpu_custom_call" | custom-call | flops 2000000 | bytes 3000000 | tf_op jit(solution)/shard_map/pallas_call | solution.py:480
  33.0 0.1 collective-permute-start.8
  33.0 0.5 %shard_map.123.keep = f32[4,2,64,256]{3,2,1,0:T(8,128)S(1)} custom-call(bf16[4,64,128]{2,1,0:T(8,128)(2,1)S(1)} %copy-done.5, bf16[4,64,128]{2,1,0:T(8,128)(2,1)S(1)} %copy-done.4, f32[4,2,32,256]{3,2,1,0:T(8,128)S(1)} %get-tuple-element.36.rest_0_, f32[1,2,32,256]{3,2,1,0:T(8,128)S(1)} %collective-permute-done.2.rest_1_, ...), custom_call_target="tpu_custom_call" | custom-call | flops 2000000 | bytes 3000000 | tf_op jit(solution)/shard_map/pallas_call | solution.py:480
  33.5 1.4 %collective-permute-done.8.arrived = f32[4,2,64,256]{3,2,1,0:T(8,128)S(1)} collective-permute-done((f32[4,2,64,256]{3,2,1,0:T(8,128)S(1)}, f32[4,2,64,256]{3,2,1,0:T(8,128)S(1)}, u32[]{:S(2)}, u32[]{:S(2)}) %collective-permute-start.8) | collective-permute-done | bytes 524320 | tf_op jit(solution)/shard_map/ppermute | solution.py:491
  34.9 0.1 shard_map.125
  35.0 1.6 %collective-permute-start.9 = (f32[4,2,16,256]{3,2,1,0:T(8,128)S(1)}, f32[4,2,16,256]{3,2,1,0:T(8,128)S(1)}, u32[]{:S(2)}, u32[]{:S(2)}) collective-permute-start(f32[4,2,16,256]{3,2,1,0:T(8,128)S(1)} %get-tuple-element.44), channel_id=1, source_target_pairs={{0,2},{1,3},{2,0},{3,1},{4,6},{5,7},{6,4},{7,5},{8,10},{9,11},{10,... | collective-permute-start | bytes 393224 | tf_op jit(solution)/shard_map/ppermute | solution.py:405
  36.6 0.5 %collective-permute-start.10 = (f32[4,2,16,256]{3,2,1,0:T(8,128)S(1)}, f32[4,2,16,256]{3,2,1,0:T(8,128)S(1)}, u32[]{:S(2)}, u32[]{:S(2)}) collective-permute-start(f32[4,2,16,256]{3,2,1,0:T(8,128)S(1)} %get-tuple-element.45), channel_id=1, source_target_pairs={{0,4},{1,5},{2,6},{3,7},{4,0},{5,1},{6,2},{7,3},{8,12},{9,13},{10,... | collective-permute-start | bytes 393224 | tf_op jit(solution)/shard_map/ppermute | solution.py:405
  37.1 1.5 %collective-permute-start.11 = (f32[4,2,16,256]{3,2,1,0:T(8,128)S(1)}, f32[4,2,16,256]{3,2,1,0:T(8,128)S(1)}, u32[]{:S(2)}, u32[]{:S(2)}) collective-permute-start(f32[4,2,16,256]{3,2,1,0:T(8,128)S(1)} %get-tuple-element.46), channel_id=1, source_target_pairs={{0,6},{1,7},{2,4},{3,5},{4,2},{5,3},{6,0},{7,1},{8,14},{9,15},{10,... | collective-permute-start | bytes 393224 | tf_op jit(solution)/shard_map/ppermute | solution.py:405
  38.6 2.5 %collective-permute-done.9.rest_1_ = f32[4,2,16,256]{3,2,1,0:T(8,128)S(1)} collective-permute-done((f32[4,2,16,256]{3,2,1,0:T(8,128)S(1)}, f32[4,2,16,256]{3,2,1,0:T(8,128)S(1)}, u32[]{:S(2)}, u32[]{:S(2)}) %collective-permute-start.9) | collective-permute-done | bytes 131104 | tf_op jit(solution)/shard_map/ppermute | solution.py:405
  41.0 3.6 %collective-permute-done.10.rest_2_ = f32[4,2,16,256]{3,2,1,0:T(8,128)S(1)} collective-permute-done((f32[4,2,16,256]{3,2,1,0:T(8,128)S(1)}, f32[4,2,16,256]{3,2,1,0:T(8,128)S(1)}, u32[]{:S(2)}, u32[]{:S(2)}) %collective-permute-start.10) | collective-permute-done | bytes 131104 | tf_op jit(solution)/shard_map/ppermute | solution.py:405
  44.6 0.0 collective-permute-done.11.rest_3_
  44.6 1.0 %shard_map.126 = f32[16,2,16,256]{3,2,1,0:T(8,128)} custom-call(s32[16,8,128]{2,1,0:T(8,128)S(1)} %get-tuple-element.35.child_of, f32[4,2,16,256]{3,2,1,0:T(8,128)S(1)} %get-tuple-element.43.rest_0_, f32[4,2,16,256]{3,2,1,0:T(8,128)S(1)} %collective-permute-done.9.rest_1_, f32[4,2,16,256]{3,2,1,0:T(8,128)S(1)} %collective-permute-done.10.rest_2_, ...), custom_call_target="tpu_custom_call" | custom-call | flops 2000000 | bytes 3000000 | tf_op jit(solution)/shard_map/pallas_call | solution.py:518
Async XLA Ops:
  0.0 6.7 %copy-start = (f32[100,2,32,512]{3,2,1,0:T(8,128)S(1)}, f32[100,2,32,512]{3,2,1,0:T(8,128)}, u32[]{:S(2)}) copy-start(f32[100,2,32,512]{3,2,1,0:T(8,128)} %operators.5) | copy-start | bytes 39321604
  0.0 6.7 %copy-start.1 = (f32[8,2,32,512]{3,2,1,0:T(8,128)S(1)}, f32[8,2,32,512]{3,2,1,0:T(8,128)}, u32[]{:S(2)}) copy-start(f32[8,2,32,512]{3,2,1,0:T(8,128)} %patterns.3) | copy-start | bytes 3145732
  0.0 12.8 %copy-start.2 = (bf16[512,256]{1,0:T(8,128)(2,1)S(1)}, bf16[512,256]{1,0:T(8,128)(2,1)}, u32[]{:S(2)}) copy-start(bf16[512,256]{1,0:T(8,128)(2,1)} %constant.9.clone.lo_in.phi_lo) | copy-start | bytes 786436
  0.0 12.8 %copy-start.3 = (bf16[512,256]{1,0:T(8,128)(2,1)S(1)}, bf16[512,256]{1,0:T(8,128)(2,1)}, u32[]{:S(2)}) copy-start(bf16[512,256]{1,0:T(8,128)(2,1)} %constant.8.clone.hi_in.phi_hi) | copy-start | bytes 786436
  1.3 8.2 %collective-permute-start = (f32[2,2,32,512]{3,2,1,0:T(8,128)S(1)}, f32[2,2,32,512]{3,2,1,0:T(8,128)S(1)}, u32[]{:S(2)}, u32[]{:S(2)}) collective-permute-start(f32[2,2,32,512]{3,2,1,0:T(8,128)S(1)} %get-tuple-element.31), channel_id=1, source_target_pairs={{0,8},{16,24},{8,0},{24,16},{1,9},{17,25},{9,1},{25,17},{2,10},{18... | collective-permute-start | bytes 786440 | tf_op jit(solution)/shard_map/ppermute | solution.py:387
  1.4 11.4 %collective-permute-start.1 = (f32[2,2,32,512]{3,2,1,0:T(8,128)S(1)}, f32[2,2,32,512]{3,2,1,0:T(8,128)S(1)}, u32[]{:S(2)}, u32[]{:S(2)}) collective-permute-start(f32[2,2,32,512]{3,2,1,0:T(8,128)S(1)} %get-tuple-element.32), channel_id=1, source_target_pairs={{8,16},{16,8},{9,17},{17,9},{10,18},{18,10},{11,19},{19,11},{12,20... | collective-permute-start | bytes 786440 | tf_op jit(solution)/shard_map/ppermute | solution.py:388
  9.5 23.0 %copy-start.4 = (bf16[4,64,128]{2,1,0:T(8,128)(2,1)S(1)}, bf16[4,64,128]{2,1,0:T(8,128)(2,1)}, u32[]{:S(2)}) copy-start(bf16[4,64,128]{2,1,0:T(8,128)(2,1)} %constant.11.clone.t_lo) | copy-start | bytes 196612
  9.5 23.0 %copy-start.5 = (bf16[4,64,128]{2,1,0:T(8,128)(2,1)S(1)}, bf16[4,64,128]{2,1,0:T(8,128)(2,1)}, u32[]{:S(2)}) copy-start(bf16[4,64,128]{2,1,0:T(8,128)(2,1)} %constant.10.clone.t_hi) | copy-start | bytes 196612
  14.7 17.7 %collective-permute-start.7 = (f32[3,2,32,256]{3,2,1,0:T(8,128)S(1)}, f32[3,2,32,256]{3,2,1,0:T(8,128)S(1)}, u32[]{:S(2)}, u32[]{:S(2)}) collective-permute-start(f32[3,2,32,256]{3,2,1,0:T(8,128)S(1)} %get-tuple-element.42), channel_id=1, source_target_pairs={{0,6},{1,7},{2,4},{3,5},{4,2},{5,3},{6,0},{7,1},{8,14},{9,15},{10,... | collective-permute-start | bytes 589832 | tf_op jit(solution)/shard_map/ppermute | solution.py:405
  18.4 14.1 %collective-permute-start.5 = (f32[3,2,32,256]{3,2,1,0:T(8,128)S(1)}, f32[3,2,32,256]{3,2,1,0:T(8,128)S(1)}, u32[]{:S(2)}, u32[]{:S(2)}) collective-permute-start(f32[3,2,32,256]{3,2,1,0:T(8,128)S(1)} %get-tuple-element.40), channel_id=1, source_target_pairs={{0,2},{1,3},{2,0},{3,1},{4,6},{5,7},{6,4},{7,5},{8,10},{9,11},{10,... | collective-permute-start | bytes 589832 | tf_op jit(solution)/shard_map/ppermute | solution.py:405
  19.0 13.5 %collective-permute-start.6 = (f32[3,2,32,256]{3,2,1,0:T(8,128)S(1)}, f32[3,2,32,256]{3,2,1,0:T(8,128)S(1)}, u32[]{:S(2)}, u32[]{:S(2)}) collective-permute-start(f32[3,2,32,256]{3,2,1,0:T(8,128)S(1)} %get-tuple-element.41), channel_id=1, source_target_pairs={{0,4},{1,5},{2,6},{3,7},{4,0},{5,1},{6,2},{7,3},{8,12},{9,13},{10,... | collective-permute-start | bytes 589832 | tf_op jit(solution)/shard_map/ppermute | solution.py:405
  19.5 7.8 %collective-permute-start.2 = (f32[1,2,32,256]{3,2,1,0:T(8,128)S(1)}, f32[1,2,32,256]{3,2,1,0:T(8,128)S(1)}, u32[]{:S(2)}, u32[]{:S(2)}) collective-permute-start(f32[1,2,32,256]{3,2,1,0:T(8,128)S(1)} %get-tuple-element.37), channel_id=1, source_target_pairs={{0,2},{1,3},{2,0},{3,1},{4,6},{5,7},{6,4},{7,5},{8,10},{9,11},{10,... | collective-permute-start | bytes 196616 | tf_op jit(solution)/shard_map/ppermute | solution.py:405
  21.0 8.8 %collective-permute-start.3 = (f32[1,2,32,256]{3,2,1,0:T(8,128)S(1)}, f32[1,2,32,256]{3,2,1,0:T(8,128)S(1)}, u32[]{:S(2)}, u32[]{:S(2)}) collective-permute-start(f32[1,2,32,256]{3,2,1,0:T(8,128)S(1)} %get-tuple-element.38), channel_id=1, source_target_pairs={{0,4},{1,5},{2,6},{3,7},{4,0},{5,1},{6,2},{7,3},{8,12},{9,13},{10,... | collective-permute-start | bytes 196616 | tf_op jit(solution)/shard_map/ppermute | solution.py:405
  27.3 5.2 %collective-permute-start.4 = (f32[1,2,32,256]{3,2,1,0:T(8,128)S(1)}, f32[1,2,32,256]{3,2,1,0:T(8,128)S(1)}, u32[]{:S(2)}, u32[]{:S(2)}) collective-permute-start(f32[1,2,32,256]{3,2,1,0:T(8,128)S(1)} %get-tuple-element.39), channel_id=1, source_target_pairs={{0,6},{1,7},{2,4},{3,5},{4,2},{5,3},{6,0},{7,1},{8,14},{9,15},{10,... | collective-permute-start | bytes 196616 | tf_op jit(solution)/shard_map/ppermute | solution.py:405
  33.0 2.0 %collective-permute-start.8 = (f32[4,2,64,256]{3,2,1,0:T(8,128)S(1)}, f32[4,2,64,256]{3,2,1,0:T(8,128)S(1)}, u32[]{:S(2)}, u32[]{:S(2)}) collective-permute-start(f32[4,2,64,256]{3,2,1,0:T(8,128)S(1)} %shard_map.124), channel_id=1, source_target_pairs={{0,1},{1,0},{2,3},{3,2},{4,5},{5,4},{6,7},{7,6},{8,9},{9,8},{10,11... | collective-permute-start | bytes 1572872 | tf_op jit(solution)/shard_map/ppermute | solution.py:491
  35.0 6.0 %collective-permute-start.9 = (f32[4,2,16,256]{3,2,1,0:T(8,128)S(1)}, f32[4,2,16,256]{3,2,1,0:T(8,128)S(1)}, u32[]{:S(2)}, u32[]{:S(2)}) collective-permute-start(f32[4,2,16,256]{3,2,1,0:T(8,128)S(1)} %get-tuple-element.44), channel_id=1, source_target_pairs={{0,2},{1,3},{2,0},{3,1},{4,6},{5,7},{6,4},{7,5},{8,10},{9,11},{10,... | collective-permute-start | bytes 393224 | tf_op jit(solution)/shard_map/ppermute | solution.py:405
  36.6 8.1 %collective-permute-start.10 = (f32[4,2,16,256]{3,2,1,0:T(8,128)S(1)}, f32[4,2,16,256]{3,2,1,0:T(8,128)S(1)}, u32[]{:S(2)}, u32[]{:S(2)}) collective-permute-start(f32[4,2,16,256]{3,2,1,0:T(8,128)S(1)} %get-tuple-element.45), channel_id=1, source_target_pairs={{0,4},{1,5},{2,6},{3,7},{4,0},{5,1},{6,2},{7,3},{8,12},{9,13},{10,... | collective-permute-start | bytes 393224 | tf_op jit(solution)/shard_map/ppermute | solution.py:405
  37.1 7.6 %collective-permute-start.11 = (f32[4,2,16,256]{3,2,1,0:T(8,128)S(1)}, f32[4,2,16,256]{3,2,1,0:T(8,128)S(1)}, u32[]{:S(2)}, u32[]{:S(2)}) collective-permute-start(f32[4,2,16,256]{3,2,1,0:T(8,128)S(1)} %get-tuple-element.46), channel_id=1, source_target_pairs={{0,6},{1,7},{2,4},{3,5},{4,2},{5,3},{6,0},{7,1},{8,14},{9,15},{10,... | collective-permute-start | bytes 393224 | tf_op jit(solution)/shard_map/ppermute | solution.py:405

commit v10 on v8

--- a/solution.py
+++ b/solution.py
@@ -101,7 +101,7 @@
     return copies
 
 
-def ends_kernel(patterns, operators, *rest):
+def ends_kernel(patterns, operators, again, *rest):
     *rest, first, second, sems = rest
     tables = len(rest) // 2
     width = first.shape[0]
@@ -116,25 +116,20 @@
         copy.wait()
 
 
-def halo_terms(partners, op_index, own, operators, first, second, total):
+def halo_terms(jobs, own, operators, first, second, total):
     clusters, _, rows, _ = own.shape
-    terms = partners.shape[1]
     width = first.shape[0]
-    group = lax.axis_index("group")
-    base = group * clusters
     total[...] = own[...]
 
-    def add(n, halo, shift):
-        c = n if n < width else n + clusters - 2 * width
-
-        @pl.loop(0, terms)
-        def _(p):
-            q = partners[c, p] - base
-
-            @pl.when((q < 0) | (q >= clusters))
-            def _():
-                e = op_index[c, p]
-                h = jnp.clip(q + shift, 0, width - 1)
+    @pl.loop(0, jobs[jobs.shape[0] - 1][0, 0])
+    def _(t):
+        code = jobs[t][0, 0]
+        e, h, n = code >> 16, (code >> 8) & 127, code & 255
+        c = jnp.where(n < width, n, n + clusters - 2 * width)
+        for source, halo in enumerate((first, second)):
+
+            @pl.when(((code >> 15) & 1) == source)
+            def _(halo=halo):
                 for r in range(rows // 8):
                     band = pl.ds(r * 8, 8)
                     ore, oim = operators[e, 0, band, :], operators[e, 1, band, :]
@@ -142,15 +137,26 @@
                     total[c, 0, band, :] += ore * pre - oim * pim
                     total[c, 1, band, :] += ore * pim + oim * pre
 
-    for odd, below, above in ((0, second, first), (1, first, second)):
-
-        @pl.when(group % 2 == odd)
-        def _():
-            for n in range(2 * width):
-                if n < width:
-                    add(n, below, width)
-                else:
-                    add(n, above, -clusters)
+
+def tile(ref, value):
+    return jnp.full(ref.shape[1:], value, jnp.int32)
+
+
+def list_halo_terms(partners, op_index, width, jobs):
+    clusters, terms = partners.shape
+    group = lax.axis_index("group")
+    count = jnp.int32(0)
+    for n in range(2 * width):
+        below = n < width
+        c = n if below else n + clusters - 2 * width
+        source = (1 - group % 2) if below else group % 2
+        for p in range(terms):
+            q = partners[c, p] - group * clusters
+            h = jnp.clip(q + width if below else q - clusters, 0, width - 1)
+            code = (op_index[c, p] << 16) + (source << 15) + (h << 8) + n
+            jobs[count] = tile(jobs, code)
+            count = count + jnp.where((q < 0) | (q >= clusters), 1, 0)
+    jobs[jobs.shape[0] - 1] = tile(jobs, count)
 
 
 def fill_slots(child_parent, slots, clusters, width, chips):
@@ -169,65 +175,55 @@
     return chip if i == 0 else chips + chip * (per_chip - 1) + i - 1
 
 
-def shift_and_phi(
-    order, first, slots, child_parent, child_octant, total, phase, phi_hi, phi_lo, outs, shifted
-):
-    clusters, _, rows, _ = total.shape
+def list_slots(child_parent, child_octant, slots, base, kids, child_of):
     chips = lax.axis_size("member") // CORES
+    chip = lax.axis_index("member") // CORES
     per_chip = slots.shape[0] // chips
-    base = lax.axis_index("group") * clusters
-    chip = lax.axis_index("member") // CORES
+    for s in range(chips):
+        for i in range(per_chip):
+            k = slots[slot_of(chip ^ s, i, chips, per_chip)]
+            at = s * per_chip + i
+            kids[at] = tile(kids, ((child_parent[k] - base) << 3) + child_octant[k])
+            child_of[at] = tile(child_of, k)
+
+
+def shift_and_phi(order, first, kids, total, phase, phi_hi, phi_lo, outs, shifted):
+    rows = total.shape[2]
+    per_chip = kids.shape[0] * CORES // lax.axis_size("member")
     count = outs[0].shape[0]
     size = count * 2 * rows
-    group = shifted.shape[0] // size
-    for start in range(0, len(order), group):
-        part = list(zip(order, outs))[start:start + group]
-        for m, (s, _) in enumerate(part):
-            for i in range(count):
-                k = slots[slot_of(chip ^ s, first + i, chips, per_chip)]
-                q = child_parent[k] - base
-                o = child_octant[k]
-                for r in range(rows // 8):
-                    band = pl.ds(r * 8, 8)
-                    pre, pim = total[q, 0, band, :], total[q, 1, band, :]
-                    ere, eim = phase[o, 0, band, :], phase[o, 1, band, :]
-                    at = m * size + i * 2 * rows + r * 8
-                    shifted[pl.ds(at, 8), :] = pre * ere - pim * eim
-                    shifted[pl.ds(at + rows, 8), :] = pre * eim + pim * ere
-        used = pl.ds(0, len(part) * size)
-        y = dot3(split(shifted[used, :]), (phi_hi[...], phi_lo[...]))
-        for m, (_, out) in enumerate(part):
-            out[...] = y[m * size:(m + 1) * size].reshape(out.shape)
+    for m, s in enumerate(order):
+        for i in range(count):
+            code = kids[s * per_chip + first + i][0, 0]
+            q, o = code >> 3, code & 7
+            for r in range(rows // 8):
+                band = pl.ds(r * 8, 8)
+                pre, pim = total[q, 0, band, :], total[q, 1, band, :]
+                ere, eim = phase[o, 0, band, :], phase[o, 1, band, :]
+                at = m * size + i * 2 * rows + r * 8
+                shifted[pl.ds(at, 8), :] = pre * ere - pim * eim
+                shifted[pl.ds(at + rows, 8), :] = pre * eim + pim * ere
+    y = dot3(split(shifted[...]), (phi_hi[...], phi_lo[...]))
+    for m, out in enumerate(outs):
+        out[...] = y[m * size:(m + 1) * size].reshape(out.shape)
 
 
 def first_kernel(
-    order, partners, op_index, child_parent, child_octant, own, operators, first, second, phase,
-    phi_hi, phi_lo, *rest
+    order, jobs, kids, own, operators, first, second, phase, phi_hi, phi_lo, *rest
 ):
-    *outs, total, slots, shifted = rest
-    chips = lax.axis_size("member") // CORES
-    fill_slots(child_parent, slots, own.shape[0], first.shape[0], chips)
-    halo_terms(partners, op_index, own, operators, first, second, total)
-    shift_and_phi(
-        order, 1, slots, child_parent, child_octant, total, phase, phi_hi, phi_lo, outs, shifted
-    )
-
-
-def later_kernel(
-    order, first, width, child_parent, child_octant, total, phase, phi_hi, phi_lo, *rest
-):
-    *outs, slots, shifted = rest
-    chips = lax.axis_size("member") // CORES
-    fill_slots(child_parent, slots, total.shape[0], width, chips)
-    shift_and_phi(
-        order, first, slots, child_parent, child_octant, total, phase, phi_hi, phi_lo, outs,
-        shifted,
-    )
+    *outs, total, shifted = rest
+    halo_terms(jobs, own, operators, first, second, total)
+    shift_and_phi(order, 1, kids, total, phase, phi_hi, phi_lo, outs, shifted)
+
+
+def later_kernel(order, first, kids, total, phase, phi_hi, phi_lo, *rest):
+    *outs, shifted = rest
+    shift_and_phi(order, first, kids, total, phase, phi_hi, phi_lo, outs, shifted)
 
 
 def own_kernel(
     theta_count, width, partners_in, op_in, parent_in, octant_in, patterns, operators, hi_in,
-    lo_in, out, phase, *rest
+    lo_in, out, phase, kids, child_of, jobs, *rest
 ):
     *early, partners, op_index, child_parent, child_octant, slots, shifted, phi_hi, phi_lo, sems = (
         rest
@@ -280,10 +276,9 @@
 
     chips = len(early) + 1
     fill_slots(child_parent, slots, clusters, width, chips)
-    shift_and_phi(
-        range(1, chips), 0, slots, child_parent, child_octant, out, phase, phi_hi, phi_lo,
-        early, shifted,
-    )
+    list_slots(child_parent, child_octant, slots, base, kids, child_of)
+    list_halo_terms(partners, op_index, width, jobs)
+    shift_and_phi(range(1, chips), 0, kids, out, phase, phi_hi, phi_lo, early, shifted)
 
 
 def theta_kernel(away, t_hi, t_lo, *rest):
@@ -314,13 +309,11 @@
         out[...] = keep[:, :, band, :] + arrived[:, :, band, :]
 
 
-def place_kernel(clusters, width, child_parent, *rest):
-    *blocks, out, slots, sems = rest
-    chips, per_chip = len(blocks), blocks[0].shape[0]
-    chip = lax.axis_index("member") // CORES
-    fill_slots(child_parent, slots, clusters, width, chips)
+def place_kernel(child_of, *rest):
+    *blocks, out, sems = rest
+    per_chip = blocks[0].shape[0]
     pairs = [
-        (block.at[i], out.at[slots[slot_of(chip ^ s, i, chips, per_chip)]])
+        (block.at[i], out.at[child_of[s * per_chip + i][0, 0]])
         for s, block in enumerate(blocks)
         for i in range(per_chip)
     ]
@@ -365,11 +358,11 @@
     *tables, first, second = pl.pallas_call(
         ends_kernel,
         out_shape=tuple(jax.ShapeDtypeStruct(x.shape, x.dtype) for x in tables) + (end, end),
-        in_specs=[HBM] * (2 + len(tables)),
+        in_specs=[HBM] * (3 + len(tables)),
         out_specs=(VMEM,) * (2 + len(tables)),
         scratch_shapes=[pltpu.SemaphoreType.DMA((2 + len(tables),))],
         compiler_params=params(4),
-    )(*map(in_hbm, (patterns, operators, *tables)))
+    )(*map(in_hbm, (patterns, operators, operators, *tables)))
     partners, operator_index, child_parent, child_octant = tables
     pairs = [[(i, i + 1) for i in range(start, groups - 1, 2)] for start in range(2)]
     pairs = [both + [(j, i) for i, j in both] for both in pairs]
@@ -394,11 +387,21 @@
             moved.append(lax.ppermute(blocks[s], "member", pairs))
         return moved[::-1]
 
-    own, phase, *early = call(
+    def tiles(count):
+        return jax.ShapeDtypeStruct((count, 8, 128), jnp.int32)
+
+    own, phase, kids, child_of, jobs, *early = call(
         functools.partial(own_kernel, theta_count, width),
-        out_shape=(total_shape, shape(8, 2, rows, lons)) + blocks_of(1, chips - 1),
+        out_shape=(
+            total_shape,
+            shape(8, 2, rows, lons),
+            tiles(children),
+            tiles(children),
+            tiles(2 * width * partners.shape[1] + 1),
+        )
+        + blocks_of(1, chips - 1),
         in_specs=[VMEM] * 6 + [HBM] * 2,
-        out_specs=(VMEM,) * (chips + 1),
+        out_specs=(VMEM,) * (chips + 4),
         scratch_shapes=[
             pltpu.SMEM(partners.shape, jnp.int32),
             pltpu.SMEM(partners.shape, jnp.int32),
@@ -424,27 +427,24 @@
     *outs, total = call(
         functools.partial(first_kernel, far),
         out_shape=blocks_of(count, len(far)) + (total_shape,),
-        in_specs=[SMEM] * 4 + [VMEM] * 7,
+        in_specs=[VMEM] * 9,
         out_specs=(VMEM,) * (len(far) + 1),
-        scratch_shapes=[slots, rows_of(count)],
+        scratch_shapes=[rows_of(count * len(far))],
         compiler_params=params(20),
         cost_estimate=cost(2),
-    )(
-        partners, operator_index, child_parent, child_octant, own, operators, first, second,
-        phase, *phi,
-    )
+    )(jobs, kids, own, operators, first, second, phase, *phi)
     late.update(zip(far, outs))
 
     def later(order, first_child, number):
         return call(
-            functools.partial(later_kernel, order, first_child, width),
+            functools.partial(later_kernel, order, first_child),
             out_shape=blocks_of(number, len(order)),
-            in_specs=[SMEM] * 2 + [VMEM] * 4,
+            in_specs=[VMEM] * 5,
             out_specs=(VMEM,) * len(order),
-            scratch_shapes=[slots, rows_of(number * len(order))],
+            scratch_shapes=[rows_of(number * len(order))],
             compiler_params=params(20),
             cost_estimate=cost(1),
-        )(child_parent, child_octant, total, phase, *phi)
+        )(kids, total, phase, *phi)
 
     late.update(zip(near, later(near, 1, count)))
     late = between_chips(late)
@@ -497,14 +497,14 @@
 
     final = [pieces[0], *between_chips(dict(enumerate(pieces)))]
     return call(
-        functools.partial(place_kernel, clusters, width),
+        place_kernel,
         out_shape=shape(children, 2, out_rows, NPC),
-        in_specs=[SMEM] + [VMEM] * chips,
+        in_specs=[VMEM] * (1 + chips),
         out_specs=HBM,
-        scratch_shapes=[slots, pltpu.SemaphoreType.DMA((children,))],
+        scratch_shapes=[pltpu.SemaphoreType.DMA((children,))],
         compiler_params=params(12),
         cost_estimate=cost(1),
-    )(child_parent, *final)
+    )(child_of, *final)
 
 
 def solution(mesh):

time: 46.3 us -> 45.1 us (0.974)
  Pallas kernels: 10.6 us -> 8.52 us
  waiting for transfers between devices: 18.3 us -> 19.2 us
    pallas_call x3, Pallas kernels: 3.67 us -> 1.87 us  [the longest x1 0.95 us: on_device(): call(place_kernel, out_shape=shape(children, 2, out_rows, NPC), in_specs=...]
    ppermute x9, waiting for transfers between devices: 13.6 us -> 14.8 us  [between_chips(): moved.append(lax.ppermute(blocks[s], 'member', pairs))]
    pallas_call x1, Pallas kernels: 1.9 us -> 1.31 us  [on_device(): call(functools.partial(first_kernel, far), out_shape=blocks_of(count, len...]
  transfers between devices with their start and end apart: 12 -> 12, of which waited for: 6 -> 6; matrix products, arithmetic and copies ran while one was open for 0% -> 0% of each run, Pallas kernels for 12% -> 10%
where the time goes in v10:
time: 45.1 us; the launch traced here: 45 us
  waiting for transfers between devices  19.2 us (43%)
  starting transfers between devices  17.1 us (38%)
  Pallas kernels  8.52 us (19%)
    ppermute x9, waiting for transfers between devices, between_chips(): moved.append(lax.ppermute(blocks[s], 'member', pairs))  14.8 us
    ppermute x9, starting transfers between devices, between_chips(): moved.append(lax.ppermute(blocks[s], 'member', pairs))  11.6 us
    ppermute x1, starting transfers between devices, on_device(): second = lax.ppermute(second, 'group', pairs[1])  5.3 us
    pallas_call x1, Pallas kernels, on_device(): call(functools.partial(own_kernel, theta_count, width), out_shape=(total_...  3.14 us
    ppermute x1, waiting for transfers between devices, on_device(): second = lax.ppermute(second, 'group', pairs[1])  2.94 us
    ppermute x1, waiting for transfers between devices, on_device(): swapped = lax.ppermute(away, 'member', swap)  1.44 us
    pallas_call x1, Pallas kernels, on_device(): call(functools.partial(first_kernel, far), out_shape=blocks_of(count, len...  1.31 us
    pallas_call x1, Pallas kernels, on_device(): pl.pallas_call(ends_kernel, out_shape=tuple((jax.ShapeDtypeStruct(x.shape...  1.24 us
  transfers between devices with their start and end apart: 12, of which 6 were waited for; matrix products, arithmetic and copies ran while one was open for 0% of the time, Pallas kernels for 10%

profile of v10, /device:TPU:8, one launch (start us, length us, event | category | flops | bytes accessed | tf_op | source)
XLA Modules:
  0.0 45.0 jit_solution(4553328444075452323)
XLA Ops:
  0.0 0.0 copy-start
  0.0 0.0 copy-start.3
  0.0 1.2 %shard_map.118 = (s32[8,8]{1,0:T(8,128)S(1)}, s32[8,8]{1,0:T(8,128)S(1)}, s32[16]{0:T(128)S(1)}, s32[16]{0:T(128)S(1)}, f32[2,2,32,512]{3,2,1,0:T(8,128)S(1)}, /*index=5*/f32[2,2,32,512]{3,2,1,0:T(8,128)S(1)}) custom-call(f32[8,2,32,512]{3,2,1,0:T(8,128)} %patterns.3, f32[100,2,32,512]{3,2,1,0:T(8,128)} %operators.5, f32[100,2,32,512]{3,2,1,0:T(8,128)} %operators.5, ...), custom_call_target="tpu_custom_call" | custom-call | tf_op jit(solution)/shard_map/pallas_call | solution.py:358
  1.2 0.0 copy-start.1
  1.3 0.0 copy-start.2
  1.3 0.1 collective-permute-start
  1.4 5.3 %collective-permute-start.1 = (f32[2,2,32,512]{3,2,1,0:T(8,128)S(1)}, f32[2,2,32,512]{3,2,1,0:T(8,128)S(1)}, u32[]{:S(2)}, u32[]{:S(2)}) collective-permute-start(f32[2,2,32,512]{3,2,1,0:T(8,128)S(1)} %get-tuple-element.36), channel_id=1, source_target_pairs={{8,16},{16,8},{9,17},{17,9},{10,18},{18,10},{11,19},{19,11},{12,20... | collective-permute-start | bytes 786440 | tf_op jit(solution)/shard_map/ppermute | solution.py:370
  6.7 0.0 copy-done
  6.7 0.0 copy-done.3
  6.7 3.1 %shard_map.119 = (f32[8,2,32,512]{3,2,1,0:T(8,128)S(1)}, f32[8,2,32,512]{3,2,1,0:T(8,128)S(1)}, s32[16,8,128]{2,1,0:T(8,128)S(1)}, s32[16,8,128]{2,1,0:T(8,128)S...) custom-call(s32[8,8]{1,0:T(8,128)S(1)} %get-tuple-element.27.partner, ...), custom_call_target="tpu_custom_call" | custom-call | flops 16000000 | bytes 24000000 | tf_op jit(solution)/shard_map/pallas_call | solution.py:393
  9.8 0.0 copy-start.4
  9.8 0.0 copy-start.5
  9.9 0.0 collective-permute-done.first
  9.9 2.9 %collective-permute-done.1.second = f32[2,2,32,512]{3,2,1,0:T(8,128)S(1)} collective-permute-done((f32[2,2,32,512]{3,2,1,0:T(8,128)S(1)}, f32[2,2,32,512]{3,2,1,0:T(8,128)S(1)}, u32[]{:S(2)}, u32[]{:S(2)}) %collective-permute-start.1) | collective-permute-done | bytes 262176 | tf_op jit(solution)/shard_map/ppermute | solution.py:370
  12.8 0.0 copy-done.1
  12.8 0.0 copy-done.2
  12.8 1.3 %shard_map.120 = (f32[3,2,32,256]{3,2,1,0:T(8,128)S(1)}, f32[8,2,32,512]{3,2,1,0:T(8,128)S(1)}) custom-call(s32[33,8,128]{2,1,0:T(8,128)S(1)} %get-tuple-element.33.jobs, s32[16,8,128]{2,1,0:T(8,128)S(1)} %get-tuple-element.32.kids, f32[8,2,32,512]{3,2,1,0:T(8,128)S(1)} %get-tuple-element.34.own, f32[100,2,32,512]{3,2,1,0:T(8,128)S(1)} %copy-done, ...), custom_call_target="tpu_custom_call" | custom-call | flops 4000000 | bytes 6000000 | tf_op jit(solution)/shard_map/pallas_call | solution.py:427
  14.1 2.5 %collective-permute-start.7 = (f32[3,2,32,256]{3,2,1,0:T(8,128)S(1)}, f32[3,2,32,256]{3,2,1,0:T(8,128)S(1)}, u32[]{:S(2)}, u32[]{:S(2)}) collective-permute-start(f32[3,2,32,256]{3,2,1,0:T(8,128)S(1)} %get-tuple-element.44), channel_id=1, source_target_pairs={{0,6},{1,7},{2,4},{3,5},{4,2},{5,3},{6,0},{7,1},{8,14},{9,15},{10,... | collective-permute-start | bytes 589832 | tf_op jit(solution)/shard_map/ppermute | solution.py:387
  16.6 0.5 %shard_map.122 = (f32[3,2,32,256]{3,2,1,0:T(8,128)S(1)}, f32[3,2,32,256]{3,2,1,0:T(8,128)S(1)}) custom-call(s32[16,8,128]{2,1,0:T(8,128)S(1)} %get-tuple-element.32.kids, f32[8,2,32,512]{3,2,1,0:T(8,128)S(1)} %get-tuple-element.38.total, f32[8,2,32,512]{3,2,1,0:T(8,128)S(1)} %get-tuple-element.37.phase, bf16[512,256]{1,0:T(8,128)(2,1)S(1)} %copy-done.2, ...), custom_call_target="tpu_custom_call" | custom-call | flops 2000000 | bytes 3000000 | tf_op jit(solution)/shard_map/pallas_call | solution.py:439
  17.2 0.6 %collective-permute-start.5 = (f32[3,2,32,256]{3,2,1,0:T(8,128)S(1)}, f32[3,2,32,256]{3,2,1,0:T(8,128)S(1)}, u32[]{:S(2)}, u32[]{:S(2)}) collective-permute-start(f32[3,2,32,256]{3,2,1,0:T(8,128)S(1)} %get-tuple-element.42), channel_id=1, source_target_pairs={{0,2},{1,3},{2,0},{3,1},{4,6},{5,7},{6,4},{7,5},{8,10},{9,11},{10,... | collective-permute-start | bytes 589832 | tf_op jit(solution)/shard_map/ppermute | solution.py:387
  17.8 0.5 %collective-permute-start.6 = (f32[3,2,32,256]{3,2,1,0:T(8,128)S(1)}, f32[3,2,32,256]{3,2,1,0:T(8,128)S(1)}, u32[]{:S(2)}, u32[]{:S(2)}) collective-permute-start(f32[3,2,32,256]{3,2,1,0:T(8,128)S(1)} %get-tuple-element.43), channel_id=1, source_target_pairs={{0,4},{1,5},{2,6},{3,7},{4,0},{5,1},{6,2},{7,3},{8,12},{9,13},{10,... | collective-permute-start | bytes 589832 | tf_op jit(solution)/shard_map/ppermute | solution.py:387
  18.3 1.5 %collective-permute-start.2 = (f32[1,2,32,256]{3,2,1,0:T(8,128)S(1)}, f32[1,2,32,256]{3,2,1,0:T(8,128)S(1)}, u32[]{:S(2)}, u32[]{:S(2)}) collective-permute-start(f32[1,2,32,256]{3,2,1,0:T(8,128)S(1)} %get-tuple-element.39), channel_id=1, source_target_pairs={{0,2},{1,3},{2,0},{3,1},{4,6},{5,7},{6,4},{7,5},{8,10},{9,11},{10,... | collective-permute-start | bytes 196616 | tf_op jit(solution)/shard_map/ppermute | solution.py:387
  19.8 1.5 %collective-permute-start.3 = (f32[1,2,32,256]{3,2,1,0:T(8,128)S(1)}, f32[1,2,32,256]{3,2,1,0:T(8,128)S(1)}, u32[]{:S(2)}, u32[]{:S(2)}) collective-permute-start(f32[1,2,32,256]{3,2,1,0:T(8,128)S(1)} %get-tuple-element.40), channel_id=1, source_target_pairs={{0,4},{1,5},{2,6},{3,7},{4,0},{5,1},{6,2},{7,3},{8,12},{9,13},{10,... | collective-permute-start | bytes 196616 | tf_op jit(solution)/shard_map/ppermute | solution.py:387
  21.3 5.4 %collective-permute-done.2.rest_1_ = f32[1,2,32,256]{3,2,1,0:T(8,128)S(1)} collective-permute-done((f32[1,2,32,256]{3,2,1,0:T(8,128)S(1)}, f32[1,2,32,256]{3,2,1,0:T(8,128)S(1)}, u32[]{:S(2)}, u32[]{:S(2)}) %collective-permute-start.2) | collective-permute-done | bytes 65568 | tf_op jit(solution)/shard_map/ppermute | solution.py:387
  26.7 1.4 %collective-permute-start.4 = (f32[1,2,32,256]{3,2,1,0:T(8,128)S(1)}, f32[1,2,32,256]{3,2,1,0:T(8,128)S(1)}, u32[]{:S(2)}, u32[]{:S(2)}) collective-permute-start(f32[1,2,32,256]{3,2,1,0:T(8,128)S(1)} %get-tuple-element.41), channel_id=1, source_target_pairs={{0,6},{1,7},{2,4},{3,5},{4,2},{5,3},{6,0},{7,1},{8,14},{9,15},{10,... | collective-permute-start | bytes 196616 | tf_op jit(solution)/shard_map/ppermute | solution.py:387
  28.1 0.4 shard_map.121.rest_0_
  28.5 0.0 collective-permute-done.3.rest_2_
  28.5 3.3 %collective-permute-done.4.rest_3_ = f32[1,2,32,256]{3,2,1,0:T(8,128)S(1)} collective-permute-done((f32[1,2,32,256]{3,2,1,0:T(8,128)S(1)}, f32[1,2,32,256]{3,2,1,0:T(8,128)S(1)}, u32[]{:S(2)}, u32[]{:S(2)}) %collective-permute-start.4) | collective-permute-done | bytes 65568 | tf_op jit(solution)/shard_map/ppermute | solution.py:387
  31.8 0.0 collective-permute-done.7.rest_6_
  31.9 0.0 collective-permute-done.5.rest_4_
  31.9 0.0 collective-permute-done.6.rest_5_
  31.9 0.0 copy-done.4
  31.9 0.0 copy-done.5
  31.9 0.5 %shard_map.124 = f32[4,2,64,256]{3,2,1,0:T(8,128)S(1)} custom-call(bf16[4,64,128]{2,1,0:T(8,128)(2,1)S(1)} %copy-done.5, bf16[4,64,128]{2,1,0:T(8,128)(2,1)S(1)} %copy-done.4, f32[4,2,32,256]{3,2,1,0:T(8,128)S(1)} %shard_map.121.rest_0_, f32[1,2,32,256]{3,2,1,0:T(8,128)S(1)} %collective-permute-done.2.rest_1_, ...), custom_call_target="tpu_custom_call" | custom-call | flops 2000000 | bytes 3000000 | tf_op jit(solution)/shard_map/pallas_call | solution.py:461
  32.3 0.1 collective-permute-start.8
  32.4 0.5 %shard_map.123.keep = f32[4,2,64,256]{3,2,1,0:T(8,128)S(1)} custom-call(bf16[4,64,128]{2,1,0:T(8,128)(2,1)S(1)} %copy-done.5, bf16[4,64,128]{2,1,0:T(8,128)(2,1)S(1)} %copy-done.4, f32[4,2,32,256]{3,2,1,0:T(8,128)S(1)} %shard_map.121.rest_0_, f32[1,2,32,256]{3,2,1,0:T(8,128)S(1)} %collective-permute-done.2.rest_1_, ...), custom_call_target="tpu_custom_call" | custom-call | flops 2000000 | bytes 3000000 | tf_op jit(solution)/shard_map/pallas_call | solution.py:461
  32.9 1.4 %collective-permute-done.8.arrived = f32[4,2,64,256]{3,2,1,0:T(8,128)S(1)} collective-permute-done((f32[4,2,64,256]{3,2,1,0:T(8,128)S(1)}, f32[4,2,64,256]{3,2,1,0:T(8,128)S(1)}, u32[]{:S(2)}, u32[]{:S(2)}) %collective-permute-start.8) | collective-permute-done | bytes 524320 | tf_op jit(solution)/shard_map/ppermute | solution.py:472
  34.3 0.1 shard_map.125
  34.4 1.6 %collective-permute-start.9 = (f32[4,2,16,256]{3,2,1,0:T(8,128)S(1)}, f32[4,2,16,256]{3,2,1,0:T(8,128)S(1)}, u32[]{:S(2)}, u32[]{:S(2)}) collective-permute-start(f32[4,2,16,256]{3,2,1,0:T(8,128)S(1)} %get-tuple-element.46), channel_id=1, source_target_pairs={{0,2},{1,3},{2,0},{3,1},{4,6},{5,7},{6,4},{7,5},{8,10},{9,11},{10,... | collective-permute-start | bytes 393224 | tf_op jit(solution)/shard_map/ppermute | solution.py:387
  35.9 0.5 %collective-permute-start.10 = (f32[4,2,16,256]{3,2,1,0:T(8,128)S(1)}, f32[4,2,16,256]{3,2,1,0:T(8,128)S(1)}, u32[]{:S(2)}, u32[]{:S(2)}) collective-permute-start(f32[4,2,16,256]{3,2,1,0:T(8,128)S(1)} %get-tuple-element.47), channel_id=1, source_target_pairs={{0,4},{1,5},{2,6},{3,7},{4,0},{5,1},{6,2},{7,3},{8,12},{9,13},{10,... | collective-permute-start | bytes 393224 | tf_op jit(solution)/shard_map/ppermute | solution.py:387
  36.4 1.5 %collective-permute-start.11 = (f32[4,2,16,256]{3,2,1,0:T(8,128)S(1)}, f32[4,2,16,256]{3,2,1,0:T(8,128)S(1)}, u32[]{:S(2)}, u32[]{:S(2)}) collective-permute-start(f32[4,2,16,256]{3,2,1,0:T(8,128)S(1)} %get-tuple-element.48), channel_id=1, source_target_pairs={{0,6},{1,7},{2,4},{3,5},{4,2},{5,3},{6,0},{7,1},{8,14},{9,15},{10,... | collective-permute-start | bytes 393224 | tf_op jit(solution)/shard_map/ppermute | solution.py:387
  37.9 2.5 %collective-permute-done.9.rest_1_ = f32[4,2,16,256]{3,2,1,0:T(8,128)S(1)} collective-permute-done((f32[4,2,16,256]{3,2,1,0:T(8,128)S(1)}, f32[4,2,16,256]{3,2,1,0:T(8,128)S(1)}, u32[]{:S(2)}, u32[]{:S(2)}) %collective-permute-start.9) | collective-permute-done | bytes 131104 | tf_op jit(solution)/shard_map/ppermute | solution.py:387
  40.4 3.6 %collective-permute-done.10.rest_2_ = f32[4,2,16,256]{3,2,1,0:T(8,128)S(1)} collective-permute-done((f32[4,2,16,256]{3,2,1,0:T(8,128)S(1)}, f32[4,2,16,256]{3,2,1,0:T(8,128)S(1)}, u32[]{:S(2)}, u32[]{:S(2)}) %collective-permute-start.10) | collective-permute-done | bytes 131104 | tf_op jit(solution)/shard_map/ppermute | solution.py:387
  44.0 0.0 collective-permute-done.11.rest_3_
  44.0 1.0 %shard_map.126 = f32[16,2,16,256]{3,2,1,0:T(8,128)} custom-call(s32[16,8,128]{2,1,0:T(8,128)S(1)} %get-tuple-element.31.child_of, f32[4,2,16,256]{3,2,1,0:T(8,128)S(1)} %get-tuple-element.45.rest_0_, f32[4,2,16,256]{3,2,1,0:T(8,128)S(1)} %collective-permute-done.9.rest_1_, f32[4,2,16,256]{3,2,1,0:T(8,128)S(1)} %collective-permute-done.10.rest_2_, ...), custom_call_target="tpu_custom_call" | custom-call | flops 2000000 | bytes 3000000 | tf_op jit(solution)/shard_map/pallas_call | solution.py:499
Async XLA Ops:
  0.0 6.7 %copy-start = (f32[100,2,32,512]{3,2,1,0:T(8,128)S(1)}, f32[100,2,32,512]{3,2,1,0:T(8,128)}, u32[]{:S(2)}) copy-start(f32[100,2,32,512]{3,2,1,0:T(8,128)} %operators.5) | copy-start | bytes 39321604
  0.0 6.7 %copy-start.3 = (f32[8,2,32,512]{3,2,1,0:T(8,128)S(1)}, f32[8,2,32,512]{3,2,1,0:T(8,128)}, u32[]{:S(2)}) copy-start(f32[8,2,32,512]{3,2,1,0:T(8,128)} %patterns.3) | copy-start | bytes 3145732
  1.2 11.6 %copy-start.1 = (bf16[512,256]{1,0:T(8,128)(2,1)S(1)}, bf16[512,256]{1,0:T(8,128)(2,1)}, u32[]{:S(2)}) copy-start(bf16[512,256]{1,0:T(8,128)(2,1)} %constant.9.clone.lo_in.phi_lo) | copy-start | bytes 786436
  1.3 11.5 %copy-start.2 = (bf16[512,256]{1,0:T(8,128)(2,1)S(1)}, bf16[512,256]{1,0:T(8,128)(2,1)}, u32[]{:S(2)}) copy-start(bf16[512,256]{1,0:T(8,128)(2,1)} %constant.8.clone.hi_in.phi_hi) | copy-start | bytes 786436
  1.3 8.6 %collective-permute-start = (f32[2,2,32,512]{3,2,1,0:T(8,128)S(1)}, f32[2,2,32,512]{3,2,1,0:T(8,128)S(1)}, u32[]{:S(2)}, u32[]{:S(2)}) collective-permute-start(f32[2,2,32,512]{3,2,1,0:T(8,128)S(1)} %get-tuple-element.35), channel_id=1, source_target_pairs={{0,8},{16,24},{8,0},{24,16},{1,9},{17,25},{9,1},{25,17},{2,10},{18... | collective-permute-start | bytes 786440 | tf_op jit(solution)/shard_map/ppermute | solution.py:369
  1.4 11.4 %collective-permute-start.1 = (f32[2,2,32,512]{3,2,1,0:T(8,128)S(1)}, f32[2,2,32,512]{3,2,1,0:T(8,128)S(1)}, u32[]{:S(2)}, u32[]{:S(2)}) collective-permute-start(f32[2,2,32,512]{3,2,1,0:T(8,128)S(1)} %get-tuple-element.36), channel_id=1, source_target_pairs={{8,16},{16,8},{9,17},{17,9},{10,18},{18,10},{11,19},{19,11},{12,20... | collective-permute-start | bytes 786440 | tf_op jit(solution)/shard_map/ppermute | solution.py:370
  9.8 22.0 %copy-start.4 = (bf16[4,64,128]{2,1,0:T(8,128)(2,1)S(1)}, bf16[4,64,128]{2,1,0:T(8,128)(2,1)}, u32[]{:S(2)}) copy-start(bf16[4,64,128]{2,1,0:T(8,128)(2,1)} %constant.11.clone.t_lo) | copy-start | bytes 196612
  9.8 22.0 %copy-start.5 = (bf16[4,64,128]{2,1,0:T(8,128)(2,1)S(1)}, bf16[4,64,128]{2,1,0:T(8,128)(2,1)}, u32[]{:S(2)}) copy-start(bf16[4,64,128]{2,1,0:T(8,128)(2,1)} %constant.10.clone.t_hi) | copy-start | bytes 196612
  14.1 17.7 %collective-permute-start.7 = (f32[3,2,32,256]{3,2,1,0:T(8,128)S(1)}, f32[3,2,32,256]{3,2,1,0:T(8,128)S(1)}, u32[]{:S(2)}, u32[]{:S(2)}) collective-permute-start(f32[3,2,32,256]{3,2,1,0:T(8,128)S(1)} %get-tuple-element.44), channel_id=1, source_target_pairs={{0,6},{1,7},{2,4},{3,5},{4,2},{5,3},{6,0},{7,1},{8,14},{9,15},{10,... | collective-permute-start | bytes 589832 | tf_op jit(solution)/shard_map/ppermute | solution.py:387
  17.2 14.7 %collective-permute-start.5 = (f32[3,2,32,256]{3,2,1,0:T(8,128)S(1)}, f32[3,2,32,256]{3,2,1,0:T(8,128)S(1)}, u32[]{:S(2)}, u32[]{:S(2)}) collective-permute-start(f32[3,2,32,256]{3,2,1,0:T(8,128)S(1)} %get-tuple-element.42), channel_id=1, source_target_pairs={{0,2},{1,3},{2,0},{3,1},{4,6},{5,7},{6,4},{7,5},{8,10},{9,11},{10,... | collective-permute-start | bytes 589832 | tf_op jit(solution)/shard_map/ppermute | solution.py:387
  17.8 14.1 %collective-permute-start.6 = (f32[3,2,32,256]{3,2,1,0:T(8,128)S(1)}, f32[3,2,32,256]{3,2,1,0:T(8,128)S(1)}, u32[]{:S(2)}, u32[]{:S(2)}) collective-permute-start(f32[3,2,32,256]{3,2,1,0:T(8,128)S(1)} %get-tuple-element.43), channel_id=1, source_target_pairs={{0,4},{1,5},{2,6},{3,7},{4,0},{5,1},{6,2},{7,3},{8,12},{9,13},{10,... | collective-permute-start | bytes 589832 | tf_op jit(solution)/shard_map/ppermute | solution.py:387
  18.3 8.4 %collective-permute-start.2 = (f32[1,2,32,256]{3,2,1,0:T(8,128)S(1)}, f32[1,2,32,256]{3,2,1,0:T(8,128)S(1)}, u32[]{:S(2)}, u32[]{:S(2)}) collective-permute-start(f32[1,2,32,256]{3,2,1,0:T(8,128)S(1)} %get-tuple-element.39), channel_id=1, source_target_pairs={{0,2},{1,3},{2,0},{3,1},{4,6},{5,7},{6,4},{7,5},{8,10},{9,11},{10,... | collective-permute-start | bytes 196616 | tf_op jit(solution)/shard_map/ppermute | solution.py:387
  19.8 8.8 %collective-permute-start.3 = (f32[1,2,32,256]{3,2,1,0:T(8,128)S(1)}, f32[1,2,32,256]{3,2,1,0:T(8,128)S(1)}, u32[]{:S(2)}, u32[]{:S(2)}) collective-permute-start(f32[1,2,32,256]{3,2,1,0:T(8,128)S(1)} %get-tuple-element.40), channel_id=1, source_target_pairs={{0,4},{1,5},{2,6},{3,7},{4,0},{5,1},{6,2},{7,3},{8,12},{9,13},{10,... | collective-permute-start | bytes 196616 | tf_op jit(solution)/shard_map/ppermute | solution.py:387
  26.7 5.2 %collective-permute-start.4 = (f32[1,2,32,256]{3,2,1,0:T(8,128)S(1)}, f32[1,2,32,256]{3,2,1,0:T(8,128)S(1)}, u32[]{:S(2)}, u32[]{:S(2)}) collective-permute-start(f32[1,2,32,256]{3,2,1,0:T(8,128)S(1)} %get-tuple-element.41), channel_id=1, source_target_pairs={{0,6},{1,7},{2,4},{3,5},{4,2},{5,3},{6,0},{7,1},{8,14},{9,15},{10,... | collective-permute-start | bytes 196616 | tf_op jit(solution)/shard_map/ppermute | solution.py:387
  32.3 2.0 %collective-permute-start.8 = (f32[4,2,64,256]{3,2,1,0:T(8,128)S(1)}, f32[4,2,64,256]{3,2,1,0:T(8,128)S(1)}, u32[]{:S(2)}, u32[]{:S(2)}) collective-permute-start(f32[4,2,64,256]{3,2,1,0:T(8,128)S(1)} %shard_map.124), channel_id=1, source_target_pairs={{0,1},{1,0},{2,3},{3,2},{4,5},{5,4},{6,7},{7,6},{8,9},{9,8},{10,11... | collective-permute-start | bytes 1572872 | tf_op jit(solution)/shard_map/ppermute | solution.py:472
  34.4 6.0 %collective-permute-start.9 = (f32[4,2,16,256]{3,2,1,0:T(8,128)S(1)}, f32[4,2,16,256]{3,2,1,0:T(8,128)S(1)}, u32[]{:S(2)}, u32[]{:S(2)}) collective-permute-start(f32[4,2,16,256]{3,2,1,0:T(8,128)S(1)} %get-tuple-element.46), channel_id=1, source_target_pairs={{0,2},{1,3},{2,0},{3,1},{4,6},{5,7},{6,4},{7,5},{8,10},{9,11},{10,... | collective-permute-start | bytes 393224 | tf_op jit(solution)/shard_map/ppermute | solution.py:387
  35.9 8.1 %collective-permute-start.10 = (f32[4,2,16,256]{3,2,1,0:T(8,128)S(1)}, f32[4,2,16,256]{3,2,1,0:T(8,128)S(1)}, u32[]{:S(2)}, u32[]{:S(2)}) collective-permute-start(f32[4,2,16,256]{3,2,1,0:T(8,128)S(1)} %get-tuple-element.47), channel_id=1, source_target_pairs={{0,4},{1,5},{2,6},{3,7},{4,0},{5,1},{6,2},{7,3},{8,12},{9,13},{10,... | collective-permute-start | bytes 393224 | tf_op jit(solution)/shard_map/ppermute | solution.py:387
  36.4 7.6 %collective-permute-start.11 = (f32[4,2,16,256]{3,2,1,0:T(8,128)S(1)}, f32[4,2,16,256]{3,2,1,0:T(8,128)S(1)}, u32[]{:S(2)}, u32[]{:S(2)}) collective-permute-start(f32[4,2,16,256]{3,2,1,0:T(8,128)S(1)} %get-tuple-element.48), channel_id=1, source_target_pairs={{0,6},{1,7},{2,4},{3,5},{4,2},{5,3},{6,0},{7,1},{8,14},{9,15},{10,... | collective-permute-start | bytes 393224 | tf_op jit(solution)/shard_map/ppermute | solution.py:387

commit v11 on v10

--- a/solution.py
+++ b/solution.py
@@ -61,7 +61,7 @@
     return dot(a[0], b[0]) + (dot(a[0], b[1]) + dot(a[1], b[0]))
 
 
-def phase_tables(member, theta_count, phase_ref):
+def phase_tables(member, theta_count, phase_ref, between):
     rows, lons = phase_ref.shape[2], phase_ref.shape[3]
     quarter = lons // 4
     row = lax.broadcasted_iota(jnp.int32, (rows, 2 * quarter), 0)
@@ -75,6 +75,7 @@
     c0, c1 = cos_x[:, :quarter], cos_x[:, quarter:]
     s0, s1 = sin_x[:, :quarter], sin_x[:, quarter:]
     x_parts = ((c0, s0), (c1, s1), (c0, -s0), (c1, -s1))
+    between()
     for q in range(4):
         ca, sa = x_parts[q]
         cb, sb = x_parts[(q + 3) % 4]
@@ -241,10 +242,17 @@
         ],
         sems,
     )
-    phase_tables(lax.axis_index("member"), theta_count, phase)
     base = lax.axis_index("group") * clusters
-    for copy in copies[:4]:
-        copy.wait()
+    chips = len(early) + 1
+
+    def lists():
+        for copy in copies[:4]:
+            copy.wait()
+        fill_slots(child_parent, slots, clusters, width, chips)
+        list_slots(child_parent, child_octant, slots, base, kids, child_of)
+        list_halo_terms(partners, op_index, width, jobs)
+
+    phase_tables(lax.axis_index("member"), theta_count, phase, lists)
 
     def translate(c, edge):
         for r in range(rows // 8):
@@ -274,10 +282,6 @@
     for copy in copies[4:]:
         copy.wait()
 
-    chips = len(early) + 1
-    fill_slots(child_parent, slots, clusters, width, chips)
-    list_slots(child_parent, child_octant, slots, base, kids, child_of)
-    list_halo_terms(partners, op_index, width, jobs)
     shift_and_phi(range(1, chips), 0, kids, out, phase, phi_hi, phi_lo, early, shifted)
 
 

time: 45.1 us -> 45.1 us (level)
  no operation moved by 1% of the time
where the time goes in v11:
time: 45.1 us; the launch traced here: 45 us
  waiting for transfers between devices  19 us (42%)
  starting transfers between devices  17.1 us (38%)
  Pallas kernels  8.64 us (19%)
    ppermute x9, waiting for transfers between devices, between_chips(): moved.append(lax.ppermute(blocks[s], 'member', pairs))  14.8 us
    ppermute x9, starting transfers between devices, between_chips(): moved.append(lax.ppermute(blocks[s], 'member', pairs))  11.6 us
    ppermute x1, starting transfers between devices, on_device(): second = lax.ppermute(second, 'group', pairs[1])  5.3 us
    pallas_call x1, Pallas kernels, on_device(): call(functools.partial(own_kernel, theta_count, width), out_shape=(total_...  3.26 us
    ppermute x1, waiting for transfers between devices, on_device(): second = lax.ppermute(second, 'group', pairs[1])  2.81 us
    ppermute x1, waiting for transfers between devices, on_device(): swapped = lax.ppermute(away, 'member', swap)  1.44 us
    pallas_call x1, Pallas kernels, on_device(): call(functools.partial(first_kernel, far), out_shape=blocks_of(count, len...  1.31 us
    pallas_call x1, Pallas kernels, on_device(): pl.pallas_call(ends_kernel, out_shape=tuple((jax.ShapeDtypeStruct(x.shape...  1.24 us
  transfers between devices with their start and end apart: 12, of which 6 were waited for; matrix products, arithmetic and copies ran while one was open for 0% of the time, Pallas kernels for 10%

profile of v11, /device:TPU:8, one launch (start us, length us, event | category | flops | bytes accessed | tf_op | source)
XLA Modules:
  0.0 45.0 jit_solution(14254745674047494171)
XLA Ops:
  0.0 0.0 copy-start
  0.0 0.0 copy-start.3
  0.0 1.2 %shard_map.118 = (s32[8,8]{1,0:T(8,128)S(1)}, s32[8,8]{1,0:T(8,128)S(1)}, s32[16]{0:T(128)S(1)}, s32[16]{0:T(128)S(1)}, f32[2,2,32,512]{3,2,1,0:T(8,128)S(1)}, /*index=5*/f32[2,2,32,512]{3,2,1,0:T(8,128)S(1)}) custom-call(f32[8,2,32,512]{3,2,1,0:T(8,128)} %patterns.3, f32[100,2,32,512]{3,2,1,0:T(8,128)} %operators.5, f32[100,2,32,512]{3,2,1,0:T(8,128)} %operators.5, ...), custom_call_target="tpu_custom_call" | custom-call | tf_op jit(solution)/shard_map/pallas_call | solution.py:362
  1.2 0.0 copy-start.1
  1.3 0.0 copy-start.2
  1.3 0.1 collective-permute-start
  1.4 5.3 %collective-permute-start.1 = (f32[2,2,32,512]{3,2,1,0:T(8,128)S(1)}, f32[2,2,32,512]{3,2,1,0:T(8,128)S(1)}, u32[]{:S(2)}, u32[]{:S(2)}) collective-permute-start(f32[2,2,32,512]{3,2,1,0:T(8,128)S(1)} %get-tuple-element.36), channel_id=1, source_target_pairs={{8,16},{16,8},{9,17},{17,9},{10,18},{18,10},{11,19},{19,11},{12,20... | collective-permute-start | bytes 786440 | tf_op jit(solution)/shard_map/ppermute | solution.py:374
  6.7 0.0 copy-done
  6.7 0.0 copy-done.3
  6.7 3.3 %shard_map.119 = (f32[8,2,32,512]{3,2,1,0:T(8,128)S(1)}, f32[8,2,32,512]{3,2,1,0:T(8,128)S(1)}, s32[16,8,128]{2,1,0:T(8,128)S(1)}, s32[16,8,128]{2,1,0:T(8,128)S...) custom-call(s32[8,8]{1,0:T(8,128)S(1)} %get-tuple-element.27.partner, ...), custom_call_target="tpu_custom_call" | custom-call | flops 16000000 | bytes 24000000 | tf_op jit(solution)/shard_map/pallas_call | solution.py:397
  10.0 0.0 copy-start.4
  10.0 0.0 copy-start.5
  10.0 0.0 collective-permute-done.first
  10.0 2.8 %collective-permute-done.1.second = f32[2,2,32,512]{3,2,1,0:T(8,128)S(1)} collective-permute-done((f32[2,2,32,512]{3,2,1,0:T(8,128)S(1)}, f32[2,2,32,512]{3,2,1,0:T(8,128)S(1)}, u32[]{:S(2)}, u32[]{:S(2)}) %collective-permute-start.1) | collective-permute-done | bytes 262176 | tf_op jit(solution)/shard_map/ppermute | solution.py:374
  12.8 0.0 copy-done.1
  12.8 0.0 copy-done.2
  12.8 1.3 %shard_map.120 = (f32[3,2,32,256]{3,2,1,0:T(8,128)S(1)}, f32[8,2,32,512]{3,2,1,0:T(8,128)S(1)}) custom-call(s32[33,8,128]{2,1,0:T(8,128)S(1)} %get-tuple-element.33.jobs, s32[16,8,128]{2,1,0:T(8,128)S(1)} %get-tuple-element.32.kids, f32[8,2,32,512]{3,2,1,0:T(8,128)S(1)} %get-tuple-element.34.own, f32[100,2,32,512]{3,2,1,0:T(8,128)S(1)} %copy-done, ...), custom_call_target="tpu_custom_call" | custom-call | flops 4000000 | bytes 6000000 | tf_op jit(solution)/shard_map/pallas_call | solution.py:431
  14.1 2.5 %collective-permute-start.7 = (f32[3,2,32,256]{3,2,1,0:T(8,128)S(1)}, f32[3,2,32,256]{3,2,1,0:T(8,128)S(1)}, u32[]{:S(2)}, u32[]{:S(2)}) collective-permute-start(f32[3,2,32,256]{3,2,1,0:T(8,128)S(1)} %get-tuple-element.44), channel_id=1, source_target_pairs={{0,6},{1,7},{2,4},{3,5},{4,2},{5,3},{6,0},{7,1},{8,14},{9,15},{10,... | collective-permute-start | bytes 589832 | tf_op jit(solution)/shard_map/ppermute | solution.py:391
  16.6 0.5 %shard_map.122 = (f32[3,2,32,256]{3,2,1,0:T(8,128)S(1)}, f32[3,2,32,256]{3,2,1,0:T(8,128)S(1)}) custom-call(s32[16,8,128]{2,1,0:T(8,128)S(1)} %get-tuple-element.32.kids, f32[8,2,32,512]{3,2,1,0:T(8,128)S(1)} %get-tuple-element.38.total, f32[8,2,32,512]{3,2,1,0:T(8,128)S(1)} %get-tuple-element.37.phase, bf16[512,256]{1,0:T(8,128)(2,1)S(1)} %copy-done.2, ...), custom_call_target="tpu_custom_call" | custom-call | flops 2000000 | bytes 3000000 | tf_op jit(solution)/shard_map/pallas_call | solution.py:443
  17.2 0.6 %collective-permute-start.5 = (f32[3,2,32,256]{3,2,1,0:T(8,128)S(1)}, f32[3,2,32,256]{3,2,1,0:T(8,128)S(1)}, u32[]{:S(2)}, u32[]{:S(2)}) collective-permute-start(f32[3,2,32,256]{3,2,1,0:T(8,128)S(1)} %get-tuple-element.42), channel_id=1, source_target_pairs={{0,2},{1,3},{2,0},{3,1},{4,6},{5,7},{6,4},{7,5},{8,10},{9,11},{10,... | collective-permute-start | bytes 589832 | tf_op jit(solution)/shard_map/ppermute | solution.py:391
  17.8 0.5 %collective-permute-start.6 = (f32[3,2,32,256]{3,2,1,0:T(8,128)S(1)}, f32[3,2,32,256]{3,2,1,0:T(8,128)S(1)}, u32[]{:S(2)}, u32[]{:S(2)}) collective-permute-start(f32[3,2,32,256]{3,2,1,0:T(8,128)S(1)} %get-tuple-element.43), channel_id=1, source_target_pairs={{0,4},{1,5},{2,6},{3,7},{4,0},{5,1},{6,2},{7,3},{8,12},{9,13},{10,... | collective-permute-start | bytes 589832 | tf_op jit(solution)/shard_map/ppermute | solution.py:391
  18.3 1.5 %collective-permute-start.2 = (f32[1,2,32,256]{3,2,1,0:T(8,128)S(1)}, f32[1,2,32,256]{3,2,1,0:T(8,128)S(1)}, u32[]{:S(2)}, u32[]{:S(2)}) collective-permute-start(f32[1,2,32,256]{3,2,1,0:T(8,128)S(1)} %get-tuple-element.39), channel_id=1, source_target_pairs={{0,2},{1,3},{2,0},{3,1},{4,6},{5,7},{6,4},{7,5},{8,10},{9,11},{10,... | collective-permute-start | bytes 196616 | tf_op jit(solution)/shard_map/ppermute | solution.py:391
  19.8 1.5 %collective-permute-start.3 = (f32[1,2,32,256]{3,2,1,0:T(8,128)S(1)}, f32[1,2,32,256]{3,2,1,0:T(8,128)S(1)}, u32[]{:S(2)}, u32[]{:S(2)}) collective-permute-start(f32[1,2,32,256]{3,2,1,0:T(8,128)S(1)} %get-tuple-element.40), channel_id=1, source_target_pairs={{0,4},{1,5},{2,6},{3,7},{4,0},{5,1},{6,2},{7,3},{8,12},{9,13},{10,... | collective-permute-start | bytes 196616 | tf_op jit(solution)/shard_map/ppermute | solution.py:391
  21.3 5.4 %collective-permute-done.2.rest_1_ = f32[1,2,32,256]{3,2,1,0:T(8,128)S(1)} collective-permute-done((f32[1,2,32,256]{3,2,1,0:T(8,128)S(1)}, f32[1,2,32,256]{3,2,1,0:T(8,128)S(1)}, u32[]{:S(2)}, u32[]{:S(2)}) %collective-permute-start.2) | collective-permute-done | bytes 65568 | tf_op jit(solution)/shard_map/ppermute | solution.py:391
  26.7 1.4 %collective-permute-start.4 = (f32[1,2,32,256]{3,2,1,0:T(8,128)S(1)}, f32[1,2,32,256]{3,2,1,0:T(8,128)S(1)}, u32[]{:S(2)}, u32[]{:S(2)}) collective-permute-start(f32[1,2,32,256]{3,2,1,0:T(8,128)S(1)} %get-tuple-element.41), channel_id=1, source_target_pairs={{0,6},{1,7},{2,4},{3,5},{4,2},{5,3},{6,0},{7,1},{8,14},{9,15},{10,... | collective-permute-start | bytes 196616 | tf_op jit(solution)/shard_map/ppermute | solution.py:391
  28.1 0.4 shard_map.121.rest_0_
  28.5 0.0 collective-permute-done.3.rest_2_
  28.5 3.3 %collective-permute-done.4.rest_3_ = f32[1,2,32,256]{3,2,1,0:T(8,128)S(1)} collective-permute-done((f32[1,2,32,256]{3,2,1,0:T(8,128)S(1)}, f32[1,2,32,256]{3,2,1,0:T(8,128)S(1)}, u32[]{:S(2)}, u32[]{:S(2)}) %collective-permute-start.4) | collective-permute-done | bytes 65568 | tf_op jit(solution)/shard_map/ppermute | solution.py:391
  31.8 0.0 collective-permute-done.7.rest_6_
  31.9 0.0 collective-permute-done.5.rest_4_
  31.9 0.0 collective-permute-done.6.rest_5_
  31.9 0.0 copy-done.4
  31.9 0.0 copy-done.5
  31.9 0.5 %shard_map.124 = f32[4,2,64,256]{3,2,1,0:T(8,128)S(1)} custom-call(bf16[4,64,128]{2,1,0:T(8,128)(2,1)S(1)} %copy-done.5, bf16[4,64,128]{2,1,0:T(8,128)(2,1)S(1)} %copy-done.4, f32[4,2,32,256]{3,2,1,0:T(8,128)S(1)} %shard_map.121.rest_0_, f32[1,2,32,256]{3,2,1,0:T(8,128)S(1)} %collective-permute-done.2.rest_1_, ...), custom_call_target="tpu_custom_call" | custom-call | flops 2000000 | bytes 3000000 | tf_op jit(solution)/shard_map/pallas_call | solution.py:465
  32.3 0.1 collective-permute-start.8
  32.4 0.5 %shard_map.123.keep = f32[4,2,64,256]{3,2,1,0:T(8,128)S(1)} custom-call(bf16[4,64,128]{2,1,0:T(8,128)(2,1)S(1)} %copy-done.5, bf16[4,64,128]{2,1,0:T(8,128)(2,1)S(1)} %copy-done.4, f32[4,2,32,256]{3,2,1,0:T(8,128)S(1)} %shard_map.121.rest_0_, f32[1,2,32,256]{3,2,1,0:T(8,128)S(1)} %collective-permute-done.2.rest_1_, ...), custom_call_target="tpu_custom_call" | custom-call | flops 2000000 | bytes 3000000 | tf_op jit(solution)/shard_map/pallas_call | solution.py:465
  32.9 1.4 %collective-permute-done.8.arrived = f32[4,2,64,256]{3,2,1,0:T(8,128)S(1)} collective-permute-done((f32[4,2,64,256]{3,2,1,0:T(8,128)S(1)}, f32[4,2,64,256]{3,2,1,0:T(8,128)S(1)}, u32[]{:S(2)}, u32[]{:S(2)}) %collective-permute-start.8) | collective-permute-done | bytes 524320 | tf_op jit(solution)/shard_map/ppermute | solution.py:476
  34.3 0.1 shard_map.125
  34.4 1.6 %collective-permute-start.9 = (f32[4,2,16,256]{3,2,1,0:T(8,128)S(1)}, f32[4,2,16,256]{3,2,1,0:T(8,128)S(1)}, u32[]{:S(2)}, u32[]{:S(2)}) collective-permute-start(f32[4,2,16,256]{3,2,1,0:T(8,128)S(1)} %get-tuple-element.46), channel_id=1, source_target_pairs={{0,2},{1,3},{2,0},{3,1},{4,6},{5,7},{6,4},{7,5},{8,10},{9,11},{10,... | collective-permute-start | bytes 393224 | tf_op jit(solution)/shard_map/ppermute | solution.py:391
  35.9 0.5 %collective-permute-start.10 = (f32[4,2,16,256]{3,2,1,0:T(8,128)S(1)}, f32[4,2,16,256]{3,2,1,0:T(8,128)S(1)}, u32[]{:S(2)}, u32[]{:S(2)}) collective-permute-start(f32[4,2,16,256]{3,2,1,0:T(8,128)S(1)} %get-tuple-element.47), channel_id=1, source_target_pairs={{0,4},{1,5},{2,6},{3,7},{4,0},{5,1},{6,2},{7,3},{8,12},{9,13},{10,... | collective-permute-start | bytes 393224 | tf_op jit(solution)/shard_map/ppermute | solution.py:391
  36.4 1.5 %collective-permute-start.11 = (f32[4,2,16,256]{3,2,1,0:T(8,128)S(1)}, f32[4,2,16,256]{3,2,1,0:T(8,128)S(1)}, u32[]{:S(2)}, u32[]{:S(2)}) collective-permute-start(f32[4,2,16,256]{3,2,1,0:T(8,128)S(1)} %get-tuple-element.48), channel_id=1, source_target_pairs={{0,6},{1,7},{2,4},{3,5},{4,2},{5,3},{6,0},{7,1},{8,14},{9,15},{10,... | collective-permute-start | bytes 393224 | tf_op jit(solution)/shard_map/ppermute | solution.py:391
  37.9 2.5 %collective-permute-done.9.rest_1_ = f32[4,2,16,256]{3,2,1,0:T(8,128)S(1)} collective-permute-done((f32[4,2,16,256]{3,2,1,0:T(8,128)S(1)}, f32[4,2,16,256]{3,2,1,0:T(8,128)S(1)}, u32[]{:S(2)}, u32[]{:S(2)}) %collective-permute-start.9) | collective-permute-done | bytes 131104 | tf_op jit(solution)/shard_map/ppermute | solution.py:391
  40.4 3.6 %collective-permute-done.10.rest_2_ = f32[4,2,16,256]{3,2,1,0:T(8,128)S(1)} collective-permute-done((f32[4,2,16,256]{3,2,1,0:T(8,128)S(1)}, f32[4,2,16,256]{3,2,1,0:T(8,128)S(1)}, u32[]{:S(2)}, u32[]{:S(2)}) %collective-permute-start.10) | collective-permute-done | bytes 131104 | tf_op jit(solution)/shard_map/ppermute | solution.py:391
  44.0 0.0 collective-permute-done.11.rest_3_
  44.0 1.0 %shard_map.126 = f32[16,2,16,256]{3,2,1,0:T(8,128)} custom-call(s32[16,8,128]{2,1,0:T(8,128)S(1)} %get-tuple-element.31.child_of, f32[4,2,16,256]{3,2,1,0:T(8,128)S(1)} %get-tuple-element.45.rest_0_, f32[4,2,16,256]{3,2,1,0:T(8,128)S(1)} %collective-permute-done.9.rest_1_, f32[4,2,16,256]{3,2,1,0:T(8,128)S(1)} %collective-permute-done.10.rest_2_, ...), custom_call_target="tpu_custom_call" | custom-call | flops 2000000 | bytes 3000000 | tf_op jit(solution)/shard_map/pallas_call | solution.py:503
Async XLA Ops:
  0.0 6.7 %copy-start = (f32[100,2,32,512]{3,2,1,0:T(8,128)S(1)}, f32[100,2,32,512]{3,2,1,0:T(8,128)}, u32[]{:S(2)}) copy-start(f32[100,2,32,512]{3,2,1,0:T(8,128)} %operators.5) | copy-start | bytes 39321604
  0.0 6.7 %copy-start.3 = (f32[8,2,32,512]{3,2,1,0:T(8,128)S(1)}, f32[8,2,32,512]{3,2,1,0:T(8,128)}, u32[]{:S(2)}) copy-start(f32[8,2,32,512]{3,2,1,0:T(8,128)} %patterns.3) | copy-start | bytes 3145732
  1.2 11.6 %copy-start.1 = (bf16[512,256]{1,0:T(8,128)(2,1)S(1)}, bf16[512,256]{1,0:T(8,128)(2,1)}, u32[]{:S(2)}) copy-start(bf16[512,256]{1,0:T(8,128)(2,1)} %constant.9.clone.lo_in.phi_lo) | copy-start | bytes 786436
  1.3 11.5 %copy-start.2 = (bf16[512,256]{1,0:T(8,128)(2,1)S(1)}, bf16[512,256]{1,0:T(8,128)(2,1)}, u32[]{:S(2)}) copy-start(bf16[512,256]{1,0:T(8,128)(2,1)} %constant.8.clone.hi_in.phi_hi) | copy-start | bytes 786436
  1.3 8.7 %collective-permute-start = (f32[2,2,32,512]{3,2,1,0:T(8,128)S(1)}, f32[2,2,32,512]{3,2,1,0:T(8,128)S(1)}, u32[]{:S(2)}, u32[]{:S(2)}) collective-permute-start(f32[2,2,32,512]{3,2,1,0:T(8,128)S(1)} %get-tuple-element.35), channel_id=1, source_target_pairs={{0,8},{16,24},{8,0},{24,16},{1,9},{17,25},{9,1},{25,17},{2,10},{18... | collective-permute-start | bytes 786440 | tf_op jit(solution)/shard_map/ppermute | solution.py:373
  1.4 11.4 %collective-permute-start.1 = (f32[2,2,32,512]{3,2,1,0:T(8,128)S(1)}, f32[2,2,32,512]{3,2,1,0:T(8,128)S(1)}, u32[]{:S(2)}, u32[]{:S(2)}) collective-permute-start(f32[2,2,32,512]{3,2,1,0:T(8,128)S(1)} %get-tuple-element.36), channel_id=1, source_target_pairs={{8,16},{16,8},{9,17},{17,9},{10,18},{18,10},{11,19},{19,11},{12,20... | collective-permute-start | bytes 786440 | tf_op jit(solution)/shard_map/ppermute | solution.py:374
  10.0 21.9 %copy-start.4 = (bf16[4,64,128]{2,1,0:T(8,128)(2,1)S(1)}, bf16[4,64,128]{2,1,0:T(8,128)(2,1)}, u32[]{:S(2)}) copy-start(bf16[4,64,128]{2,1,0:T(8,128)(2,1)} %constant.11.clone.t_lo) | copy-start | bytes 196612
  10.0 21.9 %copy-start.5 = (bf16[4,64,128]{2,1,0:T(8,128)(2,1)S(1)}, bf16[4,64,128]{2,1,0:T(8,128)(2,1)}, u32[]{:S(2)}) copy-start(bf16[4,64,128]{2,1,0:T(8,128)(2,1)} %constant.10.clone.t_hi) | copy-start | bytes 196612
  14.1 17.7 %collective-permute-start.7 = (f32[3,2,32,256]{3,2,1,0:T(8,128)S(1)}, f32[3,2,32,256]{3,2,1,0:T(8,128)S(1)}, u32[]{:S(2)}, u32[]{:S(2)}) collective-permute-start(f32[3,2,32,256]{3,2,1,0:T(8,128)S(1)} %get-tuple-element.44), channel_id=1, source_target_pairs={{0,6},{1,7},{2,4},{3,5},{4,2},{5,3},{6,0},{7,1},{8,14},{9,15},{10,... | collective-permute-start | bytes 589832 | tf_op jit(solution)/shard_map/ppermute | solution.py:391
  17.2 14.7 %collective-permute-start.5 = (f32[3,2,32,256]{3,2,1,0:T(8,128)S(1)}, f32[3,2,32,256]{3,2,1,0:T(8,128)S(1)}, u32[]{:S(2)}, u32[]{:S(2)}) collective-permute-start(f32[3,2,32,256]{3,2,1,0:T(8,128)S(1)} %get-tuple-element.42), channel_id=1, source_target_pairs={{0,2},{1,3},{2,0},{3,1},{4,6},{5,7},{6,4},{7,5},{8,10},{9,11},{10,... | collective-permute-start | bytes 589832 | tf_op jit(solution)/shard_map/ppermute | solution.py:391
  17.8 14.1 %collective-permute-start.6 = (f32[3,2,32,256]{3,2,1,0:T(8,128)S(1)}, f32[3,2,32,256]{3,2,1,0:T(8,128)S(1)}, u32[]{:S(2)}, u32[]{:S(2)}) collective-permute-start(f32[3,2,32,256]{3,2,1,0:T(8,128)S(1)} %get-tuple-element.43), channel_id=1, source_target_pairs={{0,4},{1,5},{2,6},{3,7},{4,0},{5,1},{6,2},{7,3},{8,12},{9,13},{10,... | collective-permute-start | bytes 589832 | tf_op jit(solution)/shard_map/ppermute | solution.py:391
  18.3 8.4 %collective-permute-start.2 = (f32[1,2,32,256]{3,2,1,0:T(8,128)S(1)}, f32[1,2,32,256]{3,2,1,0:T(8,128)S(1)}, u32[]{:S(2)}, u32[]{:S(2)}) collective-permute-start(f32[1,2,32,256]{3,2,1,0:T(8,128)S(1)} %get-tuple-element.39), channel_id=1, source_target_pairs={{0,2},{1,3},{2,0},{3,1},{4,6},{5,7},{6,4},{7,5},{8,10},{9,11},{10,... | collective-permute-start | bytes 196616 | tf_op jit(solution)/shard_map/ppermute | solution.py:391
  19.8 8.8 %collective-permute-start.3 = (f32[1,2,32,256]{3,2,1,0:T(8,128)S(1)}, f32[1,2,32,256]{3,2,1,0:T(8,128)S(1)}, u32[]{:S(2)}, u32[]{:S(2)}) collective-permute-start(f32[1,2,32,256]{3,2,1,0:T(8,128)S(1)} %get-tuple-element.40), channel_id=1, source_target_pairs={{0,4},{1,5},{2,6},{3,7},{4,0},{5,1},{6,2},{7,3},{8,12},{9,13},{10,... | collective-permute-start | bytes 196616 | tf_op jit(solution)/shard_map/ppermute | solution.py:391
  26.7 5.2 %collective-permute-start.4 = (f32[1,2,32,256]{3,2,1,0:T(8,128)S(1)}, f32[1,2,32,256]{3,2,1,0:T(8,128)S(1)}, u32[]{:S(2)}, u32[]{:S(2)}) collective-permute-start(f32[1,2,32,256]{3,2,1,0:T(8,128)S(1)} %get-tuple-element.41), channel_id=1, source_target_pairs={{0,6},{1,7},{2,4},{3,5},{4,2},{5,3},{6,0},{7,1},{8,14},{9,15},{10,... | collective-permute-start | bytes 196616 | tf_op jit(solution)/shard_map/ppermute | solution.py:391
  32.3 2.0 %collective-permute-start.8 = (f32[4,2,64,256]{3,2,1,0:T(8,128)S(1)}, f32[4,2,64,256]{3,2,1,0:T(8,128)S(1)}, u32[]{:S(2)}, u32[]{:S(2)}) collective-permute-start(f32[4,2,64,256]{3,2,1,0:T(8,128)S(1)} %shard_map.124), channel_id=1, source_target_pairs={{0,1},{1,0},{2,3},{3,2},{4,5},{5,4},{6,7},{7,6},{8,9},{9,8},{10,11... | collective-permute-start | bytes 1572872 | tf_op jit(solution)/shard_map/ppermute | solution.py:476
  34.4 6.0 %collective-permute-start.9 = (f32[4,2,16,256]{3,2,1,0:T(8,128)S(1)}, f32[4,2,16,256]{3,2,1,0:T(8,128)S(1)}, u32[]{:S(2)}, u32[]{:S(2)}) collective-permute-start(f32[4,2,16,256]{3,2,1,0:T(8,128)S(1)} %get-tuple-element.46), channel_id=1, source_target_pairs={{0,2},{1,3},{2,0},{3,1},{4,6},{5,7},{6,4},{7,5},{8,10},{9,11},{10,... | collective-permute-start | bytes 393224 | tf_op jit(solution)/shard_map/ppermute | solution.py:391
  35.9 8.1 %collective-permute-start.10 = (f32[4,2,16,256]{3,2,1,0:T(8,128)S(1)}, f32[4,2,16,256]{3,2,1,0:T(8,128)S(1)}, u32[]{:S(2)}, u32[]{:S(2)}) collective-permute-start(f32[4,2,16,256]{3,2,1,0:T(8,128)S(1)} %get-tuple-element.47), channel_id=1, source_target_pairs={{0,4},{1,5},{2,6},{3,7},{4,0},{5,1},{6,2},{7,3},{8,12},{9,13},{10,... | collective-permute-start | bytes 393224 | tf_op jit(solution)/shard_map/ppermute | solution.py:391
  36.4 7.6 %collective-permute-start.11 = (f32[4,2,16,256]{3,2,1,0:T(8,128)S(1)}, f32[4,2,16,256]{3,2,1,0:T(8,128)S(1)}, u32[]{:S(2)}, u32[]{:S(2)}) collective-permute-start(f32[4,2,16,256]{3,2,1,0:T(8,128)S(1)} %get-tuple-element.48), channel_id=1, source_target_pairs={{0,6},{1,7},{2,4},{3,5},{4,2},{5,3},{6,0},{7,1},{8,14},{9,15},{10,... | collective-permute-start | bytes 393224 | tf_op jit(solution)/shard_map/ppermute | solution.py:391
